TPU v7x, 32 devices: a whole 2x2x4 slice. The times are simulated.
32 devices in a mesh: seq: 4 (over y, core), wide: 8 (over z, x).
Axes of the slice: x: 2, y: 2, z: 4, core: 2. Of those that a mesh axis runs over, the one named last changes fastest.
Arguments:
- block_input: bfloat16 [16, 1024, 1024], P('wide', 'seq'), may hold values from -6 to 6
- segment_ids: int32 [16, 1024], P('wide'), may hold values from 0 to 3, never falling along the last dimension, each value on 1 to 512 neighbouring positions
- assignment: int32 [16, 1024], P('wide', 'seq'), may hold values from 0 to 7, as said below
- norm_attn: bfloat16 [1024], P(('seq', 'wide')), may hold values from 0.5 to 1.5
- weight_qkv: bfloat16 [1024, 3072], P(('seq', 'wide')), may hold values from -0.1875 to 0.1875
- weight_proj: bfloat16 [1024, 1024], P(('seq', 'wide')), may hold values from -1.5 to 1.5
- norm_ffn: bfloat16 [1024], P(('seq', 'wide')), may hold values from 0.5 to 1.5
- weight_up: bfloat16 [1024, 4096], P(('seq', 'wide')), may hold values from -0.1875 to 0.1875
- weight_down: bfloat16 [4096, 1024], P(('seq', 'wide')), may hold values from -0.09375 to 0.09375
- centroids: bfloat16 [8, 1024], P('wide'), may hold values from -0.09375 to 0.09375
- expert_norms: bfloat16 [8, 2, 1024], P('wide'), may hold values from 0.5 to 1.5
- expert_in: bfloat16 [8, 2, 1024, 4096], P('wide', None, None, 'seq'), may hold values from -0.1875 to 0.1875
- expert_out: bfloat16 [8, 2, 4096, 1024], P('wide', None, 'seq'), may hold values from -0.09375 to 0.09375
- grad_out: bfloat16 [16, 1024, 1024], P('wide', 'seq'), may hold values from -6 to 6
Outputs:
- output: bfloat16 [16, 1024, 1024], P('wide', 'seq')
- grad_input: float32 [16, 1024, 1024], P('wide', 'seq')
- grad_norm_attn: float32 [1024], P(('seq', 'wide'))
- grad_weight_qkv: float32 [1024, 3072], P(('seq', 'wide'))
- grad_weight_proj: float32 [1024, 1024], P(('seq', 'wide'))
- grad_norm_ffn: float32 [1024], P(('seq', 'wide'))
- grad_weight_up: float32 [1024, 4096], P(('seq', 'wide'))
- grad_weight_down: float32 [4096, 1024], P(('seq', 'wide'))
- grad_centroids: float32 [8, 1024], P('wide')
- grad_expert_norms: float32 [8, 2, 1024], P('wide')
- grad_expert_in: float32 [8, 2, 1024, 4096], P('wide', None, None, 'seq')
- grad_expert_out: float32 [8, 2, 4096, 1024], P('wide', None, 'seq')
- log_gate: float32 [8], P('wide')
- log_score: float32 [8], P('wide')
Inputs may be any that keep to these rules, and one draw needn't show every extreme that they name: `assignment`: in the block of one device (the 2 rows of one index of wide at the 256 positions of one index of seq) every expert is named by exactly 64 tokens.
All inputs are finite; a program needn't handle non-finite values.
Results may differ from a plain program's by a relative error of at most 0.017.
Values may be sent and summed in bfloat16 or wider, within the bound.
A program may use at most 320 MiB of HBM per device.

v0:
```python
import math

import jax
import jax.numpy as jnp
from jax import lax
from jax.sharding import PartitionSpec as P

HEADS = 16
HEAD_DIM = 64


epsilon = 1e-05
highest = lax.Precision.HIGHEST


def layer_norm(values, norm_gain):
    centered = values - jnp.mean(values, axis=-1, keepdims=True)
    variance = jnp.mean(centered * centered, axis=-1, keepdims=True)
    return centered * lax.rsqrt(variance + epsilon) * norm_gain


def gelu_exact(values):
    return jax.nn.gelu(values, approximate=False)


def product(left_side, right_side):
    return jnp.dot(left_side, right_side, preferred_element_type=jnp.float32)


def norm_back(values, norm_gain, grad_normed):
    _, pull_back = jax.vjp(layer_norm, values, norm_gain)
    return pull_back(grad_normed)


def gelu_back(pre_values, grad_active):
    _, pull_back = jax.vjp(gelu_exact, pre_values)
    return pull_back(grad_active)[0]


def split_groups(row_block, group_size, head_dim):
    row_count, length, model_width = row_block.shape
    groups = model_width // (group_size * head_dim)
    return row_block.reshape(row_count, length, groups, group_size, head_dim).transpose(
        2, 0, 1, 3, 4
    )


def merge_groups(row_block):
    groups, row_count, length, group_size, head_dim = row_block.shape
    return row_block.transpose(1, 2, 0, 3, 4).reshape(
        row_count, length, groups * group_size * head_dim
    )


def per_device(
    block_input,
    segment_ids,
    assignment,
    norm_attn,
    weight_qkv,
    weight_proj,
    norm_ffn,
    weight_up,
    weight_down,
    centroids,
    expert_norms,
    expert_in,
    expert_out,
    grad_out,
):
    row_count, local_len, model_width = block_input.shape
    token_count = row_count * local_len
    seq_devices = lax.axis_size("seq")
    full_len = local_len * seq_devices
    group_size = math.gcd(HEADS, 4)
    score_scale = 1.0 / math.sqrt(HEAD_DIM)
    gathered = (
        lax.all_gather(norm_attn, ("seq", "wide"), axis=0, tiled=True),
        lax.all_gather(weight_qkv, ("seq", "wide"), axis=0, tiled=True),
        lax.all_gather(weight_proj, ("seq", "wide"), axis=0, tiled=True),
        lax.all_gather(norm_ffn, ("seq", "wide"), axis=0, tiled=True),
        lax.all_gather(weight_up, ("seq", "wide"), axis=0, tiled=True),
        lax.all_gather(weight_down, ("seq", "wide"), axis=0, tiled=True),
    )
    gain_attn = gathered[0].astype(jnp.float32)
    qkv_full = gathered[1]
    proj_full = gathered[2]
    gain_ffn = gathered[3].astype(jnp.float32)
    up_full = gathered[4]
    down_full = gathered[5]
    tokens_flat = block_input.reshape(token_count, model_width).astype(jnp.float32)
    normed_attn = layer_norm(tokens_flat, gain_attn).astype(jnp.bfloat16)
    qkv = product(normed_attn, qkv_full).astype(jnp.bfloat16)
    qkv_rows = qkv.reshape(row_count, local_len, 3 * model_width)
    kv_whole = lax.all_gather(qkv_rows[:, :, model_width:], "seq", axis=1, tiled=True)
    offset = lax.axis_index("seq") * local_len
    query_pos = offset + jnp.arange(local_len)
    query_seg = lax.dynamic_slice_in_dim(segment_ids, offset, local_len, 1)
    key_pos = jnp.arange(full_len)
    allowed = (query_seg[:, :, None] == segment_ids[:, None, :]) & (
        key_pos[None, None, :] <= query_pos[None, :, None]
    )
    query_groups = split_groups(qkv_rows[:, :, :model_width], group_size, HEAD_DIM)
    key_groups = split_groups(kv_whole[:, :, :model_width], group_size, HEAD_DIM)
    value_groups = split_groups(kv_whole[:, :, model_width:], group_size, HEAD_DIM)

    def group_scores(query_rows, key_rows):
        scores = (
            jnp.einsum("rqhd,rkhd->rhqk", query_rows, key_rows, preferred_element_type=jnp.float32)
            * score_scale
        )
        return jnp.where(allowed[:, None], scores, -1e30)

    def attend_group(packed):
        query_rows, key_rows, value_rows = packed
        scores = group_scores(query_rows, key_rows)
        row_max = jnp.max(scores, axis=-1, keepdims=True)
        exp_scores = jnp.exp(scores - row_max)
        row_total = jnp.sum(exp_scores, axis=-1, keepdims=True)
        probs_low = (exp_scores / row_total).astype(jnp.bfloat16)
        attended_group = jnp.einsum(
            "rhqk,rkhd->rqhd", probs_low, value_rows, preferred_element_type=jnp.float32
        )
        return (attended_group, (row_max + jnp.log(row_total))[..., 0])

    attended_groups, log_totals = lax.map(attend_group, (query_groups, key_groups, value_groups))
    attended = merge_groups(attended_groups).reshape(token_count, model_width).astype(jnp.bfloat16)
    hidden = tokens_flat + product(attended, proj_full)
    normed_ffn = layer_norm(hidden, gain_ffn).astype(jnp.bfloat16)
    pre_act = product(normed_ffn, up_full)
    active = gelu_exact(pre_act).astype(jnp.bfloat16)
    dense_out = hidden + product(active, down_full)
    routed = dense_out.astype(jnp.bfloat16)
    experts = lax.axis_size("wide")
    capacity = token_count // experts
    chosen = assignment.reshape(token_count)
    one_hot = (chosen[:, None] == jnp.arange(experts, dtype=jnp.int32)[None, :]).astype(jnp.int32)
    rank_within = jnp.sum((jnp.cumsum(one_hot, axis=0) - 1) * one_hot, axis=1)
    slot_index = chosen * capacity + rank_within
    source_of = (
        jnp.zeros((token_count,), jnp.int32)
        .at[slot_index]
        .set(jnp.arange(token_count, dtype=jnp.int32))
    )
    received = lax.all_to_all(routed[source_of], "wide", split_axis=0, concat_axis=0, tiled=True)
    received_f = received.astype(jnp.float32)
    centroid_row = centroids[0]
    centroid_f = centroid_row.astype(jnp.float32)
    logit_row = jnp.dot(received, centroid_row, preferred_element_type=jnp.float32)
    gate_value = jax.nn.sigmoid(logit_row)
    gains_f = expert_norms[0].astype(jnp.float32)
    weight_pair = (
        lax.all_gather(expert_in, "seq", axis=3, tiled=True),
        lax.all_gather(expert_out, "seq", axis=2, tiled=True),
    )
    inner_weights = weight_pair[0][0]
    outer_weights = weight_pair[1][0]
    state_now = received_f
    kept_layers = []
    for sublayer in range(2):
        normed = layer_norm(state_now, gains_f[sublayer]).astype(jnp.bfloat16)
        pre_expert = product(normed, inner_weights[sublayer])
        expert_active = gelu_exact(pre_expert).astype(jnp.bfloat16)
        branch = product(expert_active, outer_weights[sublayer])
        kept_layers.append((state_now, normed, pre_expert, expert_active))
        state_now = state_now + branch
    returned = (gate_value[:, None] * state_now).astype(jnp.bfloat16)
    back_rows = lax.all_to_all(returned, "wide", split_axis=0, concat_axis=0, tiled=True)
    output = (
        (dense_out + back_rows[slot_index].astype(jnp.float32))
        .astype(jnp.bfloat16)
        .reshape(block_input.shape)
    )
    gate_sum = jnp.sum(gate_value)
    score_sum = jnp.sum(logit_row * logit_row)
    grad_flat = grad_out.reshape(token_count, model_width)
    grad_back = lax.all_to_all(
        grad_flat[source_of], "wide", split_axis=0, concat_axis=0, tiled=True
    )
    grad_ret = grad_back.astype(jnp.float32)
    grad_gate = jnp.sum(grad_ret * state_now, axis=-1)
    grad_state = grad_ret * gate_value[:, None]
    inner_grads = [None, None]
    outer_grads = [None, None]
    gain_grads = [None, None]
    for sublayer in (1, 0):
        state_in, normed_in, pre_expert, expert_active = kept_layers[sublayer]
        grad_branch = grad_state.astype(jnp.bfloat16)
        grad_act = jnp.einsum(
            "td,fd->tf", grad_branch, outer_weights[sublayer], preferred_element_type=jnp.float32
        )
        outer_grad = jnp.einsum(
            "tf,td->fd", expert_active, grad_branch, preferred_element_type=jnp.float32
        )
        grad_pre = gelu_back(pre_expert, grad_act).astype(jnp.bfloat16)
        inner_grad = jnp.einsum(
            "td,tf->df", normed_in, grad_pre, preferred_element_type=jnp.float32
        )
        grad_normed = jnp.einsum(
            "tf,df->td", grad_pre, inner_weights[sublayer], preferred_element_type=jnp.float32
        )
        inner_grad, outer_grad = (
            lax.psum_scatter(
                inner_grad.astype(jnp.bfloat16), "seq", scatter_dimension=1, tiled=True
            ).astype(jnp.float32),
            lax.psum_scatter(
                outer_grad.astype(jnp.bfloat16), "seq", scatter_dimension=0, tiled=True
            ).astype(jnp.float32),
        )
        grad_resid, gain_grad = norm_back(state_in, gains_f[sublayer], grad_normed)
        grad_state = grad_state + grad_resid
        inner_grads[sublayer] = inner_grad
        outer_grads[sublayer] = outer_grad
        gain_grads[sublayer] = gain_grad
    grad_logit = grad_gate * gate_value * (1.0 - gate_value)
    grad_routed = (grad_state + grad_logit[:, None] * centroid_f[None, :]).astype(jnp.bfloat16)
    centroid_grad = jnp.dot(grad_logit, received_f, precision=highest)
    returned_grad = lax.all_to_all(grad_routed, "wide", split_axis=0, concat_axis=0, tiled=True)
    grad_dense = grad_flat.astype(jnp.float32) + returned_grad[slot_index].astype(jnp.float32)
    grad_down_in = grad_dense.astype(jnp.bfloat16)
    grad_w_down = jnp.einsum("tf,td->fd", active, grad_down_in, preferred_element_type=jnp.float32)
    grad_active = jnp.einsum(
        "td,fd->tf", grad_down_in, down_full, preferred_element_type=jnp.float32
    )
    grad_pre_act = gelu_back(pre_act, grad_active).astype(jnp.bfloat16)
    grad_w_up = jnp.einsum(
        "td,tf->df", normed_ffn, grad_pre_act, preferred_element_type=jnp.float32
    )
    grad_normed_ffn = jnp.einsum(
        "tf,df->td", grad_pre_act, up_full, preferred_element_type=jnp.float32
    )
    grad_hidden_norm, grad_gain_ffn = norm_back(hidden, gain_ffn, grad_normed_ffn)
    grad_hidden = grad_dense + grad_hidden_norm
    grad_proj = grad_hidden.astype(jnp.bfloat16)
    grad_w_proj = jnp.einsum("tc,td->cd", attended, grad_proj, preferred_element_type=jnp.float32)
    grad_attended = jnp.einsum(
        "td,cd->tc", grad_proj, proj_full, preferred_element_type=jnp.float32
    ).astype(jnp.bfloat16)
    grad_groups = split_groups(
        grad_attended.reshape(row_count, local_len, model_width), group_size, HEAD_DIM
    )

    def attend_back(packed):
        query_rows, key_rows, value_rows, grad_att, log_total = packed
        scores = group_scores(query_rows, key_rows)
        softmax_probs = jnp.exp(scores - log_total[..., None])
        grad_probs = jnp.einsum(
            "rqhd,rkhd->rhqk", grad_att, value_rows, preferred_element_type=jnp.float32
        )
        grad_values = jnp.einsum(
            "rhqk,rqhd->rkhd",
            softmax_probs.astype(jnp.bfloat16),
            grad_att,
            preferred_element_type=jnp.float32,
        )
        inner_sum = jnp.sum(softmax_probs * grad_probs, axis=-1, keepdims=True)
        grad_scores = (softmax_probs * (grad_probs - inner_sum)).astype(jnp.bfloat16)
        grad_query = (
            jnp.einsum("rhqk,rkhd->rqhd", grad_scores, key_rows, preferred_element_type=jnp.float32)
            * score_scale
        )
        grad_keys = (
            jnp.einsum(
                "rhqk,rqhd->rkhd", grad_scores, query_rows, preferred_element_type=jnp.float32
            )
            * score_scale
        )
        return (grad_query, grad_keys, grad_values)

    grad_query_g, grad_keys_g, grad_values_g = lax.map(
        attend_back, (query_groups, key_groups, value_groups, grad_groups, log_totals)
    )
    grad_kv_whole = jnp.concatenate(
        [merge_groups(grad_keys_g), merge_groups(grad_values_g)], axis=2
    )
    grad_kv = lax.psum_scatter(
        grad_kv_whole.astype(jnp.bfloat16), "seq", scatter_dimension=1, tiled=True
    ).astype(jnp.float32)
    grad_qkv = (
        jnp.concatenate([merge_groups(grad_query_g), grad_kv], axis=2)
        .reshape(token_count, 3 * model_width)
        .astype(jnp.bfloat16)
    )
    grad_w_qkv = jnp.einsum("td,te->de", normed_attn, grad_qkv, preferred_element_type=jnp.float32)
    grad_normed_attn = jnp.einsum(
        "te,de->td", grad_qkv, qkv_full, preferred_element_type=jnp.float32
    )
    grad_input_norm, grad_gain_attn = norm_back(tokens_flat, gain_attn, grad_normed_attn)
    grad_input = (grad_hidden + grad_input_norm).reshape(block_input.shape)
    dense_grads = (
        lax.psum_scatter(grad_gain_attn, ("seq", "wide"), scatter_dimension=0, tiled=True),
        lax.psum_scatter(grad_w_qkv, ("seq", "wide"), scatter_dimension=0, tiled=True),
        lax.psum_scatter(grad_w_proj, ("seq", "wide"), scatter_dimension=0, tiled=True),
        lax.psum_scatter(grad_gain_ffn, ("seq", "wide"), scatter_dimension=0, tiled=True),
        lax.psum_scatter(grad_w_up, ("seq", "wide"), scatter_dimension=0, tiled=True),
        lax.psum_scatter(grad_w_down, ("seq", "wide"), scatter_dimension=0, tiled=True),
    )
    expert_totals = lax.psum(
        (jnp.stack(gain_grads), centroid_grad, jnp.stack([gate_sum, score_sum])), "seq"
    )
    token_total = token_count * seq_devices
    return (
        output,
        grad_input,
        dense_grads[0],
        dense_grads[1],
        dense_grads[2],
        dense_grads[3],
        dense_grads[4],
        dense_grads[5],
        expert_totals[1][None],
        expert_totals[0][None],
        jnp.stack(inner_grads)[None],
        jnp.stack(outer_grads)[None],
        (expert_totals[2][0] / token_total)[None],
        (expert_totals[2][1] / token_total)[None],
    )


def solution(mesh):
    in_specs = (
        P("wide", "seq", None),
        P("wide", None),
        P("wide", "seq"),
        P(("seq", "wide")),
        P(("seq", "wide"), None),
        P(("seq", "wide"), None),
        P(("seq", "wide")),
        P(("seq", "wide"), None),
        P(("seq", "wide"), None),
        P("wide", None),
        P("wide", None, None),
        P("wide", None, None, "seq"),
        P("wide", None, "seq", None),
        P("wide", "seq", None),
    )
    out_specs = (
        P("wide", "seq", None),
        P("wide", "seq", None),
        P(("seq", "wide")),
        P(("seq", "wide"), None),
        P(("seq", "wide"), None),
        P(("seq", "wide")),
        P(("seq", "wide"), None),
        P(("seq", "wide"), None),
        P("wide", None),
        P("wide", None, None),
        P("wide", None, None, "seq"),
        P("wide", None, "seq", None),
        P("wide"),
        P("wide"),
    )
    return jax.shard_map(
        per_device, mesh=mesh, in_specs=in_specs, out_specs=out_specs, check_vma=False
    )
```

profile of v0, /device:TPU:0, one launch (start us, length us, event | category | flops | bytes accessed | tf_op | source)
XLA Modules:
  0.0 2235.8 jit_solution(6256757369775413830)
XLA Ops:
  9.7 43.0 %all-reduce.6 = (bf16[1024]{0:T(1024)(128)(2,1)S(1)}, bf16[1024]{0:T(1024)(128)(2,1)S(1)}) all-reduce(bf16[1024]{0:T(1024)(128)(2,1)S(1)} %dynamic-update-slice, bf16[1024]{0:T(1024)(128)(2,1)S(1)} %dynamic-update-slice.1), channel_id=1, replica_groups=mesh['seq'=4,'wide'=8] {'seq','wide'}, use_global_device_ids=true, to_apply=%add | all-reduce | flops 2048 | bytes 8192
  58.5 24.6 %all-gather.8.cloned.1.call-done = bf16[1024,3072]{1,0:T(8,128)(2,1)} async-done(((bf16[32,3072]{1,0:T(8,128)(2,1)}), bf16[1024,3072]{1,0:T(8,128)(2,1)}) %all-gather.8.cloned.1.call-update) | async-done | bytes 6291472 | tf_op jit(solution)/shard_map/all_gather | solution.py:79
  104.5 47.6 %all-gather.10.cloned.1.call-done = bf16[2,1024,2048]{1,2,0:T(8,128)(2,1)} async-done(((bf16[2,256,2048]{1,2,0:T(8,128)(2,1)}), bf16[2,1024,2048]{1,2,0:T(8,128)(2,1)}) %all-gather.10.cloned.1.call-update) | async-done | bytes 8388624 | tf_op jit(solution)/shard_map/all_gather | solution.py:95
  160.9 40.1 %while.28 = (s32[]{:T(128)}, bf16[4,2,256,4,64]{2,4,3,1,0:T(8,128)(2,1)S(1)}, f32[4,2,4,256]{3,2,1,0:T(4,128)}, bf16[4,2,1024,4,64]{2,4,3,1,0:T(8,128)(2,1)}, bf...) while((s32[]{:T(128)}, ...), condition=%wide.region_5.6_spmd.clone, body=%wide.region_2.5_spmd.clone.sunk | while | flops 563083264 | bytes 30486640 | solution.py:126
  216.1 74.2 %all-gather.14.cloned.1.call-done = bf16[1024,4096]{1,0:T(8,128)(2,1)} async-done(((bf16[32,4096]{1,0:T(8,128)(2,1)}), bf16[1024,4096]{1,0:T(8,128)(2,1)}) %all-gather.14.cloned.1.call-update) | async-done | bytes 8388624 | tf_op jit(solution)/shard_map/all_gather | solution.py:82
  290.3 26.9 %multiply_convert_fusion.3 = (bf16[512,4096]{1,0:T(8,128)(2,1)}, f32[512,4096]{1,0:T(8,128)}, f32[512,4096]{1,0:T(8,128)}) fusion(bf16[1024,4096]{1,0:T(8,128)(2,1)} %all-gather.14.cloned.1.call-done, f32[512,1024]{1,0:T(8,128)} %copy-done.11, f32[1024]{0:T(1024)S(1)} %convert_element_type.169, f32[512]{0:T(512)S(1)} %fusion.123, ...), kind=kOutput, calls=%fused_computation.101 | convolution fusion | flops 4433379328 | bytes 31465472 | tf_op jit(solution)/shard_map/dot_general | solution.py:27
  317.2 51.6 %all-gather.16.cloned.1.call-done = bf16[4096,1024]{1,0:T(8,128)(2,1)} async-done(((bf16[128,1024]{1,0:T(8,128)(2,1)}), bf16[4096,1024]{1,0:T(8,128)(2,1)}) %all-gather.16.cloned.1.call-update) | async-done | bytes 8388624 | tf_op jit(solution)/shard_map/all_gather | solution.py:83
  368.9 10.5 fusion.145
  389.7 22.7 %all-to-all-done = bf16[8,64,1024]{2,1,0:T(8,128)(2,1)S(1)} async-done(((bf16[8,64,1024]{2,1,0:T(8,128)(2,1)}), bf16[8,64,1024]{2,1,0:T(8,128)(2,1)S(1)}, u32[]{:S(2)}, u32[]{:S(2)}) %all-to-all-start) | async-done | bytes 1048608 | tf_op jit(solution)/shard_map/all_to_all | solution.py:145
  418.2 56.6 %all-gather.18.cloned.1.call-done = bf16[1,2,1024,4096]{3,2,1,0:T(8,128)(2,1)} async-done(((bf16[1,2,1024,1024]{3,2,1,0:T(8,128)(2,1)}), bf16[1,2,1024,4096]{3,2,1,0:T(8,128)(2,1)}) %all-gather.18.cloned.1.call-update) | async-done | bytes 16777232 | tf_op jit(solution)/shard_map/all_gather | solution.py:153
  474.8 25.7 %multiply_convert_fusion.2 = (bf16[512,4096]{1,0:T(8,128)(2,1)}, f32[512,4096]{1,0:T(8,128)}, f32[512,4096]{1,0:T(8,128)}) fusion(bf16[512,1024]{1,0:T(8,128)(2,1)S(1)} %bitcast.337, bf16[1,2,1024,4096]{3,2,1,0:T(8,128)(2,1)} %all-gather.18.cloned.1.call-done), kind=kOutput, calls=%fused_computation.88 | convolution fusion | flops 4431282176 | bytes 30408704 | tf_op jit(solution)/shard_map/dot_general | solution.py:27
  500.5 81.8 %all-gather.20.cloned.1.call-done = bf16[1,2,4096,1024]{3,2,1,0:T(8,128)(2,1)} async-done(((bf16[1,2,1024,1024]{3,2,1,0:T(8,128)(2,1)}), bf16[1,2,4096,1024]{3,2,1,0:T(8,128)(2,1)}) %all-gather.20.cloned.1.call-update) | async-done | bytes 16777232 | tf_op jit(solution)/shard_map/all_gather | solution.py:154
  592.1 25.9 %multiply_convert_fusion.1 = (bf16[512,4096]{1,0:T(8,128)(2,1)}, f32[512,4096]{1,0:T(8,128)}, f32[512,4096]{1,0:T(8,128)}) fusion(bf16[1,2,1024,4096]{3,2,1,0:T(8,128)(2,1)S(1)} %copy-done.84, f32[512,1024]{1,0:T(8,128)S(1)} %get-tuple-element.323, f32[1024]{0:T(1024)S(1)} %bitcast.354, f32[512]{0:T(512)S(1)} %fusion.124, f32[512]{0:T(512)S(1)} %broadcast_multiply_fusion.1), kind=kOutput, calls=%fused_computation.75 | convolution fusion | flops 4433379328 | bytes 31465472 | tf_op jit(solution)/shard_map/dot_general | solution.py:27
  619.4 13.4 add_convert_fusion.2
  644.4 11.9 fusion.90
  657.2 13.5 add_convert_fusion.1
  689.0 26.1 %all-to-all-done.3 = bf16[8,64,1024]{2,1,0:T(8,128)(2,1)S(1)} async-done(((bf16[8,64,1024]{2,1,0:T(8,128)(2,1)}), bf16[8,64,1024]{2,1,0:T(8,128)(2,1)S(1)}, u32[]{:S(2)}, u32[]{:S(2)}) %all-to-all-start.3) | async-done | bytes 1048608 | tf_op jit(solution)/shard_map/all_to_all | solution.py:218
  717.4 13.5 add_convert_fusion
  746.2 80.1 %while.29 = (s32[]{:T(128)}, bf16[4,2,256,4,64]{2,4,3,1,0:T(8,128)(2,1)S(1)}, bf16[4,2,1024,4,64]{2,4,3,0,1:T(8,128)(2,1)}, bf16[4,2,1024,4,64]{2,4,3,0,1:T(8,12...) while((s32[]{:T(128)}, ...), condition=%wide.region_25.26_spmd.clone, body=%wide.region_23.25_spmd.clone.sunk | while | flops 1375336448 | bytes 108336328 | solution.py:270
  889.8 14.2 reduce-scatter.10.cloned.1.call-done
  908.3 12.4 fusion.101
  922.4 10.8 fusion.133
  934.7 10.5 fusion.113
  952.7 12.7 all-reduce.5
  981.5 71.0 %reduce-scatter.20.cloned.1.call-done = bf16[1024,1024]{1,0:T(8,128)(2,1)} async-done(((bf16[1024,4096]{1,0:T(8,128)(2,1)}), bf16[1024,1024]{1,0:T(8,128)(2,1)}) %reduce-scatter.20.cloned.1.call-update) | async-done | bytes 2097168 | tf_op jit(solution)/shard_map/reduce_scatter | solution.py:203
  1058.6 67.8 %reduce-scatter.26.cloned.1.call-done = bf16[1024,1024]{1,0:T(8,128)(2,1)} async-done(((bf16[4096,1024]{1,0:T(8,128)(2,1)}), bf16[1024,1024]{1,0:T(8,128)(2,1)}) %reduce-scatter.26.cloned.1.call-update) | async-done | bytes 2097168 | tf_op jit(solution)/shard_map/reduce_scatter | solution.py:206
  1126.5 73.9 %reduce-scatter.24.cloned.1.call-done = bf16[1024,1024]{1,0:T(8,128)(2,1)} async-done(((bf16[4096,1024]{1,0:T(8,128)(2,1)}), bf16[1024,1024]{1,0:T(8,128)(2,1)}) %reduce-scatter.24.cloned.1.call-update) | async-done | bytes 2097168 | tf_op jit(solution)/shard_map/reduce_scatter | solution.py:206
  1215.7 41.4 %all-reduce.4 = (f32[1024]{0:T(1024)S(1)}, f32[1024]{0:T(1024)S(1)}) all-reduce(f32[1024]{0:T(1024)S(1)} %get-tuple-element.232, f32[1024]{0:T(1024)S(1)} %copy-done.82), channel_id=3, replica_groups=mesh['seq'=4,'wide'=8] {'seq','wide'}, use_global_device_ids=true, to_apply=%region_30.31.clone | all-reduce | flops 2048 | bytes 16384
  1261.9 85.9 %reduce-scatter.14.cloned.1.call-done = f32[32,1024]{1,0:T(8,128)} async-done(((f32[1024,1024]{1,0:T(8,128)}), f32[32,1024]{1,0:T(8,128)}) %reduce-scatter.14.cloned.1.call-update) | async-done | bytes 131088 | tf_op jit(solution)/shard_map/reduce_scatter | solution.py:293
  1347.8 159.1 %reduce-scatter.12.cloned.1.call-done = f32[32,3072]{1,0:T(8,128)} async-done(((f32[1024,3072]{1,0:T(8,128)}), f32[32,3072]{1,0:T(8,128)}) %reduce-scatter.12.cloned.1.call-update) | async-done | bytes 393232 | tf_op jit(solution)/shard_map/reduce_scatter | solution.py:292
  1507.0 359.7 %reduce-scatter.16.cloned.1.call-done = f32[32,4096]{1,0:T(8,128)} async-done(((f32[1024,4096]{1,0:T(8,128)}), f32[32,4096]{1,0:T(8,128)}) %reduce-scatter.16.cloned.1.call-update) | async-done | bytes 524304 | tf_op jit(solution)/shard_map/reduce_scatter | solution.py:295
  1866.7 360.1 %reduce-scatter.18.cloned.1.call-done = f32[128,1024]{1,0:T(8,128)} async-done(((f32[4096,1024]{1,0:T(8,128)}), f32[128,1024]{1,0:T(8,128)}) %reduce-scatter.18.cloned.1.call-update) | async-done | bytes 524304 | tf_op jit(solution)/shard_map/reduce_scatter | solution.py:296
  (405 shorter events, 367.4 us)
Async XLA Ops:
  7.2 76.0 %all-gather.8.cloned.1.call-start = ((), (), s32[]{:S(2)}) async-start(), calls=%async_computation.13 | async-start | bytes 6488064 | tf_op jit(solution)/shard_map/all_gather | solution.py:79
  7.9 144.1 %all-gather.10.cloned.1.call-start = ((), (), s32[]{:S(2)}) async-start(), calls=%async_computation.14 | async-start | bytes 10485760 | tf_op jit(solution)/shard_map/all_gather | solution.py:95
  93.9 117.5 %all-gather.12.cloned.1.call-start = ((), (), s32[]{:S(2)}) async-start(), calls=%async_computation.15 | async-start | bytes 2162688 | tf_op jit(solution)/shard_map/all_gather | solution.py:80
  94.7 195.6 %all-gather.14.cloned.1.call-start = ((), (), s32[]{:S(2)}) async-start(), calls=%async_computation.16 | async-start | bytes 8650752 | tf_op jit(solution)/shard_map/all_gather | solution.py:82
  95.3 273.6 %all-gather.16.cloned.1.call-start = ((), (), s32[]{:S(2)}) async-start(), calls=%async_computation.17 | async-start | bytes 8650752 | tf_op jit(solution)/shard_map/all_gather | solution.py:83
  95.9 379.0 %all-gather.18.cloned.1.call-start = ((), (), s32[]{:S(2)}) async-start(), calls=%async_computation.18 | async-start | bytes 20971520 | tf_op jit(solution)/shard_map/all_gather | solution.py:153
  96.4 485.9 %all-gather.20.cloned.1.call-start = ((), (), s32[]{:S(2)}) async-start(), calls=%async_computation.19 | async-start | bytes 20971520 | tf_op jit(solution)/shard_map/all_gather | solution.py:154
  97.5 192.8 %copy-start.70 = (f32[1024]{0:T(1024)}, f32[1024]{0:T(1024)S(1)}, u32[]{:S(2)}) copy-start(f32[1024]{0:T(1024)S(1)} %convert_element_type.169) | copy-start | bytes 12292
  201.0 116.1 %copy-start.7 = (pred[256,1024]{1,0:T(8,128)(4,1)}, pred[256,1024]{1,0:T(8,128)(4,1)S(1)}, u32[]{:S(2)}) copy-start(pred[256,1024]{1,0:T(8,128)(4,1)S(1)} %get-tuple-element.561) | copy-start | bytes 786436
  201.0 116.1 %copy-start.9 = (bf16[4,2,256,4,64]{2,4,3,1,0:T(8,128)(2,1)}, bf16[4,2,256,4,64]{2,4,3,1,0:T(8,128)(2,1)S(1)}, u32[]{:S(2)}) copy-start(bf16[4,2,256,4,64]{2,4,3,1,0:T(8,128)(2,1)S(1)} %get-tuple-element.564) | copy-start | bytes 3145732
  201.0 116.1 %copy-start.35 = (s32[2,256]{1,0:T(2,128)}, s32[2,256]{1,0:T(2,128)S(1)}, u32[]{:S(2)}) copy-start(s32[2,256]{1,0:T(2,128)S(1)} %get-tuple-element.601) | copy-start | bytes 6148
  214.4 102.8 %copy-start.49 = (f32[512]{0:T(512)}, f32[512]{0:T(512)S(1)}, u32[]{:S(2)}) copy-start(f32[512]{0:T(512)S(1)} %broadcast_multiply_fusion.2) | copy-start | bytes 6148
  216.1 152.8 %copy-start.12 = (f32[512,1024]{1,0:T(8,128)S(1)}, f32[512,1024]{1,0:T(8,128)}, u32[]{:S(2)}) copy-start(f32[512,1024]{1,0:T(8,128)} %copy-done.11) | copy-start | bytes 6291460
  382.2 30.3 %all-to-all-start = ((bf16[8,64,1024]{2,1,0:T(8,128)(2,1)}), bf16[8,64,1024]{2,1,0:T(8,128)(2,1)S(1)}, u32[]{:S(2)}, u32[]{:S(2)}) async-start(bf16[8,64,1024]{2,1,0:T(8,128)(2,1)} %bitcast.13), calls=%async_computation | async-start | bytes 2097152 | tf_op jit(solution)/shard_map/all_to_all | solution.py:145
  389.7 110.9 %copy-start.39 = (f32[1,1,1024]{2,1,0:T(1,128)}, f32[1,1,1024]{2,1,0:T(1,128)S(1)}, u32[]{:S(2)}) copy-start(f32[1,1,1024]{2,1,0:T(1,128)S(1)} %get-tuple-element.308) | copy-start | bytes 12292
  389.7 252.6 %copy-start.73 = (f32[1,1,1024]{2,1,0:T(1,128)}, f32[1,1,1024]{2,1,0:T(1,128)S(1)}, u32[]{:S(2)}) copy-start(f32[1,1,1024]{2,1,0:T(1,128)S(1)} %get-tuple-element.307) | copy-start | bytes 12292
  412.4 268.7 %copy-start.3 = (bf16[8,64,1024]{2,1,0:T(8,128)(2,1)}, bf16[8,64,1024]{2,1,0:T(8,128)(2,1)S(1)}, u32[]{:S(2)}) copy-start(bf16[8,64,1024]{2,1,0:T(8,128)(2,1)S(1)} %all-to-all-done) | copy-start | bytes 3145732
  412.4 206.8 %all-to-all-start.2 = ((bf16[8,64,1024]{2,1,0:T(8,128)(2,1)}), bf16[8,64,1024]{2,1,0:T(8,128)(2,1)S(1)}, u32[]{:S(2)}, u32[]{:S(2)}) async-start(bf16[8,64,1024]{2,1,0:T(8,128)(2,1)} %bitcast.322), calls=%async_computation.2 | async-start | bytes 2097152 | tf_op jit(solution)/shard_map/all_to_all | solution.py:177
  683.4 31.7 %all-to-all-start.3 = ((bf16[8,64,1024]{2,1,0:T(8,128)(2,1)}), bf16[8,64,1024]{2,1,0:T(8,128)(2,1)S(1)}, u32[]{:S(2)}, u32[]{:S(2)}) async-start(bf16[8,64,1024]{2,1,0:T(8,128)(2,1)} %bitcast.329), calls=%async_computation.3 | async-start | bytes 2097152 | tf_op jit(solution)/shard_map/all_to_all | solution.py:218
  688.9 215.1 %reduce-scatter.10.cloned.1.call-start = ((), (), s32[]{:S(2)}) async-start(), calls=%async_computation.20 | async-start | bytes 10485760 | tf_op jit(solution)/shard_map/reduce_scatter | solution.py:276
  834.5 147.0 %reduce-scatter.22.cloned.1.call-start = ((), (), s32[]{:S(2)}) async-start(), calls=%async_computation.26 | async-start | bytes 10485760 | tf_op jit(solution)/shard_map/reduce_scatter | solution.py:203
  846.3 206.2 %reduce-scatter.20.cloned.1.call-start = ((), (), s32[]{:S(2)}) async-start(), calls=%async_computation.25 | async-start | bytes 10485760 | tf_op jit(solution)/shard_map/reduce_scatter | solution.py:203
  857.3 269.2 %reduce-scatter.26.cloned.1.call-start = ((), (), s32[]{:S(2)}) async-start(), calls=%async_computation.28 | async-start | bytes 10485760 | tf_op jit(solution)/shard_map/reduce_scatter | solution.py:206
  867.5 332.8 %reduce-scatter.24.cloned.1.call-start = ((), (), s32[]{:S(2)}) async-start(), calls=%async_computation.27 | async-start | bytes 10485760 | tf_op jit(solution)/shard_map/reduce_scatter | solution.py:206
  877.9 469.9 %reduce-scatter.14.cloned.1.call-start = ((), (), s32[]{:S(2)}) async-start(), calls=%async_computation.22 | async-start | bytes 4325376 | tf_op jit(solution)/shard_map/reduce_scatter | solution.py:293
  884.1 622.9 %reduce-scatter.12.cloned.1.call-start = ((), (), s32[]{:S(2)}) async-start(), calls=%async_computation.21 | async-start | bytes 12976128 | tf_op jit(solution)/shard_map/reduce_scatter | solution.py:292
  920.7 946.0 %reduce-scatter.16.cloned.1.call-start = ((), (), s32[]{:S(2)}) async-start(), calls=%async_computation.23 | async-start | bytes 17301504 | tf_op jit(solution)/shard_map/reduce_scatter | solution.py:295
  933.2 1293.6 %reduce-scatter.18.cloned.1.call-start = ((), (), s32[]{:S(2)}) async-start(), calls=%async_computation.24 | async-start | bytes 17301504 | tf_op jit(solution)/shard_map/reduce_scatter | solution.py:296
  945.2 31.3 %all-to-all-start.1 = ((bf16[8,64,1024]{2,1,0:T(8,128)(2,1)}), bf16[8,64,1024]{2,1,0:T(8,128)(2,1)S(1)}, u32[]{:S(2)}, u32[]{:S(2)}) async-start(bf16[8,64,1024]{2,1,0:T(8,128)(2,1)} %bitcast.23), calls=%async_computation.1 | async-start | bytes 2097152 | tf_op jit(solution)/shard_map/all_to_all | solution.py:168
  1058.6 147.9 %copy-start.6 = (bf16[2,256,1024]{2,1,0:T(8,128)(2,1)S(1)}, bf16[2,256,1024]{2,1,0:T(8,128)(2,1)}, u32[]{:S(2)}) copy-start(bf16[2,256,1024]{2,1,0:T(8,128)(2,1)} %param.18) | copy-start | bytes 3145732
  1058.6 147.9 %copy-start.38 = (f32[1024]{0:T(1024)S(1)}, f32[1024]{0:T(1024)}, u32[]{:S(2)}) copy-start(f32[1024]{0:T(1024)} %copy-done.37) | copy-start | bytes 12292
  1058.6 147.9 %copy-start.45 = (f32[1,2,2,128]{3,1,2,0:T(2,128)S(1)}, f32[1,2,2,128]{3,1,2,0:T(2,128)}, u32[]{:S(2)}) copy-start(f32[1,2,2,128]{3,1,2,0:T(2,128)} %copy-done.44) | copy-start | bytes 6148
  (85 other events, 1090.1 us)
Sparse Core Ops, SparseCore 0:
  11.0 72.1 all-gather.7
  94.1 57.8 all-gather.9
  155.0 56.3 all-gather.11
  214.3 75.9 all-gather.13
  293.1 75.7 all-gather.15
  370.3 104.5 all-gather.17
  476.4 105.8 all-gather.19
  834.6 69.3 reduce-scatter.9
  907.2 71.4 reduce-scatter.21
  981.2 71.2 reduce-scatter.19
  1055.0 71.3 reduce-scatter.25
  1128.9 71.3 reduce-scatter.23
  1203.2 144.6 reduce-scatter.13
  1354.3 152.6 reduce-scatter.11
  1509.7 356.9 reduce-scatter.15
  1869.4 357.3 reduce-scatter.17
where the time goes:
time: 2240 us
  waiting for transfers between devices  1600 us (71%)
  matrix products  354 us (16%)
  blocking collectives  97.1 us (4%)
  local copies, waits for them, and re-layouts  74.6 us (3%)
  other arithmetic  71.8 us (3%)
    reduce_scatter x1, waiting for transfers between devices, per_device(): lax.psum_scatter(grad_w_down, ('seq', 'wide'), scatter_dimension=0, tiled...  360 us
    reduce_scatter x1, waiting for transfers between devices, per_device(): lax.psum_scatter(grad_w_up, ('seq', 'wide'), scatter_dimension=0, tiled=T...  360 us
    reduce_scatter x1, waiting for transfers between devices, per_device(): lax.psum_scatter(grad_w_qkv, ('seq', 'wide'), scatter_dimension=0, tiled=...  159 us
    reduce_scatter x2, waiting for transfers between devices, per_device(): lax.psum_scatter(outer_grad.astype(jnp.bfloat16), 'seq', scatter_dimensio...  142 us
    dot_general x8, matrix products, product(): return jnp.dot(left_side, right_side, preferred_element_type=jnp.float32)  119 us
    reduce_scatter x1, waiting for transfers between devices, per_device(): lax.psum_scatter(grad_w_proj, ('seq', 'wide'), scatter_dimension=0, tiled...  85.9 us
    unnamed x2, blocking collectives  84.4 us
    all_gather x1, waiting for transfers between devices, per_device(): lax.all_gather(expert_out, 'seq', axis=2, tiled=True)  81.8 us
  transfers between devices with their start and end apart: 20, of which 18 were waited for; matrix products, arithmetic and copies ran while one was open for 13% of the time, Pallas kernels for 0%

commit v1 on v0

v1 whole, which is shorter than its diff:
```python
import functools
import math

import jax
import jax.numpy as jnp
from jax import lax
from jax.experimental import pallas as pl
from jax.experimental.pallas import tpu as pltpu
from jax.sharding import PartitionSpec as P

HEADS = 16
HEAD_DIM = 64
BLOCKS = 4

epsilon = 1e-05
highest = lax.Precision.HIGHEST
bf16 = jnp.bfloat16
f32 = jnp.float32


def layer_norm(values, norm_gain):
    centered = values - jnp.mean(values, axis=-1, keepdims=True)
    variance = jnp.mean(centered * centered, axis=-1, keepdims=True)
    return centered * lax.rsqrt(variance + epsilon) * norm_gain


def norm_back(values, norm_gain, grad_normed):
    _, pull_back = jax.vjp(layer_norm, values, norm_gain)
    return pull_back(grad_normed)


def gelu_pair(values):
    cdf = 0.5 * (1.0 + lax.erf(values * math.sqrt(0.5)))
    density = jnp.exp(values * values * -0.5) * (1.0 / math.sqrt(2.0 * math.pi))
    return values * cdf, cdf + values * density


def product(left_side, right_side):
    return jnp.dot(left_side, right_side, preferred_element_type=f32)


def product_bt(left_side, right_side):
    return lax.dot_general(
        left_side, right_side, (((1,), (1,)), ((), ())), preferred_element_type=f32
    )


def product_at(left_side, right_side):
    return lax.dot_general(
        left_side, right_side, (((0,), (0,)), ((), ())), preferred_element_type=f32
    )


def seq_send(values, pairs):
    return lax.ppermute(values, "seq", pairs)


def swap_core(values):
    return seq_send(values, [(0, 1), (1, 0), (2, 3), (3, 2)])


def swap_chip(values):
    return seq_send(values, [(0, 2), (2, 0), (1, 3), (3, 1)])


def pair_probs(query, keys, bias, score_scale):
    scores = product_bt(keys, query) * score_scale + bias
    exp_scores = jnp.exp(scores - jnp.max(scores, axis=0, keepdims=True))
    return exp_scores * (1.0 / jnp.sum(exp_scores, axis=0, keepdims=True))


def attend_kernel(score_scale, q_ref, k0, v0, k1, v1, k2, v2, bias_ref, out_ref):
    bias = bias_ref[0]
    parts = []
    for head in range(2):
        cols = slice(head * HEAD_DIM, (head + 1) * HEAD_DIM)
        keys = jnp.concatenate([k2[0][:, cols], k1[0][:, cols], k0[0][:, cols]], axis=0)
        vals = jnp.concatenate([v2[0][:, cols], v1[0][:, cols], v0[0][:, cols]], axis=0)
        probs_low = pair_probs(q_ref[0][:, cols], keys, bias, score_scale).astype(bf16)
        parts.append(product_at(vals, probs_low))
    out_ref[0] = jnp.concatenate(parts, axis=0).T.astype(bf16)


def attend_back_kernel(
    score_scale, q_ref, k0, v0, k1, v1, k2, v2, bias_ref, grad_ref, dq_ref, d0, d1, d2
):
    bias = bias_ref[0]
    dq_parts, dk_parts, dv_parts = [], [], []
    for head in range(2):
        cols = slice(head * HEAD_DIM, (head + 1) * HEAD_DIM)
        query = q_ref[0][:, cols]
        grad_att = grad_ref[0][:, cols]
        keys = jnp.concatenate([k2[0][:, cols], k1[0][:, cols], k0[0][:, cols]], axis=0)
        vals = jnp.concatenate([v2[0][:, cols], v1[0][:, cols], v0[0][:, cols]], axis=0)
        probs = pair_probs(query, keys, bias, score_scale)
        grad_probs = product_bt(vals, grad_att)
        dv_parts.append(product(probs.astype(bf16), grad_att))
        inner_sum = jnp.sum(probs * grad_probs, axis=0, keepdims=True)
        grad_scores = (probs * (grad_probs - inner_sum)).astype(bf16)
        dk_parts.append(product(grad_scores, query) * score_scale)
        dq_parts.append(product_at(keys, grad_scores) * score_scale)
    dq_ref[0] = jnp.concatenate(dq_parts, axis=0).T.astype(bf16)
    d_keys = jnp.concatenate(dk_parts, axis=1).astype(bf16)
    d_vals = jnp.concatenate(dv_parts, axis=1).astype(bf16)
    size = d_keys.shape[0] // 3
    for place, ref in enumerate((d2, d1, d0)):
        ref[0, 0] = d_keys[place * size : (place + 1) * size]
        ref[1, 0] = d_vals[place * size : (place + 1) * size]


def attention_specs(local_len, model_width, key_len):
    width = 2 * HEAD_DIM
    groups = model_width // width
    query = pl.BlockSpec((1, local_len, width), lambda row, head: (row, 0, head))
    values = pl.BlockSpec((1, local_len, width), lambda row, head: (row, 0, head + groups))
    bias = pl.BlockSpec((1, key_len, local_len), lambda row, head: (row, 0, 0))
    return groups, query, [query, query, values, query, values, query, values, bias]


def attend(query, kv_blocks, bias):
    rows, local_len, model_width = query.shape
    groups, spec, in_specs = attention_specs(local_len, model_width, bias.shape[1])
    operands = [block for block in kv_blocks for _ in range(2)]
    flops = 4 * rows * model_width * local_len * bias.shape[1]
    return pl.pallas_call(
        functools.partial(attend_kernel, 1.0 / math.sqrt(HEAD_DIM)),
        grid=(rows, groups),
        in_specs=in_specs,
        out_specs=spec,
        out_shape=jax.ShapeDtypeStruct(query.shape, bf16),
        cost_estimate=pl.CostEstimate(
            flops=flops * 6, bytes_accessed=8 * query.size * 2, transcendentals=0
        ),
        name="attend",
    )(query, *operands, bias)


def attend_back(query, kv_blocks, bias, grad_attended):
    rows, local_len, model_width = query.shape
    groups, spec, in_specs = attention_specs(local_len, model_width, bias.shape[1])
    operands = [block for block in kv_blocks for _ in range(2)]
    pair_spec = pl.BlockSpec((2, 1, local_len, 2 * HEAD_DIM), lambda row, head: (0, row, 0, head))
    pair_shape = jax.ShapeDtypeStruct((2, rows, local_len, model_width), bf16)
    flops = 10 * rows * model_width * local_len * bias.shape[1]
    return pl.pallas_call(
        functools.partial(attend_back_kernel, 1.0 / math.sqrt(HEAD_DIM)),
        grid=(rows, groups),
        in_specs=in_specs + [spec],
        out_specs=[spec, pair_spec, pair_spec, pair_spec],
        out_shape=[jax.ShapeDtypeStruct(query.shape, bf16)] + [pair_shape] * 3,
        cost_estimate=pl.CostEstimate(
            flops=flops * 6, bytes_accessed=16 * query.size * 2, transcendentals=0
        ),
        name="attend_back",
    )(query, *operands, bias, grad_attended)


def ffn_forward(normed, inner_parts, outer_parts, residual):
    kept = []
    total = residual
    for inner, outer in zip(inner_parts, outer_parts):
        act, slope = gelu_pair(product(normed, inner))
        act = act.astype(bf16)
        kept.append((act, slope.astype(bf16)))
        total = total + product(act, outer)
    return total, kept


def ffn_backward(kept, inner_parts, outer_parts, grad_branch):
    grad_pres = []
    grad_normed = None
    for (act, slope), inner, outer in zip(kept, inner_parts, outer_parts):
        grad_pre = (product_bt(grad_branch, outer) * slope.astype(f32)).astype(bf16)
        grad_pres.append(grad_pre)
        piece = product_bt(grad_pre, inner)
        grad_normed = piece if grad_normed is None else grad_normed + piece
    return grad_pres, grad_normed


def reduce_slices(own, core, chip, both):
    got_both = swap_core(both().astype(bf16))
    got_core = swap_core(core().astype(bf16))
    got_chip = swap_chip((chip() + got_both.astype(f32)).astype(bf16))
    return own() + got_core.astype(f32) + got_chip.astype(f32)


def per_device(
    block_input,
    segment_ids,
    assignment,
    norm_attn,
    weight_qkv,
    weight_proj,
    norm_ffn,
    weight_up,
    weight_down,
    centroids,
    expert_norms,
    expert_in,
    expert_out,
    grad_out,
):
    row_count, local_len, model_width = block_input.shape
    token_count = row_count * local_len
    seq_devices = lax.axis_size("seq")
    seq_index = lax.axis_index("seq")
    experts = lax.axis_size("wide")
    devices = seq_devices * experts
    every = ("seq", "wide")
    shard = weight_up.shape[0]
    hidden_width = weight_up.shape[1]

    gains_own = jnp.stack([norm_attn, norm_ffn]).astype(f32)
    gains_all = lax.all_to_all(
        jnp.broadcast_to(gains_own[None], (devices, 2, shard)), every, 0, 0, tiled=True
    )
    gains_all = gains_all.transpose(1, 0, 2).reshape(2, model_width)
    gain_attn = gains_all[0]
    gain_ffn = gains_all[1]

    qkv_full = lax.all_gather(weight_qkv, every, axis=0, tiled=True)
    up_own = (
        weight_up.reshape(shard, devices, BLOCKS, shard)
        .transpose(0, 2, 1, 3)
        .reshape(shard, hidden_width)
    )
    down_own = weight_down.reshape(BLOCKS, shard, model_width).transpose(1, 0, 2)
    rest_own = jnp.concatenate(
        [weight_proj, up_own, down_own.reshape(shard, BLOCKS * model_width)], axis=1
    )
    rest_full = lax.all_gather(rest_own, every, axis=0, tiled=True)

    def rest_block(index):
        return rest_full[:, index * model_width : (index + 1) * model_width]

    proj_full = rest_block(0)
    up_parts = [rest_block(1 + index) for index in range(BLOCKS)]
    down_parts = [rest_block(1 + BLOCKS + index) for index in range(BLOCKS)]

    inner_own = expert_in[0]
    outer_own = expert_out[0]
    inner_core = swap_core(inner_own)
    outer_core = swap_core(outer_own)
    inner_chip = swap_chip(inner_own)
    inner_both = swap_core(inner_chip)

    capacity = token_count // experts
    chosen = assignment.reshape(token_count)
    one_hot = (chosen[:, None] == jnp.arange(experts, dtype=jnp.int32)[None, :]).astype(jnp.int32)
    rank_within = jnp.sum((jnp.cumsum(one_hot, axis=0) - 1) * one_hot, axis=1)
    slot_index = chosen * capacity + rank_within
    source_of = (
        jnp.zeros((token_count,), jnp.int32)
        .at[slot_index]
        .set(jnp.arange(token_count, dtype=jnp.int32))
    )

    tokens_flat = block_input.reshape(token_count, model_width).astype(f32)
    normed_attn = layer_norm(tokens_flat, gain_attn).astype(bf16)
    kv_own = product(normed_attn, qkv_full[:, model_width:]).astype(bf16)
    kv_own = kv_own.reshape(row_count, local_len, 2 * model_width)
    query = product(normed_attn, qkv_full[:, :model_width]).astype(bf16)
    query = query.reshape(row_count, local_len, model_width)

    kv_far = seq_send(kv_own, [(0, 2), (1, 3)])
    kv_near = seq_send(
        jnp.where(seq_index == 3, kv_far, kv_own), [(0, 1), (2, 3), (3, 2)]
    )
    kv_blocks = (kv_own, kv_near, kv_far)
    outer_late, _ = lax.optimization_barrier((outer_own, kv_far))
    outer_chip = swap_chip(outer_late)
    outer_both = swap_core(outer_chip)

    before = 2 * local_len
    offset = seq_index * local_len
    padded_seg = jnp.pad(segment_ids, ((0, 0), (before, 0)), constant_values=-1)
    key_seg = lax.dynamic_slice_in_dim(padded_seg, offset, before + local_len, 1)
    query_seg = key_seg[:, before:]
    key_pos = jnp.arange(before + local_len)
    query_pos = before + jnp.arange(local_len)
    allowed = (key_seg[:, :, None] == query_seg[:, None, :]) & (
        key_pos[None, :, None] <= query_pos[None, None, :]
    )
    bias = jnp.where(allowed, 0.0, -1e30).astype(f32)

    attended_rows = attend(query, kv_blocks, bias)
    attended = attended_rows.reshape(token_count, model_width)
    hidden = tokens_flat + product(attended, proj_full)
    normed_ffn = layer_norm(hidden, gain_ffn).astype(bf16)
    dense_out, dense_kept = ffn_forward(normed_ffn, up_parts, down_parts, hidden)
    routed = dense_out.astype(bf16)

    received = lax.all_to_all(routed[source_of], "wide", split_axis=0, concat_axis=0, tiled=True)
    received_f = received.astype(f32)
    centroid_row = centroids[0]
    centroid_f = centroid_row.astype(f32)
    logit_row = jnp.dot(received, centroid_row, preferred_element_type=f32)
    gate_value = jax.nn.sigmoid(logit_row)
    gains_f = expert_norms[0].astype(f32)
    state_now = received_f
    kept_layers = []
    slices = []
    for sublayer in range(2):
        inner_parts = [part[sublayer] for part in (inner_own, inner_core, inner_chip, inner_both)]
        outer_parts = [part[sublayer] for part in (outer_own, outer_core, outer_chip, outer_both)]
        normed = layer_norm(state_now, gains_f[sublayer]).astype(bf16)
        state_next, kept = ffn_forward(normed, inner_parts, outer_parts, state_now)
        kept_layers.append((state_now, normed, kept))
        slices.append((inner_parts, outer_parts))
        state_now = state_next
    returned = (gate_value[:, None] * state_now).astype(bf16)
    back_rows = lax.all_to_all(returned, "wide", split_axis=0, concat_axis=0, tiled=True)
    output = (
        (dense_out + back_rows[slot_index].astype(f32)).astype(bf16).reshape(block_input.shape)
    )
    gate_sum = jnp.sum(gate_value)
    score_sum = jnp.sum(logit_row * logit_row)
    grad_flat = grad_out.reshape(token_count, model_width)
    grad_back = lax.all_to_all(
        grad_flat[source_of], "wide", split_axis=0, concat_axis=0, tiled=True
    )
    grad_ret = grad_back.astype(f32)
    grad_gate = jnp.sum(grad_ret * state_now, axis=-1)
    grad_state = grad_ret * gate_value[:, None]
    inner_grads = [None, None]
    outer_grads = [None, None]
    gain_grads = [None, None]
    for sublayer in (1, 0):
        state_in, normed_in, kept = kept_layers[sublayer]
        inner_parts, outer_parts = slices[sublayer]
        grad_branch = grad_state.astype(bf16)
        grad_pres, grad_normed = ffn_backward(kept, inner_parts, outer_parts, grad_branch)
        outer_grads[sublayer] = reduce_slices(
            *[functools.partial(product_at, act, grad_branch) for act, _ in kept]
        )
        inner_grads[sublayer] = reduce_slices(
            *[functools.partial(product_at, normed_in, grad_pre) for grad_pre in grad_pres]
        )
        grad_resid, gain_grad = norm_back(state_in, gains_f[sublayer], grad_normed)
        grad_state = grad_state + grad_resid
        gain_grads[sublayer] = gain_grad
    grad_logit = grad_gate * gate_value * (1.0 - gate_value)
    grad_routed = (grad_state + grad_logit[:, None] * centroid_f[None, :]).astype(bf16)
    centroid_grad = jnp.dot(grad_logit, received_f, precision=highest)
    returned_grad = lax.all_to_all(grad_routed, "wide", split_axis=0, concat_axis=0, tiled=True)
    grad_dense = grad_flat.astype(f32) + returned_grad[slot_index].astype(f32)

    grad_down_in = grad_dense.astype(bf16)
    grad_pres, grad_normed_ffn = ffn_backward(dense_kept, up_parts, down_parts, grad_down_in)
    grad_hidden_norm, grad_gain_ffn = norm_back(hidden, gain_ffn, grad_normed_ffn)
    grad_hidden = grad_dense + grad_hidden_norm
    grad_proj = grad_hidden.astype(bf16)
    rest_grad = jnp.concatenate(
        [product_at(attended, grad_proj).astype(bf16)]
        + [product_at(normed_ffn, grad_pre).astype(bf16) for grad_pre in grad_pres]
        + [product_at(act, grad_down_in).astype(bf16) for act, _ in dense_kept],
        axis=1,
    )
    rest_sum = lax.psum_scatter(rest_grad, every, scatter_dimension=0, tiled=True).astype(f32)
    grad_attended = product_bt(grad_proj, proj_full).astype(bf16)
    grad_query, grad_kv0, grad_kv1, grad_kv2 = attend_back(
        query, kv_blocks, bias, grad_attended.reshape(query.shape)
    )
    got_near = seq_send(grad_kv1, [(1, 0), (3, 2), (2, 3)])
    far_sum = jnp.where(
        seq_index == 3, (grad_kv2.astype(f32) + got_near.astype(f32)).astype(bf16), grad_kv2
    )
    got_far = seq_send(far_sum, [(2, 0), (3, 1)])
    kv_sum = grad_kv0.astype(f32) + got_far.astype(f32)
    kv_sum = kv_sum + jnp.where(seq_index % 2 == 0, got_near.astype(f32), 0.0)
    kv_sum = kv_sum.astype(bf16).reshape(2, token_count, model_width)
    grad_qkv = [grad_query.reshape(token_count, model_width), kv_sum[0], kv_sum[1]]
    qkv_grad = jnp.concatenate(
        [product_at(normed_attn, part).astype(bf16) for part in grad_qkv], axis=1
    )
    qkv_sum = lax.psum_scatter(qkv_grad, every, scatter_dimension=0, tiled=True).astype(f32)
    grad_normed_attn = sum(
        product_bt(part, qkv_full[:, index * model_width : (index + 1) * model_width])
        for index, part in enumerate(grad_qkv)
    )
    grad_input_norm, grad_gain_attn = norm_back(tokens_flat, gain_attn, grad_normed_attn)
    grad_input = (grad_hidden + grad_input_norm).reshape(block_input.shape)

    gain_terms = jnp.stack([grad_gain_attn, grad_gain_ffn]).reshape(2, devices, shard)
    gain_terms = lax.all_to_all(gain_terms.transpose(1, 0, 2), every, 0, 0, tiled=True)
    gain_sums = jnp.sum(gain_terms, axis=0)
    expert_totals = lax.psum(
        (jnp.stack(gain_grads), centroid_grad, jnp.stack([gate_sum, score_sum])), "seq"
    )
    up_grad = (
        rest_sum[:, model_width : model_width + hidden_width]
        .reshape(shard, BLOCKS, devices, shard)
        .transpose(0, 2, 1, 3)
        .reshape(shard, hidden_width)
    )
    down_grad = (
        rest_sum[:, model_width + hidden_width :]
        .reshape(shard, BLOCKS, model_width)
        .transpose(1, 0, 2)
        .reshape(BLOCKS * shard, model_width)
    )
    token_total = token_count * seq_devices
    return (
        output,
        grad_input,
        gain_sums[0],
        qkv_sum,
        rest_sum[:, :model_width],
        gain_sums[1],
        up_grad,
        down_grad,
        expert_totals[1][None],
        expert_totals[0][None],
        jnp.stack(inner_grads)[None],
        jnp.stack(outer_grads)[None],
        (expert_totals[2][0] / token_total)[None],
        (expert_totals[2][1] / token_total)[None],
    )


def solution(mesh):
    in_specs = (
        P("wide", "seq", None),
        P("wide", None),
        P("wide", "seq"),
        P(("seq", "wide")),
        P(("seq", "wide"), None),
        P(("seq", "wide"), None),
        P(("seq", "wide")),
        P(("seq", "wide"), None),
        P(("seq", "wide"), None),
        P("wide", None),
        P("wide", None, None),
        P("wide", None, None, "seq"),
        P("wide", None, "seq", None),
        P("wide", "seq", None),
    )
    out_specs = (
        P("wide", "seq", None),
        P("wide", "seq", None),
        P(("seq", "wide")),
        P(("seq", "wide"), None),
        P(("seq", "wide"), None),
        P(("seq", "wide")),
        P(("seq", "wide"), None),
        P(("seq", "wide"), None),
        P("wide", None),
        P("wide", None, None),
        P("wide", None, None, "seq"),
        P("wide", None, "seq", None),
        P("wide"),
        P("wide"),
    )
    return jax.shard_map(
        per_device, mesh=mesh, in_specs=in_specs, out_specs=out_specs, check_vma=False
    )
```

time: 2240 us -> 1100 us (0.49)
  waiting for transfers between devices: 1600 us -> 529 us
  matrix products: 354 us -> 261 us
  blocking collectives: 97.1 us -> 11.7 us
  Pallas kernels: 0 us -> 62.9 us
  starting transfers between devices: 19.9 us -> 52.7 us
    reduce_scatter x9 -> x0, waiting for transfers between devices: 1190 us -> none  [the longest x1 360 us: per_device(): lax.psum_scatter(grad_w_down, ('seq', 'wide'), scatter_dimension=0, tiled...]
    ppermute x0 -> x22, waiting for transfers between devices: none -> 437 us  [seq_send(): return lax.ppermute(values, 'seq', pairs)]
    all_gather x7 -> x2, waiting for transfers between devices: 345 us -> 53.1 us  [the longest x1 53.1 us: per_device(): qkv_full = lax.all_gather(weight_qkv, every, axis=0, tiled=True)]
    dot_general x53 -> x84, matrix products: 353 us -> 260 us  [the longest x28 89.3 us: product_bt(): lax.dot_general(left_side, right_side, (((1,), (1,)), ((), ())), preferre...]
    unnamed x2 -> x0, blocking collectives: 84.4 us -> none
    pallas_call x0 -> x2, Pallas kernels: none -> 62.9 us  [the longest x1 36.2 us: attend_back(): pl.pallas_call(functools.partial(attend_back_kernel, 1.0 / math.sqrt(HEAD...]
    all_to_all x1, waiting for transfers between devices: 22.7 us -> 0.01 us  [per_device(): lax.all_to_all(routed[source_of], 'wide', split_axis=0, concat_axis=0, ti...]
    unnamed x194 -> x283, local copies, waits for them, and re-layouts: 32.9 us -> 47.1 us
  transfers between devices with their start and end apart: 20 -> 32, of which waited for: 18 -> 14; matrix products, arithmetic and copies ran while one was open for 13% -> 22% of each run, Pallas kernels for 0% -> 2%
where the time goes in v1:
time: 1100 us; the launch traced here: 1090 us
  waiting for transfers between devices  529 us (48%)
  matrix products  261 us (24%)
  local copies, waits for them, and re-layouts  78.5 us (7%)
  other arithmetic  75.8 us (7%)
  Pallas kernels  62.9 us (6%)
  starting transfers between devices  52.7 us (5%)
  between operations  19.5 us (2%)
  blocking collectives  11.7 us (1%)
    ppermute x22, waiting for transfers between devices, seq_send(): return lax.ppermute(values, 'seq', pairs)  437 us
    dot_general x28, matrix products, product_bt(): lax.dot_general(left_side, right_side, (((1,), (1,)), ((), ())), preferre...  89.3 us
    dot_general x28, matrix products, product_at(): lax.dot_general(left_side, right_side, (((0,), (0,)), ((), ())), preferre...  86.7 us
    dot_general x27, matrix products, product(): return jnp.dot(left_side, right_side, preferred_element_type=f32)  83.9 us
    all_gather x1, waiting for transfers between devices, per_device(): qkv_full = lax.all_gather(weight_qkv, every, axis=0, tiled=True)  53.1 us
    unnamed x283, local copies, waits for them, and re-layouts  47.1 us
    pallas_call x1, Pallas kernels, attend_back(): pl.pallas_call(functools.partial(attend_back_kernel, 1.0 / math.sqrt(HEAD...  36.2 us
    pallas_call x1, Pallas kernels, attend(): pl.pallas_call(functools.partial(attend_kernel, 1.0 / math.sqrt(HEAD_DIM)...  26.7 us
  transfers between devices with their start and end apart: 32, of which 14 were waited for; matrix products, arithmetic and copies ran while one was open for 22% of the time, Pallas kernels for 2%

profile of v1, /device:TPU:0, one launch (start us, length us, event | category | flops | bytes accessed | tf_op | source)
XLA Modules:
  0.0 1091.2 jit_solution(8672386106885318962)
XLA Ops:
  13.9 7.3 all-to-all-start
  22.5 5.9 all-to-all-done
  30.0 53.1 %all-gather.3.cloned.1.call-done = bf16[1024,3072]{1,0:T(8,128)(2,1)} async-done(((bf16[32,3072]{1,0:T(8,128)(2,1)}), bf16[1024,3072]{1,0:T(8,128)(2,1)}) %all-gather.3.cloned.1.call-update) | async-done | bytes 6291472 | tf_op jit(solution)/shard_map/all_gather | solution.py:221
  83.0 4.8 fusion.6
  87.9 4.7 collective-permute-start
  92.6 57.3 %collective-permute-done.k2.v2 = bf16[2,256,2048]{2,1,0:T(8,128)(2,1)} collective-permute-done((bf16[2,256,2048]{2,1,0:T(8,128)(2,1)S(1)}, bf16[2,256,2048]{2,1,0:T(8,128)(2,1)}, u32[]{:S(2)}, u32[]{:S(2)}) %collective-permute-start) | collective-permute-done | bytes 2097184 | tf_op jit(solution)/shard_map/ppermute | solution.py:55
  159.9 113.0 %collective-permute-done.4 = bf16[2,1024,1024]{2,1,0:T(8,128)(2,1)} collective-permute-done((bf16[2,1024,1024]{2,1,0:T(8,128)(2,1)}, bf16[2,1024,1024]{2,1,0:T(8,128)(2,1)}, u32[]{:S(2)}, u32[]{:S(2)}) %collective-permute-start.4) | collective-permute-done | bytes 4194336 | tf_op jit(solution)/shard_map/ppermute | solution.py:55
  279.2 26.7 %attend.1 = bf16[2,256,1024]{2,1,0:T(8,128)(2,1)} custom-call(bf16[2,256,1024]{2,1,0:T(8,128)(2,1)} %bitcast.428, bf16[2,256,2048]{2,1,0:T(8,128)(2,1)} %bitcast.374, bf16[2,256,2048]{2,1,0:T(8,128)(2,1)} %bitcast.375, bf16[2,256,2048]{2,1,0:T(8,128)(2,1)} %collective-permute-done.1.k1.v1, bf16[2,256,2048]{2,1,0:T(8,128)(2,1)} %collective-permute-done.1.k1.v1, ...), custom_call_target="tpu_custom_call" | custom-call | flops 9663676416 | bytes 8388608 | tf_op jit(solution)/shard_map/attend/pallas_call | solution.py:125
  335.3 35.4 %collective-permute-done.5 = bf16[2,1024,1024]{2,1,0:T(8,128)(2,1)} collective-permute-done((bf16[2,1024,1024]{2,1,0:T(8,128)(2,1)}, bf16[2,1024,1024]{2,1,0:T(8,128)(2,1)}, u32[]{:S(2)}, u32[]{:S(2)}) %collective-permute-start.5) | collective-permute-done | bytes 4194336 | tf_op jit(solution)/shard_map/ppermute | solution.py:55
  387.3 5.0 multiply_convert_fusion.19
  408.5 4.6 multiply_convert_fusion.16
  463.3 5.0 fusion.32
  472.1 4.6 fusion.45
  503.5 6.0 all-to-all-start.4
  509.7 26.1 %all-to-all-done.4 = bf16[8,64,1024]{2,1,0:T(8,128)(2,1)S(1)} async-done(((bf16[8,64,1024]{2,1,0:T(8,128)(2,1)}), bf16[8,64,1024]{2,1,0:T(8,128)(2,1)S(1)}, u32[]{:S(2)}, u32[]{:S(2)}) %all-to-all-start.4) | async-done | bytes 1048608 | tf_op jit(solution)/shard_map/all_to_all | solution.py:345
  566.2 36.2 %attend_back.1 = (bf16[2,256,1024]{2,1,0:T(8,128)(2,1)}, bf16[2,2,256,1024]{3,2,1,0:T(8,128)(2,1)}, bf16[2,2,256,1024]{3,2,1,0:T(8,128)(2,1)}, bf16[2,2,256,1024]{3,2,1,0:T(8,128)(2,1)}) custom-call(bf16[2,256,1024]{2,1,0:T(8,128)(2,1)} %bitcast.429, bf16[2,256,2048]{2,1,0:T(8,128)(2,1)} %bitcast.376, bf16[2,256,2048]{2,1,0:T(8,128)(2,1)} %bitcast.377, ...), custom_call_target="tpu_custom_call" | custom-call | flops 24159191040 | bytes 16777216 | tf_op jit(solution)/shard_map/attend_back/pallas_call | solution.py:145
  603.7 5.0 collective-permute-done.8
  608.7 5.8 fusion.5
  619.0 45.4 %collective-permute-done.9 = bf16[2,2,256,1024]{3,2,1,0:T(8,128)(2,1)} collective-permute-done((bf16[2,2,256,1024]{3,2,1,0:T(8,128)(2,1)}, bf16[2,2,256,1024]{3,2,1,0:T(8,128)(2,1)}, u32[]{:S(2)}, u32[]{:S(2)}) %collective-permute-start.9) | collective-permute-done | bytes 2097184 | tf_op jit(solution)/shard_map/ppermute | solution.py:55
  670.4 13.4 %pad_maximum_fusion = bf16[1024,3072]{0,1:T(8,128)(2,1)} fusion(bf16[1024,1024]{0,1:T(8,128)(2,1)S(1)} %convolution_convert_fusion.8, bf16[1024,1024]{0,1:T(8,128)(2,1)S(1)} %convolution_convert_fusion.9, bf16[1024,1024]{0,1:T(8,128)(2,1)S(1)} %bitcast_convert_fusion), kind=kLoop, calls=%fused_computation.7 | loop fusion | flops 18874368 | bytes 12582912 | tf_op jit(solution)/shard_map/concatenate | solution.py:373
  683.8 8.6 copy.48
  692.7 4.7 convert_dynamic-update-slice_fusion.8
  719.1 24.9 %copy.50 = bf16[1024,9216]{1,0:T(8,128)(2,1)} copy(bf16[1024,9216]{0,1:T(8,128)(2,1)} %convert_dynamic-update-slice_fusion) | data formatting | bytes 37748736
  780.4 11.7 %all-reduce.1 = (f32[1,1024]{1,0:T(1,128)}, f32[1,2,1024]{2,1,0:T(2,128)}, f32[2]{0:T(128)S(1)}) all-reduce(f32[1,1024]{1,0:T(1,128)S(1)} %fusion.186, f32[1,2,1024]{2,1,0:T(2,128)S(1)} %maximum_bitcast_fusion.3, f32[2]{0:T(128)S(1)} %pad_maximum_fusion.2), channel_id=1, replica_groups=mesh['seq'=4,'wide'=8] {'seq'}, use_global_device_ids=true, to_apply=%region_26.27 | all-reduce | flops 3074 | bytes 24592 | tf_op jit(solution)/shard_map/psum | solution.py:387
  792.1 4.9 fusion.190
  815.0 4.7 fusion.123
  830.1 21.5 %collective-permute-done.15 = bf16[1024,1024]{1,0:T(8,128)(2,1)} collective-permute-done((bf16[1024,1024]{1,0:T(8,128)(2,1)}, bf16[1024,1024]{1,0:T(8,128)(2,1)}, u32[]{:S(2)}, u32[]{:S(2)}) %collective-permute-start.15) | collective-permute-done | bytes 2097184 | tf_op jit(solution)/shard_map/ppermute | solution.py:55
  854.7 5.3 add_bitcast_fusion.2
  860.0 44.0 %collective-permute-done.12 = bf16[1024,1024]{1,0:T(8,128)(2,1)} collective-permute-done((bf16[1024,1024]{1,0:T(8,128)(2,1)}, bf16[1024,1024]{1,0:T(8,128)(2,1)}, u32[]{:S(2)}, u32[]{:S(2)}) %collective-permute-start.12) | collective-permute-done | bytes 2097184 | tf_op jit(solution)/shard_map/ppermute | solution.py:55
  911.8 57.8 %collective-permute-done.21 = bf16[1024,1024]{1,0:T(8,128)(2,1)} collective-permute-done((bf16[1024,1024]{1,0:T(8,128)(2,1)}, bf16[1024,1024]{1,0:T(8,128)(2,1)}, u32[]{:S(2)}, u32[]{:S(2)}) %collective-permute-start.21) | collective-permute-done | bytes 2097184 | tf_op jit(solution)/shard_map/ppermute | solution.py:55
  973.4 57.0 %collective-permute-done.18 = bf16[1024,1024]{1,0:T(8,128)(2,1)} collective-permute-done((bf16[1024,1024]{1,0:T(8,128)(2,1)}, bf16[1024,1024]{1,0:T(8,128)(2,1)}, u32[]{:S(2)}, u32[]{:S(2)}) %collective-permute-start.18) | collective-permute-done | bytes 2097184 | tf_op jit(solution)/shard_map/ppermute | solution.py:55
  1045.4 8.1 all-to-all-start.5
  (511 shorter events, 352.9 us)
Async XLA Ops:
  7.2 75.9 %all-gather.3.cloned.1.call-start = ((), (), s32[]{:S(2)}) async-start(), calls=%async_computation.8 | async-start | bytes 6488064 | tf_op jit(solution)/shard_map/all_gather | solution.py:221
  7.9 298.0 %all-gather.5.cloned.1.call-start = ((), (), s32[]{:S(2)}) async-start(), calls=%async_computation.9 | async-start | bytes 19464192 | tf_op jit(solution)/shard_map/all_gather | solution.py:231
  13.9 14.5 %all-to-all-start = ((f32[32,2,32]{2,1,0:T(2,128)}), f32[32,2,32]{2,1,0:T(2,128)S(1)}, u32[]{:S(2)}, u32[]{:S(2)}) async-start(f32[32,2,32]{2,1,0:T(2,128)} %broadcast_in_dim.39), calls=%async_computation | async-start | bytes 65536 | tf_op jit(solution)/shard_map/all_to_all | solution.py:214
  87.9 62.0 %collective-permute-start = (bf16[2,256,2048]{2,1,0:T(8,128)(2,1)S(1)}, bf16[2,256,2048]{2,1,0:T(8,128)(2,1)}, u32[]{:S(2)}, u32[]{:S(2)}) collective-permute-start(bf16[2,256,2048]{2,1,0:T(8,128)(2,1)S(1)} %bitcast.372), channel_id=1, source_target_pairs={{0,16},{8,24},{1,17},{9,25},{2,18},{10,26},{3,19},{11,27},{4,20},{... | collective-permute-start | bytes 6291464 | tf_op jit(solution)/shard_map/ppermute | solution.py:55
  92.6 180.3 %collective-permute-start.4 = (bf16[2,1024,1024]{2,1,0:T(8,128)(2,1)}, bf16[2,1024,1024]{2,1,0:T(8,128)(2,1)}, u32[]{:S(2)}, u32[]{:S(2)}) collective-permute-start(bf16[2,1024,1024]{2,1,0:T(8,128)(2,1)} %bitcast.21), channel_id=1, source_target_pairs={{0,16},{16,0},{8,24},{24,8},{1,17},{17,1},{9,25},{25,9},{2,18},{18... | collective-permute-start | bytes 12582920 | tf_op jit(solution)/shard_map/ppermute | solution.py:55
  151.5 127.7 %collective-permute-start.1 = (bf16[2,256,2048]{2,1,0:T(8,128)(2,1)}, bf16[2,256,2048]{2,1,0:T(8,128)(2,1)}, u32[]{:S(2)}, u32[]{:S(2)}) collective-permute-start(bf16[2,256,2048]{2,1,0:T(8,128)(2,1)} %broadcast_select_fusion), channel_id=1, source_target_pairs={{0,8},{16,24},{24,16},{1,9},{17,25},{25,17},{2,10},{18,26},{26,18}... | collective-permute-start | bytes 6291464 | tf_op jit(solution)/shard_map/ppermute | solution.py:55
  272.9 111.5 %collective-permute-start.6 = (bf16[2,1024,1024]{2,1,0:T(8,128)(2,1)}, bf16[2,1024,1024]{2,1,0:T(8,128)(2,1)}, u32[]{:S(2)}, u32[]{:S(2)}) collective-permute-start(bf16[2,1024,1024]{2,1,0:T(8,128)(2,1)} %collective-permute-done.4), channel_id=1, source_target_pairs={{0,8},{8,0},{16,24},{24,16},{1,9},{9,1},{17,25},{25,17},{2,10},{10... | collective-permute-start | bytes 12582920 | tf_op jit(solution)/shard_map/ppermute | solution.py:55
  276.7 94.0 %collective-permute-start.5 = (bf16[2,1024,1024]{2,1,0:T(8,128)(2,1)}, bf16[2,1024,1024]{2,1,0:T(8,128)(2,1)}, u32[]{:S(2)}, u32[]{:S(2)}) collective-permute-start(bf16[2,1024,1024]{2,1,0:T(8,128)(2,1)} %bitcast.23), channel_id=1, source_target_pairs={{0,16},{16,0},{8,24},{24,8},{1,17},{17,1},{9,25},{25,9},{2,18},{18... | collective-permute-start | bytes 12582920 | tf_op jit(solution)/shard_map/ppermute | solution.py:55
  328.2 42.6 %all-to-all-start.1 = ((bf16[8,64,1024]{2,1,0:T(8,128)(2,1)}), bf16[8,64,1024]{2,1,0:T(8,128)(2,1)S(1)}, u32[]{:S(2)}, u32[]{:S(2)}) async-start(bf16[8,64,1024]{2,1,0:T(8,128)(2,1)} %bitcast.14), calls=%async_computation.1 | async-start | bytes 2097152 | tf_op jit(solution)/shard_map/all_to_all | solution.py:293
  331.9 63.7 %collective-permute-start.2 = (bf16[2,1024,1024]{2,1,0:T(8,128)(2,1)}, bf16[2,1024,1024]{2,1,0:T(8,128)(2,1)}, u32[]{:S(2)}, u32[]{:S(2)}) collective-permute-start(bf16[2,1024,1024]{2,1,0:T(8,128)(2,1)} %bitcast.21), channel_id=1, source_target_pairs={{0,8},{8,0},{16,24},{24,16},{1,9},{9,1},{17,25},{25,17},{2,10},{10... | collective-permute-start | bytes 12582920 | tf_op jit(solution)/shard_map/ppermute | solution.py:55
  332.2 67.7 %collective-permute-start.3 = (bf16[2,1024,1024]{2,1,0:T(8,128)(2,1)}, bf16[2,1024,1024]{2,1,0:T(8,128)(2,1)}, u32[]{:S(2)}, u32[]{:S(2)}) collective-permute-start(bf16[2,1024,1024]{2,1,0:T(8,128)(2,1)} %bitcast.23), channel_id=1, source_target_pairs={{0,8},{8,0},{16,24},{24,16},{1,9},{9,1},{17,25},{25,17},{2,10},{10... | collective-permute-start | bytes 12582920 | tf_op jit(solution)/shard_map/ppermute | solution.py:55
  370.8 32.4 %collective-permute-start.7 = (bf16[2,1024,1024]{2,1,0:T(8,128)(2,1)}, bf16[2,1024,1024]{2,1,0:T(8,128)(2,1)}, u32[]{:S(2)}, u32[]{:S(2)}) collective-permute-start(bf16[2,1024,1024]{2,1,0:T(8,128)(2,1)} %collective-permute-done.5), channel_id=1, source_target_pairs={{0,8},{8,0},{16,24},{24,16},{1,9},{9,1},{17,25},{25,17},{2,10},{10... | collective-permute-start | bytes 12582920 | tf_op jit(solution)/shard_map/ppermute | solution.py:55
  370.8 42.4 %all-to-all-start.3 = ((bf16[8,64,1024]{2,1,0:T(8,128)(2,1)}), bf16[8,64,1024]{2,1,0:T(8,128)(2,1)S(1)}, u32[]{:S(2)}, u32[]{:S(2)}) async-start(bf16[8,64,1024]{2,1,0:T(8,128)(2,1)} %bitcast.367), calls=%async_computation.3 | async-start | bytes 2097152 | tf_op jit(solution)/shard_map/all_to_all | solution.py:319
  503.5 32.2 %all-to-all-start.4 = ((bf16[8,64,1024]{2,1,0:T(8,128)(2,1)}), bf16[8,64,1024]{2,1,0:T(8,128)(2,1)S(1)}, u32[]{:S(2)}, u32[]{:S(2)}) async-start(bf16[8,64,1024]{2,1,0:T(8,128)(2,1)} %bitcast.371), calls=%async_computation.4 | async-start | bytes 2097152 | tf_op jit(solution)/shard_map/all_to_all | solution.py:345
  509.6 552.0 %reduce-scatter.7.cloned.1.call-start = ((), (), s32[]{:S(2)}) async-start(), calls=%async_computation.10 | async-start | bytes 6488064
  602.4 6.3 collective-permute-start.8
  614.5 49.9 %collective-permute-start.9 = (bf16[2,2,256,1024]{3,2,1,0:T(8,128)(2,1)}, bf16[2,2,256,1024]{3,2,1,0:T(8,128)(2,1)}, u32[]{:S(2)}, u32[]{:S(2)}) collective-permute-start(bf16[2,2,256,1024]{3,2,1,0:T(8,128)(2,1)} %fusion.5), channel_id=1, source_target_pairs={{16,0},{24,8},{17,1},{25,9},{18,2},{26,10},{19,3},{27,11},{20,4},{... | collective-permute-start | bytes 6291464 | tf_op jit(solution)/shard_map/ppermute | solution.py:55
  692.4 375.3 %reduce-scatter.9.cloned.1.call-start = ((), (), s32[]{:S(2)}) async-start(), calls=%async_computation.11 | async-start | bytes 19464192
  744.0 68.9 %all-to-all-start.2 = ((bf16[8,64,1024]{2,1,0:T(8,128)(2,1)}), bf16[8,64,1024]{2,1,0:T(8,128)(2,1)S(1)}, u32[]{:S(2)}, u32[]{:S(2)}) async-start(bf16[8,64,1024]{2,1,0:T(8,128)(2,1)} %bitcast.366), calls=%async_computation.2 | async-start | bytes 2097152 | tf_op jit(solution)/shard_map/all_to_all | solution.py:312
  752.0 45.1 %collective-permute-start.14 = (bf16[1024,1024]{1,0:T(8,128)(2,1)}, bf16[1024,1024]{1,0:T(8,128)(2,1)}, u32[]{:S(2)}, u32[]{:S(2)}) collective-permute-start(bf16[1024,1024]{1,0:T(8,128)(2,1)} %convolution_convert_fusion.4), channel_id=1, source_target_pairs={{0,8},{8,0},{16,24},{24,16},{1,9},{9,1},{17,25},{25,17},{2,10},{10... | collective-permute-start | bytes 6291464 | tf_op jit(solution)/shard_map/ppermute | solution.py:55
  765.8 58.2 %collective-permute-start.13 = (bf16[1024,1024]{1,0:T(8,128)(2,1)}, bf16[1024,1024]{1,0:T(8,128)(2,1)}, u32[]{:S(2)}, u32[]{:S(2)}) collective-permute-start(bf16[1024,1024]{1,0:T(8,128)(2,1)} %convolution_convert_fusion.5), channel_id=1, source_target_pairs={{0,8},{8,0},{16,24},{24,16},{1,9},{9,1},{17,25},{25,17},{2,10},{10... | collective-permute-start | bytes 6291464 | tf_op jit(solution)/shard_map/ppermute | solution.py:55
  766.3 35.0 %collective-permute-start.11 = (bf16[1024,1024]{1,0:T(8,128)(2,1)}, bf16[1024,1024]{1,0:T(8,128)(2,1)}, u32[]{:S(2)}, u32[]{:S(2)}) collective-permute-start(bf16[1024,1024]{1,0:T(8,128)(2,1)} %convolution_convert_fusion.6), channel_id=1, source_target_pairs={{0,8},{8,0},{16,24},{24,16},{1,9},{9,1},{17,25},{25,17},{2,10},{10... | collective-permute-start | bytes 6291464 | tf_op jit(solution)/shard_map/ppermute | solution.py:55
  766.4 63.5 %collective-permute-start.10 = (bf16[1024,1024]{1,0:T(8,128)(2,1)}, bf16[1024,1024]{1,0:T(8,128)(2,1)}, u32[]{:S(2)}, u32[]{:S(2)}) collective-permute-start(bf16[1024,1024]{1,0:T(8,128)(2,1)} %convolution_convert_fusion.7), channel_id=1, source_target_pairs={{0,8},{8,0},{16,24},{24,16},{1,9},{9,1},{17,25},{25,17},{2,10},{10... | collective-permute-start | bytes 6291464 | tf_op jit(solution)/shard_map/ppermute | solution.py:55
  766.9 43.7 %collective-permute-start.20 = (bf16[1024,1024]{1,0:T(8,128)(2,1)}, bf16[1024,1024]{1,0:T(8,128)(2,1)}, u32[]{:S(2)}, u32[]{:S(2)}) collective-permute-start(bf16[1024,1024]{1,0:T(8,128)(2,1)} %convolution_convert_fusion), channel_id=1, source_target_pairs={{0,8},{8,0},{16,24},{24,16},{1,9},{9,1},{17,25},{25,17},{2,10},{10... | collective-permute-start | bytes 6291464 | tf_op jit(solution)/shard_map/ppermute | solution.py:55
  797.0 27.1 %collective-permute-start.17 = (bf16[1024,1024]{1,0:T(8,128)(2,1)}, bf16[1024,1024]{1,0:T(8,128)(2,1)}, u32[]{:S(2)}, u32[]{:S(2)}) collective-permute-start(bf16[1024,1024]{1,0:T(8,128)(2,1)} %convolution_convert_fusion.2), channel_id=1, source_target_pairs={{0,8},{8,0},{16,24},{24,16},{1,9},{9,1},{17,25},{25,17},{2,10},{10... | collective-permute-start | bytes 6291464 | tf_op jit(solution)/shard_map/ppermute | solution.py:55
  801.3 50.3 %collective-permute-start.15 = (bf16[1024,1024]{1,0:T(8,128)(2,1)}, bf16[1024,1024]{1,0:T(8,128)(2,1)}, u32[]{:S(2)}, u32[]{:S(2)}) collective-permute-start(bf16[1024,1024]{1,0:T(8,128)(2,1)} %add_convert_fusion.2), channel_id=1, source_target_pairs={{0,16},{16,0},{8,24},{24,8},{1,17},{17,1},{9,25},{25,9},{2,18},{18... | collective-permute-start | bytes 6291464 | tf_op jit(solution)/shard_map/ppermute | solution.py:55
  810.6 93.5 %collective-permute-start.12 = (bf16[1024,1024]{1,0:T(8,128)(2,1)}, bf16[1024,1024]{1,0:T(8,128)(2,1)}, u32[]{:S(2)}, u32[]{:S(2)}) collective-permute-start(bf16[1024,1024]{1,0:T(8,128)(2,1)} %add_convert_fusion.3), channel_id=1, source_target_pairs={{0,16},{16,0},{8,24},{24,8},{1,17},{17,1},{9,25},{25,9},{2,18},{18... | collective-permute-start | bytes 6291464 | tf_op jit(solution)/shard_map/ppermute | solution.py:55
  824.1 87.8 %collective-permute-start.19 = (bf16[1024,1024]{1,0:T(8,128)(2,1)}, bf16[1024,1024]{1,0:T(8,128)(2,1)}, u32[]{:S(2)}, u32[]{:S(2)}) collective-permute-start(bf16[1024,1024]{1,0:T(8,128)(2,1)} %convolution_convert_fusion.1), channel_id=1, source_target_pairs={{0,8},{8,0},{16,24},{24,16},{1,9},{9,1},{17,25},{25,17},{2,10},{10... | collective-permute-start | bytes 6291464 | tf_op jit(solution)/shard_map/ppermute | solution.py:55
  824.1 145.6 %collective-permute-start.21 = (bf16[1024,1024]{1,0:T(8,128)(2,1)}, bf16[1024,1024]{1,0:T(8,128)(2,1)}, u32[]{:S(2)}, u32[]{:S(2)}) collective-permute-start(bf16[1024,1024]{1,0:T(8,128)(2,1)} %add_convert_fusion), channel_id=1, source_target_pairs={{0,16},{16,0},{8,24},{24,8},{1,17},{17,1},{9,25},{25,9},{2,18},{18... | collective-permute-start | bytes 6291464 | tf_op jit(solution)/shard_map/ppermute | solution.py:55
  830.0 143.4 %collective-permute-start.16 = (bf16[1024,1024]{1,0:T(8,128)(2,1)}, bf16[1024,1024]{1,0:T(8,128)(2,1)}, u32[]{:S(2)}, u32[]{:S(2)}) collective-permute-start(bf16[1024,1024]{1,0:T(8,128)(2,1)} %convolution_convert_fusion.3), channel_id=1, source_target_pairs={{0,8},{8,0},{16,24},{24,16},{1,9},{9,1},{17,25},{25,17},{2,10},{10... | collective-permute-start | bytes 6291464 | tf_op jit(solution)/shard_map/ppermute | solution.py:55
  851.6 178.8 %collective-permute-start.18 = (bf16[1024,1024]{1,0:T(8,128)(2,1)}, bf16[1024,1024]{1,0:T(8,128)(2,1)}, u32[]{:S(2)}, u32[]{:S(2)}) collective-permute-start(bf16[1024,1024]{1,0:T(8,128)(2,1)} %add_convert_fusion.1), channel_id=1, source_target_pairs={{0,16},{16,0},{8,24},{24,8},{1,17},{17,1},{9,25},{25,9},{2,18},{18... | collective-permute-start | bytes 6291464 | tf_op jit(solution)/shard_map/ppermute | solution.py:55
  1045.4 15.6 %all-to-all-start.5 = ((f32[32,2,32]{2,1,0:T(2,128)}), f32[32,2,32]{2,1,0:T(2,128)S(1)}, u32[]{:S(2)}, u32[]{:S(2)}) async-start(f32[32,2,32]{2,1,0:T(2,128)} %maximum_bitcast_fusion.2), calls=%async_computation.5 | async-start | bytes 65536 | tf_op jit(solution)/shard_map/all_to_all | solution.py:385
  (136 other events, 1441.0 us)
Sparse Core Ops, SparseCore 0:
  11.0 72.0 all-gather.2
  86.6 161.8 all-gather.4
  692.6 129.2 reduce-scatter.6
  828.2 239.5 reduce-scatter.8

commit v2 on v1

--- a/solution.py
+++ b/solution.py
@@ -5,6 +5,7 @@
 import jax.numpy as jnp
 from jax import lax
 from jax.experimental import pallas as pl
+from jax.experimental.layout import Layout, with_layout_constraint
 from jax.experimental.pallas import tpu as pltpu
 from jax.sharding import PartitionSpec as P
 
@@ -49,6 +50,14 @@
     return lax.dot_general(
         left_side, right_side, (((0,), (0,)), ((), ())), preferred_element_type=f32
     )
+
+
+def row_major(values):
+    return with_layout_constraint(values, Layout(major_to_minor=(0, 1)))
+
+
+def weight_grad(left_side, right_side):
+    return row_major(product_at(left_side, right_side).astype(bf16))
 
 
 def seq_send(values, pairs):
@@ -177,11 +186,214 @@
     return grad_pres, grad_normed
 
 
-def reduce_slices(own, core, chip, both):
-    got_both = swap_core(both().astype(bf16))
-    got_core = swap_core(core().astype(bf16))
-    got_chip = swap_chip((chip() + got_both.astype(f32)).astype(bf16))
-    return own() + got_core.astype(f32) + got_chip.astype(f32)
+class SliceSum:
+    def __init__(self, operands):
+        self.operands = operands
+
+    def terms(self):
+        return [weight_grad(left, right) for left, right in self.operands]
+
+    def send_core(self, terms):
+        self.own, core, self.chip, both = terms
+        self.got_core = swap_core(core)
+        self.got_both = swap_core(both)
+
+    def chip_sum(self):
+        return (self.chip.astype(f32) + self.got_both.astype(f32)).astype(bf16)
+
+    def send_chip(self, values):
+        self.got_chip = swap_chip(values)
+
+    def total(self):
+        return self.own.astype(f32) + self.got_core.astype(f32) + self.got_chip.astype(f32)
+
+
+def cube_bits():
+    bits = []
+    for axis in ("seq", "wide"):
+        count = lax.axis_size(axis).bit_length() - 1
+        bits += [(axis, bit) for bit in reversed(range(count))]
+    return bits
+
+
+def cube_orders(bits):
+    core = bits.index(("seq", 0))
+    chip = bits.index(("seq", 1))
+    wide = [place for place, (axis, _) in enumerate(bits) if axis == "wide"]
+    if len(wide) == 3:
+        far, near, across = wide
+        return (
+            (far, chip, near, across, core),
+            (near, across, far, chip, core),
+            (chip, far, across, near, core),
+        )
+    return (
+        (chip, *wide, core),
+        (*wide, chip, core),
+        (*wide[1:], chip, wide[0], core),
+    )
+
+
+def cube_place(bits):
+    index = {axis: lax.axis_index(axis) for axis in ("seq", "wide")}
+    mine = [lax.rem(index[axis] // (1 << bit), 2) for axis, bit in bits]
+
+    def partner(place):
+        axis, bit = bits[place]
+        other = dict(index)
+        other[axis] = index[axis] + (1 - 2 * mine[place]) * (1 << bit)
+        return (other["seq"], other["wide"])
+
+    return mine, partner
+
+
+def cube_barrier(bits, partner):
+    barrier = pltpu.get_barrier_semaphore()
+    for place in range(len(bits)):
+        pl.semaphore_signal(
+            barrier, inc=1, device_id=partner(place), device_id_type=pl.DeviceIdType.MESH
+        )
+    pl.semaphore_wait(barrier, len(bits))
+
+
+def gather_kernel(bits, orders, own_ref, out_ref, send_sem, recv_sem, copy_sem):
+    mine, partner = cube_place(bits)
+    own_copy = pltpu.make_async_copy(own_ref, out_ref.at[tuple(mine)], copy_sem)
+    own_copy.start()
+    cube_barrier(bits, partner)
+    own_copy.wait()
+    width = own_ref.shape[1] // len(orders)
+    copies = []
+    held = [[False] * len(bits) for _ in orders]
+    for stage in range(len(bits)):
+        for color, order in enumerate(orders):
+            if stage:
+                copies[(stage - 1) * len(orders) + color].wait_recv()
+                held[color][order[stage - 1]] = True
+            place = tuple(
+                slice(None) if whole else mine[axis] for axis, whole in enumerate(held[color])
+            )
+            ref = out_ref.at[place + (slice(None), pl.ds(color * width, width))]
+            copy = pltpu.make_async_remote_copy(
+                src_ref=ref,
+                dst_ref=ref,
+                send_sem=send_sem.at[color, stage],
+                recv_sem=recv_sem.at[color, stage],
+                device_id=partner(order[stage]),
+                device_id_type=pl.DeviceIdType.MESH,
+            )
+            copy.start()
+            copies.append(copy)
+    for copy in copies:
+        copy.wait_send()
+    for copy in copies[-len(orders) :]:
+        copy.wait_recv()
+
+
+def gather_rows(own):
+    bits = cube_bits()
+    orders = cube_orders(bits)
+    rows, width = own.shape
+    out = pl.pallas_call(
+        functools.partial(gather_kernel, bits, orders),
+        in_specs=[pl.BlockSpec(memory_space=pltpu.VMEM)],
+        out_specs=pl.BlockSpec(memory_space=pl.ANY),
+        out_shape=jax.ShapeDtypeStruct((2,) * len(bits) + (rows, width), own.dtype),
+        scratch_shapes=[
+            pltpu.SemaphoreType.DMA((len(orders), len(bits))),
+            pltpu.SemaphoreType.DMA((len(orders), len(bits))),
+            pltpu.SemaphoreType.DMA,
+        ],
+        compiler_params=pltpu.CompilerParams(collective_id=0, has_side_effects=True),
+        name="gather_rows",
+    )(own)
+    return out.reshape(rows << len(bits), width)
+
+
+def scatter_kernel(bits, orders, terms_ref, out_ref, *scratch):
+    stages = len(bits)
+    colors = len(orders)
+    got = scratch[: colors * stages]
+    sums = scratch[colors * stages : colors * (2 * stages - 1)]
+    send_sem, recv_sem = scratch[colors * (2 * stages - 1) :]
+    mine, partner = cube_place(bits)
+    cube_barrier(bits, partner)
+    width = terms_ref.shape[-1] // colors
+    copies = []
+
+    def half(color, stage, keep):
+        done = orders[color][:stage]
+        place = []
+        for axis in range(stages):
+            if axis in done:
+                continue
+            if axis == orders[color][stage]:
+                place.append(mine[axis] if keep else 1 - mine[axis])
+            else:
+                place.append(slice(None))
+        if stage == 0:
+            return terms_ref.at[tuple(place) + (slice(None), pl.ds(color * width, width))]
+        return sums[color * (stages - 1) + stage - 1].at[tuple(place)]
+
+    for stage in range(stages + 1):
+        for color in range(colors):
+            if stage:
+                copies[(stage - 1) * colors + color].wait_recv()
+                kept = half(color, stage - 1, True)[...].astype(f32)
+                total = kept + got[color * stages + stage - 1][...].astype(f32)
+                if stage == stages:
+                    out_ref[:, pl.ds(color * width, width)] = total
+                    continue
+                sums[color * (stages - 1) + stage - 1][...] = total.astype(bf16)
+            copy = pltpu.make_async_remote_copy(
+                src_ref=half(color, stage, False),
+                dst_ref=got[color * stages + stage],
+                send_sem=send_sem.at[color, stage],
+                recv_sem=recv_sem.at[color, stage],
+                device_id=partner(orders[color][stage]),
+                device_id_type=pl.DeviceIdType.MESH,
+            )
+            copy.start()
+            copies.append(copy)
+    for copy in copies:
+        copy.wait_send()
+
+
+def scatter_rows(terms):
+    bits = cube_bits()
+    orders = [order[::-1] for order in cube_orders(bits)]
+    colors = len(orders)
+    stages = len(bits)
+    rows = terms.shape[0] >> stages
+    width = terms.shape[1]
+    got = [
+        pltpu.VMEM((2,) * (stages - 1 - stage) + (rows, width // colors), bf16)
+        for _ in range(colors)
+        for stage in range(stages)
+    ]
+    sums = [
+        pltpu.VMEM((2,) * (stages - 1 - stage) + (rows, width // colors), bf16)
+        for _ in range(colors)
+        for stage in range(stages - 1)
+    ]
+    return pl.pallas_call(
+        functools.partial(scatter_kernel, bits, orders),
+        in_specs=[pl.BlockSpec(memory_space=pltpu.VMEM)],
+        out_specs=pl.BlockSpec(memory_space=pltpu.VMEM),
+        out_shape=jax.ShapeDtypeStruct((rows, width), f32),
+        scratch_shapes=got
+        + sums
+        + [
+            pltpu.SemaphoreType.DMA((colors, stages)),
+            pltpu.SemaphoreType.DMA((colors, stages)),
+        ],
+        compiler_params=pltpu.CompilerParams(collective_id=1, has_side_effects=True),
+        name="scatter_rows",
+    )(terms.reshape((2,) * stages + (rows, width)))
+
+
+def together(*values):
+    return lax.optimization_barrier(values)
 
 
 def per_device(
@@ -218,7 +430,7 @@
     gain_attn = gains_all[0]
     gain_ffn = gains_all[1]
 
-    qkv_full = lax.all_gather(weight_qkv, every, axis=0, tiled=True)
+    qkv_full = gather_rows(weight_qkv)
     up_own = (
         weight_up.reshape(shard, devices, BLOCKS, shard)
         .transpose(0, 2, 1, 3)
@@ -241,8 +453,8 @@
     outer_own = expert_out[0]
     inner_core = swap_core(inner_own)
     outer_core = swap_core(outer_own)
-    inner_chip = swap_chip(inner_own)
-    inner_both = swap_core(inner_chip)
+    inner_chip = [swap_chip(inner_own[0]), None]
+    outer_chip = [None, None]
 
     capacity = token_count // experts
     chosen = assignment.reshape(token_count)
@@ -267,9 +479,8 @@
         jnp.where(seq_index == 3, kv_far, kv_own), [(0, 1), (2, 3), (3, 2)]
     )
     kv_blocks = (kv_own, kv_near, kv_far)
-    outer_late, _ = lax.optimization_barrier((outer_own, kv_far))
-    outer_chip = swap_chip(outer_late)
-    outer_both = swap_core(outer_chip)
+    late = together(outer_own[0], inner_own[1], outer_own[1], kv_far)
+    outer_chip[0], inner_chip[1], outer_chip[1] = [swap_chip(part) for part in late[:3]]
 
     before = 2 * local_len
     offset = seq_index * local_len
@@ -292,6 +503,10 @@
 
     received = lax.all_to_all(routed[source_of], "wide", split_axis=0, concat_axis=0, tiled=True)
     received_f = received.astype(f32)
+    inner_both = [swap_core(together(inner_chip[0], attended)[0]), None]
+    outer_both = [swap_core(together(outer_chip[0], received)[0]), None]
+    inner_both[1] = swap_core(together(inner_chip[1], received)[0])
+    outer_both[1] = swap_core(together(outer_chip[1], received)[0])
     centroid_row = centroids[0]
     centroid_f = centroid_row.astype(f32)
     logit_row = jnp.dot(received, centroid_row, preferred_element_type=f32)
@@ -322,19 +537,16 @@
     grad_ret = grad_back.astype(f32)
     grad_gate = jnp.sum(grad_ret * state_now, axis=-1)
     grad_state = grad_ret * gate_value[:, None]
-    inner_grads = [None, None]
-    outer_grads = [None, None]
     gain_grads = [None, None]
+    weight_terms = [None, None]
     for sublayer in (1, 0):
         state_in, normed_in, kept = kept_layers[sublayer]
         inner_parts, outer_parts = slices[sublayer]
         grad_branch = grad_state.astype(bf16)
         grad_pres, grad_normed = ffn_backward(kept, inner_parts, outer_parts, grad_branch)
-        outer_grads[sublayer] = reduce_slices(
-            *[functools.partial(product_at, act, grad_branch) for act, _ in kept]
-        )
-        inner_grads[sublayer] = reduce_slices(
-            *[functools.partial(product_at, normed_in, grad_pre) for grad_pre in grad_pres]
+        weight_terms[sublayer] = (
+            [(act, grad_branch) for act, _ in kept],
+            [(normed_in, grad_pre) for grad_pre in grad_pres],
         )
         grad_resid, gain_grad = norm_back(state_in, gains_f[sublayer], grad_normed)
         grad_state = grad_state + grad_resid
@@ -343,6 +555,11 @@
     grad_routed = (grad_state + grad_logit[:, None] * centroid_f[None, :]).astype(bf16)
     centroid_grad = jnp.dot(grad_logit, received_f, precision=highest)
     returned_grad = lax.all_to_all(grad_routed, "wide", split_axis=0, concat_axis=0, tiled=True)
+    outer_sum1 = SliceSum(weight_terms[1][0])
+    inner_sum1 = SliceSum(weight_terms[1][1])
+    returned_grad, *held = together(returned_grad, *outer_sum1.terms(), *inner_sum1.terms())
+    outer_sum1.send_core(held[:4])
+    inner_sum1.send_core(held[4:])
     grad_dense = grad_flat.astype(f32) + returned_grad[slot_index].astype(f32)
 
     grad_down_in = grad_dense.astype(bf16)
@@ -351,13 +568,19 @@
     grad_hidden = grad_dense + grad_hidden_norm
     grad_proj = grad_hidden.astype(bf16)
     rest_grad = jnp.concatenate(
-        [product_at(attended, grad_proj).astype(bf16)]
-        + [product_at(normed_ffn, grad_pre).astype(bf16) for grad_pre in grad_pres]
-        + [product_at(act, grad_down_in).astype(bf16) for act, _ in dense_kept],
+        [weight_grad(attended, grad_proj)]
+        + [weight_grad(normed_ffn, grad_pre) for grad_pre in grad_pres]
+        + [weight_grad(act, grad_down_in) for act, _ in dense_kept],
         axis=1,
     )
+    rest_grad = row_major(rest_grad)
+    grad_attended = product_bt(grad_proj, proj_full).astype(bf16)
+    grad_attended, rest_grad, *held = together(
+        grad_attended, rest_grad, outer_sum1.chip_sum(), inner_sum1.chip_sum()
+    )
+    outer_sum1.send_chip(held[0])
+    inner_sum1.send_chip(held[1])
     rest_sum = lax.psum_scatter(rest_grad, every, scatter_dimension=0, tiled=True).astype(f32)
-    grad_attended = product_bt(grad_proj, proj_full).astype(bf16)
     grad_query, grad_kv0, grad_kv1, grad_kv2 = attend_back(
         query, kv_blocks, bias, grad_attended.reshape(query.shape)
     )
@@ -365,15 +588,24 @@
     far_sum = jnp.where(
         seq_index == 3, (grad_kv2.astype(f32) + got_near.astype(f32)).astype(bf16), grad_kv2
     )
+    far_sum, outer_sum1.got_chip, inner_sum1.got_chip = together(
+        far_sum, outer_sum1.got_chip, inner_sum1.got_chip
+    )
     got_far = seq_send(far_sum, [(2, 0), (3, 1)])
+    outer_sum0 = SliceSum(weight_terms[0][0])
+    inner_sum0 = SliceSum(weight_terms[0][1])
+    got_far, *held = together(got_far, *outer_sum0.terms(), *inner_sum0.terms())
+    outer_sum0.send_core(held[:4])
+    inner_sum0.send_core(held[4:])
+    outer_sum0.send_chip(outer_sum0.chip_sum())
+    inner_sum0.send_chip(inner_sum0.chip_sum())
     kv_sum = grad_kv0.astype(f32) + got_far.astype(f32)
     kv_sum = kv_sum + jnp.where(seq_index % 2 == 0, got_near.astype(f32), 0.0)
     kv_sum = kv_sum.astype(bf16).reshape(2, token_count, model_width)
     grad_qkv = [grad_query.reshape(token_count, model_width), kv_sum[0], kv_sum[1]]
-    qkv_grad = jnp.concatenate(
-        [product_at(normed_attn, part).astype(bf16) for part in grad_qkv], axis=1
-    )
-    qkv_sum = lax.psum_scatter(qkv_grad, every, scatter_dimension=0, tiled=True).astype(f32)
+    qkv_grad = row_major(
+        jnp.concatenate([weight_grad(normed_attn, part) for part in grad_qkv], axis=1)
+    )
     grad_normed_attn = sum(
         product_bt(part, qkv_full[:, index * model_width : (index + 1) * model_width])
         for index, part in enumerate(grad_qkv)
@@ -382,7 +614,9 @@
     grad_input = (grad_hidden + grad_input_norm).reshape(block_input.shape)
 
     gain_terms = jnp.stack([grad_gain_attn, grad_gain_ffn]).reshape(2, devices, shard)
-    gain_terms = lax.all_to_all(gain_terms.transpose(1, 0, 2), every, 0, 0, tiled=True)
+    gain_terms, qkv_grad = together(gain_terms.transpose(1, 0, 2), qkv_grad)
+    gain_terms = lax.all_to_all(gain_terms, every, 0, 0, tiled=True)
+    qkv_sum = scatter_rows(qkv_grad)
     gain_sums = jnp.sum(gain_terms, axis=0)
     expert_totals = lax.psum(
         (jnp.stack(gain_grads), centroid_grad, jnp.stack([gate_sum, score_sum])), "seq"
@@ -411,8 +645,8 @@
         down_grad,
         expert_totals[1][None],
         expert_totals[0][None],
-        jnp.stack(inner_grads)[None],
-        jnp.stack(outer_grads)[None],
+        jnp.stack([inner_sum0.total(), inner_sum1.total()])[None],
+        jnp.stack([outer_sum0.total(), outer_sum1.total()])[None],
         (expert_totals[2][0] / token_total)[None],
         (expert_totals[2][1] / token_total)[None],
     )

time: 1100 us -> 1050 us (0.955)
  waiting for transfers between devices: 529 us -> 233 us
  Pallas kernels: 62.9 us -> 249 us
  blocking collectives: 11.7 us -> 112 us
  matrix products: 261 us -> 231 us
  local copies, waits for them, and re-layouts: 78.5 us -> 52.5 us
  other arithmetic: 75.8 us -> 88 us
    ppermute x22 -> x26, waiting for transfers between devices: 437 us -> 213 us  [seq_send(): return lax.ppermute(values, 'seq', pairs)]
    pallas_call x0 -> x2, Pallas kernels: none -> 186 us  [the longest x1 110 us: scatter_rows(): pl.pallas_call(functools.partial(scatter_kernel, bits, orders), in_specs=...]
    psum x1, blocking collectives: 11.7 us -> 112 us  [per_device(): lax.psum((jnp.stack(gain_grads), centroid_grad, jnp.stack([gate_sum, scor...]
    all_gather x1 -> x0, waiting for transfers between devices: 53.1 us -> none  [per_device(): qkv_full = lax.all_gather(weight_qkv, every, axis=0, tiled=True)]
    unnamed x283 -> x242, local copies, waits for them, and re-layouts: 47.1 us -> 12.5 us
    all_to_all x1, waiting for transfers between devices: 26.1 us -> 7.99 us  [per_device(): lax.all_to_all(grad_routed, 'wide', split_axis=0, concat_axis=0, tiled=True)]
    convert_element_type x0 -> x4, other arithmetic: none -> 16 us  [chip_sum(): return (self.chip.astype(f32) + self.got_both.astype(f32)).astype(bf16)]
    dot_general x27, matrix products: 83.9 us -> 71.5 us  [product(): return jnp.dot(left_side, right_side, preferred_element_type=f32)]
  transfers between devices with their start and end apart: 32 -> 34, of which waited for: 14 -> 7; matrix products, arithmetic and copies ran while one was open for 22% -> 24% of each run, Pallas kernels for 2% -> 24%
where the time goes in v2:
time: 1050 us; the launch traced here: 1040 us
  Pallas kernels  249 us (24%)
  waiting for transfers between devices  233 us (22%)
  matrix products  231 us (22%)
  blocking collectives  112 us (11%)
  other arithmetic  88 us (8%)
  starting transfers between devices  56.4 us (5%)
  local copies, waits for them, and re-layouts  52.5 us (5%)
  between operations  19.7 us (2%)
    ppermute x26, waiting for transfers between devices, seq_send(): return lax.ppermute(values, 'seq', pairs)  213 us
    psum x1, blocking collectives, per_device(): lax.psum((jnp.stack(gain_grads), centroid_grad, jnp.stack([gate_sum, scor...  112 us
    pallas_call x1, Pallas kernels, scatter_rows(): pl.pallas_call(functools.partial(scatter_kernel, bits, orders), in_specs=...  110 us
    dot_general x28, matrix products, product_bt(): lax.dot_general(left_side, right_side, (((1,), (1,)), ((), ())), preferre...  80.4 us
    dot_general x28, matrix products, product_at(): lax.dot_general(left_side, right_side, (((0,), (0,)), ((), ())), preferre...  78.2 us
    pallas_call x1, Pallas kernels, gather_rows(): pl.pallas_call(functools.partial(gather_kernel, bits, orders), in_specs=[...  75.8 us
    dot_general x27, matrix products, product(): return jnp.dot(left_side, right_side, preferred_element_type=f32)  71.5 us
    pallas_call x1, Pallas kernels, attend_back(): pl.pallas_call(functools.partial(attend_back_kernel, 1.0 / math.sqrt(HEAD...  36.3 us
  transfers between devices with their start and end apart: 34, of which 7 were waited for; matrix products, arithmetic and copies ran while one was open for 24% of the time, Pallas kernels for 24%

profile of v2, /device:TPU:0, one launch (start us, length us, event | category | flops | bytes accessed | tf_op | source)
XLA Modules:
  0.0 1041.4 jit_solution(7835708431490602952)
XLA Ops:
  13.2 7.3 all-to-all-start
  21.8 75.8 %gather_rows.1 = bf16[2,2,2,2,2,32,3072]{6,5,4,3,2,1,0:T(8,128)(2,1)} custom-call(bf16[32,3072]{1,0:T(8,128)(2,1)} %own_ref.1), custom_call_target="tpu_custom_call" | custom-call | tf_op jit(solution)/shard_map/gather_rows/pallas_call | solution.py:297
  98.4 5.0 fusion.6
  103.4 5.2 collective-permute-start
  111.1 69.4 %collective-permute-done.k2.v2 = bf16[2,256,2048]{2,1,0:T(8,128)(2,1)} collective-permute-done((bf16[2,256,2048]{2,1,0:T(8,128)(2,1)S(1)}, bf16[2,256,2048]{2,1,0:T(8,128)(2,1)}, u32[]{:S(2)}, u32[]{:S(2)}) %collective-permute-start) | collective-permute-done | bytes 2097184 | tf_op jit(solution)/shard_map/ppermute | solution.py:64
  194.9 26.7 %attend.1 = bf16[2,256,1024]{2,1,0:T(8,128)(2,1)} custom-call(bf16[2,256,1024]{2,1,0:T(8,128)(2,1)} %bitcast.378, bf16[2,256,2048]{2,1,0:T(8,128)(2,1)} %bitcast.332, bf16[2,256,2048]{2,1,0:T(8,128)(2,1)} %bitcast.333, bf16[2,256,2048]{2,1,0:T(8,128)(2,1)} %collective-permute-done.1.k1.v1, bf16[2,256,2048]{2,1,0:T(8,128)(2,1)} %collective-permute-done.1.k1.v1, ...), custom_call_target="tpu_custom_call" | custom-call | flops 9663676416 | bytes 8388608 | tf_op jit(solution)/shard_map/attend/pallas_call | solution.py:134
  243.9 5.7 all-to-all-start.1
  250.2 4.7 slice_bitcast_fusion.4
  262.8 11.1 %all-to-all-done.1 = bf16[8,64,1024]{2,1,0:T(8,128)(2,1)S(1)} async-done(((bf16[8,64,1024]{2,1,0:T(8,128)(2,1)}), bf16[8,64,1024]{2,1,0:T(8,128)(2,1)S(1)}, u32[]{:S(2)}, u32[]{:S(2)}) %all-to-all-start.1) | async-done | bytes 1048608 | tf_op jit(solution)/shard_map/all_to_all | solution.py:504
  286.9 20.6 %collective-permute-done.5 = bf16[1024,1024]{1,0:T(8,128)(2,1)} collective-permute-done((bf16[1024,1024]{1,0:T(8,128)(2,1)}, bf16[1024,1024]{1,0:T(8,128)(2,1)}, u32[]{:S(2)}, u32[]{:S(2)}) %collective-permute-start.5) | collective-permute-done | bytes 2097184 | tf_op jit(solution)/shard_map/ppermute | solution.py:64
  309.0 43.5 %collective-permute-done.9 = bf16[1024,1024]{1,0:T(8,128)(2,1)} collective-permute-done((bf16[1024,1024]{1,0:T(8,128)(2,1)}, bf16[1024,1024]{1,0:T(8,128)(2,1)}, u32[]{:S(2)}, u32[]{:S(2)}) %collective-permute-start.9) | collective-permute-done | bytes 2097184 | tf_op jit(solution)/shard_map/ppermute | solution.py:64
  352.5 44.3 %collective-permute-done.8 = bf16[1024,1024]{1,0:T(8,128)(2,1)} collective-permute-done((bf16[1024,1024]{1,0:T(8,128)(2,1)}, bf16[1024,1024]{1,0:T(8,128)(2,1)}, u32[]{:S(2)}, u32[]{:S(2)}) %collective-permute-start.8) | collective-permute-done | bytes 2097184 | tf_op jit(solution)/shard_map/ppermute | solution.py:64
  397.5 4.8 multiply_convert_fusion.19
  406.1 4.3 multiply_convert_fusion.20
  413.7 4.4 multiply_convert_fusion.18
  499.7 5.9 all-to-all-start.4
  505.8 4.4 convolution_convert_fusion.15
  523.5 8.0 all-to-all-done.4
  590.0 4.2 fusion.100
  594.2 4.1 add_convert_fusion.3
  611.3 36.3 %attend_back.1 = (bf16[2,256,1024]{2,1,0:T(8,128)(2,1)}, bf16[2,2,256,1024]{3,2,1,0:T(8,128)(2,1)}, bf16[2,2,256,1024]{3,2,1,0:T(8,128)(2,1)}, bf16[2,2,256,1024]{3,2,1,0:T(8,128)(2,1)}) custom-call(bf16[2,256,1024]{2,1,0:T(8,128)(2,1)} %bitcast.379, bf16[2,256,2048]{2,1,0:T(8,128)(2,1)} %bitcast.334, bf16[2,256,2048]{2,1,0:T(8,128)(2,1)} %bitcast.335, ...), custom_call_target="tpu_custom_call" | custom-call | flops 24159191040 | bytes 16777216 | tf_op jit(solution)/shard_map/attend_back/pallas_call | solution.py:154
  662.0 4.4 convolution_convert_fusion.5
  676.1 112.2 %all-reduce.1 = (f32[1,1024]{1,0:T(1,128)}, f32[1,2,1024]{2,1,0:T(2,128)}, f32[2]{0:T(128)S(1)}) all-reduce(f32[1,1024]{1,0:T(1,128)S(1)} %fusion.154, f32[1,2,1024]{2,1,0:T(2,128)S(1)} %maximum_bitcast_fusion.3, f32[2]{0:T(128)S(1)} %pad_maximum_fusion.2), channel_id=1, replica_groups=mesh['seq'=4,'wide'=8] {'seq'}, use_global_device_ids=true, to_apply=%region_25.26 | all-reduce | flops 3074 | bytes 24592 | tf_op jit(solution)/shard_map/psum | solution.py:621
  788.4 5.7 fusion.5
  808.8 5.8 add_bitcast_fusion.2
  814.6 5.8 add_bitcast_fusion
  820.5 35.5 %collective-permute-done.17 = bf16[2,2,256,1024]{3,2,1,0:T(8,128)(2,1)} collective-permute-done((bf16[2,2,256,1024]{3,2,1,0:T(8,128)(2,1)}, bf16[2,2,256,1024]{3,2,1,0:T(8,128)(2,1)}, u32[]{:S(2)}, u32[]{:S(2)}) %collective-permute-start.17) | collective-permute-done | bytes 2097184 | tf_op jit(solution)/shard_map/ppermute | solution.py:64
  883.8 4.8 all-to-all-start.5
  892.1 110.1 %scatter_rows.1 = f32[32,3072]{1,0:T(8,128)} custom-call(bf16[2,2,2,2,2,32,3072]{6,5,4,3,2,1,0:T(8,128)(2,1)} %bitcast.313), custom_call_target="tpu_custom_call" | custom-call | tf_op jit(solution)/shard_map/scatter_rows/pallas_call | solution.py:379
  1006.7 4.3 maximum_bitcast_fusion
  1014.8 4.2 maximum_bitcast_fusion.1
  1023.9 4.5 reshape.482
  (485 shorter events, 328.4 us)
Async XLA Ops:
  7.2 214.5 %all-gather.2.cloned.1.call-start = ((), (), s32[]{:S(2)}) async-start(), calls=%async_computation.7 | async-start | bytes 19464192 | tf_op jit(solution)/shard_map/all_gather | solution.py:443
  13.2 84.5 %all-to-all-start = ((f32[32,2,32]{2,1,0:T(2,128)}), f32[32,2,32]{2,1,0:T(2,128)S(1)}, u32[]{:S(2)}, u32[]{:S(2)}) async-start(f32[32,2,32]{2,1,0:T(2,128)} %broadcast_in_dim.39), calls=%async_computation | async-start | bytes 65536 | tf_op jit(solution)/shard_map/all_to_all | solution.py:426
  103.4 77.1 %collective-permute-start = (bf16[2,256,2048]{2,1,0:T(8,128)(2,1)S(1)}, bf16[2,256,2048]{2,1,0:T(8,128)(2,1)}, u32[]{:S(2)}, u32[]{:S(2)}) collective-permute-start(bf16[2,256,2048]{2,1,0:T(8,128)(2,1)S(1)} %bitcast.330), channel_id=1, source_target_pairs={{0,16},{8,24},{1,17},{9,25},{2,18},{10,26},{3,19},{11,27},{4,20},{... | collective-permute-start | bytes 6291464 | tf_op jit(solution)/shard_map/ppermute | solution.py:64
  111.1 149.8 %collective-permute-start.4 = (bf16[1024,1024]{1,0:T(8,128)(2,1)}, bf16[1024,1024]{1,0:T(8,128)(2,1)}, u32[]{:S(2)}, u32[]{:S(2)}) collective-permute-start(bf16[1024,1024]{1,0:T(8,128)(2,1)} %get-tuple-element.121), channel_id=1, source_target_pairs={{0,16},{16,0},{8,24},{24,8},{1,17},{17,1},{9,25},{25,9},{2,18},{18... | collective-permute-start | bytes 6291464 | tf_op jit(solution)/shard_map/ppermute | solution.py:64
  243.9 30.0 %all-to-all-start.1 = ((bf16[8,64,1024]{2,1,0:T(8,128)(2,1)}), bf16[8,64,1024]{2,1,0:T(8,128)(2,1)S(1)}, u32[]{:S(2)}, u32[]{:S(2)}) async-start(bf16[8,64,1024]{2,1,0:T(8,128)(2,1)} %bitcast.15), calls=%async_computation.1 | async-start | bytes 2097152 | tf_op jit(solution)/shard_map/all_to_all | solution.py:504
  249.7 155.9 %collective-permute-start.2 = (bf16[2,1024,1024]{2,1,0:T(8,128)(2,1)}, bf16[2,1024,1024]{2,1,0:T(8,128)(2,1)}, u32[]{:S(2)}, u32[]{:S(2)}) collective-permute-start(bf16[2,1024,1024]{2,1,0:T(8,128)(2,1)} %bitcast.325), channel_id=1, source_target_pairs={{0,8},{8,0},{16,24},{24,16},{1,9},{9,1},{17,25},{25,17},{2,10},{10... | collective-permute-start | bytes 12582920 | tf_op jit(solution)/shard_map/ppermute | solution.py:64
  249.7 160.7 %collective-permute-start.3 = (bf16[2,1024,1024]{2,1,0:T(8,128)(2,1)}, bf16[2,1024,1024]{2,1,0:T(8,128)(2,1)}, u32[]{:S(2)}, u32[]{:S(2)}) collective-permute-start(bf16[2,1024,1024]{2,1,0:T(8,128)(2,1)} %bitcast.324), channel_id=1, source_target_pairs={{0,8},{8,0},{16,24},{24,16},{1,9},{9,1},{17,25},{25,17},{2,10},{10... | collective-permute-start | bytes 12582920 | tf_op jit(solution)/shard_map/ppermute | solution.py:64
  257.8 49.8 %collective-permute-start.5 = (bf16[1024,1024]{1,0:T(8,128)(2,1)}, bf16[1024,1024]{1,0:T(8,128)(2,1)}, u32[]{:S(2)}, u32[]{:S(2)}) collective-permute-start(bf16[1024,1024]{1,0:T(8,128)(2,1)} %get-tuple-element.52), channel_id=1, source_target_pairs={{0,16},{16,0},{8,24},{24,8},{1,17},{17,1},{9,25},{25,9},{2,18},{18... | collective-permute-start | bytes 6291464 | tf_op jit(solution)/shard_map/ppermute | solution.py:64
  260.8 91.7 %collective-permute-start.9 = (bf16[1024,1024]{1,0:T(8,128)(2,1)}, bf16[1024,1024]{1,0:T(8,128)(2,1)}, u32[]{:S(2)}, u32[]{:S(2)}) collective-permute-start(bf16[1024,1024]{1,0:T(8,128)(2,1)} %get-tuple-element.56), channel_id=1, source_target_pairs={{0,16},{16,0},{8,24},{24,8},{1,17},{17,1},{9,25},{25,9},{2,18},{18... | collective-permute-start | bytes 6291464 | tf_op jit(solution)/shard_map/ppermute | solution.py:64
  260.8 136.0 %collective-permute-start.8 = (bf16[1024,1024]{1,0:T(8,128)(2,1)}, bf16[1024,1024]{1,0:T(8,128)(2,1)}, u32[]{:S(2)}, u32[]{:S(2)}) collective-permute-start(bf16[1024,1024]{1,0:T(8,128)(2,1)} %get-tuple-element.55), channel_id=1, source_target_pairs={{0,16},{16,0},{8,24},{24,8},{1,17},{17,1},{9,25},{25,9},{2,18},{18... | collective-permute-start | bytes 6291464 | tf_op jit(solution)/shard_map/ppermute | solution.py:64
  273.9 33.6 %all-to-all-start.3 = ((bf16[8,64,1024]{2,1,0:T(8,128)(2,1)}), bf16[8,64,1024]{2,1,0:T(8,128)(2,1)S(1)}, u32[]{:S(2)}, u32[]{:S(2)}) async-start(bf16[8,64,1024]{2,1,0:T(8,128)(2,1)} %bitcast.322), calls=%async_computation.3 | async-start | bytes 2097152 | tf_op jit(solution)/shard_map/all_to_all | solution.py:534
  307.6 106.1 %collective-permute-start.6 = (bf16[1024,1024]{1,0:T(8,128)(2,1)}, bf16[1024,1024]{1,0:T(8,128)(2,1)}, u32[]{:S(2)}, u32[]{:S(2)}) collective-permute-start(bf16[1024,1024]{1,0:T(8,128)(2,1)} %collective-permute-done.4), channel_id=1, source_target_pairs={{0,8},{8,0},{16,24},{24,16},{1,9},{9,1},{17,25},{25,17},{2,10},{10... | collective-permute-start | bytes 6291464 | tf_op jit(solution)/shard_map/ppermute | solution.py:64
  352.5 65.6 %collective-permute-start.7 = (bf16[1024,1024]{1,0:T(8,128)(2,1)}, bf16[1024,1024]{1,0:T(8,128)(2,1)S(1)}, u32[]{:S(2)}, u32[]{:S(2)}) collective-permute-start(bf16[1024,1024]{1,0:T(8,128)(2,1)} %collective-permute-done.5), channel_id=1, source_target_pairs={{0,8},{8,0},{16,24},{24,16},{1,9},{9,1},{17,25},{25,17},{2,10},{10... | collective-permute-start | bytes 6291464 | tf_op jit(solution)/shard_map/ppermute | solution.py:64
  396.8 58.2 %collective-permute-start.11 = (bf16[1024,1024]{1,0:T(8,128)(2,1)}, bf16[1024,1024]{1,0:T(8,128)(2,1)S(1)}, u32[]{:S(2)}, u32[]{:S(2)}) collective-permute-start(bf16[1024,1024]{1,0:T(8,128)(2,1)} %collective-permute-done.9), channel_id=1, source_target_pairs={{0,8},{8,0},{16,24},{24,16},{1,9},{9,1},{17,25},{25,17},{2,10},{10... | collective-permute-start | bytes 6291464 | tf_op jit(solution)/shard_map/ppermute | solution.py:64
  405.5 48.1 %collective-permute-start.10 = (bf16[1024,1024]{1,0:T(8,128)(2,1)}, bf16[1024,1024]{1,0:T(8,128)(2,1)S(1)}, u32[]{:S(2)}, u32[]{:S(2)}) collective-permute-start(bf16[1024,1024]{1,0:T(8,128)(2,1)} %collective-permute-done.8), channel_id=1, source_target_pairs={{0,8},{8,0},{16,24},{24,16},{1,9},{9,1},{17,25},{25,17},{2,10},{10... | collective-permute-start | bytes 6291464 | tf_op jit(solution)/shard_map/ppermute | solution.py:64
  499.7 31.9 %all-to-all-start.4 = ((bf16[8,64,1024]{2,1,0:T(8,128)(2,1)}), bf16[8,64,1024]{2,1,0:T(8,128)(2,1)S(1)}, u32[]{:S(2)}, u32[]{:S(2)}) async-start(bf16[8,64,1024]{2,1,0:T(8,128)(2,1)} %bitcast.329), calls=%async_computation.4 | async-start | bytes 2097152 | tf_op jit(solution)/shard_map/all_to_all | solution.py:557
  505.6 513.4 %reduce-scatter.2.cloned.1.call-start = ((), (), s32[]{:S(2)}) async-start(), calls=%async_computation.8 | async-start | bytes 19464192 | tf_op jit(solution)/shard_map/reduce_scatter | solution.py:583
  575.9 18.2 %collective-permute-start.12 = (bf16[1024,1024]{1,0:T(8,128)(2,1)}, bf16[1024,1024]{1,0:T(8,128)(2,1)}, u32[]{:S(2)}, u32[]{:S(2)}) collective-permute-start(bf16[1024,1024]{1,0:T(8,128)(2,1)} %convolution_convert_fusion.14), channel_id=1, source_target_pairs={{0,8},{8,0},{16,24},{24,16},{1,9},{9,1},{17,25},{25,17},{2,10},{10... | collective-permute-start | bytes 6291464 | tf_op jit(solution)/shard_map/ppermute | solution.py:64
  578.6 19.6 %collective-permute-start.13 = (bf16[1024,1024]{1,0:T(8,128)(2,1)}, bf16[1024,1024]{1,0:T(8,128)(2,1)}, u32[]{:S(2)}, u32[]{:S(2)}) collective-permute-start(bf16[1024,1024]{1,0:T(8,128)(2,1)} %convolution_convert_fusion.10), channel_id=1, source_target_pairs={{0,8},{8,0},{16,24},{24,16},{1,9},{9,1},{17,25},{25,17},{2,10},{10... | collective-permute-start | bytes 6291464 | tf_op jit(solution)/shard_map/ppermute | solution.py:64
  647.6 140.8 %collective-permute-start.14 = (bf16[2,2,256,1024]{3,2,1,0:T(8,128)(2,1)}, bf16[2,2,256,1024]{3,2,1,0:T(8,128)(2,1)}, u32[]{:S(2)}, u32[]{:S(2)}) collective-permute-start(bf16[2,2,256,1024]{3,2,1,0:T(8,128)(2,1)} %get-tuple-element.68), channel_id=1, source_target_pairs={{8,0},{24,16},{16,24},{9,1},{25,17},{17,25},{10,2},{26,18},{18,26}... | collective-permute-start | bytes 6291464 | tf_op jit(solution)/shard_map/ppermute | solution.py:64
  653.0 141.1 %collective-permute-start.15 = (bf16[1024,1024]{1,0:T(8,128)(2,1)}, bf16[1024,1024]{1,0:T(8,128)(2,1)}, u32[]{:S(2)}, u32[]{:S(2)}) collective-permute-start(bf16[1024,1024]{1,0:T(8,128)(2,1)} %add_convert_fusion.3), channel_id=1, source_target_pairs={{0,16},{16,0},{8,24},{24,8},{1,17},{17,1},{9,25},{25,9},{2,18},{18... | collective-permute-start | bytes 6291464 | tf_op jit(solution)/shard_map/ppermute | solution.py:64
  655.5 138.7 %collective-permute-start.16 = (bf16[1024,1024]{1,0:T(8,128)(2,1)}, bf16[1024,1024]{1,0:T(8,128)(2,1)}, u32[]{:S(2)}, u32[]{:S(2)}) collective-permute-start(bf16[1024,1024]{1,0:T(8,128)(2,1)} %add_convert_fusion.2), channel_id=1, source_target_pairs={{0,16},{16,0},{8,24},{24,8},{1,17},{17,1},{9,25},{25,9},{2,18},{18... | collective-permute-start | bytes 6291464 | tf_op jit(solution)/shard_map/ppermute | solution.py:64
  658.1 139.2 %all-to-all-start.2 = ((bf16[8,64,1024]{2,1,0:T(8,128)(2,1)}), bf16[8,64,1024]{2,1,0:T(8,128)(2,1)S(1)}, u32[]{:S(2)}, u32[]{:S(2)}) async-start(bf16[8,64,1024]{2,1,0:T(8,128)(2,1)} %bitcast.328), calls=%async_computation.2 | async-start | bytes 2097152 | tf_op jit(solution)/shard_map/all_to_all | solution.py:527
  671.6 137.1 %collective-permute-start.21 = (bf16[1024,1024]{1,0:T(8,128)(2,1)}, bf16[1024,1024]{1,0:T(8,128)(2,1)}, u32[]{:S(2)}, u32[]{:S(2)}) collective-permute-start(bf16[1024,1024]{1,0:T(8,128)(2,1)} %convolution_convert_fusion.12), channel_id=1, source_target_pairs={{0,8},{8,0},{16,24},{24,16},{1,9},{9,1},{17,25},{25,17},{2,10},{10... | collective-permute-start | bytes 6291464 | tf_op jit(solution)/shard_map/ppermute | solution.py:64
  676.1 138.5 %collective-permute-start.25 = (bf16[1024,1024]{1,0:T(8,128)(2,1)}, bf16[1024,1024]{1,0:T(8,128)(2,1)}, u32[]{:S(2)}, u32[]{:S(2)}) collective-permute-start(bf16[1024,1024]{1,0:T(8,128)(2,1)} %convolution_convert_fusion.16), channel_id=1, source_target_pairs={{0,8},{8,0},{16,24},{24,16},{1,9},{9,1},{17,25},{25,17},{2,10},{10... | collective-permute-start | bytes 6291464 | tf_op jit(solution)/shard_map/ppermute | solution.py:64
  794.1 61.9 %collective-permute-start.17 = (bf16[2,2,256,1024]{3,2,1,0:T(8,128)(2,1)}, bf16[2,2,256,1024]{3,2,1,0:T(8,128)(2,1)}, u32[]{:S(2)}, u32[]{:S(2)}) collective-permute-start(bf16[2,2,256,1024]{3,2,1,0:T(8,128)(2,1)} %fusion.5), channel_id=1, source_target_pairs={{16,0},{24,8},{17,1},{25,9},{18,2},{26,10},{19,3},{27,11},{20,4},{... | collective-permute-start | bytes 6291464 | tf_op jit(solution)/shard_map/ppermute | solution.py:64
  856.0 18.4 %collective-permute-start.23 = (bf16[1024,1024]{1,0:T(8,128)(2,1)}, bf16[1024,1024]{1,0:T(8,128)(2,1)}, u32[]{:S(2)}, u32[]{:S(2)}) collective-permute-start(bf16[1024,1024]{1,0:T(8,128)(2,1)} %convolution_convert_fusion.6), channel_id=1, source_target_pairs={{0,8},{8,0},{16,24},{24,16},{1,9},{9,1},{17,25},{25,17},{2,10},{10... | collective-permute-start | bytes 6291464 | tf_op jit(solution)/shard_map/ppermute | solution.py:64
  864.8 138.0 %collective-permute-start.18 = (bf16[1024,1024]{1,0:T(8,128)(2,1)}, bf16[1024,1024]{1,0:T(8,128)(2,1)}, u32[]{:S(2)}, u32[]{:S(2)}) collective-permute-start(bf16[1024,1024]{1,0:T(8,128)(2,1)} %convolution_convert_fusion.4), channel_id=1, source_target_pairs={{0,8},{8,0},{16,24},{24,16},{1,9},{9,1},{17,25},{25,17},{2,10},{10... | collective-permute-start | bytes 6291464 | tf_op jit(solution)/shard_map/ppermute | solution.py:64
  864.9 146.0 %collective-permute-start.22 = (bf16[1024,1024]{1,0:T(8,128)(2,1)}, bf16[1024,1024]{1,0:T(8,128)(2,1)}, u32[]{:S(2)}, u32[]{:S(2)}) collective-permute-start(bf16[1024,1024]{1,0:T(8,128)(2,1)} %convolution_convert_fusion.8), channel_id=1, source_target_pairs={{0,8},{8,0},{16,24},{24,16},{1,9},{9,1},{17,25},{25,17},{2,10},{10... | collective-permute-start | bytes 6291464 | tf_op jit(solution)/shard_map/ppermute | solution.py:64
  872.5 130.4 %collective-permute-start.20 = (bf16[1024,1024]{1,0:T(8,128)(2,1)}, bf16[1024,1024]{1,0:T(8,128)(2,1)}, u32[]{:S(2)}, u32[]{:S(2)}) collective-permute-start(bf16[1024,1024]{1,0:T(8,128)(2,1)} %add_convert_fusion.1), channel_id=1, source_target_pairs={{0,16},{16,0},{8,24},{24,8},{1,17},{17,1},{9,25},{25,9},{2,18},{18... | collective-permute-start | bytes 6291464 | tf_op jit(solution)/shard_map/ppermute | solution.py:64
  878.8 132.2 %collective-permute-start.24 = (bf16[1024,1024]{1,0:T(8,128)(2,1)}, bf16[1024,1024]{1,0:T(8,128)(2,1)}, u32[]{:S(2)}, u32[]{:S(2)}) collective-permute-start(bf16[1024,1024]{1,0:T(8,128)(2,1)} %add_convert_fusion), channel_id=1, source_target_pairs={{0,16},{16,0},{8,24},{24,8},{1,17},{17,1},{9,25},{25,9},{2,18},{18... | collective-permute-start | bytes 6291464 | tf_op jit(solution)/shard_map/ppermute | solution.py:64
  883.8 118.5 %all-to-all-start.5 = ((f32[32,2,32]{2,1,0:T(2,128)}), f32[32,2,32]{2,1,0:T(2,128)S(1)}, u32[]{:S(2)}, u32[]{:S(2)}) async-start(f32[32,2,32]{2,1,0:T(2,128)} %maximum_bitcast_fusion.2), calls=%async_computation.5 | async-start | bytes 65536 | tf_op jit(solution)/shard_map/all_to_all | solution.py:618
  (120 other events, 1181.6 us)
Sparse Core Ops, SparseCore 0:
  12.6 177.8 all-gather.1
  602.3 259.0 reduce-scatter.1

commit v3 on v2

--- a/solution.py
+++ b/solution.py
@@ -78,7 +78,50 @@
     return exp_scores * (1.0 / jnp.sum(exp_scores, axis=0, keepdims=True))
 
 
-def attend_kernel(score_scale, q_ref, k0, v0, k1, v1, k2, v2, bias_ref, out_ref):
+def ride_chip(source, target, send_sem, recv_sem):
+    seq = lax.axis_index("seq")
+    other = (lax.rem(seq + 2, 4), lax.axis_index("wide"))
+    step = pl.program_id(0) * pl.num_programs(1) + pl.program_id(1)
+    copy = pltpu.make_async_remote_copy(
+        src_ref=source,
+        dst_ref=target,
+        send_sem=send_sem,
+        recv_sem=recv_sem,
+        device_id=other,
+        device_id_type=pl.DeviceIdType.MESH,
+    )
+
+    @pl.when(step == 0)
+    def _():
+        barrier = pltpu.get_barrier_semaphore()
+        pl.semaphore_signal(
+            barrier, inc=1, device_id=other, device_id_type=pl.DeviceIdType.MESH
+        )
+        pl.semaphore_wait(barrier, 1)
+        copy.start()
+
+    @pl.when(step == pl.num_programs(0) * pl.num_programs(1) - 1)
+    def _():
+        copy.wait()
+
+
+def attend_kernel(
+    score_scale,
+    q_ref,
+    k0,
+    v0,
+    k1,
+    v1,
+    k2,
+    v2,
+    bias_ref,
+    ride_ref,
+    out_ref,
+    rode_ref,
+    send_sem,
+    recv_sem,
+):
+    ride_chip(ride_ref.at[0], rode_ref, send_sem, recv_sem)
     bias = bias_ref[0]
     parts = []
     for head in range(2):
@@ -91,8 +134,26 @@
 
 
 def attend_back_kernel(
-    score_scale, q_ref, k0, v0, k1, v1, k2, v2, bias_ref, grad_ref, dq_ref, d0, d1, d2
+    score_scale,
+    q_ref,
+    k0,
+    v0,
+    k1,
+    v1,
+    k2,
+    v2,
+    bias_ref,
+    grad_ref,
+    ride_ref,
+    dq_ref,
+    d0,
+    d1,
+    d2,
+    rode_ref,
+    send_sem,
+    recv_sem,
 ):
+    ride_chip(ride_ref, rode_ref, send_sem, recv_sem)
     bias = bias_ref[0]
     dq_parts, dk_parts, dv_parts = [], [], []
     for head in range(2):
@@ -126,7 +187,7 @@
     return groups, query, [query, query, values, query, values, query, values, bias]
 
 
-def attend(query, kv_blocks, bias):
+def attend(query, kv_blocks, bias, ride):
     rows, local_len, model_width = query.shape
     groups, spec, in_specs = attention_specs(local_len, model_width, bias.shape[1])
     operands = [block for block in kv_blocks for _ in range(2)]
@@ -134,17 +195,22 @@
     return pl.pallas_call(
         functools.partial(attend_kernel, 1.0 / math.sqrt(HEAD_DIM)),
         grid=(rows, groups),
-        in_specs=in_specs,
-        out_specs=spec,
-        out_shape=jax.ShapeDtypeStruct(query.shape, bf16),
+        in_specs=in_specs + [pl.BlockSpec(memory_space=pl.ANY)],
+        out_specs=[spec, pl.BlockSpec(memory_space=pl.ANY)],
+        out_shape=[
+            jax.ShapeDtypeStruct(query.shape, bf16),
+            jax.ShapeDtypeStruct(ride.shape[1:], ride.dtype),
+        ],
+        scratch_shapes=[pltpu.SemaphoreType.DMA, pltpu.SemaphoreType.DMA],
+        compiler_params=pltpu.CompilerParams(collective_id=2, has_side_effects=True),
         cost_estimate=pl.CostEstimate(
             flops=flops * 6, bytes_accessed=8 * query.size * 2, transcendentals=0
         ),
         name="attend",
-    )(query, *operands, bias)
-
-
-def attend_back(query, kv_blocks, bias, grad_attended):
+    )(query, *operands, bias, ride)
+
+
+def attend_back(query, kv_blocks, bias, grad_attended, ride):
     rows, local_len, model_width = query.shape
     groups, spec, in_specs = attention_specs(local_len, model_width, bias.shape[1])
     operands = [block for block in kv_blocks for _ in range(2)]
@@ -154,14 +220,18 @@
     return pl.pallas_call(
         functools.partial(attend_back_kernel, 1.0 / math.sqrt(HEAD_DIM)),
         grid=(rows, groups),
-        in_specs=in_specs + [spec],
-        out_specs=[spec, pair_spec, pair_spec, pair_spec],
-        out_shape=[jax.ShapeDtypeStruct(query.shape, bf16)] + [pair_shape] * 3,
+        in_specs=in_specs + [spec, pl.BlockSpec(memory_space=pl.ANY)],
+        out_specs=[spec, pair_spec, pair_spec, pair_spec, pl.BlockSpec(memory_space=pl.ANY)],
+        out_shape=[jax.ShapeDtypeStruct(query.shape, bf16)]
+        + [pair_shape] * 3
+        + [jax.ShapeDtypeStruct(ride.shape, ride.dtype)],
+        scratch_shapes=[pltpu.SemaphoreType.DMA, pltpu.SemaphoreType.DMA],
+        compiler_params=pltpu.CompilerParams(collective_id=3, has_side_effects=True),
         cost_estimate=pl.CostEstimate(
             flops=flops * 6, bytes_accessed=16 * query.size * 2, transcendentals=0
         ),
         name="attend_back",
-    )(query, *operands, bias, grad_attended)
+    )(query, *operands, bias, grad_attended, ride)
 
 
 def ffn_forward(normed, inner_parts, outer_parts, residual):
@@ -190,16 +260,18 @@
     def __init__(self, operands):
         self.operands = operands
 
-    def terms(self):
-        return [weight_grad(left, right) for left, right in self.operands]
-
-    def send_core(self, terms):
-        self.own, core, self.chip, both = terms
-        self.got_core = swap_core(core)
-        self.got_both = swap_core(both)
+    def term(self, place):
+        return weight_grad(*self.operands[place])
+
+    def send_both(self, values):
+        self.got_both = swap_core(values)
+
+    def send_core(self, values):
+        self.got_core = swap_core(values)
 
     def chip_sum(self):
-        return (self.chip.astype(f32) + self.got_both.astype(f32)).astype(bf16)
+        values = product_at(*self.operands[2]) + self.got_both.astype(f32)
+        return row_major(values.astype(bf16))
 
     def send_chip(self, values):
         self.got_chip = swap_chip(values)
@@ -222,16 +294,8 @@
     wide = [place for place, (axis, _) in enumerate(bits) if axis == "wide"]
     if len(wide) == 3:
         far, near, across = wide
-        return (
-            (far, chip, near, across, core),
-            (near, across, far, chip, core),
-            (chip, far, across, near, core),
-        )
-    return (
-        (chip, *wide, core),
-        (*wide, chip, core),
-        (*wide[1:], chip, wide[0], core),
-    )
+        return ((chip, far, near, across, core), (chip, across, far, near, core))
+    return ((chip, *wide, core), (chip, *wide[2:], *wide[:2], core))
 
 
 def cube_place(bits):
@@ -256,13 +320,46 @@
     pl.semaphore_wait(barrier, len(bits))
 
 
-def gather_kernel(bits, orders, own_ref, out_ref, send_sem, recv_sem, copy_sem):
+def gather_kernel(
+    bits,
+    orders,
+    own_ref,
+    inner_ref,
+    outer_ref,
+    out_ref,
+    inner_core_ref,
+    outer_core_ref,
+    inner_chip_ref,
+    send_sem,
+    recv_sem,
+    copy_sem,
+    ride_send,
+    ride_recv,
+):
     mine, partner = cube_place(bits)
     own_copy = pltpu.make_async_copy(own_ref, out_ref.at[tuple(mine)], copy_sem)
     own_copy.start()
     cube_barrier(bits, partner)
     own_copy.wait()
     width = own_ref.shape[1] // len(orders)
+    core = partner(bits.index(("seq", 0)))
+    chip = partner(bits.index(("seq", 1)))
+    rides = [
+        (inner_ref.at[0, 0], inner_chip_ref, chip),
+        (inner_ref.at[0], inner_core_ref, core),
+        (outer_ref.at[0], outer_core_ref, core),
+    ]
+    rides = [
+        pltpu.make_async_remote_copy(
+            src_ref=source,
+            dst_ref=target,
+            send_sem=ride_send.at[place],
+            recv_sem=ride_recv.at[place],
+            device_id=device,
+            device_id_type=pl.DeviceIdType.MESH,
+        )
+        for place, (source, target, device) in enumerate(rides)
+    ]
     copies = []
     held = [[False] * len(bits) for _ in orders]
     for stage in range(len(bits)):
@@ -284,30 +381,44 @@
             )
             copy.start()
             copies.append(copy)
+        if stage == 0:
+            for ride in rides:
+                ride.start()
     for copy in copies:
         copy.wait_send()
     for copy in copies[-len(orders) :]:
         copy.wait_recv()
-
-
-def gather_rows(own):
+    for ride in rides:
+        ride.wait()
+
+
+def gather_rows(own, expert_in, expert_out):
     bits = cube_bits()
     orders = cube_orders(bits)
     rows, width = own.shape
-    out = pl.pallas_call(
+    anywhere = pl.BlockSpec(memory_space=pl.ANY)
+    out, inner_core, outer_core, inner_chip = pl.pallas_call(
         functools.partial(gather_kernel, bits, orders),
-        in_specs=[pl.BlockSpec(memory_space=pltpu.VMEM)],
-        out_specs=pl.BlockSpec(memory_space=pl.ANY),
-        out_shape=jax.ShapeDtypeStruct((2,) * len(bits) + (rows, width), own.dtype),
+        in_specs=[pl.BlockSpec(memory_space=pltpu.VMEM), anywhere, anywhere],
+        out_specs=[anywhere] * 4,
+        out_shape=[
+            jax.ShapeDtypeStruct((2,) * len(bits) + (rows, width), own.dtype),
+            jax.ShapeDtypeStruct(expert_in.shape[1:], expert_in.dtype),
+            jax.ShapeDtypeStruct(expert_out.shape[1:], expert_out.dtype),
+            jax.ShapeDtypeStruct(expert_in.shape[2:], expert_in.dtype),
+        ],
         scratch_shapes=[
             pltpu.SemaphoreType.DMA((len(orders), len(bits))),
             pltpu.SemaphoreType.DMA((len(orders), len(bits))),
             pltpu.SemaphoreType.DMA,
+            pltpu.SemaphoreType.DMA((3,)),
+            pltpu.SemaphoreType.DMA((3,)),
         ],
         compiler_params=pltpu.CompilerParams(collective_id=0, has_side_effects=True),
+        cost_estimate=pl.CostEstimate(flops=0, bytes_accessed=25 * own.size << 5, transcendentals=0),
         name="gather_rows",
-    )(own)
-    return out.reshape(rows << len(bits), width)
+    )(own, expert_in, expert_out)
+    return out.reshape(rows << len(bits), width), inner_core, outer_core, inner_chip
 
 
 def scatter_kernel(bits, orders, terms_ref, out_ref, *scratch):
@@ -388,6 +499,7 @@
             pltpu.SemaphoreType.DMA((colors, stages)),
         ],
         compiler_params=pltpu.CompilerParams(collective_id=1, has_side_effects=True),
+        cost_estimate=pl.CostEstimate(flops=0, bytes_accessed=50 * terms.size, transcendentals=0),
         name="scatter_rows",
     )(terms.reshape((2,) * stages + (rows, width)))
 
@@ -430,7 +542,7 @@
     gain_attn = gains_all[0]
     gain_ffn = gains_all[1]
 
-    qkv_full = gather_rows(weight_qkv)
+    qkv_full, inner_core, outer_core, inner_first = gather_rows(weight_qkv, expert_in, expert_out)
     up_own = (
         weight_up.reshape(shard, devices, BLOCKS, shard)
         .transpose(0, 2, 1, 3)
@@ -451,9 +563,7 @@
 
     inner_own = expert_in[0]
     outer_own = expert_out[0]
-    inner_core = swap_core(inner_own)
-    outer_core = swap_core(outer_own)
-    inner_chip = [swap_chip(inner_own[0]), None]
+    inner_chip = [inner_first, None]
     outer_chip = [None, None]
 
     capacity = token_count // experts
@@ -479,9 +589,6 @@
         jnp.where(seq_index == 3, kv_far, kv_own), [(0, 1), (2, 3), (3, 2)]
     )
     kv_blocks = (kv_own, kv_near, kv_far)
-    late = together(outer_own[0], inner_own[1], outer_own[1], kv_far)
-    outer_chip[0], inner_chip[1], outer_chip[1] = [swap_chip(part) for part in late[:3]]
-
     before = 2 * local_len
     offset = seq_index * local_len
     padded_seg = jnp.pad(segment_ids, ((0, 0), (before, 0)), constant_values=-1)
@@ -494,7 +601,9 @@
     )
     bias = jnp.where(allowed, 0.0, -1e30).astype(f32)
 
-    attended_rows = attend(query, kv_blocks, bias)
+    attended_rows, outer_chip[0] = attend(query, kv_blocks, bias, outer_own)
+    late = together(inner_own[1], outer_own[1], attended_rows)
+    inner_chip[1], outer_chip[1] = [swap_chip(part) for part in late[:2]]
     attended = attended_rows.reshape(token_count, model_width)
     hidden = tokens_flat + product(attended, proj_full)
     normed_ffn = layer_norm(hidden, gain_ffn).astype(bf16)
@@ -504,9 +613,7 @@
     received = lax.all_to_all(routed[source_of], "wide", split_axis=0, concat_axis=0, tiled=True)
     received_f = received.astype(f32)
     inner_both = [swap_core(together(inner_chip[0], attended)[0]), None]
-    outer_both = [swap_core(together(outer_chip[0], received)[0]), None]
-    inner_both[1] = swap_core(together(inner_chip[1], received)[0])
-    outer_both[1] = swap_core(together(outer_chip[1], received)[0])
+    outer_both = [swap_core(together(outer_chip[0], attended)[0]), None]
     centroid_row = centroids[0]
     centroid_f = centroid_row.astype(f32)
     logit_row = jnp.dot(received, centroid_row, preferred_element_type=f32)
@@ -516,6 +623,9 @@
     kept_layers = []
     slices = []
     for sublayer in range(2):
+        if sublayer:
+            inner_both[1] = swap_core(together(inner_chip[1], state_now)[0])
+            outer_both[1] = swap_core(together(outer_chip[1], state_now)[0])
         inner_parts = [part[sublayer] for part in (inner_own, inner_core, inner_chip, inner_both)]
         outer_parts = [part[sublayer] for part in (outer_own, outer_core, outer_chip, outer_both)]
         normed = layer_norm(state_now, gains_f[sublayer]).astype(bf16)
@@ -539,6 +649,7 @@
     grad_state = grad_ret * gate_value[:, None]
     gain_grads = [None, None]
     weight_terms = [None, None]
+    sums = [None, None]
     for sublayer in (1, 0):
         state_in, normed_in, kept = kept_layers[sublayer]
         inner_parts, outer_parts = slices[sublayer]
@@ -551,15 +662,30 @@
         grad_resid, gain_grad = norm_back(state_in, gains_f[sublayer], grad_normed)
         grad_state = grad_state + grad_resid
         gain_grads[sublayer] = gain_grad
+        sums[sublayer] = [SliceSum(operands) for operands in weight_terms[sublayer]]
+        if sublayer:
+            grad_state, *held = together(grad_state, *[part.term(3) for part in sums[1]])
+            for part, values in zip(sums[1], held):
+                part.send_both(values)
     grad_logit = grad_gate * gate_value * (1.0 - gate_value)
     grad_routed = (grad_state + grad_logit[:, None] * centroid_f[None, :]).astype(bf16)
     centroid_grad = jnp.dot(grad_logit, received_f, precision=highest)
+    grad_routed, *held = together(grad_routed, *[part.chip_sum() for part in sums[1]])
+    for part, values in zip(sums[1], held):
+        part.send_chip(values)
     returned_grad = lax.all_to_all(grad_routed, "wide", split_axis=0, concat_axis=0, tiled=True)
-    outer_sum1 = SliceSum(weight_terms[1][0])
-    inner_sum1 = SliceSum(weight_terms[1][1])
-    returned_grad, *held = together(returned_grad, *outer_sum1.terms(), *inner_sum1.terms())
-    outer_sum1.send_core(held[:4])
-    inner_sum1.send_core(held[4:])
+    returned_grad, *held = together(
+        returned_grad,
+        *[part.term(3) for part in sums[0]],
+        *[part.term(1) for part in sums[1]],
+        *[part.term(0) for part in sums[1]],
+    )
+    for part, values in zip(sums[0], held[:2]):
+        part.send_both(values)
+    for part, values in zip(sums[1], held[2:4]):
+        part.send_core(values)
+    for part, values in zip(sums[1], held[4:]):
+        part.own = values
     grad_dense = grad_flat.astype(f32) + returned_grad[slot_index].astype(f32)
 
     grad_down_in = grad_dense.astype(bf16)
@@ -575,30 +701,33 @@
     )
     rest_grad = row_major(rest_grad)
     grad_attended = product_bt(grad_proj, proj_full).astype(bf16)
-    grad_attended, rest_grad, *held = together(
-        grad_attended, rest_grad, outer_sum1.chip_sum(), inner_sum1.chip_sum()
-    )
-    outer_sum1.send_chip(held[0])
-    inner_sum1.send_chip(held[1])
+    outer1, inner1 = sums[1]
+    outer0, inner0 = sums[0]
+    grad_attended, rest_grad, outer1.got_chip, inner1.got_chip, outer_send, inner_send = together(
+        grad_attended,
+        rest_grad,
+        outer1.got_chip,
+        inner1.got_chip,
+        outer0.chip_sum(),
+        inner0.chip_sum(),
+    )
     rest_sum = lax.psum_scatter(rest_grad, every, scatter_dimension=0, tiled=True).astype(f32)
-    grad_query, grad_kv0, grad_kv1, grad_kv2 = attend_back(
-        query, kv_blocks, bias, grad_attended.reshape(query.shape)
+    grad_query, grad_kv0, grad_kv1, grad_kv2, outer0.got_chip = attend_back(
+        query, kv_blocks, bias, grad_attended.reshape(query.shape), outer_send
     )
     got_near = seq_send(grad_kv1, [(1, 0), (3, 2), (2, 3)])
     far_sum = jnp.where(
         seq_index == 3, (grad_kv2.astype(f32) + got_near.astype(f32)).astype(bf16), grad_kv2
     )
-    far_sum, outer_sum1.got_chip, inner_sum1.got_chip = together(
-        far_sum, outer_sum1.got_chip, inner_sum1.got_chip
-    )
     got_far = seq_send(far_sum, [(2, 0), (3, 1)])
-    outer_sum0 = SliceSum(weight_terms[0][0])
-    inner_sum0 = SliceSum(weight_terms[0][1])
-    got_far, *held = together(got_far, *outer_sum0.terms(), *inner_sum0.terms())
-    outer_sum0.send_core(held[:4])
-    inner_sum0.send_core(held[4:])
-    outer_sum0.send_chip(outer_sum0.chip_sum())
-    inner_sum0.send_chip(inner_sum0.chip_sum())
+    got_far, *held = together(
+        got_far, *[part.term(1) for part in sums[0]], *[part.term(0) for part in sums[0]]
+    )
+    for part, values in zip(sums[0], held[:2]):
+        part.send_core(values)
+    for part, values in zip(sums[0], held[2:]):
+        part.own = values
+    inner0.send_chip(together(inner_send, got_far)[0])
     kv_sum = grad_kv0.astype(f32) + got_far.astype(f32)
     kv_sum = kv_sum + jnp.where(seq_index % 2 == 0, got_near.astype(f32), 0.0)
     kv_sum = kv_sum.astype(bf16).reshape(2, token_count, model_width)
@@ -618,9 +747,15 @@
     gain_terms = lax.all_to_all(gain_terms, every, 0, 0, tiled=True)
     qkv_sum = scatter_rows(qkv_grad)
     gain_sums = jnp.sum(gain_terms, axis=0)
-    expert_totals = lax.psum(
-        (jnp.stack(gain_grads), centroid_grad, jnp.stack([gate_sum, score_sum])), "seq"
-    )
+    totals = jnp.concatenate(
+        [
+            jnp.stack(gain_grads),
+            centroid_grad.reshape(1, model_width),
+            jnp.pad(jnp.stack([gate_sum, score_sum]), (0, model_width - 2))[None],
+        ]
+    )
+    totals = totals + swap_core(totals)
+    totals = totals + swap_chip(totals)
     up_grad = (
         rest_sum[:, model_width : model_width + hidden_width]
         .reshape(shard, BLOCKS, devices, shard)
@@ -643,12 +778,12 @@
         gain_sums[1],
         up_grad,
         down_grad,
-        expert_totals[1][None],
-        expert_totals[0][None],
-        jnp.stack([inner_sum0.total(), inner_sum1.total()])[None],
-        jnp.stack([outer_sum0.total(), outer_sum1.total()])[None],
-        (expert_totals[2][0] / token_total)[None],
-        (expert_totals[2][1] / token_total)[None],
+        totals[2:3],
+        totals[:2][None],
+        jnp.stack([inner0.total(), inner1.total()])[None],
+        jnp.stack([outer0.total(), outer1.total()])[None],
+        totals[3, :1] / token_total,
+        totals[3, 1:2] / token_total,
     )
 
 

time: 1050 us -> 879 us (0.84)
  blocking collectives: 112 us -> 0 us
  waiting for transfers between devices: 233 us -> 174 us
  Pallas kernels: 249 us -> 271 us
  other arithmetic: 88 us -> 67 us
    psum x1 -> x0, blocking collectives: 112 us -> none  [per_device(): lax.psum((jnp.stack(gain_grads), centroid_grad, jnp.stack([gate_sum, scor...]
    ppermute x26 -> x23, waiting for transfers between devices: 213 us -> 151 us  [seq_send(): return lax.ppermute(values, 'seq', pairs)]
    pallas_call x1, Pallas kernels: 110 us -> 76.5 us  [scatter_rows(): pl.pallas_call(functools.partial(scatter_kernel, bits, orders), in_specs=...]
    pallas_call x1, Pallas kernels: 26.7 us -> 52.7 us  [attend(): pl.pallas_call(functools.partial(attend_kernel, 1.0 / math.sqrt(HEAD_DIM)...]
    convert_element_type x4 -> x0, other arithmetic: 16 us -> none  [chip_sum(): return (self.chip.astype(f32) + self.got_both.astype(f32)).astype(bf16)]
    pallas_call x1, Pallas kernels: 75.8 us -> 91.2 us  [gather_rows(): pl.pallas_call(functools.partial(gather_kernel, bits, orders), in_specs=[...]
    pallas_call x1, Pallas kernels: 36.3 us -> 50.9 us  [attend_back(): pl.pallas_call(functools.partial(attend_back_kernel, 1.0 / math.sqrt(HEAD...]
    ppermute x26 -> x23, starting transfers between devices: 24.5 us -> 18.9 us  [seq_send(): return lax.ppermute(values, 'seq', pairs)]
  transfers between devices with their start and end apart: 34 -> 31, of which waited for: 7 -> 6; matrix products, arithmetic and copies ran while one was open for 24% -> 30% of each run, Pallas kernels for 24% -> 31%
where the time goes in v3:
time: 879 us; the launch traced here: 870 us
  Pallas kernels  271 us (31%)
  matrix products  229 us (26%)
  waiting for transfers between devices  174 us (20%)
  other arithmetic  67 us (8%)
  starting transfers between devices  54.5 us (6%)
  local copies, waits for them, and re-layouts  54.4 us (6%)
  between operations  19.8 us (2%)
    ppermute x23, waiting for transfers between devices, seq_send(): return lax.ppermute(values, 'seq', pairs)  151 us
    pallas_call x1, Pallas kernels, gather_rows(): pl.pallas_call(functools.partial(gather_kernel, bits, orders), in_specs=[...  91.2 us
    dot_general x28, matrix products, product_at(): lax.dot_general(left_side, right_side, (((0,), (0,)), ((), ())), preferre...  81.4 us
    dot_general x28, matrix products, product_bt(): lax.dot_general(left_side, right_side, (((1,), (1,)), ((), ())), preferre...  78.4 us
    pallas_call x1, Pallas kernels, scatter_rows(): pl.pallas_call(functools.partial(scatter_kernel, bits, orders), in_specs=...  76.5 us
    dot_general x27, matrix products, product(): return jnp.dot(left_side, right_side, preferred_element_type=f32)  68.7 us
    pallas_call x1, Pallas kernels, attend(): pl.pallas_call(functools.partial(attend_kernel, 1.0 / math.sqrt(HEAD_DIM)...  52.7 us
    pallas_call x1, Pallas kernels, attend_back(): pl.pallas_call(functools.partial(attend_back_kernel, 1.0 / math.sqrt(HEAD...  50.9 us
  transfers between devices with their start and end apart: 31, of which 6 were waited for; matrix products, arithmetic and copies ran while one was open for 30% of the time, Pallas kernels for 31%

profile of v3, /device:TPU:0, one launch (start us, length us, event | category | flops | bytes accessed | tf_op | source)
XLA Modules:
  0.0 870.1 jit_solution(17717702920103016114)
XLA Ops:
  13.2 7.3 all-to-all-start
  21.8 91.2 %gather_rows.1 = (bf16[2,2,2,2,2,32,3072]{6,5,4,3,2,1,0:T(8,128)(2,1)}, bf16[2,1024,1024]{2,1,0:T(8,128)(2,1)}, bf16[2,1024,1024]{2,1,0:T(8,128)(2,1)}, bf16[1024,1024]{1,0:T(8,128)(2,1)}) custom-call(bf16[32,3072]{1,0:T(8,128)(2,1)} %own_ref.1, bf16[1,2,1024,1024]{3,2,1,0:T(8,128)(2,1)} %inner_ref.1, bf16[1,2,1024,1024]{3,2,1,0:T(8,128)(2,1)} %outer_ref.1), custom_call_target="tpu_custom_call" | custom-call | bytes 78643200 | tf_op jit(solution)/shard_map/gather_rows/pallas_call | solution.py:400
  113.8 4.7 fusion.6
  121.9 66.9 %collective-permute-done.k2.v2 = bf16[2,256,2048]{2,1,0:T(8,128)(2,1)} collective-permute-done((bf16[2,256,2048]{2,1,0:T(8,128)(2,1)S(1)}, bf16[2,256,2048]{2,1,0:T(8,128)(2,1)}, u32[]{:S(2)}, u32[]{:S(2)}) %collective-permute-start) | collective-permute-done | bytes 2097184 | tf_op jit(solution)/shard_map/ppermute | solution.py:64
  203.1 52.7 %attend.1 = (bf16[2,256,1024]{2,1,0:T(8,128)(2,1)}, bf16[1024,1024]{1,0:T(8,128)(2,1)}) custom-call(bf16[2,256,1024]{2,1,0:T(8,128)(2,1)} %bitcast.390, bf16[2,256,2048]{2,1,0:T(8,128)(2,1)} %bitcast.330, bf16[2,256,2048]{2,1,0:T(8,128)(2,1)} %bitcast.331, bf16[2,256,2048]{2,1,0:T(8,128)(2,1)} %collective-permute-done.1.k1.v1, ...), custom_call_target="tpu_custom_call" | custom-call | flops 9663676416 | bytes 8388608 | tf_op jit(solution)/shard_map/attend/pallas_call | solution.py:195
  260.3 4.1 fusion.77
  278.1 6.2 all-to-all-start.1
  287.2 4.6 slice_bitcast_fusion
  294.4 15.4 %all-to-all-done.1 = bf16[8,64,1024]{2,1,0:T(8,128)(2,1)S(1)} async-done(((bf16[8,64,1024]{2,1,0:T(8,128)(2,1)}), bf16[8,64,1024]{2,1,0:T(8,128)(2,1)S(1)}, u32[]{:S(2)}, u32[]{:S(2)}) %all-to-all-start.1) | async-done | bytes 1048608 | tf_op jit(solution)/shard_map/all_to_all | solution.py:613
  314.6 5.0 multiply_convert_fusion.19
  333.8 4.3 multiply_convert_fusion.18
  361.1 24.0 %collective-permute-done.4 = bf16[1024,1024]{1,0:T(8,128)(2,1)} collective-permute-done((bf16[1024,1024]{1,0:T(8,128)(2,1)}, bf16[1024,1024]{1,0:T(8,128)(2,1)}, u32[]{:S(2)}, u32[]{:S(2)}) %collective-permute-start.4) | collective-permute-done | bytes 2097184 | tf_op jit(solution)/shard_map/ppermute | solution.py:64
  392.6 4.1 multiply_convert_fusion.9
  455.9 6.4 all-to-all-start.4
  462.4 4.3 convolution_convert_fusion.9
  482.0 6.7 all-to-all-done.4
  547.1 4.2 fusion.128
  551.3 4.4 add_convert_fusion.1.ride_ref
  555.7 4.2 add_convert_fusion
  559.9 13.0 %collective-permute-done.11 = bf16[1024,1024]{1,0:T(8,128)(2,1)} collective-permute-done((bf16[1024,1024]{1,0:T(8,128)(2,1)}, bf16[1024,1024]{1,0:T(8,128)(2,1)}, u32[]{:S(2)}, u32[]{:S(2)}) %collective-permute-start.11) | collective-permute-done | bytes 2097184 | tf_op jit(solution)/shard_map/ppermute | solution.py:64
  575.8 5.7 all-to-all-start.2
  582.0 50.9 %attend_back.1 = (bf16[2,256,1024]{2,1,0:T(8,128)(2,1)}, bf16[2,2,256,1024]{3,2,1,0:T(8,128)(2,1)}, bf16[2,2,256,1024]{3,2,1,0:T(8,128)(2,1)}, bf16[2,2,256,1024]{3,2,1,0:T(8,128)(2,1)}, bf16[1024,1024]{1,0:T(8,128)(2,1)}) custom-call(bf16[2,256,1024]{2,1,0:T(8,128)(2,1)} %bitcast.391, bf16[2,256,2048]{2,1,0:T(8,128)(2,1)} %bitcast.332, ...), custom_call_target="tpu_custom_call" | custom-call | flops 24159191040 | bytes 16777216 | tf_op jit(solution)/shard_map/attend_back/pallas_call | solution.py:220
  634.4 4.1 convolution_convert_fusion.5
  662.3 4.0 bitcast_convert_fusion
  669.4 5.8 add_bitcast_fusion.2
  675.2 5.8 add_bitcast_fusion
  681.1 47.5 %collective-permute-done.15 = bf16[2,2,256,1024]{3,2,1,0:T(8,128)(2,1)} collective-permute-done((bf16[2,2,256,1024]{3,2,1,0:T(8,128)(2,1)}, bf16[2,2,256,1024]{3,2,1,0:T(8,128)(2,1)}, u32[]{:S(2)}, u32[]{:S(2)}) %collective-permute-start.15) | collective-permute-done | bytes 2097184 | tf_op jit(solution)/shard_map/ppermute | solution.py:64
  745.1 6.4 all-to-all-start.5
  755.1 76.5 %scatter_rows.1 = f32[32,3072]{1,0:T(8,128)} custom-call(bf16[2,2,2,2,2,32,3072]{6,5,4,3,2,1,0:T(8,128)(2,1)} %bitcast.319), custom_call_target="tpu_custom_call" | custom-call | bytes 157286400 | tf_op jit(solution)/shard_map/scatter_rows/pallas_call | solution.py:490
  836.0 4.3 maximum_bitcast_fusion
  843.5 4.2 maximum_bitcast_fusion.1
  852.6 4.5 reshape.483
  (499 shorter events, 296.7 us)
Async XLA Ops:
  7.2 248.7 %all-gather.2.cloned.1.call-start = ((), (), s32[]{:S(2)}) async-start(), calls=%async_computation.7 | async-start | bytes 19464192 | tf_op jit(solution)/shard_map/all_gather | solution.py:555
  13.2 99.9 %all-to-all-start = ((f32[32,2,32]{2,1,0:T(2,128)}), f32[32,2,32]{2,1,0:T(2,128)S(1)}, u32[]{:S(2)}, u32[]{:S(2)}) async-start(f32[32,2,32]{2,1,0:T(2,128)} %broadcast_in_dim.39), calls=%async_computation | async-start | bytes 65536 | tf_op jit(solution)/shard_map/all_to_all | solution.py:538
  21.8 91.5 %copy-start.71 = (f32[512]{0:T(512)}, f32[512]{0:T(512)S(1)}, u32[]{:S(2)}) copy-start(f32[512]{0:T(512)S(1)} %rsqrt.50) | copy-start | bytes 6148
  118.6 70.2 %collective-permute-start = (bf16[2,256,2048]{2,1,0:T(8,128)(2,1)S(1)}, bf16[2,256,2048]{2,1,0:T(8,128)(2,1)}, u32[]{:S(2)}, u32[]{:S(2)}) collective-permute-start(bf16[2,256,2048]{2,1,0:T(8,128)(2,1)S(1)} %bitcast.328), channel_id=1, source_target_pairs={{0,16},{8,24},{1,17},{9,25},{2,18},{10,26},{3,19},{11,27},{4,20},{... | collective-permute-start | bytes 6291464 | tf_op jit(solution)/shard_map/ppermute | solution.py:64
  190.3 12.8 %collective-permute-start.1 = (bf16[2,256,2048]{2,1,0:T(8,128)(2,1)}, bf16[2,256,2048]{2,1,0:T(8,128)(2,1)}, u32[]{:S(2)}, u32[]{:S(2)}) collective-permute-start(bf16[2,256,2048]{2,1,0:T(8,128)(2,1)} %broadcast_select_fusion), channel_id=1, source_target_pairs={{0,8},{16,24},{24,16},{1,9},{17,25},{25,17},{2,10},{18,26},{26,18}... | collective-permute-start | bytes 6291464 | tf_op jit(solution)/shard_map/ppermute | solution.py:64
  278.1 31.7 %all-to-all-start.1 = ((bf16[8,64,1024]{2,1,0:T(8,128)(2,1)}), bf16[8,64,1024]{2,1,0:T(8,128)(2,1)S(1)}, u32[]{:S(2)}, u32[]{:S(2)}) async-start(bf16[8,64,1024]{2,1,0:T(8,128)(2,1)} %bitcast.16), calls=%async_computation.1 | async-start | bytes 2097152 | tf_op jit(solution)/shard_map/all_to_all | solution.py:613
  291.9 41.8 %collective-permute-start.2 = (bf16[1024,1024]{1,0:T(8,128)(2,1)}, bf16[1024,1024]{1,0:T(8,128)(2,1)}, u32[]{:S(2)}, u32[]{:S(2)}) collective-permute-start(bf16[1024,1024]{1,0:T(8,128)(2,1)} %get-tuple-element.64), channel_id=1, source_target_pairs={{0,8},{8,0},{16,24},{24,16},{1,9},{9,1},{17,25},{25,17},{2,10},{10... | collective-permute-start | bytes 6291464 | tf_op jit(solution)/shard_map/ppermute | solution.py:64
  291.9 46.2 %collective-permute-start.3 = (bf16[1024,1024]{1,0:T(8,128)(2,1)}, bf16[1024,1024]{1,0:T(8,128)(2,1)}, u32[]{:S(2)}, u32[]{:S(2)}) collective-permute-start(bf16[1024,1024]{1,0:T(8,128)(2,1)} %get-tuple-element.65), channel_id=1, source_target_pairs={{0,8},{8,0},{16,24},{24,16},{1,9},{9,1},{17,25},{25,17},{2,10},{10... | collective-permute-start | bytes 6291464 | tf_op jit(solution)/shard_map/ppermute | solution.py:64
  292.4 49.2 %collective-permute-start.5 = (bf16[1024,1024]{1,0:T(8,128)(2,1)}, bf16[1024,1024]{1,0:T(8,128)(2,1)}, u32[]{:S(2)}, u32[]{:S(2)}) collective-permute-start(bf16[1024,1024]{1,0:T(8,128)(2,1)} %get-tuple-element.67), channel_id=1, source_target_pairs={{0,16},{16,0},{8,24},{24,8},{1,17},{17,1},{9,25},{25,9},{2,18},{18... | collective-permute-start | bytes 6291464 | tf_op jit(solution)/shard_map/ppermute | solution.py:64
  294.1 91.1 %collective-permute-start.4 = (bf16[1024,1024]{1,0:T(8,128)(2,1)}, bf16[1024,1024]{1,0:T(8,128)(2,1)}, u32[]{:S(2)}, u32[]{:S(2)}) collective-permute-start(bf16[1024,1024]{1,0:T(8,128)(2,1)} %get-tuple-element.66), channel_id=1, source_target_pairs={{0,16},{16,0},{8,24},{24,8},{1,17},{17,1},{9,25},{25,9},{2,18},{18... | collective-permute-start | bytes 6291464 | tf_op jit(solution)/shard_map/ppermute | solution.py:64
  309.8 37.2 %all-to-all-start.3 = ((bf16[8,64,1024]{2,1,0:T(8,128)(2,1)}), bf16[8,64,1024]{2,1,0:T(8,128)(2,1)S(1)}, u32[]{:S(2)}, u32[]{:S(2)}) async-start(bf16[8,64,1024]{2,1,0:T(8,128)(2,1)} %bitcast.322), calls=%async_computation.3 | async-start | bytes 2097152 | tf_op jit(solution)/shard_map/all_to_all | solution.py:644
  341.6 63.6 %collective-permute-start.7 = (bf16[1024,1024]{1,0:T(8,128)(2,1)}, bf16[1024,1024]{1,0:T(8,128)(2,1)}, u32[]{:S(2)}, u32[]{:S(2)}) collective-permute-start(bf16[1024,1024]{1,0:T(8,128)(2,1)} %collective-permute-done.5), channel_id=1, source_target_pairs={{0,8},{8,0},{16,24},{24,16},{1,9},{9,1},{17,25},{25,17},{2,10},{10... | collective-permute-start | bytes 6291464 | tf_op jit(solution)/shard_map/ppermute | solution.py:64
  385.2 17.7 %collective-permute-start.6 = (bf16[1024,1024]{1,0:T(8,128)(2,1)}, bf16[1024,1024]{1,0:T(8,128)(2,1)S(1)}, u32[]{:S(2)}, u32[]{:S(2)}) collective-permute-start(bf16[1024,1024]{1,0:T(8,128)(2,1)} %collective-permute-done.4), channel_id=1, source_target_pairs={{0,8},{8,0},{16,24},{24,16},{1,9},{9,1},{17,25},{25,17},{2,10},{10... | collective-permute-start | bytes 6291464 | tf_op jit(solution)/shard_map/ppermute | solution.py:64
  438.7 11.8 %collective-permute-start.8 = (bf16[1024,1024]{1,0:T(8,128)(2,1)S(1)}, bf16[1024,1024]{1,0:T(8,128)(2,1)S(1)}, u32[]{:S(2)}, u32[]{:S(2)}) collective-permute-start(bf16[1024,1024]{1,0:T(8,128)(2,1)S(1)} %convolution_convert_fusion.13), channel_id=1, source_target_pairs={{0,8},{8,0},{16,24},{24,16},{1,9},{9,1},{17,25},{25,17},{2,10},{10... | collective-permute-start | bytes 6291464 | tf_op jit(solution)/shard_map/ppermute | solution.py:64
  439.3 13.8 %collective-permute-start.9 = (bf16[1024,1024]{1,0:T(8,128)(2,1)S(1)}, bf16[1024,1024]{1,0:T(8,128)(2,1)S(1)}, u32[]{:S(2)}, u32[]{:S(2)}) collective-permute-start(bf16[1024,1024]{1,0:T(8,128)(2,1)S(1)} %copy-done.90), channel_id=1, source_target_pairs={{0,8},{8,0},{16,24},{24,16},{1,9},{9,1},{17,25},{25,17},{2,10},{10... | collective-permute-start | bytes 6291464 | tf_op jit(solution)/shard_map/ppermute | solution.py:64
  455.9 32.7 %all-to-all-start.4 = ((bf16[8,64,1024]{2,1,0:T(8,128)(2,1)}), bf16[8,64,1024]{2,1,0:T(8,128)(2,1)S(1)}, u32[]{:S(2)}, u32[]{:S(2)}) async-start(bf16[8,64,1024]{2,1,0:T(8,128)(2,1)} %bitcast.326), calls=%async_computation.4 | async-start | bytes 2097152 | tf_op jit(solution)/shard_map/all_to_all | solution.py:676
  462.3 385.4 %reduce-scatter.2.cloned.1.call-start = ((), (), s32[]{:S(2)}) async-start(), calls=%async_computation.8 | async-start | bytes 19464192 | tf_op jit(solution)/shard_map/reduce_scatter | solution.py:714
  480.0 79.9 %collective-permute-start.10 = (bf16[1024,1024]{1,0:T(8,128)(2,1)}, bf16[1024,1024]{1,0:T(8,128)(2,1)}, u32[]{:S(2)}, u32[]{:S(2)}) collective-permute-start(bf16[1024,1024]{1,0:T(8,128)(2,1)} %add_convert_fusion.3), channel_id=1, source_target_pairs={{0,16},{16,0},{8,24},{24,8},{1,17},{17,1},{9,25},{25,9},{2,18},{18... | collective-permute-start | bytes 6291464 | tf_op jit(solution)/shard_map/ppermute | solution.py:64
  481.7 91.2 %collective-permute-start.11 = (bf16[1024,1024]{1,0:T(8,128)(2,1)}, bf16[1024,1024]{1,0:T(8,128)(2,1)}, u32[]{:S(2)}, u32[]{:S(2)}) collective-permute-start(bf16[1024,1024]{1,0:T(8,128)(2,1)} %add_convert_fusion.2), channel_id=1, source_target_pairs={{0,16},{16,0},{8,24},{24,8},{1,17},{17,1},{9,25},{25,9},{2,18},{18... | collective-permute-start | bytes 6291464 | tf_op jit(solution)/shard_map/ppermute | solution.py:64
  533.0 18.3 %collective-permute-start.12 = (bf16[1024,1024]{1,0:T(8,128)(2,1)}, bf16[1024,1024]{1,0:T(8,128)(2,1)}, u32[]{:S(2)}, u32[]{:S(2)}) collective-permute-start(bf16[1024,1024]{1,0:T(8,128)(2,1)} %convolution_convert_fusion.11), channel_id=1, source_target_pairs={{0,8},{8,0},{16,24},{24,16},{1,9},{9,1},{17,25},{25,17},{2,10},{10... | collective-permute-start | bytes 6291464 | tf_op jit(solution)/shard_map/ppermute | solution.py:64
  535.7 19.9 %collective-permute-start.13 = (bf16[1024,1024]{1,0:T(8,128)(2,1)}, bf16[1024,1024]{1,0:T(8,128)(2,1)}, u32[]{:S(2)}, u32[]{:S(2)}) collective-permute-start(bf16[1024,1024]{1,0:T(8,128)(2,1)} %convolution_convert_fusion.10), channel_id=1, source_target_pairs={{0,8},{8,0},{16,24},{24,16},{1,9},{9,1},{17,25},{25,17},{2,10},{10... | collective-permute-start | bytes 6291464 | tf_op jit(solution)/shard_map/ppermute | solution.py:64
  575.8 80.9 %all-to-all-start.2 = ((bf16[8,64,1024]{2,1,0:T(8,128)(2,1)}), bf16[8,64,1024]{2,1,0:T(8,128)(2,1)S(1)}, u32[]{:S(2)}, u32[]{:S(2)}) async-start(bf16[8,64,1024]{2,1,0:T(8,128)(2,1)} %bitcast.327), calls=%async_computation.2 | async-start | bytes 2097152 | tf_op jit(solution)/shard_map/all_to_all | solution.py:637
  632.9 18.2 %collective-permute-start.14 = (bf16[2,2,256,1024]{3,2,1,0:T(8,128)(2,1)}, bf16[2,2,256,1024]{3,2,1,0:T(8,128)(2,1)S(1)}, u32[]{:S(2)}, u32[]{:S(2)}) collective-permute-start(bf16[2,2,256,1024]{3,2,1,0:T(8,128)(2,1)} %get-tuple-element.84), channel_id=1, source_target_pairs={{8,0},{24,16},{16,24},{9,1},{25,17},{17,25},{10,2},{26,18},{18,26}... | collective-permute-start | bytes 6291464 | tf_op jit(solution)/shard_map/ppermute | solution.py:64
  641.1 3.7 collective-permute-start.16
  644.9 4.3 collective-permute-start.17
  646.6 22.8 %collective-permute-start.20 = (bf16[1024,1024]{1,0:T(8,128)(2,1)}, bf16[1024,1024]{1,0:T(8,128)(2,1)}, u32[]{:S(2)}, u32[]{:S(2)}) collective-permute-start(bf16[1024,1024]{1,0:T(8,128)(2,1)} %convolution_convert_fusion.8), channel_id=1, source_target_pairs={{0,8},{8,0},{16,24},{24,16},{1,9},{9,1},{17,25},{25,17},{2,10},{10... | collective-permute-start | bytes 6291464 | tf_op jit(solution)/shard_map/ppermute | solution.py:64
  649.3 25.9 %collective-permute-start.22 = (bf16[1024,1024]{1,0:T(8,128)(2,1)}, bf16[1024,1024]{1,0:T(8,128)(2,1)}, u32[]{:S(2)}, u32[]{:S(2)}) collective-permute-start(bf16[1024,1024]{1,0:T(8,128)(2,1)} %convolution_convert_fusion.9), channel_id=1, source_target_pairs={{0,8},{8,0},{16,24},{24,16},{1,9},{9,1},{17,25},{25,17},{2,10},{10... | collective-permute-start | bytes 6291464 | tf_op jit(solution)/shard_map/ppermute | solution.py:64
  653.5 75.0 %collective-permute-start.15 = (bf16[2,2,256,1024]{3,2,1,0:T(8,128)(2,1)}, bf16[2,2,256,1024]{3,2,1,0:T(8,128)(2,1)}, u32[]{:S(2)}, u32[]{:S(2)}) collective-permute-start(bf16[2,2,256,1024]{3,2,1,0:T(8,128)(2,1)} %fusion.5), channel_id=1, source_target_pairs={{16,0},{24,8},{17,1},{25,9},{18,2},{26,10},{19,3},{27,11},{20,4},{... | collective-permute-start | bytes 6291464 | tf_op jit(solution)/shard_map/ppermute | solution.py:64
  736.2 96.0 %collective-permute-start.19 = (bf16[1024,1024]{1,0:T(8,128)(2,1)}, bf16[1024,1024]{1,0:T(8,128)(2,1)}, u32[]{:S(2)}, u32[]{:S(2)}) collective-permute-start(bf16[1024,1024]{1,0:T(8,128)(2,1)} %add_convert_fusion), channel_id=1, source_target_pairs={{0,16},{16,0},{8,24},{24,8},{1,17},{17,1},{9,25},{25,9},{2,18},{18... | collective-permute-start | bytes 6291464 | tf_op jit(solution)/shard_map/ppermute | solution.py:64
  736.3 95.9 %collective-permute-start.18 = (bf16[1024,1024]{1,0:T(8,128)(2,1)}, bf16[1024,1024]{1,0:T(8,128)(2,1)}, u32[]{:S(2)}, u32[]{:S(2)}) collective-permute-start(bf16[1024,1024]{1,0:T(8,128)(2,1)} %convolution_convert_fusion.4), channel_id=1, source_target_pairs={{0,8},{8,0},{16,24},{24,16},{1,9},{9,1},{17,25},{25,17},{2,10},{10... | collective-permute-start | bytes 6291464 | tf_op jit(solution)/shard_map/ppermute | solution.py:64
  736.4 103.9 %collective-permute-start.21 = (bf16[1024,1024]{1,0:T(8,128)(2,1)}, bf16[1024,1024]{1,0:T(8,128)(2,1)}, u32[]{:S(2)}, u32[]{:S(2)}) collective-permute-start(bf16[1024,1024]{1,0:T(8,128)(2,1)} %convolution_convert_fusion.5), channel_id=1, source_target_pairs={{0,8},{8,0},{16,24},{24,16},{1,9},{9,1},{17,25},{25,17},{2,10},{10... | collective-permute-start | bytes 6291464 | tf_op jit(solution)/shard_map/ppermute | solution.py:64
  745.1 86.5 %all-to-all-start.5 = ((f32[32,2,32]{2,1,0:T(2,128)}), f32[32,2,32]{2,1,0:T(2,128)S(1)}, u32[]{:S(2)}, u32[]{:S(2)}) async-start(f32[32,2,32]{2,1,0:T(2,128)} %maximum_bitcast_fusion.2), calls=%async_computation.5 | async-start | bytes 65536 | tf_op jit(solution)/shard_map/all_to_all | solution.py:747
  (127 other events, 1213.2 us)
Sparse Core Ops, SparseCore 0:
  12.6 156.3 all-gather.1
  573.1 246.2 reduce-scatter.1

commit v4 on v3

--- a/solution.py
+++ b/solution.py
@@ -12,6 +12,7 @@
 HEADS = 16
 HEAD_DIM = 64
 BLOCKS = 4
+LANES = 128
 
 epsilon = 1e-05
 highest = lax.Precision.HIGHEST
@@ -534,15 +535,14 @@
     shard = weight_up.shape[0]
     hidden_width = weight_up.shape[1]
 
-    gains_own = jnp.stack([norm_attn, norm_ffn]).astype(f32)
-    gains_all = lax.all_to_all(
-        jnp.broadcast_to(gains_own[None], (devices, 2, shard)), every, 0, 0, tiled=True
-    )
-    gains_all = gains_all.transpose(1, 0, 2).reshape(2, model_width)
+    gains_own = jnp.stack([norm_attn, norm_ffn], axis=1)
+    first_own = jnp.concatenate(
+        [weight_qkv, jnp.pad(gains_own, ((0, 0), (0, 2 * LANES - gains_own.shape[1])))], axis=1
+    )
+    qkv_full, inner_core, outer_core, inner_first = gather_rows(first_own, expert_in, expert_out)
+    gains_all = qkv_full[:, 3 * model_width : 3 * model_width + 2].astype(f32).T
     gain_attn = gains_all[0]
     gain_ffn = gains_all[1]
-
-    qkv_full, inner_core, outer_core, inner_first = gather_rows(weight_qkv, expert_in, expert_out)
     up_own = (
         weight_up.reshape(shard, devices, BLOCKS, shard)
         .transpose(0, 2, 1, 3)
@@ -552,6 +552,7 @@
     rest_own = jnp.concatenate(
         [weight_proj, up_own, down_own.reshape(shard, BLOCKS * model_width)], axis=1
     )
+    rest_own, _ = together(rest_own, qkv_full)
     rest_full = lax.all_gather(rest_own, every, axis=0, tiled=True)
 
     def rest_block(index):
@@ -579,7 +580,7 @@
 
     tokens_flat = block_input.reshape(token_count, model_width).astype(f32)
     normed_attn = layer_norm(tokens_flat, gain_attn).astype(bf16)
-    kv_own = product(normed_attn, qkv_full[:, model_width:]).astype(bf16)
+    kv_own = product(normed_attn, qkv_full[:, model_width : 3 * model_width]).astype(bf16)
     kv_own = kv_own.reshape(row_count, local_len, 2 * model_width)
     query = product(normed_attn, qkv_full[:, :model_width]).astype(bf16)
     query = query.reshape(row_count, local_len, model_width)
@@ -611,6 +612,7 @@
     routed = dense_out.astype(bf16)
 
     received = lax.all_to_all(routed[source_of], "wide", split_axis=0, concat_axis=0, tiled=True)
+    received, inner_chip[1] = together(received, inner_chip[1])
     received_f = received.astype(f32)
     inner_both = [swap_core(together(inner_chip[0], attended)[0]), None]
     outer_both = [swap_core(together(outer_chip[0], attended)[0]), None]
@@ -692,6 +694,9 @@
     grad_pres, grad_normed_ffn = ffn_backward(dense_kept, up_parts, down_parts, grad_down_in)
     grad_hidden_norm, grad_gain_ffn = norm_back(hidden, gain_ffn, grad_normed_ffn)
     grad_hidden = grad_dense + grad_hidden_norm
+    outer1, inner1 = sums[1]
+    outer0, inner0 = sums[0]
+    grad_hidden, outer1.got_chip = together(grad_hidden, outer1.got_chip)
     grad_proj = grad_hidden.astype(bf16)
     rest_grad = jnp.concatenate(
         [weight_grad(attended, grad_proj)]
@@ -701,15 +706,9 @@
     )
     rest_grad = row_major(rest_grad)
     grad_attended = product_bt(grad_proj, proj_full).astype(bf16)
-    outer1, inner1 = sums[1]
-    outer0, inner0 = sums[0]
-    grad_attended, rest_grad, outer1.got_chip, inner1.got_chip, outer_send, inner_send = together(
-        grad_attended,
-        rest_grad,
-        outer1.got_chip,
-        inner1.got_chip,
-        outer0.chip_sum(),
-        inner0.chip_sum(),
+    grad_attended, rest_grad = together(grad_attended, rest_grad)
+    grad_attended, inner1.got_chip, outer_send, inner_send = together(
+        grad_attended, inner1.got_chip, outer0.chip_sum(), inner0.chip_sum()
     )
     rest_sum = lax.psum_scatter(rest_grad, every, scatter_dimension=0, tiled=True).astype(f32)
     grad_query, grad_kv0, grad_kv1, grad_kv2, outer0.got_chip = attend_back(

time: 879 us -> 838 us (0.953)
  waiting for transfers between devices: 174 us -> 152 us
    ppermute x23, waiting for transfers between devices: 151 us -> 125 us  [seq_send(): return lax.ppermute(values, 'seq', pairs)]
    pallas_call x1, Pallas kernels: 91.2 us -> 64.9 us  [gather_rows(): pl.pallas_call(functools.partial(gather_kernel, bits, orders), in_specs=[...]
    pallas_call x1, Pallas kernels: 50.9 us -> 68.2 us  [attend_back(): pl.pallas_call(functools.partial(attend_back_kernel, 1.0 / math.sqrt(HEAD...]
    pallas_call x1, Pallas kernels: 52.7 us -> 67.3 us  [attend(): pl.pallas_call(functools.partial(attend_kernel, 1.0 / math.sqrt(HEAD_DIM)...]
    pallas_call x1, Pallas kernels: 76.5 us -> 65.8 us  [scatter_rows(): pl.pallas_call(functools.partial(scatter_kernel, bits, orders), in_specs=...]
    unnamed x262 -> x265, local copies, waits for them, and re-layouts: 15.9 us -> 17.8 us
  transfers between devices with their start and end apart: 31 -> 30, of which waited for: 6 -> 6; matrix products, arithmetic and copies ran while one was open for 30% -> 31% of each run, Pallas kernels for 31% -> 24%
where the time goes in v4:
time: 838 us; the launch traced here: 830 us
  Pallas kernels  266 us (32%)
  matrix products  222 us (26%)
  waiting for transfers between devices  152 us (18%)
  other arithmetic  68.7 us (8%)
  local copies, waits for them, and re-layouts  53.3 us (6%)
  starting transfers between devices  47.5 us (6%)
  between operations  19.8 us (2%)
    ppermute x23, waiting for transfers between devices, seq_send(): return lax.ppermute(values, 'seq', pairs)  125 us
    dot_general x28, matrix products, product_at(): lax.dot_general(left_side, right_side, (((0,), (0,)), ((), ())), preferre...  81 us
    dot_general x28, matrix products, product_bt(): lax.dot_general(left_side, right_side, (((1,), (1,)), ((), ())), preferre...  71.6 us
    dot_general x27, matrix products, product(): return jnp.dot(left_side, right_side, preferred_element_type=f32)  68.7 us
    pallas_call x1, Pallas kernels, attend_back(): pl.pallas_call(functools.partial(attend_back_kernel, 1.0 / math.sqrt(HEAD...  68.2 us
    pallas_call x1, Pallas kernels, attend(): pl.pallas_call(functools.partial(attend_kernel, 1.0 / math.sqrt(HEAD_DIM)...  67.3 us
    pallas_call x1, Pallas kernels, scatter_rows(): pl.pallas_call(functools.partial(scatter_kernel, bits, orders), in_specs=...  65.8 us
    pallas_call x1, Pallas kernels, gather_rows(): pl.pallas_call(functools.partial(gather_kernel, bits, orders), in_specs=[...  64.9 us
  transfers between devices with their start and end apart: 30, of which 6 were waited for; matrix products, arithmetic and copies ran while one was open for 31% of the time, Pallas kernels for 24%

profile of v4, /device:TPU:0, one launch (start us, length us, event | category | flops | bytes accessed | tf_op | source)
XLA Modules:
  0.0 829.8 jit_solution(16113711185603652663)
XLA Ops:
  13.3 64.9 %gather_rows.1 = (bf16[2,2,2,2,2,32,3328]{6,5,4,3,2,1,0:T(8,128)(2,1)}, bf16[2,1024,1024]{2,1,0:T(8,128)(2,1)}, bf16[2,1024,1024]{2,1,0:T(8,128)(2,1)}, bf16[1024,1024]{1,0:T(8,128)(2,1)}) custom-call(bf16[32,3328]{1,0:T(8,128)(2,1)} %fusion.149.own_ref, bf16[1,2,1024,1024]{3,2,1,0:T(8,128)(2,1)} %inner_ref.1, bf16[1,2,1024,1024]{3,2,1,0:T(8,128)(2,1)} %outer_ref.1), custom_call_target="tpu_custom_call" | custom-call | bytes 85196800 | tf_op jit(solution)/shard_map/gather_rows/pallas_call | solution.py:401
  82.4 5.2 fusion.10
  91.7 51.3 %collective-permute-done.k2.v2 = bf16[2,256,2048]{2,1,0:T(8,128)(2,1)} collective-permute-done((bf16[2,256,2048]{2,1,0:T(8,128)(2,1)S(1)}, bf16[2,256,2048]{2,1,0:T(8,128)(2,1)}, u32[]{:S(2)}, u32[]{:S(2)}) %collective-permute-start) | collective-permute-done | bytes 2097184 | tf_op jit(solution)/shard_map/ppermute | solution.py:65
  151.8 4.3 fusion.122
  159.1 67.3 %attend.1 = (bf16[2,256,1024]{2,1,0:T(8,128)(2,1)}, bf16[1024,1024]{1,0:T(8,128)(2,1)}) custom-call(bf16[2,256,1024]{2,1,0:T(8,128)(2,1)} %bitcast.400, bf16[2,256,2048]{2,1,0:T(8,128)(2,1)} %bitcast.327, bf16[2,256,2048]{2,1,0:T(8,128)(2,1)} %bitcast.328, bf16[2,256,2048]{2,1,0:T(8,128)(2,1)} %collective-permute-done.1.k1.v1, ...), custom_call_target="tpu_custom_call" | custom-call | flops 9663676416 | bytes 8388608 | tf_op jit(solution)/shard_map/attend/pallas_call | solution.py:196
  231.2 4.1 fusion.74
  249.2 6.3 all-to-all-start
  260.4 20.6 %all-to-all-done = bf16[8,64,1024]{2,1,0:T(8,128)(2,1)S(1)} async-done(((bf16[8,64,1024]{2,1,0:T(8,128)(2,1)}), bf16[8,64,1024]{2,1,0:T(8,128)(2,1)S(1)}, u32[]{:S(2)}, u32[]{:S(2)}) %all-to-all-start) | async-done | bytes 1048608 | tf_op jit(solution)/shard_map/all_to_all | solution.py:614
  292.6 4.5 multiply_convert_fusion.21
  303.7 4.5 multiply_convert_fusion.18
  314.1 4.6 multiply_convert_fusion.14
  394.2 5.9 all-to-all-start.3
  400.2 4.3 convolution_convert_fusion.9
  419.4 6.8 all-to-all-done.3
  459.2 6.3 collective-permute-done.10
  489.9 4.3 fusion.125
  499.1 5.7 all-to-all-start.1
  505.3 5.3 add_convert_fusion.1.ride_ref
  510.5 4.6 add_convert_fusion
  515.1 27.6 %collective-permute-done.11 = bf16[1024,1024]{1,0:T(8,128)(2,1)} collective-permute-done((bf16[1024,1024]{1,0:T(8,128)(2,1)}, bf16[1024,1024]{1,0:T(8,128)(2,1)}, u32[]{:S(2)}, u32[]{:S(2)}) %collective-permute-start.11) | collective-permute-done | bytes 2097184 | tf_op jit(solution)/shard_map/ppermute | solution.py:65
  542.7 68.2 %attend_back.1 = (bf16[2,256,1024]{2,1,0:T(8,128)(2,1)}, bf16[2,2,256,1024]{3,2,1,0:T(8,128)(2,1)}, bf16[2,2,256,1024]{3,2,1,0:T(8,128)(2,1)}, bf16[2,2,256,1024]{3,2,1,0:T(8,128)(2,1)}, bf16[1024,1024]{1,0:T(8,128)(2,1)}) custom-call(bf16[2,256,1024]{2,1,0:T(8,128)(2,1)} %bitcast.401, bf16[2,256,2048]{2,1,0:T(8,128)(2,1)} %bitcast.329, ...), custom_call_target="tpu_custom_call" | custom-call | flops 24159191040 | bytes 16777216 | tf_op jit(solution)/shard_map/attend_back/pallas_call | solution.py:221
  612.3 4.1 convolution_convert_fusion.4
  640.2 3.9 bitcast_convert_fusion
  647.1 5.8 add_bitcast_fusion.2
  653.0 5.8 add_bitcast_fusion
  658.8 39.4 %collective-permute-done.15 = bf16[2,2,256,1024]{3,2,1,0:T(8,128)(2,1)} collective-permute-done((bf16[2,2,256,1024]{3,2,1,0:T(8,128)(2,1)}, bf16[2,2,256,1024]{3,2,1,0:T(8,128)(2,1)}, u32[]{:S(2)}, u32[]{:S(2)}) %collective-permute-start.15) | collective-permute-done | bytes 2097184 | tf_op jit(solution)/shard_map/ppermute | solution.py:65
  714.8 6.4 all-to-all-start.4
  721.2 4.2 add_add_fusion.4
  725.5 65.8 %scatter_rows.1 = f32[32,3072]{1,0:T(8,128)} custom-call(bf16[2,2,2,2,2,32,3072]{6,5,4,3,2,1,0:T(8,128)(2,1)} %bitcast.316), custom_call_target="tpu_custom_call" | custom-call | bytes 157286400 | tf_op jit(solution)/shard_map/scatter_rows/pallas_call | solution.py:491
  795.7 4.3 maximum_bitcast_fusion
  803.1 4.2 maximum_bitcast_fusion.1
  812.3 4.5 reshape.410
  (495 shorter events, 285.1 us)
Async XLA Ops:
  7.2 219.6 %all-gather.2.cloned.1.call-start = ((), (), s32[]{:S(2)}) async-start(), calls=%async_computation.6 | async-start | bytes 19464192 | tf_op jit(solution)/shard_map/all_gather | solution.py:556
  81.4 149.2 %copy-start.57 = (f32[1,1024]{1,0:T(1,128)}, f32[1,1024]{1,0:T(1,128)S(1)}, u32[]{:S(2)}) copy-start(f32[1,1024]{1,0:T(1,128)S(1)} %get-tuple-element.141) | copy-start | bytes 12292
  87.6 55.4 %collective-permute-start = (bf16[2,256,2048]{2,1,0:T(8,128)(2,1)S(1)}, bf16[2,256,2048]{2,1,0:T(8,128)(2,1)}, u32[]{:S(2)}, u32[]{:S(2)}) collective-permute-start(bf16[2,256,2048]{2,1,0:T(8,128)(2,1)S(1)} %bitcast.325), channel_id=1, source_target_pairs={{0,16},{8,24},{1,17},{9,25},{2,18},{10,26},{3,19},{11,27},{4,20},{... | collective-permute-start | bytes 6291464 | tf_op jit(solution)/shard_map/ppermute | solution.py:65
  144.6 14.5 %collective-permute-start.1 = (bf16[2,256,2048]{2,1,0:T(8,128)(2,1)}, bf16[2,256,2048]{2,1,0:T(8,128)(2,1)}, u32[]{:S(2)}, u32[]{:S(2)}) collective-permute-start(bf16[2,256,2048]{2,1,0:T(8,128)(2,1)} %broadcast_select_fusion), channel_id=1, source_target_pairs={{0,8},{16,24},{24,16},{1,9},{17,25},{25,17},{2,10},{18,26},{26,18}... | collective-permute-start | bytes 6291464 | tf_op jit(solution)/shard_map/ppermute | solution.py:65
  226.4 58.2 %collective-permute-start.2 = (bf16[1024,1024]{1,0:T(8,128)(2,1)}, bf16[1024,1024]{1,0:T(8,128)(2,1)}, u32[]{:S(2)}, u32[]{:S(2)}) collective-permute-start(bf16[1024,1024]{1,0:T(8,128)(2,1)} %get-tuple-element.66), channel_id=1, source_target_pairs={{0,16},{16,0},{8,24},{24,8},{1,17},{17,1},{9,25},{25,9},{2,18},{18... | collective-permute-start | bytes 6291464 | tf_op jit(solution)/shard_map/ppermute | solution.py:65
  249.2 31.8 %all-to-all-start = ((bf16[8,64,1024]{2,1,0:T(8,128)(2,1)}), bf16[8,64,1024]{2,1,0:T(8,128)(2,1)S(1)}, u32[]{:S(2)}, u32[]{:S(2)}) async-start(bf16[8,64,1024]{2,1,0:T(8,128)(2,1)} %bitcast.18), calls=%async_computation | async-start | bytes 2097152 | tf_op jit(solution)/shard_map/all_to_all | solution.py:614
  258.3 45.4 %collective-permute-start.3 = (bf16[1024,1024]{1,0:T(8,128)(2,1)}, bf16[1024,1024]{1,0:T(8,128)(2,1)}, u32[]{:S(2)}, u32[]{:S(2)}) collective-permute-start(bf16[1024,1024]{1,0:T(8,128)(2,1)} %get-tuple-element.72), channel_id=1, source_target_pairs={{0,8},{8,0},{16,24},{24,16},{1,9},{9,1},{17,25},{25,17},{2,10},{10... | collective-permute-start | bytes 6291464 | tf_op jit(solution)/shard_map/ppermute | solution.py:65
  258.4 49.8 %collective-permute-start.4 = (bf16[1024,1024]{1,0:T(8,128)(2,1)}, bf16[1024,1024]{1,0:T(8,128)(2,1)}, u32[]{:S(2)}, u32[]{:S(2)}) collective-permute-start(bf16[1024,1024]{1,0:T(8,128)(2,1)} %get-tuple-element.73), channel_id=1, source_target_pairs={{0,8},{8,0},{16,24},{24,16},{1,9},{9,1},{17,25},{25,17},{2,10},{10... | collective-permute-start | bytes 6291464 | tf_op jit(solution)/shard_map/ppermute | solution.py:65
  258.9 70.9 %collective-permute-start.5 = (bf16[1024,1024]{1,0:T(8,128)(2,1)}, bf16[1024,1024]{1,0:T(8,128)(2,1)}, u32[]{:S(2)}, u32[]{:S(2)}) collective-permute-start(bf16[1024,1024]{1,0:T(8,128)(2,1)} %get-tuple-element.75), channel_id=1, source_target_pairs={{0,16},{16,0},{8,24},{24,8},{1,17},{17,1},{9,25},{25,9},{2,18},{18... | collective-permute-start | bytes 6291464 | tf_op jit(solution)/shard_map/ppermute | solution.py:65
  281.0 37.7 %all-to-all-start.2 = ((bf16[8,64,1024]{2,1,0:T(8,128)(2,1)}), bf16[8,64,1024]{2,1,0:T(8,128)(2,1)S(1)}, u32[]{:S(2)}, u32[]{:S(2)}) async-start(bf16[8,64,1024]{2,1,0:T(8,128)(2,1)} %bitcast.319), calls=%async_computation.2 | async-start | bytes 2097152 | tf_op jit(solution)/shard_map/all_to_all | solution.py:646
  329.8 19.7 %collective-permute-start.7 = (bf16[1024,1024]{1,0:T(8,128)(2,1)}, bf16[1024,1024]{1,0:T(8,128)(2,1)S(1)}, u32[]{:S(2)}, u32[]{:S(2)}) collective-permute-start(bf16[1024,1024]{1,0:T(8,128)(2,1)} %collective-permute-done.5), channel_id=1, source_target_pairs={{0,8},{8,0},{16,24},{24,16},{1,9},{9,1},{17,25},{25,17},{2,10},{10... | collective-permute-start | bytes 6291464 | tf_op jit(solution)/shard_map/ppermute | solution.py:65
  329.9 17.2 %collective-permute-start.6 = (bf16[1024,1024]{1,0:T(8,128)(2,1)}, bf16[1024,1024]{1,0:T(8,128)(2,1)S(1)}, u32[]{:S(2)}, u32[]{:S(2)}) collective-permute-start(bf16[1024,1024]{1,0:T(8,128)(2,1)} %collective-permute-done.2), channel_id=1, source_target_pairs={{0,8},{8,0},{16,24},{24,16},{1,9},{9,1},{17,25},{25,17},{2,10},{10... | collective-permute-start | bytes 6291464 | tf_op jit(solution)/shard_map/ppermute | solution.py:65
  377.1 11.8 %collective-permute-start.8 = (bf16[1024,1024]{1,0:T(8,128)(2,1)S(1)}, bf16[1024,1024]{1,0:T(8,128)(2,1)S(1)}, u32[]{:S(2)}, u32[]{:S(2)}) collective-permute-start(bf16[1024,1024]{1,0:T(8,128)(2,1)S(1)} %convolution_convert_fusion.13), channel_id=1, source_target_pairs={{0,8},{8,0},{16,24},{24,16},{1,9},{9,1},{17,25},{25,17},{2,10},{10... | collective-permute-start | bytes 6291464 | tf_op jit(solution)/shard_map/ppermute | solution.py:65
  377.2 14.4 %collective-permute-start.9 = (bf16[1024,1024]{1,0:T(8,128)(2,1)S(1)}, bf16[1024,1024]{1,0:T(8,128)(2,1)S(1)}, u32[]{:S(2)}, u32[]{:S(2)}) collective-permute-start(bf16[1024,1024]{1,0:T(8,128)(2,1)S(1)} %copy-done.87), channel_id=1, source_target_pairs={{0,8},{8,0},{16,24},{24,16},{1,9},{9,1},{17,25},{25,17},{2,10},{10... | collective-permute-start | bytes 6291464 | tf_op jit(solution)/shard_map/ppermute | solution.py:65
  394.2 32.0 %all-to-all-start.3 = ((bf16[8,64,1024]{2,1,0:T(8,128)(2,1)}), bf16[8,64,1024]{2,1,0:T(8,128)(2,1)S(1)}, u32[]{:S(2)}, u32[]{:S(2)}) async-start(bf16[8,64,1024]{2,1,0:T(8,128)(2,1)} %bitcast.323), calls=%async_computation.3 | async-start | bytes 2097152 | tf_op jit(solution)/shard_map/all_to_all | solution.py:678
  400.2 407.2 %reduce-scatter.2.cloned.1.call-start = ((), (), s32[]{:S(2)}) async-start(), calls=%async_computation.7 | async-start | bytes 19464192 | tf_op jit(solution)/shard_map/reduce_scatter | solution.py:713
  417.8 47.7 %collective-permute-start.10 = (bf16[1024,1024]{1,0:T(8,128)(2,1)}, bf16[1024,1024]{1,0:T(8,128)(2,1)}, u32[]{:S(2)}, u32[]{:S(2)}) collective-permute-start(bf16[1024,1024]{1,0:T(8,128)(2,1)} %add_convert_fusion.3), channel_id=1, source_target_pairs={{0,16},{16,0},{8,24},{24,8},{1,17},{17,1},{9,25},{25,9},{2,18},{18... | collective-permute-start | bytes 6291464 | tf_op jit(solution)/shard_map/ppermute | solution.py:65
  494.2 11.1 %collective-permute-start.12 = (bf16[1024,1024]{1,0:T(8,128)(2,1)}, bf16[1024,1024]{1,0:T(8,128)(2,1)}, u32[]{:S(2)}, u32[]{:S(2)}) collective-permute-start(bf16[1024,1024]{1,0:T(8,128)(2,1)} %convolution_convert_fusion.11), channel_id=1, source_target_pairs={{0,8},{8,0},{16,24},{24,16},{1,9},{9,1},{17,25},{25,17},{2,10},{10... | collective-permute-start | bytes 6291464 | tf_op jit(solution)/shard_map/ppermute | solution.py:65
  494.3 16.3 %collective-permute-start.13 = (bf16[1024,1024]{1,0:T(8,128)(2,1)}, bf16[1024,1024]{1,0:T(8,128)(2,1)}, u32[]{:S(2)}, u32[]{:S(2)}) collective-permute-start(bf16[1024,1024]{1,0:T(8,128)(2,1)} %convolution_convert_fusion.10), channel_id=1, source_target_pairs={{0,8},{8,0},{16,24},{24,16},{1,9},{9,1},{17,25},{25,17},{2,10},{10... | collective-permute-start | bytes 6291464 | tf_op jit(solution)/shard_map/ppermute | solution.py:65
  494.8 47.9 %collective-permute-start.11 = (bf16[1024,1024]{1,0:T(8,128)(2,1)}, bf16[1024,1024]{1,0:T(8,128)(2,1)}, u32[]{:S(2)}, u32[]{:S(2)}) collective-permute-start(bf16[1024,1024]{1,0:T(8,128)(2,1)} %add_convert_fusion.2), channel_id=1, source_target_pairs={{0,16},{16,0},{8,24},{24,8},{1,17},{17,1},{9,25},{25,9},{2,18},{18... | collective-permute-start | bytes 6291464 | tf_op jit(solution)/shard_map/ppermute | solution.py:65
  499.1 135.7 %all-to-all-start.1 = ((bf16[8,64,1024]{2,1,0:T(8,128)(2,1)}), bf16[8,64,1024]{2,1,0:T(8,128)(2,1)S(1)}, u32[]{:S(2)}, u32[]{:S(2)}) async-start(bf16[8,64,1024]{2,1,0:T(8,128)(2,1)} %bitcast.324), calls=%async_computation.1 | async-start | bytes 2097152 | tf_op jit(solution)/shard_map/all_to_all | solution.py:639
  610.9 18.3 %collective-permute-start.14 = (bf16[2,2,256,1024]{3,2,1,0:T(8,128)(2,1)}, bf16[2,2,256,1024]{3,2,1,0:T(8,128)(2,1)S(1)}, u32[]{:S(2)}, u32[]{:S(2)}) collective-permute-start(bf16[2,2,256,1024]{3,2,1,0:T(8,128)(2,1)} %get-tuple-element.94), channel_id=1, source_target_pairs={{8,0},{24,16},{16,24},{9,1},{25,17},{17,25},{10,2},{26,18},{18,26}... | collective-permute-start | bytes 6291464 | tf_op jit(solution)/shard_map/ppermute | solution.py:65
  619.2 4.0 collective-permute-start.16
  623.2 4.1 collective-permute-start.17
  624.7 22.5 %collective-permute-start.20 = (bf16[1024,1024]{1,0:T(8,128)(2,1)}, bf16[1024,1024]{1,0:T(8,128)(2,1)}, u32[]{:S(2)}, u32[]{:S(2)}) collective-permute-start(bf16[1024,1024]{1,0:T(8,128)(2,1)} %convolution_convert_fusion.8), channel_id=1, source_target_pairs={{0,8},{8,0},{16,24},{24,16},{1,9},{9,1},{17,25},{25,17},{2,10},{10... | collective-permute-start | bytes 6291464 | tf_op jit(solution)/shard_map/ppermute | solution.py:65
  627.4 25.6 %collective-permute-start.22 = (bf16[1024,1024]{1,0:T(8,128)(2,1)}, bf16[1024,1024]{1,0:T(8,128)(2,1)}, u32[]{:S(2)}, u32[]{:S(2)}) collective-permute-start(bf16[1024,1024]{1,0:T(8,128)(2,1)} %convolution_convert_fusion.9), channel_id=1, source_target_pairs={{0,8},{8,0},{16,24},{24,16},{1,9},{9,1},{17,25},{25,17},{2,10},{10... | collective-permute-start | bytes 6291464 | tf_op jit(solution)/shard_map/ppermute | solution.py:65
  631.6 66.6 %collective-permute-start.15 = (bf16[2,2,256,1024]{3,2,1,0:T(8,128)(2,1)}, bf16[2,2,256,1024]{3,2,1,0:T(8,128)(2,1)}, u32[]{:S(2)}, u32[]{:S(2)}) collective-permute-start(bf16[2,2,256,1024]{3,2,1,0:T(8,128)(2,1)} %fusion.5), channel_id=1, source_target_pairs={{16,0},{24,8},{17,1},{25,9},{18,2},{26,10},{19,3},{27,11},{20,4},{... | collective-permute-start | bytes 6291464 | tf_op jit(solution)/shard_map/ppermute | solution.py:65
  707.5 84.3 %collective-permute-start.19 = (bf16[1024,1024]{1,0:T(8,128)(2,1)}, bf16[1024,1024]{1,0:T(8,128)(2,1)}, u32[]{:S(2)}, u32[]{:S(2)}) collective-permute-start(bf16[1024,1024]{1,0:T(8,128)(2,1)} %add_convert_fusion), channel_id=1, source_target_pairs={{0,16},{16,0},{8,24},{24,8},{1,17},{17,1},{9,25},{25,9},{2,18},{18... | collective-permute-start | bytes 6291464 | tf_op jit(solution)/shard_map/ppermute | solution.py:65
  707.6 84.3 %collective-permute-start.18 = (bf16[1024,1024]{1,0:T(8,128)(2,1)}, bf16[1024,1024]{1,0:T(8,128)(2,1)}, u32[]{:S(2)}, u32[]{:S(2)}) collective-permute-start(bf16[1024,1024]{1,0:T(8,128)(2,1)} %convolution_convert_fusion.4), channel_id=1, source_target_pairs={{0,8},{8,0},{16,24},{24,16},{1,9},{9,1},{17,25},{25,17},{2,10},{10... | collective-permute-start | bytes 6291464 | tf_op jit(solution)/shard_map/ppermute | solution.py:65
  707.7 92.3 %collective-permute-start.21 = (bf16[1024,1024]{1,0:T(8,128)(2,1)}, bf16[1024,1024]{1,0:T(8,128)(2,1)}, u32[]{:S(2)}, u32[]{:S(2)}) collective-permute-start(bf16[1024,1024]{1,0:T(8,128)(2,1)} %convolution_convert_fusion.5), channel_id=1, source_target_pairs={{0,8},{8,0},{16,24},{24,16},{1,9},{9,1},{17,25},{25,17},{2,10},{10... | collective-permute-start | bytes 6291464 | tf_op jit(solution)/shard_map/ppermute | solution.py:65
  714.8 76.5 %all-to-all-start.4 = ((f32[32,2,32]{2,1,0:T(2,128)}), f32[32,2,32]{2,1,0:T(2,128)S(1)}, u32[]{:S(2)}, u32[]{:S(2)}) async-start(f32[32,2,32]{2,1,0:T(2,128)} %maximum_bitcast_fusion.2), calls=%async_computation.4 | async-start | bytes 65536 | tf_op jit(solution)/shard_map/all_to_all | solution.py:746
  725.5 66.4 %copy-start.26 = (bf16[1024,1024]{1,0:T(8,128)(2,1)S(1)}, bf16[1024,1024]{1,0:T(8,128)(2,1)}, u32[]{:S(2)}) copy-start(bf16[1024,1024]{1,0:T(8,128)(2,1)} %convolution_convert_fusion.2) | copy-start | bytes 6291460
  (127 other events, 763.2 us)
Sparse Core Ops, SparseCore 0:
  78.4 137.2 all-gather.1
  494.3 221.7 reduce-scatter.1

commit v5 on v4

--- a/solution.py
+++ b/solution.py
@@ -145,16 +145,11 @@
     v2,
     bias_ref,
     grad_ref,
-    ride_ref,
     dq_ref,
     d0,
     d1,
     d2,
-    rode_ref,
-    send_sem,
-    recv_sem,
 ):
-    ride_chip(ride_ref, rode_ref, send_sem, recv_sem)
     bias = bias_ref[0]
     dq_parts, dk_parts, dv_parts = [], [], []
     for head in range(2):
@@ -211,7 +206,7 @@
     )(query, *operands, bias, ride)
 
 
-def attend_back(query, kv_blocks, bias, grad_attended, ride):
+def attend_back(query, kv_blocks, bias, grad_attended):
     rows, local_len, model_width = query.shape
     groups, spec, in_specs = attention_specs(local_len, model_width, bias.shape[1])
     operands = [block for block in kv_blocks for _ in range(2)]
@@ -221,18 +216,14 @@
     return pl.pallas_call(
         functools.partial(attend_back_kernel, 1.0 / math.sqrt(HEAD_DIM)),
         grid=(rows, groups),
-        in_specs=in_specs + [spec, pl.BlockSpec(memory_space=pl.ANY)],
-        out_specs=[spec, pair_spec, pair_spec, pair_spec, pl.BlockSpec(memory_space=pl.ANY)],
-        out_shape=[jax.ShapeDtypeStruct(query.shape, bf16)]
-        + [pair_shape] * 3
-        + [jax.ShapeDtypeStruct(ride.shape, ride.dtype)],
-        scratch_shapes=[pltpu.SemaphoreType.DMA, pltpu.SemaphoreType.DMA],
-        compiler_params=pltpu.CompilerParams(collective_id=3, has_side_effects=True),
+        in_specs=in_specs + [spec],
+        out_specs=[spec, pair_spec, pair_spec, pair_spec],
+        out_shape=[jax.ShapeDtypeStruct(query.shape, bf16)] + [pair_shape] * 3,
         cost_estimate=pl.CostEstimate(
             flops=flops * 6, bytes_accessed=16 * query.size * 2, transcendentals=0
         ),
         name="attend_back",
-    )(query, *operands, bias, grad_attended, ride)
+    )(query, *operands, bias, grad_attended)
 
 
 def ffn_forward(normed, inner_parts, outer_parts, residual):
@@ -707,13 +698,11 @@
     rest_grad = row_major(rest_grad)
     grad_attended = product_bt(grad_proj, proj_full).astype(bf16)
     grad_attended, rest_grad = together(grad_attended, rest_grad)
-    grad_attended, inner1.got_chip, outer_send, inner_send = together(
-        grad_attended, inner1.got_chip, outer0.chip_sum(), inner0.chip_sum()
-    )
     rest_sum = lax.psum_scatter(rest_grad, every, scatter_dimension=0, tiled=True).astype(f32)
-    grad_query, grad_kv0, grad_kv1, grad_kv2, outer0.got_chip = attend_back(
-        query, kv_blocks, bias, grad_attended.reshape(query.shape), outer_send
-    )
+    grad_query, grad_kv0, grad_kv1, grad_kv2 = attend_back(
+        query, kv_blocks, bias, grad_attended.reshape(query.shape)
+    )
+    grad_kv1, inner1.got_chip = together(grad_kv1, inner1.got_chip)
     got_near = seq_send(grad_kv1, [(1, 0), (3, 2), (2, 3)])
     far_sum = jnp.where(
         seq_index == 3, (grad_kv2.astype(f32) + got_near.astype(f32)).astype(bf16), grad_kv2
@@ -726,7 +715,9 @@
         part.send_core(values)
     for part, values in zip(sums[0], held[2:]):
         part.own = values
-    inner0.send_chip(together(inner_send, got_far)[0])
+    outer_send, inner_send, got_far = together(outer0.chip_sum(), inner0.chip_sum(), got_far)
+    outer0.send_chip(outer_send)
+    inner0.send_chip(inner_send)
     kv_sum = grad_kv0.astype(f32) + got_far.astype(f32)
     kv_sum = kv_sum + jnp.where(seq_index % 2 == 0, got_near.astype(f32), 0.0)
     kv_sum = kv_sum.astype(bf16).reshape(2, token_count, model_width)

time: 838 us -> 828 us (0.988)
    pallas_call x1, Pallas kernels: 68.2 us -> 36.3 us  [attend_back(): pl.pallas_call(functools.partial(attend_back_kernel, 1.0 / math.sqrt(HEAD...]
    pallas_call x1, Pallas kernels: 65.8 us -> 90.1 us  [scatter_rows(): pl.pallas_call(functools.partial(scatter_kernel, bits, orders), in_specs=...]
    ppermute x23 -> x24, waiting for transfers between devices: 125 us -> 117 us  [seq_send(): return lax.ppermute(values, 'seq', pairs)]
    ppermute x23 -> x24, starting transfers between devices: 19.5 us -> 21.8 us  [seq_send(): return lax.ppermute(values, 'seq', pairs)]
    unnamed x265 -> x261, local copies, waits for them, and re-layouts: 17.8 us -> 18.4 us
  transfers between devices with their start and end apart: 30 -> 31, of which waited for: 6 -> 6; matrix products, arithmetic and copies ran while one was open for 31% -> 31% of each run, Pallas kernels for 24% -> 24%
where the time goes in v5:
time: 828 us; the launch traced here: 819 us
  Pallas kernels  260 us (31%)
  matrix products  221 us (27%)
  waiting for transfers between devices  145 us (18%)
  other arithmetic  69.3 us (8%)
  local copies, waits for them, and re-layouts  54.4 us (7%)
  starting transfers between devices  49.4 us (6%)
  between operations  20 us (2%)
    ppermute x24, waiting for transfers between devices, seq_send(): return lax.ppermute(values, 'seq', pairs)  117 us
    pallas_call x1, Pallas kernels, scatter_rows(): pl.pallas_call(functools.partial(scatter_kernel, bits, orders), in_specs=...  90.1 us
    dot_general x28, matrix products, product_at(): lax.dot_general(left_side, right_side, (((0,), (0,)), ((), ())), preferre...  80.6 us
    dot_general x28, matrix products, product_bt(): lax.dot_general(left_side, right_side, (((1,), (1,)), ((), ())), preferre...  71.2 us
    dot_general x27, matrix products, product(): return jnp.dot(left_side, right_side, preferred_element_type=f32)  68.6 us
    pallas_call x1, Pallas kernels, attend(): pl.pallas_call(functools.partial(attend_kernel, 1.0 / math.sqrt(HEAD_DIM)...  68.6 us
    pallas_call x1, Pallas kernels, gather_rows(): pl.pallas_call(functools.partial(gather_kernel, bits, orders), in_specs=[...  64.9 us
    pallas_call x1, Pallas kernels, attend_back(): pl.pallas_call(functools.partial(attend_back_kernel, 1.0 / math.sqrt(HEAD...  36.3 us
  transfers between devices with their start and end apart: 31, of which 6 were waited for; matrix products, arithmetic and copies ran while one was open for 31% of the time, Pallas kernels for 24%

profile of v5, /device:TPU:0, one launch (start us, length us, event | category | flops | bytes accessed | tf_op | source)
XLA Modules:
  0.0 818.9 jit_solution(17146843936700361157)
XLA Ops:
  13.3 64.9 %gather_rows.1 = (bf16[2,2,2,2,2,32,3328]{6,5,4,3,2,1,0:T(8,128)(2,1)}, bf16[2,1024,1024]{2,1,0:T(8,128)(2,1)}, bf16[2,1024,1024]{2,1,0:T(8,128)(2,1)}, bf16[1024,1024]{1,0:T(8,128)(2,1)}) custom-call(bf16[32,3328]{1,0:T(8,128)(2,1)} %fusion.149.own_ref, bf16[1,2,1024,1024]{3,2,1,0:T(8,128)(2,1)} %inner_ref.1, bf16[1,2,1024,1024]{3,2,1,0:T(8,128)(2,1)} %outer_ref.1), custom_call_target="tpu_custom_call" | custom-call | bytes 85196800 | tf_op jit(solution)/shard_map/gather_rows/pallas_call | solution.py:392
  81.8 5.2 fusion.10
  91.2 51.3 %collective-permute-done.k2.v2 = bf16[2,256,2048]{2,1,0:T(8,128)(2,1)} collective-permute-done((bf16[2,256,2048]{2,1,0:T(8,128)(2,1)S(1)}, bf16[2,256,2048]{2,1,0:T(8,128)(2,1)}, u32[]{:S(2)}, u32[]{:S(2)}) %collective-permute-start) | collective-permute-done | bytes 2097184 | tf_op jit(solution)/shard_map/ppermute | solution.py:65
  151.2 4.3 fusion.122
  158.4 68.6 %attend.1 = (bf16[2,256,1024]{2,1,0:T(8,128)(2,1)}, bf16[1024,1024]{1,0:T(8,128)(2,1)}) custom-call(bf16[2,256,1024]{2,1,0:T(8,128)(2,1)} %bitcast.400, bf16[2,256,2048]{2,1,0:T(8,128)(2,1)} %bitcast.327, bf16[2,256,2048]{2,1,0:T(8,128)(2,1)} %bitcast.328, bf16[2,256,2048]{2,1,0:T(8,128)(2,1)} %collective-permute-done.1.k1.v1, ...), custom_call_target="tpu_custom_call" | custom-call | flops 9663676416 | bytes 8388608 | tf_op jit(solution)/shard_map/attend/pallas_call | solution.py:191
  232.1 4.0 fusion.74
  249.6 6.4 all-to-all-start
  260.9 20.6 %all-to-all-done = bf16[8,64,1024]{2,1,0:T(8,128)(2,1)S(1)} async-done(((bf16[8,64,1024]{2,1,0:T(8,128)(2,1)}), bf16[8,64,1024]{2,1,0:T(8,128)(2,1)S(1)}, u32[]{:S(2)}, u32[]{:S(2)}) %all-to-all-start) | async-done | bytes 1048608 | tf_op jit(solution)/shard_map/all_to_all | solution.py:605
  293.2 4.5 multiply_convert_fusion.21
  304.3 4.5 multiply_convert_fusion.18
  314.7 4.6 multiply_convert_fusion.14
  394.2 5.9 all-to-all-start.3
  400.2 4.3 convolution_convert_fusion.9
  419.5 6.7 all-to-all-done.3
  459.2 6.4 collective-permute-done.10
  490.0 4.3 fusion.125
  498.3 5.7 all-to-all-start.1
  504.6 4.1 convolution_convert_fusion.4
  513.1 36.3 %attend_back.1 = (bf16[2,256,1024]{2,1,0:T(8,128)(2,1)}, bf16[2,2,256,1024]{3,2,1,0:T(8,128)(2,1)}, bf16[2,2,256,1024]{3,2,1,0:T(8,128)(2,1)}, bf16[2,2,256,1024]{3,2,1,0:T(8,128)(2,1)}) custom-call(bf16[2,256,1024]{2,1,0:T(8,128)(2,1)} %bitcast.401, bf16[2,256,2048]{2,1,0:T(8,128)(2,1)} %bitcast.329, bf16[2,256,2048]{2,1,0:T(8,128)(2,1)} %bitcast.330, ...), custom_call_target="tpu_custom_call" | custom-call | flops 24159191040 | bytes 16777216 | tf_op jit(solution)/shard_map/attend_back/pallas_call | solution.py:216
  549.4 13.1 %collective-permute-done.13 = bf16[1024,1024]{1,0:T(8,128)(2,1)} collective-permute-done((bf16[1024,1024]{1,0:T(8,128)(2,1)}, bf16[1024,1024]{1,0:T(8,128)(2,1)}, u32[]{:S(2)}, u32[]{:S(2)}) %collective-permute-start.13) | collective-permute-done | bytes 2097184 | tf_op jit(solution)/shard_map/ppermute | solution.py:65
  564.0 4.2 convolution_convert_fusion.5
  594.7 4.3 add_convert_fusion.1
  599.0 4.6 add_convert_fusion
  603.7 5.9 add_bitcast_fusion.2
  609.6 5.3 add_bitcast_fusion
  614.9 46.4 %collective-permute-done.15 = bf16[2,2,256,1024]{3,2,1,0:T(8,128)(2,1)S(1)} collective-permute-done((bf16[2,2,256,1024]{3,2,1,0:T(8,128)(2,1)S(1)}, bf16[2,2,256,1024]{3,2,1,0:T(8,128)(2,1)S(1)}, u32[]{:S(2)}, u32[]{:S(2)}) %collective-permute-start.15) | collective-permute-done | bytes 2097184 | tf_op jit(solution)/shard_map/ppermute | solution.py:65
  679.2 6.1 all-to-all-start.4
  685.3 4.2 add_add_fusion.4
  689.5 90.1 %scatter_rows.1 = f32[32,3072]{1,0:T(8,128)} custom-call(bf16[2,2,2,2,2,32,3072]{6,5,4,3,2,1,0:T(8,128)(2,1)} %bitcast.316), custom_call_target="tpu_custom_call" | custom-call | bytes 157286400 | tf_op jit(solution)/shard_map/scatter_rows/pallas_call | solution.py:482
  784.0 4.3 maximum_bitcast_fusion
  792.1 4.2 maximum_bitcast_fusion.1
  801.2 4.5 reshape.410
  (493 shorter events, 289.2 us)
Async XLA Ops:
  7.2 220.2 %all-gather.2.cloned.1.call-start = ((), (), s32[]{:S(2)}) async-start(), calls=%async_computation.6 | async-start | bytes 19464192 | tf_op jit(solution)/shard_map/all_gather | solution.py:547
  80.9 150.8 %copy-start.54 = (f32[1,1024]{1,0:T(1,128)}, f32[1,1024]{1,0:T(1,128)S(1)}, u32[]{:S(2)}) copy-start(f32[1,1024]{1,0:T(1,128)S(1)} %get-tuple-element.139) | copy-start | bytes 12292
  87.1 55.4 %collective-permute-start = (bf16[2,256,2048]{2,1,0:T(8,128)(2,1)S(1)}, bf16[2,256,2048]{2,1,0:T(8,128)(2,1)}, u32[]{:S(2)}, u32[]{:S(2)}) collective-permute-start(bf16[2,256,2048]{2,1,0:T(8,128)(2,1)S(1)} %bitcast.325), channel_id=1, source_target_pairs={{0,16},{8,24},{1,17},{9,25},{2,18},{10,26},{3,19},{11,27},{4,20},{... | collective-permute-start | bytes 6291464 | tf_op jit(solution)/shard_map/ppermute | solution.py:65
  144.0 14.4 %collective-permute-start.1 = (bf16[2,256,2048]{2,1,0:T(8,128)(2,1)}, bf16[2,256,2048]{2,1,0:T(8,128)(2,1)}, u32[]{:S(2)}, u32[]{:S(2)}) collective-permute-start(bf16[2,256,2048]{2,1,0:T(8,128)(2,1)} %broadcast_select_fusion), channel_id=1, source_target_pairs={{0,8},{16,24},{24,16},{1,9},{17,25},{25,17},{2,10},{18,26},{26,18}... | collective-permute-start | bytes 6291464 | tf_op jit(solution)/shard_map/ppermute | solution.py:65
  226.9 58.2 %collective-permute-start.2 = (bf16[1024,1024]{1,0:T(8,128)(2,1)}, bf16[1024,1024]{1,0:T(8,128)(2,1)}, u32[]{:S(2)}, u32[]{:S(2)}) collective-permute-start(bf16[1024,1024]{1,0:T(8,128)(2,1)} %get-tuple-element.65), channel_id=1, source_target_pairs={{0,16},{16,0},{8,24},{24,8},{1,17},{17,1},{9,25},{25,9},{2,18},{18... | collective-permute-start | bytes 6291464 | tf_op jit(solution)/shard_map/ppermute | solution.py:65
  249.6 31.9 %all-to-all-start = ((bf16[8,64,1024]{2,1,0:T(8,128)(2,1)}), bf16[8,64,1024]{2,1,0:T(8,128)(2,1)S(1)}, u32[]{:S(2)}, u32[]{:S(2)}) async-start(bf16[8,64,1024]{2,1,0:T(8,128)(2,1)} %bitcast.18), calls=%async_computation | async-start | bytes 2097152 | tf_op jit(solution)/shard_map/all_to_all | solution.py:605
  258.9 45.4 %collective-permute-start.3 = (bf16[1024,1024]{1,0:T(8,128)(2,1)}, bf16[1024,1024]{1,0:T(8,128)(2,1)}, u32[]{:S(2)}, u32[]{:S(2)}) collective-permute-start(bf16[1024,1024]{1,0:T(8,128)(2,1)} %get-tuple-element.71), channel_id=1, source_target_pairs={{0,8},{8,0},{16,24},{24,16},{1,9},{9,1},{17,25},{25,17},{2,10},{10... | collective-permute-start | bytes 6291464 | tf_op jit(solution)/shard_map/ppermute | solution.py:65
  259.0 49.8 %collective-permute-start.4 = (bf16[1024,1024]{1,0:T(8,128)(2,1)}, bf16[1024,1024]{1,0:T(8,128)(2,1)}, u32[]{:S(2)}, u32[]{:S(2)}) collective-permute-start(bf16[1024,1024]{1,0:T(8,128)(2,1)} %get-tuple-element.72), channel_id=1, source_target_pairs={{0,8},{8,0},{16,24},{24,16},{1,9},{9,1},{17,25},{25,17},{2,10},{10... | collective-permute-start | bytes 6291464 | tf_op jit(solution)/shard_map/ppermute | solution.py:65
  259.5 70.9 %collective-permute-start.5 = (bf16[1024,1024]{1,0:T(8,128)(2,1)}, bf16[1024,1024]{1,0:T(8,128)(2,1)}, u32[]{:S(2)}, u32[]{:S(2)}) collective-permute-start(bf16[1024,1024]{1,0:T(8,128)(2,1)} %get-tuple-element.74), channel_id=1, source_target_pairs={{0,16},{16,0},{8,24},{24,8},{1,17},{17,1},{9,25},{25,9},{2,18},{18... | collective-permute-start | bytes 6291464 | tf_op jit(solution)/shard_map/ppermute | solution.py:65
  281.5 37.8 %all-to-all-start.2 = ((bf16[8,64,1024]{2,1,0:T(8,128)(2,1)}), bf16[8,64,1024]{2,1,0:T(8,128)(2,1)S(1)}, u32[]{:S(2)}, u32[]{:S(2)}) async-start(bf16[8,64,1024]{2,1,0:T(8,128)(2,1)} %bitcast.319), calls=%async_computation.2 | async-start | bytes 2097152 | tf_op jit(solution)/shard_map/all_to_all | solution.py:637
  330.4 19.7 %collective-permute-start.7 = (bf16[1024,1024]{1,0:T(8,128)(2,1)}, bf16[1024,1024]{1,0:T(8,128)(2,1)S(1)}, u32[]{:S(2)}, u32[]{:S(2)}) collective-permute-start(bf16[1024,1024]{1,0:T(8,128)(2,1)} %collective-permute-done.5), channel_id=1, source_target_pairs={{0,8},{8,0},{16,24},{24,16},{1,9},{9,1},{17,25},{25,17},{2,10},{10... | collective-permute-start | bytes 6291464 | tf_op jit(solution)/shard_map/ppermute | solution.py:65
  330.5 17.2 %collective-permute-start.6 = (bf16[1024,1024]{1,0:T(8,128)(2,1)}, bf16[1024,1024]{1,0:T(8,128)(2,1)S(1)}, u32[]{:S(2)}, u32[]{:S(2)}) collective-permute-start(bf16[1024,1024]{1,0:T(8,128)(2,1)} %collective-permute-done.2), channel_id=1, source_target_pairs={{0,8},{8,0},{16,24},{24,16},{1,9},{9,1},{17,25},{25,17},{2,10},{10... | collective-permute-start | bytes 6291464 | tf_op jit(solution)/shard_map/ppermute | solution.py:65
  377.1 11.8 %collective-permute-start.8 = (bf16[1024,1024]{1,0:T(8,128)(2,1)S(1)}, bf16[1024,1024]{1,0:T(8,128)(2,1)S(1)}, u32[]{:S(2)}, u32[]{:S(2)}) collective-permute-start(bf16[1024,1024]{1,0:T(8,128)(2,1)S(1)} %convolution_convert_fusion.13), channel_id=1, source_target_pairs={{0,8},{8,0},{16,24},{24,16},{1,9},{9,1},{17,25},{25,17},{2,10},{10... | collective-permute-start | bytes 6291464 | tf_op jit(solution)/shard_map/ppermute | solution.py:65
  377.2 14.4 %collective-permute-start.9 = (bf16[1024,1024]{1,0:T(8,128)(2,1)S(1)}, bf16[1024,1024]{1,0:T(8,128)(2,1)S(1)}, u32[]{:S(2)}, u32[]{:S(2)}) collective-permute-start(bf16[1024,1024]{1,0:T(8,128)(2,1)S(1)} %copy-done.84), channel_id=1, source_target_pairs={{0,8},{8,0},{16,24},{24,16},{1,9},{9,1},{17,25},{25,17},{2,10},{10... | collective-permute-start | bytes 6291464 | tf_op jit(solution)/shard_map/ppermute | solution.py:65
  394.2 32.0 %all-to-all-start.3 = ((bf16[8,64,1024]{2,1,0:T(8,128)(2,1)}), bf16[8,64,1024]{2,1,0:T(8,128)(2,1)S(1)}, u32[]{:S(2)}, u32[]{:S(2)}) async-start(bf16[8,64,1024]{2,1,0:T(8,128)(2,1)} %bitcast.323), calls=%async_computation.3 | async-start | bytes 2097152 | tf_op jit(solution)/shard_map/all_to_all | solution.py:669
  400.2 396.2 %reduce-scatter.2.cloned.1.call-start = ((), (), s32[]{:S(2)}) async-start(), calls=%async_computation.7 | async-start | bytes 19464192 | tf_op jit(solution)/shard_map/reduce_scatter | solution.py:701
  418.0 47.6 %collective-permute-start.10 = (bf16[1024,1024]{1,0:T(8,128)(2,1)}, bf16[1024,1024]{1,0:T(8,128)(2,1)}, u32[]{:S(2)}, u32[]{:S(2)}) collective-permute-start(bf16[1024,1024]{1,0:T(8,128)(2,1)} %add_convert_fusion.3), channel_id=1, source_target_pairs={{0,16},{16,0},{8,24},{24,8},{1,17},{17,1},{9,25},{25,9},{2,18},{18... | collective-permute-start | bytes 6291464 | tf_op jit(solution)/shard_map/ppermute | solution.py:65
  498.3 79.4 %all-to-all-start.1 = ((bf16[8,64,1024]{2,1,0:T(8,128)(2,1)}), bf16[8,64,1024]{2,1,0:T(8,128)(2,1)S(1)}, u32[]{:S(2)}, u32[]{:S(2)}) async-start(bf16[8,64,1024]{2,1,0:T(8,128)(2,1)} %bitcast.324), calls=%async_computation.1 | async-start | bytes 2097152 | tf_op jit(solution)/shard_map/all_to_all | solution.py:630
  504.5 63.7 %collective-permute-start.16 = (f32[4,1024]{1,0:T(4,128)S(1)}, f32[4,1024]{1,0:T(4,128)S(1)}, u32[]{:S(2)}, u32[]{:S(2)}) collective-permute-start(f32[4,1024]{1,0:T(4,128)S(1)} %pad_maximum_fusion.2), channel_id=1, source_target_pairs={{0,8},{8,0},{16,24},{24,16},{1,9},{9,1},{17,25},{25,17},{2,10},{10... | collective-permute-start | bytes 49160 | tf_op jit(solution)/shard_map/ppermute | solution.py:65
  511.6 51.0 %collective-permute-start.13 = (bf16[1024,1024]{1,0:T(8,128)(2,1)}, bf16[1024,1024]{1,0:T(8,128)(2,1)}, u32[]{:S(2)}, u32[]{:S(2)}) collective-permute-start(bf16[1024,1024]{1,0:T(8,128)(2,1)} %add_convert_fusion.2), channel_id=1, source_target_pairs={{0,16},{16,0},{8,24},{24,8},{1,17},{17,1},{9,25},{25,9},{2,18},{18... | collective-permute-start | bytes 6291464 | tf_op jit(solution)/shard_map/ppermute | solution.py:65
  562.6 25.1 %collective-permute-start.14 = (bf16[2,2,256,1024]{3,2,1,0:T(8,128)(2,1)}, bf16[2,2,256,1024]{3,2,1,0:T(8,128)(2,1)}, u32[]{:S(2)}, u32[]{:S(2)}) collective-permute-start(bf16[2,2,256,1024]{3,2,1,0:T(8,128)(2,1)} %get-tuple-element.92), channel_id=1, source_target_pairs={{8,0},{24,16},{16,24},{9,1},{25,17},{17,25},{10,2},{26,18},{18,26}... | collective-permute-start | bytes 6291464 | tf_op jit(solution)/shard_map/ppermute | solution.py:65
  568.2 6.1 collective-permute-start.17
  571.4 23.3 %collective-permute-start.11 = (bf16[1024,1024]{1,0:T(8,128)(2,1)}, bf16[1024,1024]{1,0:T(8,128)(2,1)}, u32[]{:S(2)}, u32[]{:S(2)}) collective-permute-start(bf16[1024,1024]{1,0:T(8,128)(2,1)} %convolution_convert_fusion.11), channel_id=1, source_target_pairs={{0,8},{8,0},{16,24},{24,16},{1,9},{9,1},{17,25},{25,17},{2,10},{10... | collective-permute-start | bytes 6291464 | tf_op jit(solution)/shard_map/ppermute | solution.py:65
  574.2 24.8 %collective-permute-start.12 = (bf16[1024,1024]{1,0:T(8,128)(2,1)}, bf16[1024,1024]{1,0:T(8,128)(2,1)}, u32[]{:S(2)}, u32[]{:S(2)}) collective-permute-start(bf16[1024,1024]{1,0:T(8,128)(2,1)} %convolution_convert_fusion.10), channel_id=1, source_target_pairs={{0,8},{8,0},{16,24},{24,16},{1,9},{9,1},{17,25},{25,17},{2,10},{10... | collective-permute-start | bytes 6291464 | tf_op jit(solution)/shard_map/ppermute | solution.py:65
  580.5 23.2 %collective-permute-start.20 = (bf16[1024,1024]{1,0:T(8,128)(2,1)}, bf16[1024,1024]{1,0:T(8,128)(2,1)}, u32[]{:S(2)}, u32[]{:S(2)}) collective-permute-start(bf16[1024,1024]{1,0:T(8,128)(2,1)} %convolution_convert_fusion.8), channel_id=1, source_target_pairs={{0,8},{8,0},{16,24},{24,16},{1,9},{9,1},{17,25},{25,17},{2,10},{10... | collective-permute-start | bytes 6291464 | tf_op jit(solution)/shard_map/ppermute | solution.py:65
  584.2 25.4 %collective-permute-start.23 = (bf16[1024,1024]{1,0:T(8,128)(2,1)}, bf16[1024,1024]{1,0:T(8,128)(2,1)S(1)}, u32[]{:S(2)}, u32[]{:S(2)}) collective-permute-start(bf16[1024,1024]{1,0:T(8,128)(2,1)} %convolution_convert_fusion.9), channel_id=1, source_target_pairs={{0,8},{8,0},{16,24},{24,16},{1,9},{9,1},{17,25},{25,17},{2,10},{10... | collective-permute-start | bytes 6291464 | tf_op jit(solution)/shard_map/ppermute | solution.py:65
  590.4 70.9 %collective-permute-start.15 = (bf16[2,2,256,1024]{3,2,1,0:T(8,128)(2,1)S(1)}, bf16[2,2,256,1024]{3,2,1,0:T(8,128)(2,1)S(1)}, u32[]{:S(2)}, u32[]{:S(2)}) collective-permute-start(bf16[2,2,256,1024]{3,2,1,0:T(8,128)(2,1)S(1)} %fusion.5), channel_id=1, source_target_pairs={{16,0},{24,8},{17,1},{25,9},{18,2},{26,10},{19,3},{27,11},{20,4},{... | collective-permute-start | bytes 6291464 | tf_op jit(solution)/shard_map/ppermute | solution.py:65
  670.3 109.9 %collective-permute-start.19 = (bf16[1024,1024]{1,0:T(8,128)(2,1)}, bf16[1024,1024]{1,0:T(8,128)(2,1)}, u32[]{:S(2)}, u32[]{:S(2)}) collective-permute-start(bf16[1024,1024]{1,0:T(8,128)(2,1)} %add_convert_fusion), channel_id=1, source_target_pairs={{0,16},{16,0},{8,24},{24,8},{1,17},{17,1},{9,25},{25,9},{2,18},{18... | collective-permute-start | bytes 6291464 | tf_op jit(solution)/shard_map/ppermute | solution.py:65
  670.4 109.8 %collective-permute-start.18 = (bf16[1024,1024]{1,0:T(8,128)(2,1)}, bf16[1024,1024]{1,0:T(8,128)(2,1)}, u32[]{:S(2)}, u32[]{:S(2)}) collective-permute-start(bf16[1024,1024]{1,0:T(8,128)(2,1)} %convolution_convert_fusion.4), channel_id=1, source_target_pairs={{0,8},{8,0},{16,24},{24,16},{1,9},{9,1},{17,25},{25,17},{2,10},{10... | collective-permute-start | bytes 6291464 | tf_op jit(solution)/shard_map/ppermute | solution.py:65
  670.5 117.8 %collective-permute-start.22 = (bf16[1024,1024]{1,0:T(8,128)(2,1)}, bf16[1024,1024]{1,0:T(8,128)(2,1)}, u32[]{:S(2)}, u32[]{:S(2)}) collective-permute-start(bf16[1024,1024]{1,0:T(8,128)(2,1)} %add_convert_fusion.1), channel_id=1, source_target_pairs={{0,16},{16,0},{8,24},{24,8},{1,17},{17,1},{9,25},{25,9},{2,18},{18... | collective-permute-start | bytes 6291464 | tf_op jit(solution)/shard_map/ppermute | solution.py:65
  672.4 115.9 %collective-permute-start.21 = (bf16[1024,1024]{1,0:T(8,128)(2,1)}, bf16[1024,1024]{1,0:T(8,128)(2,1)}, u32[]{:S(2)}, u32[]{:S(2)}) collective-permute-start(bf16[1024,1024]{1,0:T(8,128)(2,1)} %convolution_convert_fusion.5), channel_id=1, source_target_pairs={{0,8},{8,0},{16,24},{24,16},{1,9},{9,1},{17,25},{25,17},{2,10},{10... | collective-permute-start | bytes 6291464 | tf_op jit(solution)/shard_map/ppermute | solution.py:65
  679.2 100.4 %all-to-all-start.4 = ((f32[32,2,32]{2,1,0:T(2,128)}), f32[32,2,32]{2,1,0:T(2,128)S(1)}, u32[]{:S(2)}, u32[]{:S(2)}) async-start(f32[32,2,32]{2,1,0:T(2,128)} %maximum_bitcast_fusion.2), calls=%async_computation.4 | async-start | bytes 65536 | tf_op jit(solution)/shard_map/all_to_all | solution.py:737
  (126 other events, 819.0 us)
Sparse Core Ops, SparseCore 0:
  78.4 138.8 all-gather.1
  494.4 237.8 reduce-scatter.1

commit v6 on v5

--- a/solution.py
+++ b/solution.py
@@ -206,21 +206,31 @@
     )(query, *operands, bias, ride)
 
 
-def attend_back(query, kv_blocks, bias, grad_attended):
-    rows, local_len, model_width = query.shape
-    groups, spec, in_specs = attention_specs(local_len, model_width, bias.shape[1])
+def attend_back(query, kv_blocks, bias, grad_attended, row):
+    _, local_len, model_width = query.shape
+    key_len = bias.shape[1]
+    width = 2 * HEAD_DIM
+    groups = model_width // width
+    spec = pl.BlockSpec((1, local_len, width), lambda head: (row, 0, head))
+    value_spec = pl.BlockSpec((1, local_len, width), lambda head: (row, 0, head + groups))
+    bias_spec = pl.BlockSpec((1, key_len, local_len), lambda head: (row, 0, 0))
     operands = [block for block in kv_blocks for _ in range(2)]
-    pair_spec = pl.BlockSpec((2, 1, local_len, 2 * HEAD_DIM), lambda row, head: (0, row, 0, head))
-    pair_shape = jax.ShapeDtypeStruct((2, rows, local_len, model_width), bf16)
-    flops = 10 * rows * model_width * local_len * bias.shape[1]
+    pair_spec = pl.BlockSpec((2, 1, local_len, width), lambda head: (0, 0, 0, head))
+    pair_shape = jax.ShapeDtypeStruct((2, 1, local_len, model_width), bf16)
+    flops = 10 * model_width * local_len * key_len
     return pl.pallas_call(
         functools.partial(attend_back_kernel, 1.0 / math.sqrt(HEAD_DIM)),
-        grid=(rows, groups),
-        in_specs=in_specs + [spec],
-        out_specs=[spec, pair_spec, pair_spec, pair_spec],
-        out_shape=[jax.ShapeDtypeStruct(query.shape, bf16)] + [pair_shape] * 3,
+        grid=(groups,),
+        in_specs=[spec] + [spec, value_spec] * 3 + [bias_spec, spec],
+        out_specs=[
+            pl.BlockSpec((1, local_len, width), lambda head: (0, 0, head)),
+            pair_spec,
+            pair_spec,
+            pair_spec,
+        ],
+        out_shape=[jax.ShapeDtypeStruct((1, local_len, model_width), bf16)] + [pair_shape] * 3,
         cost_estimate=pl.CostEstimate(
-            flops=flops * 6, bytes_accessed=16 * query.size * 2, transcendentals=0
+            flops=flops * 12, bytes_accessed=8 * query.size * 2, transcendentals=0
         ),
         name="attend_back",
     )(query, *operands, bias, grad_attended)
@@ -698,16 +708,30 @@
     rest_grad = row_major(rest_grad)
     grad_attended = product_bt(grad_proj, proj_full).astype(bf16)
     grad_attended, rest_grad = together(grad_attended, rest_grad)
+    grad_attended, inner1.got_chip = together(grad_attended, inner1.got_chip)
     rest_sum = lax.psum_scatter(rest_grad, every, scatter_dimension=0, tiled=True).astype(f32)
-    grad_query, grad_kv0, grad_kv1, grad_kv2 = attend_back(
-        query, kv_blocks, bias, grad_attended.reshape(query.shape)
-    )
-    grad_kv1, inner1.got_chip = together(grad_kv1, inner1.got_chip)
-    got_near = seq_send(grad_kv1, [(1, 0), (3, 2), (2, 3)])
-    far_sum = jnp.where(
-        seq_index == 3, (grad_kv2.astype(f32) + got_near.astype(f32)).astype(bf16), grad_kv2
-    )
-    got_far = seq_send(far_sum, [(2, 0), (3, 1)])
+    grad_rows = grad_attended.reshape(query.shape)
+    query_rows, kv_rows, far_rows = [], [], []
+    for row in range(row_count):
+        if row:
+            grad_rows, far_rows[-1] = together(grad_rows, far_rows[-1])
+            far_rows[-1] = seq_send(far_rows[-1], [(2, 0), (3, 1)])
+        grad_query, grad_kv0, grad_kv1, grad_kv2 = attend_back(
+            query, kv_blocks, bias, grad_rows, row
+        )
+        if row:
+            grad_kv1, far_rows[-1] = together(grad_kv1, far_rows[-1])
+        got_near = seq_send(grad_kv1, [(1, 0), (3, 2), (2, 3)])
+        far_sum = jnp.where(
+            seq_index == 3, (grad_kv2.astype(f32) + got_near.astype(f32)).astype(bf16), grad_kv2
+        )
+        near_sum = grad_kv0.astype(f32) + jnp.where(
+            seq_index % 2 == 0, got_near.astype(f32), 0.0
+        )
+        query_rows.append(grad_query)
+        kv_rows.append(near_sum)
+        far_rows.append(far_sum)
+    got_far = seq_send(far_rows[-1], [(2, 0), (3, 1)])
     got_far, *held = together(
         got_far, *[part.term(1) for part in sums[0]], *[part.term(0) for part in sums[0]]
     )
@@ -718,9 +742,11 @@
     outer_send, inner_send, got_far = together(outer0.chip_sum(), inner0.chip_sum(), got_far)
     outer0.send_chip(outer_send)
     inner0.send_chip(inner_send)
-    kv_sum = grad_kv0.astype(f32) + got_far.astype(f32)
-    kv_sum = kv_sum + jnp.where(seq_index % 2 == 0, got_near.astype(f32), 0.0)
-    kv_sum = kv_sum.astype(bf16).reshape(2, token_count, model_width)
+    far_rows[-1] = got_far
+    kv_sum = jnp.concatenate(
+        [(near + far.astype(f32)).astype(bf16) for near, far in zip(kv_rows, far_rows)], axis=1
+    ).reshape(2, token_count, model_width)
+    grad_query = jnp.concatenate(query_rows, axis=0)
     grad_qkv = [grad_query.reshape(token_count, model_width), kv_sum[0], kv_sum[1]]
     qkv_grad = row_major(
         jnp.concatenate([weight_grad(normed_attn, part) for part in grad_qkv], axis=1)

time: 828 us -> 831 us (level)
  Pallas kernels: 260 us -> 238 us
  local copies, waits for them, and re-layouts: 54.4 us -> 75.5 us
    pallas_call x0 -> x1, local copies, waits for them, and re-layouts: none -> 19.3 us  [attend_back(): pl.pallas_call(functools.partial(attend_back_kernel, 1.0 / math.sqrt(HEAD...]
    pallas_call x1, Pallas kernels: 36.3 us -> 19.3 us  [attend_back(): pl.pallas_call(functools.partial(attend_back_kernel, 1.0 / math.sqrt(HEAD...]
    ppermute x24 -> x26, starting transfers between devices: 21.8 us -> 24.3 us  [seq_send(): return lax.ppermute(values, 'seq', pairs)]
    unnamed x261 -> x266, local copies, waits for them, and re-layouts: 18.4 us -> 20 us
    ppermute x24 -> x26, waiting for transfers between devices: 117 us -> 119 us  [seq_send(): return lax.ppermute(values, 'seq', pairs)]
  transfers between devices with their start and end apart: 31 -> 33, of which waited for: 6 -> 7; matrix products, arithmetic and copies ran while one was open for 31% -> 34% of each run, Pallas kernels for 24% -> 21%
where the time goes in v6:
time: 831 us; the launch traced here: 822 us
  Pallas kernels  238 us (29%)
  matrix products  223 us (27%)
  waiting for transfers between devices  146 us (18%)
  local copies, waits for them, and re-layouts  75.5 us (9%)
  other arithmetic  70.2 us (8%)
  starting transfers between devices  49.8 us (6%)
  between operations  19.8 us (2%)
    ppermute x26, waiting for transfers between devices, seq_send(): return lax.ppermute(values, 'seq', pairs)  119 us
    pallas_call x1, Pallas kernels, scatter_rows(): pl.pallas_call(functools.partial(scatter_kernel, bits, orders), in_specs=...  89.9 us
    dot_general x28, matrix products, product_at(): lax.dot_general(left_side, right_side, (((0,), (0,)), ((), ())), preferre...  80.5 us
    dot_general x28, matrix products, product_bt(): lax.dot_general(left_side, right_side, (((1,), (1,)), ((), ())), preferre...  71.9 us
    dot_general x27, matrix products, product(): return jnp.dot(left_side, right_side, preferred_element_type=f32)  69.4 us
    pallas_call x1, Pallas kernels, gather_rows(): pl.pallas_call(functools.partial(gather_kernel, bits, orders), in_specs=[...  64.9 us
    pallas_call x1, Pallas kernels, attend(): pl.pallas_call(functools.partial(attend_kernel, 1.0 / math.sqrt(HEAD_DIM)...  63.8 us
    ppermute x26, starting transfers between devices, seq_send(): return lax.ppermute(values, 'seq', pairs)  24.3 us
  transfers between devices with their start and end apart: 33, of which 7 were waited for; matrix products, arithmetic and copies ran while one was open for 34% of the time, Pallas kernels for 21%

profile of v6, /device:TPU:0, one launch (start us, length us, event | category | flops | bytes accessed | tf_op | source)
XLA Modules:
  0.0 822.2 jit_solution(5354184358388938240)
XLA Ops:
  13.3 64.9 %gather_rows.1 = (bf16[2,2,2,2,2,32,3328]{6,5,4,3,2,1,0:T(8,128)(2,1)}, bf16[2,1024,1024]{2,1,0:T(8,128)(2,1)}, bf16[2,1024,1024]{2,1,0:T(8,128)(2,1)}, bf16[1024,1024]{1,0:T(8,128)(2,1)}) custom-call(bf16[32,3328]{1,0:T(8,128)(2,1)} %fusion.158.own_ref, bf16[1,2,1024,1024]{3,2,1,0:T(8,128)(2,1)} %inner_ref.1, bf16[1,2,1024,1024]{3,2,1,0:T(8,128)(2,1)} %outer_ref.1), custom_call_target="tpu_custom_call" | custom-call | bytes 85196800 | tf_op jit(solution)/shard_map/gather_rows/pallas_call | solution.py:402
  81.8 6.2 fusion.6
  92.2 52.6 %collective-permute-done.k2.v2 = bf16[2,256,2048]{2,1,0:T(8,128)(2,1)} collective-permute-done((bf16[2,256,2048]{2,1,0:T(8,128)(2,1)}, bf16[2,256,2048]{2,1,0:T(8,128)(2,1)}, u32[]{:S(2)}, u32[]{:S(2)}) %collective-permute-start) | collective-permute-done | bytes 2097184 | tf_op jit(solution)/shard_map/ppermute | solution.py:65
  162.0 63.8 %attend.1 = (bf16[2,256,1024]{2,1,0:T(8,128)(2,1)}, bf16[1024,1024]{1,0:T(8,128)(2,1)}) custom-call(bf16[2,256,1024]{2,1,0:T(8,128)(2,1)} %bitcast.395, bf16[2,256,2048]{2,1,0:T(8,128)(2,1)} %bitcast.7.k0.v0, bf16[2,256,2048]{2,1,0:T(8,128)(2,1)} %bitcast.7.k0.v0, bf16[2,256,2048]{2,1,0:T(8,128)(2,1)} %collective-permute-done.1.k1.v1, ...), custom_call_target="tpu_custom_call" | custom-call | flops 9663676416 | bytes 8388608 | tf_op jit(solution)/shard_map/attend/pallas_call | solution.py:191
  249.3 5.5 all-to-all-start
  259.7 20.7 %all-to-all-done = bf16[8,64,1024]{2,1,0:T(8,128)(2,1)S(1)} async-done(((bf16[8,64,1024]{2,1,0:T(8,128)(2,1)}), bf16[8,64,1024]{2,1,0:T(8,128)(2,1)S(1)}, u32[]{:S(2)}, u32[]{:S(2)}) %all-to-all-start) | async-done | bytes 1048608 | tf_op jit(solution)/shard_map/all_to_all | solution.py:615
  292.0 4.5 multiply_convert_fusion.21
  303.2 4.5 multiply_convert_fusion.18
  313.6 4.6 multiply_convert_fusion.14
  393.1 6.0 all-to-all-start.3
  399.1 4.3 convolution_convert_fusion.9
  418.2 6.9 all-to-all-done.3
  458.3 6.2 collective-permute-done.10
  488.8 4.7 fusion.133
  497.7 5.7 all-to-all-start.1
  504.0 4.2 convolution_convert_fusion.4
  511.0 29.4 %collective-permute-done.11 = bf16[1024,1024]{1,0:T(8,128)(2,1)} collective-permute-done((bf16[1024,1024]{1,0:T(8,128)(2,1)}, bf16[1024,1024]{1,0:T(8,128)(2,1)}, u32[]{:S(2)}, u32[]{:S(2)}) %collective-permute-start.11) | collective-permute-done | bytes 2097184 | tf_op jit(solution)/shard_map/ppermute | solution.py:65
  540.4 19.3 %attend_back.2 = (bf16[1,256,1024]{2,1,0:T(8,128)(2,1)}, bf16[2,1,256,1024]{3,2,1,0:T(8,128)(2,1)}, bf16[2,1,256,1024]{3,2,1,0:T(8,128)(2,1)}, bf16[2,1,256,1024]{3,2,1,0:T(8,128)(2,1)}) custom-call(bf16[2,256,1024]{2,1,0:T(8,128)(2,1)} %bitcast.396, bf16[2,256,2048]{2,1,0:T(8,128)(2,1)} %bitcast.7.k0.v0, bf16[2,256,2048]{2,1,0:T(8,128)(2,1)} %bitcast.7.k0.v0, ...), custom_call_target="tpu_custom_call" | custom-call | flops 24159191040 | bytes 8388608 | tf_op jit(solution)/shard_map/attend_back/pallas_call | solution.py:221
  561.2 4.3 convolution_convert_fusion.5
  584.9 19.3 %attend_back.3 = (bf16[2,256,1024]{2,1,0:T(8,128)(2,1)}, bf16[2,1,256,1024]{3,2,1,0:T(8,128)(2,1)}, bf16[2,1,256,1024]{3,2,1,0:T(8,128)(2,1)S(1)}, bf16[2,1,256,1024]{3,2,1,0:T(8,128)(2,1)}) fusion(bf16[2,256,1024]{2,1,0:T(8,128)(2,1)} %constant_dynamic-update-slice_fusion.1, bf16[2,256,1024]{2,1,0:T(8,128)(2,1)} %bitcast.397, ...), kind=kCustom, calls=%fused_computation.270 | custom fusion | bytes 13631488 | tf_op jit(solution)/shard_map/attend_back/pallas_call | solution.py:221
  607.6 7.8 collective-permute-done.13
  619.4 4.6 add_convert_fusion
  624.1 5.9 add_bitcast_fusion.2
  632.2 4.2 add_convert_fusion.1
  636.5 5.8 add_bitcast_fusion
  644.4 22.6 %collective-permute-done.17 = bf16[2,1,256,1024]{3,2,1,0:T(8,128)(2,1)S(1)} collective-permute-done((bf16[2,1,256,1024]{3,2,1,0:T(8,128)(2,1)S(1)}, bf16[2,1,256,1024]{3,2,1,0:T(8,128)(2,1)S(1)}, u32[]{:S(2)}, u32[]{:S(2)}) %collective-permute-start.17) | collective-permute-done | bytes 1048608 | tf_op jit(solution)/shard_map/ppermute | solution.py:65
  684.2 4.8 all-to-all-start.4
  689.0 4.2 add_add_fusion.4
  693.2 89.9 %scatter_rows.1 = f32[32,3072]{1,0:T(8,128)} custom-call(bf16[2,2,2,2,2,32,3072]{6,5,4,3,2,1,0:T(8,128)(2,1)} %bitcast.316), custom_call_target="tpu_custom_call" | custom-call | bytes 157286400 | tf_op jit(solution)/shard_map/scatter_rows/pallas_call | solution.py:492
  787.5 4.3 maximum_bitcast_fusion
  795.6 4.2 maximum_bitcast_fusion.1
  804.7 4.5 reshape.410
  (505 shorter events, 302.1 us)
Async XLA Ops:
  7.2 219.8 %all-gather.2.cloned.1.call-start = ((), (), s32[]{:S(2)}) async-start(), calls=%async_computation.6 | async-start | bytes 19464192 | tf_op jit(solution)/shard_map/all_gather | solution.py:557
  88.0 56.8 %collective-permute-start = (bf16[2,256,2048]{2,1,0:T(8,128)(2,1)}, bf16[2,256,2048]{2,1,0:T(8,128)(2,1)}, u32[]{:S(2)}, u32[]{:S(2)}) collective-permute-start(bf16[2,256,2048]{2,1,0:T(8,128)(2,1)} %bitcast.7.k0.v0), channel_id=1, source_target_pairs={{0,16},{8,24},{1,17},{9,25},{2,18},{10,26},{3,19},{11,27},{4,20},{... | collective-permute-start | bytes 6291464 | tf_op jit(solution)/shard_map/ppermute | solution.py:65
  147.9 14.1 %collective-permute-start.1 = (bf16[2,256,2048]{2,1,0:T(8,128)(2,1)}, bf16[2,256,2048]{2,1,0:T(8,128)(2,1)}, u32[]{:S(2)}, u32[]{:S(2)}) collective-permute-start(bf16[2,256,2048]{2,1,0:T(8,128)(2,1)} %broadcast_select_fusion), channel_id=1, source_target_pairs={{0,8},{16,24},{24,16},{1,9},{17,25},{25,17},{2,10},{18,26},{26,18}... | collective-permute-start | bytes 6291464 | tf_op jit(solution)/shard_map/ppermute | solution.py:65
  225.8 58.2 %collective-permute-start.2 = (bf16[1024,1024]{1,0:T(8,128)(2,1)}, bf16[1024,1024]{1,0:T(8,128)(2,1)}, u32[]{:S(2)}, u32[]{:S(2)}) collective-permute-start(bf16[1024,1024]{1,0:T(8,128)(2,1)} %get-tuple-element.73), channel_id=1, source_target_pairs={{0,16},{16,0},{8,24},{24,8},{1,17},{17,1},{9,25},{25,9},{2,18},{18... | collective-permute-start | bytes 6291464 | tf_op jit(solution)/shard_map/ppermute | solution.py:65
  249.3 31.1 %all-to-all-start = ((bf16[8,64,1024]{2,1,0:T(8,128)(2,1)}), bf16[8,64,1024]{2,1,0:T(8,128)(2,1)S(1)}, u32[]{:S(2)}, u32[]{:S(2)}) async-start(bf16[8,64,1024]{2,1,0:T(8,128)(2,1)} %bitcast.18), calls=%async_computation | async-start | bytes 2097152 | tf_op jit(solution)/shard_map/all_to_all | solution.py:615
  257.7 45.5 %collective-permute-start.3 = (bf16[1024,1024]{1,0:T(8,128)(2,1)}, bf16[1024,1024]{1,0:T(8,128)(2,1)}, u32[]{:S(2)}, u32[]{:S(2)}) collective-permute-start(bf16[1024,1024]{1,0:T(8,128)(2,1)} %get-tuple-element.79), channel_id=1, source_target_pairs={{0,8},{8,0},{16,24},{24,16},{1,9},{9,1},{17,25},{25,17},{2,10},{10... | collective-permute-start | bytes 6291464 | tf_op jit(solution)/shard_map/ppermute | solution.py:65
  257.8 49.9 %collective-permute-start.4 = (bf16[1024,1024]{1,0:T(8,128)(2,1)}, bf16[1024,1024]{1,0:T(8,128)(2,1)}, u32[]{:S(2)}, u32[]{:S(2)}) collective-permute-start(bf16[1024,1024]{1,0:T(8,128)(2,1)} %get-tuple-element.80), channel_id=1, source_target_pairs={{0,8},{8,0},{16,24},{24,16},{1,9},{9,1},{17,25},{25,17},{2,10},{10... | collective-permute-start | bytes 6291464 | tf_op jit(solution)/shard_map/ppermute | solution.py:65
  258.2 71.0 %collective-permute-start.5 = (bf16[1024,1024]{1,0:T(8,128)(2,1)}, bf16[1024,1024]{1,0:T(8,128)(2,1)}, u32[]{:S(2)}, u32[]{:S(2)}) collective-permute-start(bf16[1024,1024]{1,0:T(8,128)(2,1)} %get-tuple-element.82), channel_id=1, source_target_pairs={{0,16},{16,0},{8,24},{24,8},{1,17},{17,1},{9,25},{25,9},{2,18},{18... | collective-permute-start | bytes 6291464 | tf_op jit(solution)/shard_map/ppermute | solution.py:65
  280.4 37.8 %all-to-all-start.2 = ((bf16[8,64,1024]{2,1,0:T(8,128)(2,1)}), bf16[8,64,1024]{2,1,0:T(8,128)(2,1)S(1)}, u32[]{:S(2)}, u32[]{:S(2)}) async-start(bf16[8,64,1024]{2,1,0:T(8,128)(2,1)} %bitcast.319), calls=%async_computation.2 | async-start | bytes 2097152 | tf_op jit(solution)/shard_map/all_to_all | solution.py:647
  329.3 19.7 %collective-permute-start.7 = (bf16[1024,1024]{1,0:T(8,128)(2,1)}, bf16[1024,1024]{1,0:T(8,128)(2,1)S(1)}, u32[]{:S(2)}, u32[]{:S(2)}) collective-permute-start(bf16[1024,1024]{1,0:T(8,128)(2,1)} %collective-permute-done.5), channel_id=1, source_target_pairs={{0,8},{8,0},{16,24},{24,16},{1,9},{9,1},{17,25},{25,17},{2,10},{10... | collective-permute-start | bytes 6291464 | tf_op jit(solution)/shard_map/ppermute | solution.py:65
  329.3 17.2 %collective-permute-start.6 = (bf16[1024,1024]{1,0:T(8,128)(2,1)}, bf16[1024,1024]{1,0:T(8,128)(2,1)S(1)}, u32[]{:S(2)}, u32[]{:S(2)}) collective-permute-start(bf16[1024,1024]{1,0:T(8,128)(2,1)} %collective-permute-done.2), channel_id=1, source_target_pairs={{0,8},{8,0},{16,24},{24,16},{1,9},{9,1},{17,25},{25,17},{2,10},{10... | collective-permute-start | bytes 6291464 | tf_op jit(solution)/shard_map/ppermute | solution.py:65
  376.0 11.8 %collective-permute-start.8 = (bf16[1024,1024]{1,0:T(8,128)(2,1)S(1)}, bf16[1024,1024]{1,0:T(8,128)(2,1)S(1)}, u32[]{:S(2)}, u32[]{:S(2)}) collective-permute-start(bf16[1024,1024]{1,0:T(8,128)(2,1)S(1)} %convolution_convert_fusion.13), channel_id=1, source_target_pairs={{0,8},{8,0},{16,24},{24,16},{1,9},{9,1},{17,25},{25,17},{2,10},{10... | collective-permute-start | bytes 6291464 | tf_op jit(solution)/shard_map/ppermute | solution.py:65
  376.1 14.4 %collective-permute-start.9 = (bf16[1024,1024]{1,0:T(8,128)(2,1)S(1)}, bf16[1024,1024]{1,0:T(8,128)(2,1)S(1)}, u32[]{:S(2)}, u32[]{:S(2)}) collective-permute-start(bf16[1024,1024]{1,0:T(8,128)(2,1)S(1)} %copy-done.87), channel_id=1, source_target_pairs={{0,8},{8,0},{16,24},{24,16},{1,9},{9,1},{17,25},{25,17},{2,10},{10... | collective-permute-start | bytes 6291464 | tf_op jit(solution)/shard_map/ppermute | solution.py:65
  393.1 32.0 %all-to-all-start.3 = ((bf16[8,64,1024]{2,1,0:T(8,128)(2,1)}), bf16[8,64,1024]{2,1,0:T(8,128)(2,1)S(1)}, u32[]{:S(2)}, u32[]{:S(2)}) async-start(bf16[8,64,1024]{2,1,0:T(8,128)(2,1)} %bitcast.323), calls=%async_computation.3 | async-start | bytes 2097152 | tf_op jit(solution)/shard_map/all_to_all | solution.py:679
  399.1 400.8 %reduce-scatter.2.cloned.1.call-start = ((), (), s32[]{:S(2)}) async-start(), calls=%async_computation.7 | async-start | bytes 19464192 | tf_op jit(solution)/shard_map/reduce_scatter | solution.py:712
  416.8 47.6 %collective-permute-start.10 = (bf16[1024,1024]{1,0:T(8,128)(2,1)}, bf16[1024,1024]{1,0:T(8,128)(2,1)}, u32[]{:S(2)}, u32[]{:S(2)}) collective-permute-start(bf16[1024,1024]{1,0:T(8,128)(2,1)} %add_convert_fusion.3), channel_id=1, source_target_pairs={{0,16},{16,0},{8,24},{24,8},{1,17},{17,1},{9,25},{25,9},{2,18},{18... | collective-permute-start | bytes 6291464 | tf_op jit(solution)/shard_map/ppermute | solution.py:65
  493.5 46.9 %collective-permute-start.11 = (bf16[1024,1024]{1,0:T(8,128)(2,1)}, bf16[1024,1024]{1,0:T(8,128)(2,1)}, u32[]{:S(2)}, u32[]{:S(2)}) collective-permute-start(bf16[1024,1024]{1,0:T(8,128)(2,1)} %add_convert_fusion.2), channel_id=1, source_target_pairs={{0,16},{16,0},{8,24},{24,8},{1,17},{17,1},{9,25},{25,9},{2,18},{18... | collective-permute-start | bytes 6291464 | tf_op jit(solution)/shard_map/ppermute | solution.py:65
  497.7 79.0 %all-to-all-start.1 = ((bf16[8,64,1024]{2,1,0:T(8,128)(2,1)}), bf16[8,64,1024]{2,1,0:T(8,128)(2,1)S(1)}, u32[]{:S(2)}, u32[]{:S(2)}) async-start(bf16[8,64,1024]{2,1,0:T(8,128)(2,1)} %bitcast.324), calls=%async_computation.1 | async-start | bytes 2097152 | tf_op jit(solution)/shard_map/all_to_all | solution.py:640
  503.9 61.5 %collective-permute-start.18 = (f32[4,1024]{1,0:T(4,128)S(1)}, f32[4,1024]{1,0:T(4,128)S(1)}, u32[]{:S(2)}, u32[]{:S(2)}) collective-permute-start(f32[4,1024]{1,0:T(4,128)S(1)} %pad_maximum_fusion.3), channel_id=1, source_target_pairs={{0,8},{8,0},{16,24},{24,16},{1,9},{9,1},{17,25},{25,17},{2,10},{10... | collective-permute-start | bytes 49160 | tf_op jit(solution)/shard_map/ppermute | solution.py:65
  559.8 13.6 %collective-permute-start.12 = (bf16[2,1,256,1024]{3,2,1,0:T(8,128)(2,1)}, bf16[2,1,256,1024]{3,2,1,0:T(8,128)(2,1)S(1)}, u32[]{:S(2)}, u32[]{:S(2)}) collective-permute-start(bf16[2,1,256,1024]{3,2,1,0:T(8,128)(2,1)} %get-tuple-element.97), channel_id=1, source_target_pairs={{8,0},{24,16},{16,24},{9,1},{25,17},{17,25},{10,2},{26,18},{18,26}... | collective-permute-start | bytes 3145736 | tf_op jit(solution)/shard_map/ppermute | solution.py:65
  567.6 51.8 %collective-permute-start.16 = (bf16[1024,1024]{1,0:T(8,128)(2,1)}, bf16[1024,1024]{1,0:T(8,128)(2,1)}, u32[]{:S(2)}, u32[]{:S(2)}) collective-permute-start(bf16[1024,1024]{1,0:T(8,128)(2,1)} %convolution_convert_fusion.10), channel_id=1, source_target_pairs={{0,8},{8,0},{16,24},{24,16},{1,9},{9,1},{17,25},{25,17},{2,10},{10... | collective-permute-start | bytes 6291464 | tf_op jit(solution)/shard_map/ppermute | solution.py:65
  573.0 51.1 %collective-permute-start.22 = (bf16[1024,1024]{1,0:T(8,128)(2,1)}, bf16[1024,1024]{1,0:T(8,128)(2,1)}, u32[]{:S(2)}, u32[]{:S(2)}) collective-permute-start(bf16[1024,1024]{1,0:T(8,128)(2,1)} %convolution_convert_fusion.8), channel_id=1, source_target_pairs={{0,8},{8,0},{16,24},{24,16},{1,9},{9,1},{17,25},{25,17},{2,10},{10... | collective-permute-start | bytes 6291464 | tf_op jit(solution)/shard_map/ppermute | solution.py:65
  574.8 40.5 %collective-permute-start.13 = (bf16[2,1,256,1024]{3,2,1,0:T(8,128)(2,1)}, bf16[2,1,256,1024]{3,2,1,0:T(8,128)(2,1)}, u32[]{:S(2)}, u32[]{:S(2)}) collective-permute-start(bf16[2,1,256,1024]{3,2,1,0:T(8,128)(2,1)} %fusion.125), channel_id=1, source_target_pairs={{16,0},{24,8},{17,1},{25,9},{18,2},{26,10},{19,3},{27,11},{20,4},{... | collective-permute-start | bytes 3145736 | tf_op jit(solution)/shard_map/ppermute | solution.py:65
  579.9 52.3 %collective-permute-start.15 = (bf16[1024,1024]{1,0:T(8,128)(2,1)}, bf16[1024,1024]{1,0:T(8,128)(2,1)}, u32[]{:S(2)}, u32[]{:S(2)}) collective-permute-start(bf16[1024,1024]{1,0:T(8,128)(2,1)} %convolution_convert_fusion.11), channel_id=1, source_target_pairs={{0,8},{8,0},{16,24},{24,16},{1,9},{9,1},{17,25},{25,17},{2,10},{10... | collective-permute-start | bytes 6291464 | tf_op jit(solution)/shard_map/ppermute | solution.py:65
  583.6 52.8 %collective-permute-start.25 = (bf16[1024,1024]{1,0:T(8,128)(2,1)}, bf16[1024,1024]{1,0:T(8,128)(2,1)}, u32[]{:S(2)}, u32[]{:S(2)}) collective-permute-start(bf16[1024,1024]{1,0:T(8,128)(2,1)} %convolution_convert_fusion.9), channel_id=1, source_target_pairs={{0,8},{8,0},{16,24},{24,16},{1,9},{9,1},{17,25},{25,17},{2,10},{10... | collective-permute-start | bytes 6291464 | tf_op jit(solution)/shard_map/ppermute | solution.py:65
  615.4 14.7 %collective-permute-start.14 = (bf16[2,1,256,1024]{3,2,1,0:T(8,128)(2,1)S(1)}, bf16[2,1,256,1024]{3,2,1,0:T(8,128)(2,1)S(1)}, u32[]{:S(2)}, u32[]{:S(2)}) collective-permute-start(bf16[2,1,256,1024]{3,2,1,0:T(8,128)(2,1)S(1)} %copy-done.90), channel_id=1, source_target_pairs={{8,0},{24,16},{16,24},{9,1},{25,17},{17,25},{10,2},{26,18},{18,26}... | collective-permute-start | bytes 3145736 | tf_op jit(solution)/shard_map/ppermute | solution.py:65
  630.5 36.5 %collective-permute-start.17 = (bf16[2,1,256,1024]{3,2,1,0:T(8,128)(2,1)S(1)}, bf16[2,1,256,1024]{3,2,1,0:T(8,128)(2,1)S(1)}, u32[]{:S(2)}, u32[]{:S(2)}) collective-permute-start(bf16[2,1,256,1024]{3,2,1,0:T(8,128)(2,1)S(1)} %fusion.124), channel_id=1, source_target_pairs={{16,0},{24,8},{17,1},{25,9},{18,2},{26,10},{19,3},{27,11},{20,4},{... | collective-permute-start | bytes 3145736 | tf_op jit(solution)/shard_map/ppermute | solution.py:65
  675.2 108.4 %collective-permute-start.21 = (bf16[1024,1024]{1,0:T(8,128)(2,1)}, bf16[1024,1024]{1,0:T(8,128)(2,1)}, u32[]{:S(2)}, u32[]{:S(2)}) collective-permute-start(bf16[1024,1024]{1,0:T(8,128)(2,1)} %add_convert_fusion), channel_id=1, source_target_pairs={{0,16},{16,0},{8,24},{24,8},{1,17},{17,1},{9,25},{25,9},{2,18},{18... | collective-permute-start | bytes 6291464 | tf_op jit(solution)/shard_map/ppermute | solution.py:65
  675.3 108.3 %collective-permute-start.20 = (bf16[1024,1024]{1,0:T(8,128)(2,1)}, bf16[1024,1024]{1,0:T(8,128)(2,1)}, u32[]{:S(2)}, u32[]{:S(2)}) collective-permute-start(bf16[1024,1024]{1,0:T(8,128)(2,1)} %convolution_convert_fusion.4), channel_id=1, source_target_pairs={{0,8},{8,0},{16,24},{24,16},{1,9},{9,1},{17,25},{25,17},{2,10},{10... | collective-permute-start | bytes 6291464 | tf_op jit(solution)/shard_map/ppermute | solution.py:65
  675.6 116.1 %collective-permute-start.24 = (bf16[1024,1024]{1,0:T(8,128)(2,1)}, bf16[1024,1024]{1,0:T(8,128)(2,1)}, u32[]{:S(2)}, u32[]{:S(2)}) collective-permute-start(bf16[1024,1024]{1,0:T(8,128)(2,1)} %add_convert_fusion.1), channel_id=1, source_target_pairs={{0,16},{16,0},{8,24},{24,8},{1,17},{17,1},{9,25},{25,9},{2,18},{18... | collective-permute-start | bytes 6291464 | tf_op jit(solution)/shard_map/ppermute | solution.py:65
  677.3 114.4 %collective-permute-start.23 = (bf16[1024,1024]{1,0:T(8,128)(2,1)}, bf16[1024,1024]{1,0:T(8,128)(2,1)}, u32[]{:S(2)}, u32[]{:S(2)}) collective-permute-start(bf16[1024,1024]{1,0:T(8,128)(2,1)} %convolution_convert_fusion.5), channel_id=1, source_target_pairs={{0,8},{8,0},{16,24},{24,16},{1,9},{9,1},{17,25},{25,17},{2,10},{10... | collective-permute-start | bytes 6291464 | tf_op jit(solution)/shard_map/ppermute | solution.py:65
  684.2 98.9 %all-to-all-start.4 = ((f32[32,2,32]{2,1,0:T(2,128)}), f32[32,2,32]{2,1,0:T(2,128)S(1)}, u32[]{:S(2)}, u32[]{:S(2)}) async-start(f32[32,2,32]{2,1,0:T(2,128)} %maximum_bitcast_fusion.2), calls=%async_computation.4 | async-start | bytes 65536 | tf_op jit(solution)/shard_map/all_to_all | solution.py:763
  (130 other events, 894.3 us)
Sparse Core Ops, SparseCore 0:
  78.3 136.0 all-gather.1
  493.7 234.0 reduce-scatter.1

commit v7 on v5

--- a/solution.py
+++ b/solution.py
@@ -248,6 +248,18 @@
     return grad_pres, grad_normed
 
 
+def slices_in_order(operands):
+    seq = lax.axis_index("seq")
+    terms = None
+    for place, (left, right) in enumerate(operands):
+        values = weight_grad(left, right)
+        owner = seq + (1 - 2 * (seq % 2)) * (place % 2) + (2 - 4 * (seq // 2)) * (place // 2)
+        if terms is None:
+            terms = jnp.zeros((len(operands),) + values.shape, values.dtype)
+        terms = lax.dynamic_update_index_in_dim(terms, values, owner, 0)
+    return terms
+
+
 class SliceSum:
     def __init__(self, operands):
         self.operands = operands
@@ -255,11 +267,13 @@
     def term(self, place):
         return weight_grad(*self.operands[place])
 
-    def send_both(self, values):
-        self.got_both = swap_core(values)
-
-    def send_core(self, values):
-        self.got_core = swap_core(values)
+    def take(self, place, values):
+        if place == 0:
+            self.own = values
+        elif place == 1:
+            self.got_core = swap_core(values)
+        else:
+            self.got_both = swap_core(values)
 
     def chip_sum(self):
         values = product_at(*self.operands[2]) + self.got_both.astype(f32)
@@ -641,58 +655,53 @@
     grad_gate = jnp.sum(grad_ret * state_now, axis=-1)
     grad_state = grad_ret * gate_value[:, None]
     gain_grads = [None, None]
-    weight_terms = [None, None]
-    sums = [None, None]
+    second_sums = []
     for sublayer in (1, 0):
         state_in, normed_in, kept = kept_layers[sublayer]
         inner_parts, outer_parts = slices[sublayer]
         grad_branch = grad_state.astype(bf16)
+        outer_terms = [(act, grad_branch) for act, _ in kept]
+        if sublayer:
+            terms, grad_branch = together(slices_in_order(outer_terms), grad_branch)
+            second_sums.append(lax.psum_scatter(terms, "seq", scatter_dimension=0, tiled=True))
         grad_pres, grad_normed = ffn_backward(kept, inner_parts, outer_parts, grad_branch)
-        weight_terms[sublayer] = (
-            [(act, grad_branch) for act, _ in kept],
-            [(normed_in, grad_pre) for grad_pre in grad_pres],
-        )
+        inner_terms = [(normed_in, grad_pre) for grad_pre in grad_pres]
         grad_resid, gain_grad = norm_back(state_in, gains_f[sublayer], grad_normed)
         grad_state = grad_state + grad_resid
         gain_grads[sublayer] = gain_grad
-        sums[sublayer] = [SliceSum(operands) for operands in weight_terms[sublayer]]
         if sublayer:
-            grad_state, *held = together(grad_state, *[part.term(3) for part in sums[1]])
-            for part, values in zip(sums[1], held):
-                part.send_both(values)
+            terms, grad_state = together(slices_in_order(inner_terms), grad_state)
+            second_sums.append(lax.psum_scatter(terms, "seq", scatter_dimension=0, tiled=True))
+    outer0 = SliceSum(outer_terms)
+    inner0 = SliceSum(inner_terms)
     grad_logit = grad_gate * gate_value * (1.0 - gate_value)
     grad_routed = (grad_state + grad_logit[:, None] * centroid_f[None, :]).astype(bf16)
     centroid_grad = jnp.dot(grad_logit, received_f, precision=highest)
-    grad_routed, *held = together(grad_routed, *[part.chip_sum() for part in sums[1]])
-    for part, values in zip(sums[1], held):
-        part.send_chip(values)
     returned_grad = lax.all_to_all(grad_routed, "wide", split_axis=0, concat_axis=0, tiled=True)
+    firsts = (outer0, inner0)
+    for part in firsts:
+        part.take(3, part.term(3))
     returned_grad, *held = together(
         returned_grad,
-        *[part.term(3) for part in sums[0]],
-        *[part.term(1) for part in sums[1]],
-        *[part.term(0) for part in sums[1]],
-    )
-    for part, values in zip(sums[0], held[:2]):
-        part.send_both(values)
-    for part, values in zip(sums[1], held[2:4]):
-        part.send_core(values)
-    for part, values in zip(sums[1], held[4:]):
-        part.own = values
+        *[part.term(place) for place in (1, 0) for part in firsts],
+        *[part.chip_sum() for part in firsts],
+    )
+    for part, core, own, chip in zip(firsts, held[:2], held[2:4], held[4:]):
+        part.take(1, core)
+        part.take(0, own)
+        part.send_chip(chip)
     grad_dense = grad_flat.astype(f32) + returned_grad[slot_index].astype(f32)
 
     grad_down_in = grad_dense.astype(bf16)
     grad_pres, grad_normed_ffn = ffn_backward(dense_kept, up_parts, down_parts, grad_down_in)
     grad_hidden_norm, grad_gain_ffn = norm_back(hidden, gain_ffn, grad_normed_ffn)
     grad_hidden = grad_dense + grad_hidden_norm
-    outer1, inner1 = sums[1]
-    outer0, inner0 = sums[0]
-    grad_hidden, outer1.got_chip = together(grad_hidden, outer1.got_chip)
+    grad_down_late, outer0.got_chip = together(grad_down_in, outer0.got_chip)
     grad_proj = grad_hidden.astype(bf16)
     rest_grad = jnp.concatenate(
         [weight_grad(attended, grad_proj)]
         + [weight_grad(normed_ffn, grad_pre) for grad_pre in grad_pres]
-        + [weight_grad(act, grad_down_in) for act, _ in dense_kept],
+        + [weight_grad(act, grad_down_late) for act, _ in dense_kept],
         axis=1,
     )
     rest_grad = row_major(rest_grad)
@@ -702,22 +711,15 @@
     grad_query, grad_kv0, grad_kv1, grad_kv2 = attend_back(
         query, kv_blocks, bias, grad_attended.reshape(query.shape)
     )
-    grad_kv1, inner1.got_chip = together(grad_kv1, inner1.got_chip)
+    grad_kv1, inner0.got_chip = together(grad_kv1, inner0.got_chip)
     got_near = seq_send(grad_kv1, [(1, 0), (3, 2), (2, 3)])
     far_sum = jnp.where(
         seq_index == 3, (grad_kv2.astype(f32) + got_near.astype(f32)).astype(bf16), grad_kv2
     )
     got_far = seq_send(far_sum, [(2, 0), (3, 1)])
-    got_far, *held = together(
-        got_far, *[part.term(1) for part in sums[0]], *[part.term(0) for part in sums[0]]
-    )
-    for part, values in zip(sums[0], held[:2]):
-        part.send_core(values)
-    for part, values in zip(sums[0], held[2:]):
-        part.own = values
-    outer_send, inner_send, got_far = together(outer0.chip_sum(), inner0.chip_sum(), got_far)
-    outer0.send_chip(outer_send)
-    inner0.send_chip(inner_send)
+    outer_total = jnp.stack([outer0.total(), second_sums[0][0].astype(f32)])
+    inner_total = jnp.stack([inner0.total(), second_sums[1][0].astype(f32)])
+    got_far, outer_total, inner_total = together(got_far, outer_total, inner_total)
     kv_sum = grad_kv0.astype(f32) + got_far.astype(f32)
     kv_sum = kv_sum + jnp.where(seq_index % 2 == 0, got_near.astype(f32), 0.0)
     kv_sum = kv_sum.astype(bf16).reshape(2, token_count, model_width)
@@ -770,8 +772,8 @@
         down_grad,
         totals[2:3],
         totals[:2][None],
-        jnp.stack([inner0.total(), inner1.total()])[None],
-        jnp.stack([outer0.total(), outer1.total()])[None],
+        inner_total[None],
+        outer_total[None],
         totals[3, :1] / token_total,
         totals[3, 1:2] / token_total,
     )

time: 828 us -> 897 us (1.083)
  waiting for transfers between devices: 145 us -> 208 us
  local copies, waits for them, and re-layouts: 54.4 us -> 71.4 us
  Pallas kernels: 260 us -> 246 us
    ppermute x24 -> x18, waiting for transfers between devices: 117 us -> 180 us  [seq_send(): return lax.ppermute(values, 'seq', pairs)]
    pallas_call x1, Pallas kernels: 90.1 us -> 77.3 us  [scatter_rows(): pl.pallas_call(functools.partial(scatter_kernel, bits, orders), in_specs=...]
    dot_general x27, matrix products: 68.6 us -> 78.1 us  [product(): return jnp.dot(left_side, right_side, preferred_element_type=f32)]
    unnamed x261, local copies, waits for them, and re-layouts: 18.4 us -> 27.5 us
    ppermute x24 -> x18, starting transfers between devices: 21.8 us -> 17.2 us  [seq_send(): return lax.ppermute(values, 'seq', pairs)]
  transfers between devices with their start and end apart: 31 -> 27, of which waited for: 6 -> 9; matrix products, arithmetic and copies ran while one was open for 31% -> 36% of each run, Pallas kernels for 24% -> 20%
where the time goes in v7:
time: 897 us; the launch traced here: 889 us
  Pallas kernels  246 us (27%)
  matrix products  225 us (25%)
  waiting for transfers between devices  208 us (23%)
  other arithmetic  74.8 us (8%)
  local copies, waits for them, and re-layouts  71.4 us (8%)
  starting transfers between devices  44.4 us (5%)
  between operations  19.5 us (2%)
    ppermute x18, waiting for transfers between devices, seq_send(): return lax.ppermute(values, 'seq', pairs)  180 us
    dot_general x27, matrix products, product(): return jnp.dot(left_side, right_side, preferred_element_type=f32)  78.1 us
    pallas_call x1, Pallas kernels, scatter_rows(): pl.pallas_call(functools.partial(scatter_kernel, bits, orders), in_specs=...  77.3 us
    dot_general x28, matrix products, product_at(): lax.dot_general(left_side, right_side, (((0,), (0,)), ((), ())), preferre...  77 us
    dot_general x28, matrix products, product_bt(): lax.dot_general(left_side, right_side, (((1,), (1,)), ((), ())), preferre...  69 us
    pallas_call x1, Pallas kernels, attend(): pl.pallas_call(functools.partial(attend_kernel, 1.0 / math.sqrt(HEAD_DIM)...  67.3 us
    pallas_call x1, Pallas kernels, gather_rows(): pl.pallas_call(functools.partial(gather_kernel, bits, orders), in_specs=[...  64.9 us
    pallas_call x1, Pallas kernels, attend_back(): pl.pallas_call(functools.partial(attend_back_kernel, 1.0 / math.sqrt(HEAD...  36.4 us
  transfers between devices with their start and end apart: 27, of which 9 were waited for; matrix products, arithmetic and copies ran while one was open for 36% of the time, Pallas kernels for 20%

profile of v7, /device:TPU:0, one launch (start us, length us, event | category | flops | bytes accessed | tf_op | source)
XLA Modules:
  0.0 888.6 jit_solution(8619002188815176754)
XLA Ops:
  13.3 64.9 %gather_rows.1 = (bf16[2,2,2,2,2,32,3328]{6,5,4,3,2,1,0:T(8,128)(2,1)}, bf16[2,1024,1024]{2,1,0:T(8,128)(2,1)}, bf16[2,1024,1024]{2,1,0:T(8,128)(2,1)}, bf16[1024,1024]{1,0:T(8,128)(2,1)}) custom-call(bf16[32,3328]{1,0:T(8,128)(2,1)} %fusion.148.own_ref, bf16[1,2,1024,1024]{3,2,1,0:T(8,128)(2,1)} %inner_ref.1, bf16[1,2,1024,1024]{3,2,1,0:T(8,128)(2,1)} %outer_ref.1), custom_call_target="tpu_custom_call" | custom-call | bytes 85196800 | tf_op jit(solution)/shard_map/gather_rows/pallas_call | solution.py:406
  82.4 5.1 fusion.10
  91.7 51.3 %collective-permute-done.k2.v2 = bf16[2,256,2048]{2,1,0:T(8,128)(2,1)} collective-permute-done((bf16[2,256,2048]{2,1,0:T(8,128)(2,1)S(1)}, bf16[2,256,2048]{2,1,0:T(8,128)(2,1)}, u32[]{:S(2)}, u32[]{:S(2)}) %collective-permute-start) | collective-permute-done | bytes 2097184 | tf_op jit(solution)/shard_map/ppermute | solution.py:65
  151.8 4.3 fusion.121
  159.0 67.3 %attend.1 = (bf16[2,256,1024]{2,1,0:T(8,128)(2,1)}, bf16[1024,1024]{1,0:T(8,128)(2,1)}) custom-call(bf16[2,256,1024]{2,1,0:T(8,128)(2,1)} %bitcast.390, bf16[2,256,2048]{2,1,0:T(8,128)(2,1)} %bitcast.319, bf16[2,256,2048]{2,1,0:T(8,128)(2,1)} %bitcast.320, bf16[2,256,2048]{2,1,0:T(8,128)(2,1)} %collective-permute-done.1.k1.v1, ...), custom_call_target="tpu_custom_call" | custom-call | flops 9663676416 | bytes 8388608 | tf_op jit(solution)/shard_map/attend/pallas_call | solution.py:191
  249.1 6.1 all-to-all-start
  258.6 22.1 %all-to-all-done = bf16[8,64,1024]{2,1,0:T(8,128)(2,1)S(1)} async-done(((bf16[8,64,1024]{2,1,0:T(8,128)(2,1)}), bf16[8,64,1024]{2,1,0:T(8,128)(2,1)S(1)}, u32[]{:S(2)}, u32[]{:S(2)}) %all-to-all-start) | async-done | bytes 1048608 | tf_op jit(solution)/shard_map/all_to_all | solution.py:619
  322.4 4.5 broadcast.298.clone
  343.5 69.3 %collective-permute-done.5 = bf16[1024,1024]{1,0:T(8,128)(2,1)} collective-permute-done((bf16[1024,1024]{1,0:T(8,128)(2,1)}, bf16[1024,1024]{1,0:T(8,128)(2,1)}, u32[]{:S(2)}, u32[]{:S(2)}) %collective-permute-start.5) | collective-permute-done | bytes 2097184 | tf_op jit(solution)/shard_map/ppermute | solution.py:65
  412.9 5.1 fusion.31
  420.6 4.3 fusion.167
  448.7 4.5 broadcast.298
  463.6 7.7 fusion.19
  476.4 4.3 multiply_convert_fusion.4
  506.3 6.0 all-to-all-start.3
  524.7 4.3 add_convert_fusion.1
  529.0 4.5 add_convert_fusion
  533.5 4.9 all-to-all-done.3
  585.9 9.0 %collective-permute-done.10 = bf16[1024,1024]{1,0:T(8,128)(2,1)} collective-permute-done((bf16[1024,1024]{1,0:T(8,128)(2,1)}, bf16[1024,1024]{1,0:T(8,128)(2,1)}, u32[]{:S(2)}, u32[]{:S(2)}) %collective-permute-start.10) | collective-permute-done | bytes 2097184 | tf_op jit(solution)/shard_map/ppermute | solution.py:65
  605.9 5.5 all-to-all-start.1
  612.0 36.4 %attend_back.1 = (bf16[2,256,1024]{2,1,0:T(8,128)(2,1)}, bf16[2,2,256,1024]{3,2,1,0:T(8,128)(2,1)}, bf16[2,2,256,1024]{3,2,1,0:T(8,128)(2,1)}, bf16[2,2,256,1024]{3,2,1,0:T(8,128)(2,1)}) custom-call(bf16[2,256,1024]{2,1,0:T(8,128)(2,1)} %bitcast.391, bf16[2,256,2048]{2,1,0:T(8,128)(2,1)} %bitcast.321, bf16[2,256,2048]{2,1,0:T(8,128)(2,1)} %bitcast.322, ...), custom_call_target="tpu_custom_call" | custom-call | flops 24159191040 | bytes 16777216 | tf_op jit(solution)/shard_map/attend_back/pallas_call | solution.py:216
  648.4 10.5 %collective-permute-done.11 = bf16[1024,1024]{1,0:T(8,128)(2,1)} collective-permute-done((bf16[1024,1024]{1,0:T(8,128)(2,1)}, bf16[1024,1024]{1,0:T(8,128)(2,1)}, u32[]{:S(2)}, u32[]{:S(2)}) %collective-permute-start.11) | collective-permute-done | bytes 2097184 | tf_op jit(solution)/shard_map/ppermute | solution.py:65
  677.9 5.9 fusion.5
  687.9 4.3 fusion.103
  692.3 5.9 add_bitcast_fusion.1
  698.1 5.6 add_bitcast_fusion
  710.7 7.2 pad_maximum_fusion
  722.1 37.3 %collective-permute-done.13 = bf16[2,2,256,1024]{3,2,1,0:T(8,128)(2,1)} collective-permute-done((bf16[2,2,256,1024]{3,2,1,0:T(8,128)(2,1)}, bf16[2,2,256,1024]{3,2,1,0:T(8,128)(2,1)}, u32[]{:S(2)}, u32[]{:S(2)}) %collective-permute-start.13) | collective-permute-done | bytes 2097184 | tf_op jit(solution)/shard_map/ppermute | solution.py:65
  779.3 4.9 all-to-all-start.4
  784.1 4.3 add_add_fusion.4
  788.4 77.3 %scatter_rows.1 = f32[32,3072]{1,0:T(8,128)} custom-call(bf16[2,2,2,2,2,32,3072]{6,5,4,3,2,1,0:T(8,128)(2,1)} %bitcast.309), custom_call_target="tpu_custom_call" | custom-call | bytes 157286400 | tf_op jit(solution)/shard_map/scatter_rows/pallas_call | solution.py:496
  871.2 4.5 reshape.400
  (486 shorter events, 310.1 us)
Async XLA Ops:
  7.2 219.6 %all-gather.2.cloned.1.call-start = ((), (), s32[]{:S(2)}) async-start(), calls=%async_computation.8 | async-start | bytes 19464192 | tf_op jit(solution)/shard_map/all_gather | solution.py:561
  81.4 149.2 %copy-start.54 = (f32[1,1024]{1,0:T(1,128)}, f32[1,1024]{1,0:T(1,128)S(1)}, u32[]{:S(2)}) copy-start(f32[1,1024]{1,0:T(1,128)S(1)} %get-tuple-element.124) | copy-start | bytes 12292
  87.5 57.1 %copy-start.21 = (bf16[512,2048]{1,0:T(8,128)(2,1)}, bf16[512,2048]{1,0:T(8,128)(2,1)S(1)}, u32[]{:S(2)}) copy-start(bf16[512,2048]{1,0:T(8,128)(2,1)S(1)} %fusion.10) | copy-start | bytes 6291460
  87.6 55.4 %collective-permute-start = (bf16[2,256,2048]{2,1,0:T(8,128)(2,1)S(1)}, bf16[2,256,2048]{2,1,0:T(8,128)(2,1)}, u32[]{:S(2)}, u32[]{:S(2)}) collective-permute-start(bf16[2,256,2048]{2,1,0:T(8,128)(2,1)S(1)} %bitcast.317), channel_id=1, source_target_pairs={{0,16},{8,24},{1,17},{9,25},{2,18},{10,26},{3,19},{11,27},{4,20},{... | collective-permute-start | bytes 6291464 | tf_op jit(solution)/shard_map/ppermute | solution.py:65
  91.7 58.4 %copy-start.62 = (s32[2,1024]{1,0:T(2,128)S(1)}, s32[2,1024]{1,0:T(2,128)}, u32[]{:S(2)}) copy-start(s32[2,1024]{1,0:T(2,128)} %param.15) | copy-start | bytes 24580
  144.6 14.4 %collective-permute-start.1 = (bf16[2,256,2048]{2,1,0:T(8,128)(2,1)}, bf16[2,256,2048]{2,1,0:T(8,128)(2,1)}, u32[]{:S(2)}, u32[]{:S(2)}) collective-permute-start(bf16[2,256,2048]{2,1,0:T(8,128)(2,1)} %broadcast_select_fusion), channel_id=1, source_target_pairs={{0,8},{16,24},{24,16},{1,9},{17,25},{25,17},{2,10},{18,26},{26,18}... | collective-permute-start | bytes 6291464 | tf_op jit(solution)/shard_map/ppermute | solution.py:65
  226.4 58.7 %collective-permute-start.2 = (bf16[1024,1024]{1,0:T(8,128)(2,1)}, bf16[1024,1024]{1,0:T(8,128)(2,1)}, u32[]{:S(2)}, u32[]{:S(2)}) collective-permute-start(bf16[1024,1024]{1,0:T(8,128)(2,1)} %get-tuple-element.58), channel_id=1, source_target_pairs={{0,16},{16,0},{8,24},{24,8},{1,17},{17,1},{9,25},{25,9},{2,18},{18... | collective-permute-start | bytes 6291464 | tf_op jit(solution)/shard_map/ppermute | solution.py:65
  249.1 31.6 %all-to-all-start = ((bf16[8,64,1024]{2,1,0:T(8,128)(2,1)}), bf16[8,64,1024]{2,1,0:T(8,128)(2,1)S(1)}, u32[]{:S(2)}, u32[]{:S(2)}) async-start(bf16[8,64,1024]{2,1,0:T(8,128)(2,1)} %bitcast.18), calls=%async_computation | async-start | bytes 2097152 | tf_op jit(solution)/shard_map/all_to_all | solution.py:619
  258.0 43.4 %collective-permute-start.3 = (bf16[1024,1024]{1,0:T(8,128)(2,1)}, bf16[1024,1024]{1,0:T(8,128)(2,1)S(1)}, u32[]{:S(2)}, u32[]{:S(2)}) collective-permute-start(bf16[1024,1024]{1,0:T(8,128)(2,1)} %get-tuple-element.64), channel_id=1, source_target_pairs={{0,8},{8,0},{16,24},{24,16},{1,9},{9,1},{17,25},{25,17},{2,10},{10... | collective-permute-start | bytes 6291464 | tf_op jit(solution)/shard_map/ppermute | solution.py:65
  258.1 46.6 %collective-permute-start.4 = (bf16[1024,1024]{1,0:T(8,128)(2,1)}, bf16[1024,1024]{1,0:T(8,128)(2,1)}, u32[]{:S(2)}, u32[]{:S(2)}) collective-permute-start(bf16[1024,1024]{1,0:T(8,128)(2,1)} %get-tuple-element.65), channel_id=1, source_target_pairs={{0,8},{8,0},{16,24},{24,16},{1,9},{9,1},{17,25},{25,17},{2,10},{10... | collective-permute-start | bytes 6291464 | tf_op jit(solution)/shard_map/ppermute | solution.py:65
  280.7 33.2 %all-to-all-start.2 = ((bf16[8,64,1024]{2,1,0:T(8,128)(2,1)}), bf16[8,64,1024]{2,1,0:T(8,128)(2,1)}, u32[]{:S(2)}, u32[]{:S(2)}) async-start(bf16[8,64,1024]{2,1,0:T(8,128)(2,1)} %bitcast.35), calls=%async_computation.2 | async-start | bytes 2097152 | tf_op jit(solution)/shard_map/all_to_all | solution.py:651
  285.0 418.8 %reduce-scatter.4.cloned.1.call-start = ((), (), s32[]{:S(2)}) async-start(), calls=%async_computation.9 | async-start | bytes 10485760 | tf_op jit(solution)/shard_map/reduce_scatter | solution.py:666
  308.2 26.5 %collective-permute-start.6 = (bf16[1024,1024]{1,0:T(8,128)(2,1)}, bf16[1024,1024]{1,0:T(8,128)(2,1)}, u32[]{:S(2)}, u32[]{:S(2)}) collective-permute-start(bf16[1024,1024]{1,0:T(8,128)(2,1)} %collective-permute-done.2), channel_id=1, source_target_pairs={{0,8},{8,0},{16,24},{24,16},{1,9},{9,1},{17,25},{25,17},{2,10},{10... | collective-permute-start | bytes 6291464 | tf_op jit(solution)/shard_map/ppermute | solution.py:65
  341.7 366.2 %reduce-scatter.6.cloned.1.call-start = ((), (), s32[]{:S(2)}) async-start(), calls=%async_computation.10 | async-start | bytes 10485760 | tf_op jit(solution)/shard_map/reduce_scatter | solution.py:674
  341.9 71.0 %collective-permute-start.5 = (bf16[1024,1024]{1,0:T(8,128)(2,1)}, bf16[1024,1024]{1,0:T(8,128)(2,1)}, u32[]{:S(2)}, u32[]{:S(2)}) collective-permute-start(bf16[1024,1024]{1,0:T(8,128)(2,1)} %get-tuple-element.67), channel_id=1, source_target_pairs={{0,16},{16,0},{8,24},{24,8},{1,17},{17,1},{9,25},{25,9},{2,18},{18... | collective-permute-start | bytes 6291464 | tf_op jit(solution)/shard_map/ppermute | solution.py:65
  343.5 74.4 %copy-start.14 = (bf16[1,2,1024,1024]{3,2,1,0:T(8,128)(2,1)S(1)}, bf16[1,2,1024,1024]{3,2,1,0:T(8,128)(2,1)}, u32[]{:S(2)}) copy-start(bf16[1,2,1024,1024]{3,2,1,0:T(8,128)(2,1)} %outer_ref.1) | copy-start | bytes 12582916
  343.5 74.4 %copy-start.101 = (f32[512,1024]{1,0:T(8,128)S(1)}, f32[512,1024]{1,0:T(8,128)}, u32[]{:S(2)}) copy-start(f32[512,1024]{1,0:T(8,128)} %fusion.163) | copy-start | bytes 6291460
  412.9 27.2 %collective-permute-start.7 = (bf16[1024,1024]{1,0:T(8,128)(2,1)}, bf16[1024,1024]{1,0:T(8,128)(2,1)S(1)}, u32[]{:S(2)}, u32[]{:S(2)}) collective-permute-start(bf16[1024,1024]{1,0:T(8,128)(2,1)} %collective-permute-done.5), channel_id=1, source_target_pairs={{0,8},{8,0},{16,24},{24,16},{1,9},{9,1},{17,25},{25,17},{2,10},{10... | collective-permute-start | bytes 6291464 | tf_op jit(solution)/shard_map/ppermute | solution.py:65
  475.9 48.8 %collective-permute-start.8 = (bf16[1024,1024]{1,0:T(8,128)(2,1)}, bf16[1024,1024]{1,0:T(8,128)(2,1)}, u32[]{:S(2)}, u32[]{:S(2)}) collective-permute-start(bf16[1024,1024]{1,0:T(8,128)(2,1)} %convolution_convert_fusion.3), channel_id=1, source_target_pairs={{0,8},{8,0},{16,24},{24,16},{1,9},{9,1},{17,25},{25,17},{2,10},{10... | collective-permute-start | bytes 6291464 | tf_op jit(solution)/shard_map/ppermute | solution.py:65
  483.5 45.6 %collective-permute-start.9 = (bf16[1024,1024]{1,0:T(8,128)(2,1)}, bf16[1024,1024]{1,0:T(8,128)(2,1)}, u32[]{:S(2)}, u32[]{:S(2)}) collective-permute-start(bf16[1024,1024]{1,0:T(8,128)(2,1)} %convolution_convert_fusion.2), channel_id=1, source_target_pairs={{0,8},{8,0},{16,24},{24,16},{1,9},{9,1},{17,25},{25,17},{2,10},{10... | collective-permute-start | bytes 6291464 | tf_op jit(solution)/shard_map/ppermute | solution.py:65
  506.3 32.1 %all-to-all-start.3 = ((bf16[8,64,1024]{2,1,0:T(8,128)(2,1)}), bf16[8,64,1024]{2,1,0:T(8,128)(2,1)S(1)}, u32[]{:S(2)}, u32[]{:S(2)}) async-start(bf16[8,64,1024]{2,1,0:T(8,128)(2,1)} %bitcast.46), calls=%async_computation.3 | async-start | bytes 2097152 | tf_op jit(solution)/shard_map/all_to_all | solution.py:680
  512.3 354.0 %reduce-scatter.8.cloned.1.call-start = ((), (), s32[]{:S(2)}) async-start(), calls=%async_computation.11 | async-start | bytes 19464192 | tf_op jit(solution)/shard_map/reduce_scatter | solution.py:710
  538.5 56.4 %collective-permute-start.10 = (bf16[1024,1024]{1,0:T(8,128)(2,1)}, bf16[1024,1024]{1,0:T(8,128)(2,1)}, u32[]{:S(2)}, u32[]{:S(2)}) collective-permute-start(bf16[1024,1024]{1,0:T(8,128)(2,1)} %add_convert_fusion.1), channel_id=1, source_target_pairs={{0,16},{16,0},{8,24},{24,8},{1,17},{17,1},{9,25},{25,9},{2,18},{18... | collective-permute-start | bytes 6291464 | tf_op jit(solution)/shard_map/ppermute | solution.py:65
  605.9 66.9 %all-to-all-start.1 = ((bf16[8,64,1024]{2,1,0:T(8,128)(2,1)}), bf16[8,64,1024]{2,1,0:T(8,128)(2,1)S(1)}, u32[]{:S(2)}, u32[]{:S(2)}) async-start(bf16[8,64,1024]{2,1,0:T(8,128)(2,1)} %bitcast.31), calls=%async_computation.1 | async-start | bytes 2097152 | tf_op jit(solution)/shard_map/all_to_all | solution.py:644
  611.4 47.5 %collective-permute-start.11 = (bf16[1024,1024]{1,0:T(8,128)(2,1)}, bf16[1024,1024]{1,0:T(8,128)(2,1)}, u32[]{:S(2)}, u32[]{:S(2)}) collective-permute-start(bf16[1024,1024]{1,0:T(8,128)(2,1)} %add_convert_fusion), channel_id=1, source_target_pairs={{0,16},{16,0},{8,24},{24,8},{1,17},{17,1},{9,25},{25,9},{2,18},{18... | collective-permute-start | bytes 6291464 | tf_op jit(solution)/shard_map/ppermute | solution.py:65
  658.9 18.9 %collective-permute-start.12 = (bf16[2,2,256,1024]{3,2,1,0:T(8,128)(2,1)}, bf16[2,2,256,1024]{3,2,1,0:T(8,128)(2,1)}, u32[]{:S(2)}, u32[]{:S(2)}) collective-permute-start(bf16[2,2,256,1024]{3,2,1,0:T(8,128)(2,1)} %get-tuple-element.81), channel_id=1, source_target_pairs={{8,0},{24,16},{16,24},{9,1},{25,17},{17,25},{10,2},{26,18},{18,26}... | collective-permute-start | bytes 6291464 | tf_op jit(solution)/shard_map/ppermute | solution.py:65
  662.1 3.4 collective-permute-start.16
  665.6 4.0 collective-permute-start.17
  665.9 26.4 %collective-permute-start.14 = (bf16[1024,1024]{1,0:T(8,128)(2,1)}, bf16[1024,1024]{1,0:T(8,128)(2,1)}, u32[]{:S(2)}, u32[]{:S(2)}) collective-permute-start(bf16[1024,1024]{1,0:T(8,128)(2,1)} %convolution_convert_fusion.7), channel_id=1, source_target_pairs={{0,8},{8,0},{16,24},{24,16},{1,9},{9,1},{17,25},{25,17},{2,10},{10... | collective-permute-start | bytes 6291464 | tf_op jit(solution)/shard_map/ppermute | solution.py:65
  672.1 26.1 %collective-permute-start.15 = (bf16[1024,1024]{1,0:T(8,128)(2,1)}, bf16[1024,1024]{1,0:T(8,128)(2,1)}, u32[]{:S(2)}, u32[]{:S(2)}) collective-permute-start(bf16[1024,1024]{1,0:T(8,128)(2,1)} %convolution_convert_fusion.6), channel_id=1, source_target_pairs={{0,8},{8,0},{16,24},{24,16},{1,9},{9,1},{17,25},{25,17},{2,10},{10... | collective-permute-start | bytes 6291464 | tf_op jit(solution)/shard_map/ppermute | solution.py:65
  683.8 75.6 %collective-permute-start.13 = (bf16[2,2,256,1024]{3,2,1,0:T(8,128)(2,1)}, bf16[2,2,256,1024]{3,2,1,0:T(8,128)(2,1)}, u32[]{:S(2)}, u32[]{:S(2)}) collective-permute-start(bf16[2,2,256,1024]{3,2,1,0:T(8,128)(2,1)} %fusion.5), channel_id=1, source_target_pairs={{16,0},{24,8},{17,1},{25,9},{18,2},{26,10},{19,3},{27,11},{20,4},{... | collective-permute-start | bytes 6291464 | tf_op jit(solution)/shard_map/ppermute | solution.py:65
  779.3 86.5 %all-to-all-start.4 = ((f32[32,2,32]{2,1,0:T(2,128)}), f32[32,2,32]{2,1,0:T(2,128)S(1)}, u32[]{:S(2)}, u32[]{:S(2)}) async-start(f32[32,2,32]{2,1,0:T(2,128)} %maximum_bitcast_fusion), calls=%async_computation.6 | async-start | bytes 65536 | tf_op jit(solution)/shard_map/all_to_all | solution.py:739
  (122 other events, 755.0 us)
Sparse Core Ops, SparseCore 0:
  78.4 137.1 all-gather.1
  341.8 94.5 reduce-scatter.3
  476.5 83.7 reduce-scatter.5
  606.0 227.1 reduce-scatter.7

commit v8 on v7

--- a/solution.py
+++ b/solution.py
@@ -248,15 +248,15 @@
     return grad_pres, grad_normed
 
 
-def slices_in_order(operands):
+def slice_owner(place):
     seq = lax.axis_index("seq")
-    terms = None
+    return seq + (1 - 2 * (seq % 2)) * (place % 2) + (2 - 4 * (seq // 2)) * (place // 2)
+
+
+def slices_in_order(terms, operands):
     for place, (left, right) in enumerate(operands):
         values = weight_grad(left, right)
-        owner = seq + (1 - 2 * (seq % 2)) * (place % 2) + (2 - 4 * (seq // 2)) * (place // 2)
-        if terms is None:
-            terms = jnp.zeros((len(operands),) + values.shape, values.dtype)
-        terms = lax.dynamic_update_index_in_dim(terms, values, owner, 0)
+        terms = lax.dynamic_update_index_in_dim(terms, values, slice_owner(place), 0)
     return terms
 
 
@@ -608,8 +608,10 @@
     bias = jnp.where(allowed, 0.0, -1e30).astype(f32)
 
     attended_rows, outer_chip[0] = attend(query, kv_blocks, bias, outer_own)
-    late = together(inner_own[1], outer_own[1], attended_rows)
-    inner_chip[1], outer_chip[1] = [swap_chip(part) for part in late[:2]]
+    inner_chip[1] = swap_chip(together(inner_own[1], attended_rows)[0])
+    outer_late, _ = together(outer_own[1], rest_full)
+    outer_all = lax.all_gather(outer_late, "seq", axis=0)
+
     attended = attended_rows.reshape(token_count, model_width)
     hidden = tokens_flat + product(attended, proj_full)
     normed_ffn = layer_norm(hidden, gain_ffn).astype(bf16)
@@ -617,7 +619,8 @@
     routed = dense_out.astype(bf16)
 
     received = lax.all_to_all(routed[source_of], "wide", split_axis=0, concat_axis=0, tiled=True)
-    received, inner_chip[1] = together(received, inner_chip[1])
+    fresh = [jnp.zeros((seq_devices,) + part.shape[1:], bf16) for part in (outer_own, inner_own)]
+    received, inner_chip[1], *fresh = together(received, inner_chip[1], *fresh)
     received_f = received.astype(f32)
     inner_both = [swap_core(together(inner_chip[0], attended)[0]), None]
     outer_both = [swap_core(together(outer_chip[0], attended)[0]), None]
@@ -632,9 +635,14 @@
     for sublayer in range(2):
         if sublayer:
             inner_both[1] = swap_core(together(inner_chip[1], state_now)[0])
-            outer_both[1] = swap_core(together(outer_chip[1], state_now)[0])
         inner_parts = [part[sublayer] for part in (inner_own, inner_core, inner_chip, inner_both)]
-        outer_parts = [part[sublayer] for part in (outer_own, outer_core, outer_chip, outer_both)]
+        if sublayer:
+            outer_parts = [
+                lax.dynamic_index_in_dim(outer_all, slice_owner(place), 0, keepdims=False)
+                for place in range(len(inner_parts))
+            ]
+        else:
+            outer_parts = [part[0] for part in (outer_own, outer_core, outer_chip, outer_both)]
         normed = layer_norm(state_now, gains_f[sublayer]).astype(bf16)
         state_next, kept = ffn_forward(normed, inner_parts, outer_parts, state_now)
         kept_layers.append((state_now, normed, kept))
@@ -662,7 +670,7 @@
         grad_branch = grad_state.astype(bf16)
         outer_terms = [(act, grad_branch) for act, _ in kept]
         if sublayer:
-            terms, grad_branch = together(slices_in_order(outer_terms), grad_branch)
+            terms, grad_branch = together(slices_in_order(fresh[0], outer_terms), grad_branch)
             second_sums.append(lax.psum_scatter(terms, "seq", scatter_dimension=0, tiled=True))
         grad_pres, grad_normed = ffn_backward(kept, inner_parts, outer_parts, grad_branch)
         inner_terms = [(normed_in, grad_pre) for grad_pre in grad_pres]
@@ -670,7 +678,7 @@
         grad_state = grad_state + grad_resid
         gain_grads[sublayer] = gain_grad
         if sublayer:
-            terms, grad_state = together(slices_in_order(inner_terms), grad_state)
+            terms, grad_state = together(slices_in_order(fresh[1], inner_terms), grad_state)
             second_sums.append(lax.psum_scatter(terms, "seq", scatter_dimension=0, tiled=True))
     outer0 = SliceSum(outer_terms)
     inner0 = SliceSum(inner_terms)

time: 897 us -> 861 us (0.960)
  waiting for transfers between devices: 208 us -> 177 us
    ppermute x18 -> x16, waiting for transfers between devices: 180 us -> 151 us  [seq_send(): return lax.ppermute(values, 'seq', pairs)]
    unnamed x261 -> x266, local copies, waits for them, and re-layouts: 27.5 us -> 32 us
  transfers between devices with their start and end apart: 27 -> 26, of which waited for: 9 -> 9; matrix products, arithmetic and copies ran while one was open for 36% -> 39% of each run, Pallas kernels for 20% -> 21%
where the time goes in v8:
time: 861 us; the launch traced here: 852 us
  Pallas kernels  244 us (28%)
  matrix products  223 us (26%)
  waiting for transfers between devices  177 us (21%)
  other arithmetic  75 us (9%)
  local copies, waits for them, and re-layouts  72.9 us (8%)
  starting transfers between devices  40 us (5%)
  between operations  19.5 us (2%)
    ppermute x16, waiting for transfers between devices, seq_send(): return lax.ppermute(values, 'seq', pairs)  151 us
    dot_general x28, matrix products, product_at(): lax.dot_general(left_side, right_side, (((0,), (0,)), ((), ())), preferre...  78.6 us
    pallas_call x1, Pallas kernels, scatter_rows(): pl.pallas_call(functools.partial(scatter_kernel, bits, orders), in_specs=...  77.2 us
    dot_general x27, matrix products, product(): return jnp.dot(left_side, right_side, preferred_element_type=f32)  74.4 us
    dot_general x28, matrix products, product_bt(): lax.dot_general(left_side, right_side, (((1,), (1,)), ((), ())), preferre...  69 us
    pallas_call x1, Pallas kernels, attend(): pl.pallas_call(functools.partial(attend_kernel, 1.0 / math.sqrt(HEAD_DIM)...  66 us
    pallas_call x1, Pallas kernels, gather_rows(): pl.pallas_call(functools.partial(gather_kernel, bits, orders), in_specs=[...  64.9 us
    pallas_call x1, Pallas kernels, attend_back(): pl.pallas_call(functools.partial(attend_back_kernel, 1.0 / math.sqrt(HEAD...  36.4 us
  transfers between devices with their start and end apart: 26, of which 9 were waited for; matrix products, arithmetic and copies ran while one was open for 39% of the time, Pallas kernels for 21%

profile of v8, /device:TPU:0, one launch (start us, length us, event | category | flops | bytes accessed | tf_op | source)
XLA Modules:
  0.0 852.2 jit_solution(16939108436884576244)
XLA Ops:
  12.2 64.9 %gather_rows.1 = (bf16[2,2,2,2,2,32,3328]{6,5,4,3,2,1,0:T(8,128)(2,1)}, bf16[2,1024,1024]{2,1,0:T(8,128)(2,1)}, bf16[2,1024,1024]{2,1,0:T(8,128)(2,1)}, bf16[1024,1024]{1,0:T(8,128)(2,1)}) custom-call(bf16[32,3328]{1,0:T(8,128)(2,1)} %fusion.170.own_ref, bf16[1,2,1024,1024]{3,2,1,0:T(8,128)(2,1)} %inner_ref.1, bf16[1,2,1024,1024]{3,2,1,0:T(8,128)(2,1)} %outer_ref.1), custom_call_target="tpu_custom_call" | custom-call | bytes 85196800 | tf_op jit(solution)/shard_map/gather_rows/pallas_call | solution.py:406
  82.1 5.2 fusion.10
  91.4 51.3 %collective-permute-done.k2.v2 = bf16[2,256,2048]{2,1,0:T(8,128)(2,1)} collective-permute-done((bf16[2,256,2048]{2,1,0:T(8,128)(2,1)S(1)}, bf16[2,256,2048]{2,1,0:T(8,128)(2,1)}, u32[]{:S(2)}, u32[]{:S(2)}) %collective-permute-start) | collective-permute-done | bytes 2097184 | tf_op jit(solution)/shard_map/ppermute | solution.py:65
  160.1 66.0 %attend.1 = (bf16[2,256,1024]{2,1,0:T(8,128)(2,1)}, bf16[1024,1024]{1,0:T(8,128)(2,1)}) custom-call(bf16[2,256,1024]{2,1,0:T(8,128)(2,1)} %bitcast.421, bf16[2,256,2048]{2,1,0:T(8,128)(2,1)} %bitcast.338, bf16[2,256,2048]{2,1,0:T(8,128)(2,1)} %bitcast.339, bf16[2,256,2048]{2,1,0:T(8,128)(2,1)} %collective-permute-done.1.k1.v1, ...), custom_call_target="tpu_custom_call" | custom-call | flops 9663676416 | bytes 8388608 | tf_op jit(solution)/shard_map/attend/pallas_call | solution.py:191
  234.3 4.5 fusion.101
  238.8 4.8 fusion.93
  254.3 6.1 all-to-all-start
  263.9 22.0 %all-to-all-done = bf16[8,64,1024]{2,1,0:T(8,128)(2,1)S(1)} async-done(((bf16[8,64,1024]{2,1,0:T(8,128)(2,1)}), bf16[8,64,1024]{2,1,0:T(8,128)(2,1)S(1)}, u32[]{:S(2)}, u32[]{:S(2)}) %all-to-all-start) | async-done | bytes 1048608 | tf_op jit(solution)/shard_map/all_to_all | solution.py:621
  290.2 15.6 %collective-permute-done.2 = bf16[1024,1024]{1,0:T(8,128)(2,1)} collective-permute-done((bf16[1024,1024]{1,0:T(8,128)(2,1)}, bf16[1024,1024]{1,0:T(8,128)(2,1)}, u32[]{:S(2)}, u32[]{:S(2)}) %collective-permute-start.2) | collective-permute-done | bytes 2097184 | tf_op jit(solution)/shard_map/ppermute | solution.py:65
  306.5 4.5 multiply_convert_fusion.21
  329.7 4.5 broadcast.298
  334.1 7.8 copy.62
  371.1 4.4 multiply_convert_fusion.10
  423.3 4.7 multiply_convert_fusion.4
  454.0 5.6 all-to-all-start.3
  471.9 4.4 add_convert_fusion.1
  476.3 4.4 add_convert_fusion
  480.7 4.7 all-to-all-done.3
  530.9 29.5 %collective-permute-done.8 = bf16[1024,1024]{1,0:T(8,128)(2,1)} collective-permute-done((bf16[1024,1024]{1,0:T(8,128)(2,1)}, bf16[1024,1024]{1,0:T(8,128)(2,1)}, u32[]{:S(2)}, u32[]{:S(2)}) %collective-permute-start.8) | collective-permute-done | bytes 2097184 | tf_op jit(solution)/shard_map/ppermute | solution.py:65
  571.6 5.5 all-to-all-start.1
  577.7 36.4 %attend_back.1 = (bf16[2,256,1024]{2,1,0:T(8,128)(2,1)}, bf16[2,2,256,1024]{3,2,1,0:T(8,128)(2,1)}, bf16[2,2,256,1024]{3,2,1,0:T(8,128)(2,1)}, bf16[2,2,256,1024]{3,2,1,0:T(8,128)(2,1)}) custom-call(bf16[2,256,1024]{2,1,0:T(8,128)(2,1)} %bitcast.422, bf16[2,256,2048]{2,1,0:T(8,128)(2,1)} %bitcast.340, bf16[2,256,2048]{2,1,0:T(8,128)(2,1)} %bitcast.341, ...), custom_call_target="tpu_custom_call" | custom-call | flops 24159191040 | bytes 16777216 | tf_op jit(solution)/shard_map/attend_back/pallas_call | solution.py:216
  614.1 10.4 %collective-permute-done.9 = bf16[1024,1024]{1,0:T(8,128)(2,1)} collective-permute-done((bf16[1024,1024]{1,0:T(8,128)(2,1)}, bf16[1024,1024]{1,0:T(8,128)(2,1)}, u32[]{:S(2)}, u32[]{:S(2)}) %collective-permute-start.9) | collective-permute-done | bytes 2097184 | tf_op jit(solution)/shard_map/ppermute | solution.py:65
  643.4 5.9 fusion.5
  653.4 4.3 fusion.115
  657.7 5.7 add_bitcast_fusion
  663.5 5.6 add_bitcast_fusion.1
  679.2 4.7 pad_maximum_fusion.1
  684.0 40.9 %collective-permute-done.11 = bf16[2,2,256,1024]{3,2,1,0:T(8,128)(2,1)} collective-permute-done((bf16[2,2,256,1024]{3,2,1,0:T(8,128)(2,1)}, bf16[2,2,256,1024]{3,2,1,0:T(8,128)(2,1)}, u32[]{:S(2)}, u32[]{:S(2)}) %collective-permute-start.11) | collective-permute-done | bytes 2097184 | tf_op jit(solution)/shard_map/ppermute | solution.py:65
  743.0 4.8 all-to-all-start.4
  747.8 4.3 add_add_fusion.4
  752.1 77.2 %scatter_rows.1 = f32[32,3072]{1,0:T(8,128)} custom-call(bf16[2,2,2,2,2,32,3072]{6,5,4,3,2,1,0:T(8,128)(2,1)} %bitcast.327), custom_call_target="tpu_custom_call" | custom-call | bytes 157286400 | tf_op jit(solution)/shard_map/scatter_rows/pallas_call | solution.py:496
  834.8 4.5 reshape.400
  (493 shorter events, 307.7 us)
Async XLA Ops:
  7.2 219.3 %all-gather.4.cloned.1.call-start = ((), (), s32[]{:S(2)}) async-start(), calls=%async_computation.8 | async-start | bytes 19464192 | tf_op jit(solution)/shard_map/all_gather | solution.py:561
  12.2 64.9 %copy-start.54 = (bf16[32,1024]{1,0:T(8,128)(2,1)S(1)}, bf16[32,1024]{1,0:T(8,128)(2,1)}, u32[]{:S(2)}) copy-start(bf16[32,1024]{1,0:T(8,128)(2,1)} %param.19) | copy-start | bytes 196612
  78.0 293.1 %all-gather.6.cloned.1.call-start = ((), (), s32[]{:S(2)}) async-start(), calls=%async_computation.12 | async-start | bytes 10485760 | tf_op jit(solution)/shard_map/all_gather | solution.py:613
  81.1 149.1 %copy-start.55 = (f32[1,1024]{1,0:T(1,128)}, f32[1,1024]{1,0:T(1,128)S(1)}, u32[]{:S(2)}) copy-start(f32[1,1024]{1,0:T(1,128)S(1)} %get-tuple-element.126) | copy-start | bytes 12292
  87.2 57.0 %copy-start.18 = (bf16[512,2048]{1,0:T(8,128)(2,1)}, bf16[512,2048]{1,0:T(8,128)(2,1)S(1)}, u32[]{:S(2)}) copy-start(bf16[512,2048]{1,0:T(8,128)(2,1)S(1)} %fusion.10) | copy-start | bytes 6291460
  87.3 55.4 %collective-permute-start = (bf16[2,256,2048]{2,1,0:T(8,128)(2,1)S(1)}, bf16[2,256,2048]{2,1,0:T(8,128)(2,1)}, u32[]{:S(2)}, u32[]{:S(2)}) collective-permute-start(bf16[2,256,2048]{2,1,0:T(8,128)(2,1)S(1)} %bitcast.336), channel_id=1, source_target_pairs={{0,16},{8,24},{1,17},{9,25},{2,18},{10,26},{3,19},{11,27},{4,20},{... | collective-permute-start | bytes 6291464 | tf_op jit(solution)/shard_map/ppermute | solution.py:65
  91.4 58.4 %copy-start.63 = (s32[2,1024]{1,0:T(2,128)S(1)}, s32[2,1024]{1,0:T(2,128)}, u32[]{:S(2)}) copy-start(s32[2,1024]{1,0:T(2,128)} %param.15) | copy-start | bytes 24580
  144.3 15.9 %collective-permute-start.1 = (bf16[2,256,2048]{2,1,0:T(8,128)(2,1)}, bf16[2,256,2048]{2,1,0:T(8,128)(2,1)}, u32[]{:S(2)}, u32[]{:S(2)}) collective-permute-start(bf16[2,256,2048]{2,1,0:T(8,128)(2,1)} %broadcast_select_fusion), channel_id=1, source_target_pairs={{0,8},{16,24},{24,16},{1,9},{17,25},{25,17},{2,10},{18,26},{26,18}... | collective-permute-start | bytes 6291464 | tf_op jit(solution)/shard_map/ppermute | solution.py:65
  226.1 79.7 %collective-permute-start.2 = (bf16[1024,1024]{1,0:T(8,128)(2,1)}, bf16[1024,1024]{1,0:T(8,128)(2,1)}, u32[]{:S(2)}, u32[]{:S(2)}) collective-permute-start(bf16[1024,1024]{1,0:T(8,128)(2,1)} %slice_bitcast_fusion.1), channel_id=1, source_target_pairs={{0,16},{16,0},{8,24},{24,8},{1,17},{17,1},{9,25},{25,9},{2,18},{18... | collective-permute-start | bytes 6291464 | tf_op jit(solution)/shard_map/ppermute | solution.py:65
  254.3 31.6 %all-to-all-start = ((bf16[8,64,1024]{2,1,0:T(8,128)(2,1)}), bf16[8,64,1024]{2,1,0:T(8,128)(2,1)S(1)}, u32[]{:S(2)}, u32[]{:S(2)}) async-start(bf16[8,64,1024]{2,1,0:T(8,128)(2,1)} %bitcast.18), calls=%async_computation | async-start | bytes 2097152 | tf_op jit(solution)/shard_map/all_to_all | solution.py:621
  263.3 59.0 %collective-permute-start.3 = (bf16[1024,1024]{1,0:T(8,128)(2,1)}, bf16[1024,1024]{1,0:T(8,128)(2,1)S(1)}, u32[]{:S(2)}, u32[]{:S(2)}) collective-permute-start(bf16[1024,1024]{1,0:T(8,128)(2,1)} %get-tuple-element.65), channel_id=1, source_target_pairs={{0,8},{8,0},{16,24},{24,16},{1,9},{9,1},{17,25},{25,17},{2,10},{10... | collective-permute-start | bytes 6291464 | tf_op jit(solution)/shard_map/ppermute | solution.py:65
  263.4 62.1 %collective-permute-start.4 = (bf16[1024,1024]{1,0:T(8,128)(2,1)}, bf16[1024,1024]{1,0:T(8,128)(2,1)}, u32[]{:S(2)}, u32[]{:S(2)}) collective-permute-start(bf16[1024,1024]{1,0:T(8,128)(2,1)} %get-tuple-element.66), channel_id=1, source_target_pairs={{0,8},{8,0},{16,24},{24,16},{1,9},{9,1},{17,25},{25,17},{2,10},{10... | collective-permute-start | bytes 6291464 | tf_op jit(solution)/shard_map/ppermute | solution.py:65
  285.9 61.6 %all-to-all-start.2 = ((bf16[8,64,1024]{2,1,0:T(8,128)(2,1)}), bf16[8,64,1024]{2,1,0:T(8,128)(2,1)}, u32[]{:S(2)}, u32[]{:S(2)}) async-start(bf16[8,64,1024]{2,1,0:T(8,128)(2,1)} %bitcast.39), calls=%async_computation.2 | async-start | bytes 2097152 | tf_op jit(solution)/shard_map/all_to_all | solution.py:659
  290.2 378.9 %reduce-scatter.4.cloned.1.call-start = ((), (), s32[]{:S(2)}) async-start(), calls=%async_computation.9 | async-start | bytes 10485760 | tf_op jit(solution)/shard_map/reduce_scatter | solution.py:674
  341.9 22.0 %collective-permute-start.5 = (bf16[1024,1024]{1,0:T(8,128)(2,1)}, bf16[1024,1024]{1,0:T(8,128)(2,1)}, u32[]{:S(2)}, u32[]{:S(2)}) collective-permute-start(bf16[1024,1024]{1,0:T(8,128)(2,1)} %collective-permute-done.2), channel_id=1, source_target_pairs={{0,8},{8,0},{16,24},{24,16},{1,9},{9,1},{17,25},{25,17},{2,10},{10... | collective-permute-start | bytes 6291464 | tf_op jit(solution)/shard_map/ppermute | solution.py:65
  371.0 305.2 %reduce-scatter.6.cloned.1.call-start = ((), (), s32[]{:S(2)}) async-start(), calls=%async_computation.10 | async-start | bytes 10485760 | tf_op jit(solution)/shard_map/reduce_scatter | solution.py:682
  430.9 45.4 %collective-permute-start.7 = (bf16[1024,1024]{1,0:T(8,128)(2,1)}, bf16[1024,1024]{1,0:T(8,128)(2,1)}, u32[]{:S(2)}, u32[]{:S(2)}) collective-permute-start(bf16[1024,1024]{1,0:T(8,128)(2,1)} %convolution_convert_fusion.2), channel_id=1, source_target_pairs={{0,8},{8,0},{16,24},{24,16},{1,9},{9,1},{17,25},{25,17},{2,10},{10... | collective-permute-start | bytes 6291464 | tf_op jit(solution)/shard_map/ppermute | solution.py:65
  433.8 38.2 %collective-permute-start.6 = (bf16[1024,1024]{1,0:T(8,128)(2,1)}, bf16[1024,1024]{1,0:T(8,128)(2,1)}, u32[]{:S(2)}, u32[]{:S(2)}) collective-permute-start(bf16[1024,1024]{1,0:T(8,128)(2,1)} %convolution_convert_fusion.3), channel_id=1, source_target_pairs={{0,8},{8,0},{16,24},{24,16},{1,9},{9,1},{17,25},{25,17},{2,10},{10... | collective-permute-start | bytes 6291464 | tf_op jit(solution)/shard_map/ppermute | solution.py:65
  454.0 31.4 %all-to-all-start.3 = ((bf16[8,64,1024]{2,1,0:T(8,128)(2,1)}), bf16[8,64,1024]{2,1,0:T(8,128)(2,1)S(1)}, u32[]{:S(2)}, u32[]{:S(2)}) async-start(bf16[8,64,1024]{2,1,0:T(8,128)(2,1)} %bitcast.335), calls=%async_computation.3 | async-start | bytes 2097152 | tf_op jit(solution)/shard_map/all_to_all | solution.py:688
  459.5 370.3 %reduce-scatter.8.cloned.1.call-start = ((), (), s32[]{:S(2)}) async-start(), calls=%async_computation.11 | async-start | bytes 19464192 | tf_op jit(solution)/shard_map/reduce_scatter | solution.py:718
  485.4 75.0 %collective-permute-start.8 = (bf16[1024,1024]{1,0:T(8,128)(2,1)}, bf16[1024,1024]{1,0:T(8,128)(2,1)}, u32[]{:S(2)}, u32[]{:S(2)}) collective-permute-start(bf16[1024,1024]{1,0:T(8,128)(2,1)} %add_convert_fusion.1), channel_id=1, source_target_pairs={{0,16},{16,0},{8,24},{24,8},{1,17},{17,1},{9,25},{25,9},{2,18},{18... | collective-permute-start | bytes 6291464 | tf_op jit(solution)/shard_map/ppermute | solution.py:65
  571.6 66.7 %all-to-all-start.1 = ((bf16[8,64,1024]{2,1,0:T(8,128)(2,1)}), bf16[8,64,1024]{2,1,0:T(8,128)(2,1)S(1)}, u32[]{:S(2)}, u32[]{:S(2)}) async-start(bf16[8,64,1024]{2,1,0:T(8,128)(2,1)} %bitcast.35), calls=%async_computation.1 | async-start | bytes 2097152 | tf_op jit(solution)/shard_map/all_to_all | solution.py:652
  577.1 47.4 %collective-permute-start.9 = (bf16[1024,1024]{1,0:T(8,128)(2,1)}, bf16[1024,1024]{1,0:T(8,128)(2,1)}, u32[]{:S(2)}, u32[]{:S(2)}) collective-permute-start(bf16[1024,1024]{1,0:T(8,128)(2,1)} %add_convert_fusion), channel_id=1, source_target_pairs={{0,16},{16,0},{8,24},{24,8},{1,17},{17,1},{9,25},{25,9},{2,18},{18... | collective-permute-start | bytes 6291464 | tf_op jit(solution)/shard_map/ppermute | solution.py:65
  577.6 54.0 %copy-start.70 = (f32[2,256]{1,0:T(2,128)S(1)}, f32[2,256]{1,0:T(2,128)}, u32[]{:S(2)}) copy-start(f32[2,256]{1,0:T(2,128)} %copy-done.69) | copy-start | bytes 6148
  577.7 54.0 %copy-start.75 = (f32[2,256]{1,0:T(2,128)S(1)}, f32[2,256]{1,0:T(2,128)}, u32[]{:S(2)}) copy-start(f32[2,256]{1,0:T(2,128)} %get-tuple-element.131) | copy-start | bytes 6148
  624.5 18.8 %collective-permute-start.10 = (bf16[2,2,256,1024]{3,2,1,0:T(8,128)(2,1)}, bf16[2,2,256,1024]{3,2,1,0:T(8,128)(2,1)}, u32[]{:S(2)}, u32[]{:S(2)}) collective-permute-start(bf16[2,2,256,1024]{3,2,1,0:T(8,128)(2,1)} %get-tuple-element.83), channel_id=1, source_target_pairs={{8,0},{24,16},{16,24},{9,1},{25,17},{17,25},{10,2},{26,18},{18,26}... | collective-permute-start | bytes 6291464 | tf_op jit(solution)/shard_map/ppermute | solution.py:65
  627.7 3.4 collective-permute-start.14
  631.1 4.0 collective-permute-start.15
  631.6 26.1 %collective-permute-start.13 = (bf16[1024,1024]{1,0:T(8,128)(2,1)}, bf16[1024,1024]{1,0:T(8,128)(2,1)}, u32[]{:S(2)}, u32[]{:S(2)}) collective-permute-start(bf16[1024,1024]{1,0:T(8,128)(2,1)} %convolution_convert_fusion.6), channel_id=1, source_target_pairs={{0,8},{8,0},{16,24},{24,16},{1,9},{9,1},{17,25},{25,17},{2,10},{10... | collective-permute-start | bytes 6291464 | tf_op jit(solution)/shard_map/ppermute | solution.py:65
  637.6 25.9 %collective-permute-start.12 = (bf16[1024,1024]{1,0:T(8,128)(2,1)}, bf16[1024,1024]{1,0:T(8,128)(2,1)}, u32[]{:S(2)}, u32[]{:S(2)}) collective-permute-start(bf16[1024,1024]{1,0:T(8,128)(2,1)} %convolution_convert_fusion.7), channel_id=1, source_target_pairs={{0,8},{8,0},{16,24},{24,16},{1,9},{9,1},{17,25},{25,17},{2,10},{10... | collective-permute-start | bytes 6291464 | tf_op jit(solution)/shard_map/ppermute | solution.py:65
  649.2 75.6 %collective-permute-start.11 = (bf16[2,2,256,1024]{3,2,1,0:T(8,128)(2,1)}, bf16[2,2,256,1024]{3,2,1,0:T(8,128)(2,1)}, u32[]{:S(2)}, u32[]{:S(2)}) collective-permute-start(bf16[2,2,256,1024]{3,2,1,0:T(8,128)(2,1)} %fusion.5), channel_id=1, source_target_pairs={{16,0},{24,8},{17,1},{25,9},{18,2},{26,10},{19,3},{27,11},{20,4},{... | collective-permute-start | bytes 6291464 | tf_op jit(solution)/shard_map/ppermute | solution.py:65
  743.0 86.3 %all-to-all-start.4 = ((f32[32,2,32]{2,1,0:T(2,128)}), f32[32,2,32]{2,1,0:T(2,128)S(1)}, u32[]{:S(2)}, u32[]{:S(2)}) async-start(f32[32,2,32]{2,1,0:T(2,128)} %maximum_bitcast_fusion), calls=%async_computation.6 | async-start | bytes 65536 | tf_op jit(solution)/shard_map/all_to_all | solution.py:747
  (123 other events, 771.9 us)
Sparse Core Ops, SparseCore 0:
  78.1 135.9 all-gather.3
  230.3 90.2 all-gather.5
  371.1 71.3 reduce-scatter.3
  445.5 99.2 reduce-scatter.5
  571.7 230.2 reduce-scatter.7

commit v9 on v5

--- a/solution.py
+++ b/solution.py
@@ -246,6 +246,18 @@
         piece = product_bt(grad_pre, inner)
         grad_normed = piece if grad_normed is None else grad_normed + piece
     return grad_pres, grad_normed
+
+
+def slice_owner(place):
+    seq = lax.axis_index("seq")
+    return seq + (1 - 2 * (seq % 2)) * (place % 2) + (2 - 4 * (seq // 2)) * (place // 2)
+
+
+def slices_in_order(terms, operands):
+    for place, (left, right) in enumerate(operands):
+        values = weight_grad(left, right)
+        terms = lax.dynamic_update_index_in_dim(terms, values, slice_owner(place), 0)
+    return terms
 
 
 class SliceSum:
@@ -603,7 +615,8 @@
     routed = dense_out.astype(bf16)
 
     received = lax.all_to_all(routed[source_of], "wide", split_axis=0, concat_axis=0, tiled=True)
-    received, inner_chip[1] = together(received, inner_chip[1])
+    fresh = jnp.zeros((seq_devices,) + inner_own.shape[1:], bf16)
+    received, inner_chip[1], fresh = together(received, inner_chip[1], fresh)
     received_f = received.astype(f32)
     inner_both = [swap_core(together(inner_chip[0], attended)[0]), None]
     outer_both = [swap_core(together(outer_chip[0], attended)[0]), None]
@@ -657,36 +670,40 @@
         gain_grads[sublayer] = gain_grad
         sums[sublayer] = [SliceSum(operands) for operands in weight_terms[sublayer]]
         if sublayer:
-            grad_state, *held = together(grad_state, *[part.term(3) for part in sums[1]])
-            for part, values in zip(sums[1], held):
-                part.send_both(values)
+            outer1 = sums[1][0]
+            grad_state, both, fresh = together(
+                grad_state, outer1.term(3), slices_in_order(fresh, weight_terms[1][1])
+            )
+            outer1.send_both(both)
+            inner_second = lax.psum_scatter(fresh, "seq", scatter_dimension=0, tiled=True)
     grad_logit = grad_gate * gate_value * (1.0 - gate_value)
     grad_routed = (grad_state + grad_logit[:, None] * centroid_f[None, :]).astype(bf16)
     centroid_grad = jnp.dot(grad_logit, received_f, precision=highest)
-    grad_routed, *held = together(grad_routed, *[part.chip_sum() for part in sums[1]])
-    for part, values in zip(sums[1], held):
-        part.send_chip(values)
+    grad_routed, held = together(grad_routed, outer1.chip_sum())
+    outer1.send_chip(held)
     returned_grad = lax.all_to_all(grad_routed, "wide", split_axis=0, concat_axis=0, tiled=True)
+    outer0, inner0 = sums[0]
     returned_grad, *held = together(
         returned_grad,
-        *[part.term(3) for part in sums[0]],
-        *[part.term(1) for part in sums[1]],
-        *[part.term(0) for part in sums[1]],
-    )
-    for part, values in zip(sums[0], held[:2]):
-        part.send_both(values)
-    for part, values in zip(sums[1], held[2:4]):
-        part.send_core(values)
-    for part, values in zip(sums[1], held[4:]):
-        part.own = values
+        outer0.term(3),
+        inner0.term(3),
+        outer1.term(1),
+        outer0.term(1),
+        inner0.term(1),
+        outer1.term(0),
+    )
+    outer0.send_both(held[0])
+    inner0.send_both(held[1])
+    outer1.send_core(held[2])
+    outer0.send_core(held[3])
+    inner0.send_core(held[4])
+    outer1.own = held[5]
     grad_dense = grad_flat.astype(f32) + returned_grad[slot_index].astype(f32)
 
     grad_down_in = grad_dense.astype(bf16)
     grad_pres, grad_normed_ffn = ffn_backward(dense_kept, up_parts, down_parts, grad_down_in)
     grad_hidden_norm, grad_gain_ffn = norm_back(hidden, gain_ffn, grad_normed_ffn)
     grad_hidden = grad_dense + grad_hidden_norm
-    outer1, inner1 = sums[1]
-    outer0, inner0 = sums[0]
     grad_hidden, outer1.got_chip = together(grad_hidden, outer1.got_chip)
     grad_proj = grad_hidden.astype(bf16)
     rest_grad = jnp.concatenate(
@@ -698,25 +715,25 @@
     rest_grad = row_major(rest_grad)
     grad_attended = product_bt(grad_proj, proj_full).astype(bf16)
     grad_attended, rest_grad = together(grad_attended, rest_grad)
+    grad_attended, held = together(grad_attended, outer0.chip_sum())
+    outer0.send_chip(held)
     rest_sum = lax.psum_scatter(rest_grad, every, scatter_dimension=0, tiled=True).astype(f32)
     grad_query, grad_kv0, grad_kv1, grad_kv2 = attend_back(
         query, kv_blocks, bias, grad_attended.reshape(query.shape)
     )
-    grad_kv1, inner1.got_chip = together(grad_kv1, inner1.got_chip)
+    grad_kv1, outer0.got_chip = together(grad_kv1, outer0.got_chip)
     got_near = seq_send(grad_kv1, [(1, 0), (3, 2), (2, 3)])
     far_sum = jnp.where(
         seq_index == 3, (grad_kv2.astype(f32) + got_near.astype(f32)).astype(bf16), grad_kv2
     )
     got_far = seq_send(far_sum, [(2, 0), (3, 1)])
-    got_far, *held = together(
-        got_far, *[part.term(1) for part in sums[0]], *[part.term(0) for part in sums[0]]
-    )
-    for part, values in zip(sums[0], held[:2]):
-        part.send_core(values)
-    for part, values in zip(sums[0], held[2:]):
-        part.own = values
-    outer_send, inner_send, got_far = together(outer0.chip_sum(), inner0.chip_sum(), got_far)
-    outer0.send_chip(outer_send)
+    outer0.own = outer0.term(0)
+    got_far, inner0.own, inner_send, outer_total = together(
+        got_far,
+        inner0.term(0),
+        inner0.chip_sum(),
+        jnp.stack([outer0.total(), outer1.total()]),
+    )
     inner0.send_chip(inner_send)
     kv_sum = grad_kv0.astype(f32) + got_far.astype(f32)
     kv_sum = kv_sum + jnp.where(seq_index % 2 == 0, got_near.astype(f32), 0.0)
@@ -770,8 +787,8 @@
         down_grad,
         totals[2:3],
         totals[:2][None],
-        jnp.stack([inner0.total(), inner1.total()])[None],
-        jnp.stack([outer0.total(), outer1.total()])[None],
+        jnp.stack([inner0.total(), inner_second[0].astype(f32)])[None],
+        outer_total[None],
         totals[3, :1] / token_total,
         totals[3, 1:2] / token_total,
     )

time: 828 us -> 832 us (level)
  Pallas kernels: 260 us -> 247 us
    pallas_call x1, Pallas kernels: 90.1 us -> 77.3 us  [scatter_rows(): pl.pallas_call(functools.partial(scatter_kernel, bits, orders), in_specs=...]
    ppermute x24 -> x21, waiting for transfers between devices: 117 us -> 124 us  [seq_send(): return lax.ppermute(values, 'seq', pairs)]
    ppermute x24 -> x21, starting transfers between devices: 21.8 us -> 17.5 us  [seq_send(): return lax.ppermute(values, 'seq', pairs)]
    unnamed x261 -> x251, local copies, waits for them, and re-layouts: 18.4 us -> 20.6 us
  transfers between devices with their start and end apart: 31 -> 29, of which waited for: 6 -> 8; matrix products, arithmetic and copies ran while one was open for 31% -> 35% of each run, Pallas kernels for 24% -> 22%
where the time goes in v9:
time: 832 us; the launch traced here: 824 us
  Pallas kernels  247 us (30%)
  matrix products  225 us (27%)
  waiting for transfers between devices  152 us (18%)
  other arithmetic  74.3 us (9%)
  local copies, waits for them, and re-layouts  61 us (7%)
  starting transfers between devices  43.9 us (5%)
  between operations  19.4 us (2%)
    ppermute x21, waiting for transfers between devices, seq_send(): return lax.ppermute(values, 'seq', pairs)  124 us
    dot_general x28, matrix products, product_at(): lax.dot_general(left_side, right_side, (((0,), (0,)), ((), ())), preferre...  79.7 us
    dot_general x28, matrix products, product_bt(): lax.dot_general(left_side, right_side, (((1,), (1,)), ((), ())), preferre...  78.9 us
    pallas_call x1, Pallas kernels, scatter_rows(): pl.pallas_call(functools.partial(scatter_kernel, bits, orders), in_specs=...  77.3 us
    pallas_call x1, Pallas kernels, attend(): pl.pallas_call(functools.partial(attend_kernel, 1.0 / math.sqrt(HEAD_DIM)...  68.7 us
    dot_general x27, matrix products, product(): return jnp.dot(left_side, right_side, preferred_element_type=f32)  65.9 us
    pallas_call x1, Pallas kernels, gather_rows(): pl.pallas_call(functools.partial(gather_kernel, bits, orders), in_specs=[...  64.9 us
    pallas_call x1, Pallas kernels, attend_back(): pl.pallas_call(functools.partial(attend_back_kernel, 1.0 / math.sqrt(HEAD...  36.4 us
  transfers between devices with their start and end apart: 29, of which 8 were waited for; matrix products, arithmetic and copies ran while one was open for 35% of the time, Pallas kernels for 22%

profile of v9, /device:TPU:0, one launch (start us, length us, event | category | flops | bytes accessed | tf_op | source)
XLA Modules:
  0.0 823.7 jit_solution(9577926915378290633)
XLA Ops:
  13.3 64.9 %gather_rows.1 = (bf16[2,2,2,2,2,32,3328]{6,5,4,3,2,1,0:T(8,128)(2,1)}, bf16[2,1024,1024]{2,1,0:T(8,128)(2,1)}, bf16[2,1024,1024]{2,1,0:T(8,128)(2,1)}, bf16[1024,1024]{1,0:T(8,128)(2,1)}) custom-call(bf16[32,3328]{1,0:T(8,128)(2,1)} %fusion.149.own_ref, bf16[1,2,1024,1024]{3,2,1,0:T(8,128)(2,1)} %inner_ref.1, bf16[1,2,1024,1024]{3,2,1,0:T(8,128)(2,1)} %outer_ref.1), custom_call_target="tpu_custom_call" | custom-call | bytes 85196800 | tf_op jit(solution)/shard_map/gather_rows/pallas_call | solution.py:404
  81.8 5.2 fusion.10
  91.2 51.3 %collective-permute-done.k2.v2 = bf16[2,256,2048]{2,1,0:T(8,128)(2,1)} collective-permute-done((bf16[2,256,2048]{2,1,0:T(8,128)(2,1)S(1)}, bf16[2,256,2048]{2,1,0:T(8,128)(2,1)}, u32[]{:S(2)}, u32[]{:S(2)}) %collective-permute-start) | collective-permute-done | bytes 2097184 | tf_op jit(solution)/shard_map/ppermute | solution.py:65
  151.2 4.3 fusion.122
  158.4 68.7 %attend.1 = (bf16[2,256,1024]{2,1,0:T(8,128)(2,1)}, bf16[1024,1024]{1,0:T(8,128)(2,1)}) custom-call(bf16[2,256,1024]{2,1,0:T(8,128)(2,1)} %bitcast.404, bf16[2,256,2048]{2,1,0:T(8,128)(2,1)} %bitcast.333, bf16[2,256,2048]{2,1,0:T(8,128)(2,1)} %bitcast.334, bf16[2,256,2048]{2,1,0:T(8,128)(2,1)} %collective-permute-done.1.k1.v1, ...), custom_call_target="tpu_custom_call" | custom-call | flops 9663676416 | bytes 8388608 | tf_op jit(solution)/shard_map/attend/pallas_call | solution.py:191
  249.8 6.3 all-to-all-start
  260.9 20.7 %all-to-all-done = bf16[8,64,1024]{2,1,0:T(8,128)(2,1)S(1)} async-done(((bf16[8,64,1024]{2,1,0:T(8,128)(2,1)}), bf16[8,64,1024]{2,1,0:T(8,128)(2,1)S(1)}, u32[]{:S(2)}, u32[]{:S(2)}) %all-to-all-start) | async-done | bytes 1048608 | tf_op jit(solution)/shard_map/all_to_all | solution.py:617
  296.3 4.5 multiply_convert_fusion.18
  313.4 4.4 multiply_convert_fusion.14
  337.2 4.5 broadcast_in_dim.99
  359.5 4.0 multiply_convert_fusion.8
  377.0 4.3 fusion.26
  414.2 5.1 all-to-all-start.3
  419.3 4.4 convolution_convert_fusion.6
  438.9 6.7 all-to-all-done.3
  478.6 18.3 %collective-permute-done.9 = bf16[1024,1024]{1,0:T(8,128)(2,1)} collective-permute-done((bf16[1024,1024]{1,0:T(8,128)(2,1)}, bf16[1024,1024]{1,0:T(8,128)(2,1)}, u32[]{:S(2)}, u32[]{:S(2)}) %collective-permute-start.9) | collective-permute-done | bytes 2097184 | tf_op jit(solution)/shard_map/ppermute | solution.py:65
  521.2 4.1 fusion.125
  529.2 5.5 all-to-all-start.1
  534.8 5.2 add_convert_fusion.1
  540.5 36.4 %attend_back.1 = (bf16[2,256,1024]{2,1,0:T(8,128)(2,1)}, bf16[2,2,256,1024]{3,2,1,0:T(8,128)(2,1)}, bf16[2,2,256,1024]{3,2,1,0:T(8,128)(2,1)}, bf16[2,2,256,1024]{3,2,1,0:T(8,128)(2,1)}) custom-call(bf16[2,256,1024]{2,1,0:T(8,128)(2,1)} %bitcast.405, bf16[2,256,2048]{2,1,0:T(8,128)(2,1)} %bitcast.335, bf16[2,256,2048]{2,1,0:T(8,128)(2,1)} %bitcast.336, ...), custom_call_target="tpu_custom_call" | custom-call | flops 24159191040 | bytes 16777216 | tf_op jit(solution)/shard_map/attend_back/pallas_call | solution.py:216
  576.9 10.4 %collective-permute-done.11 = bf16[1024,1024]{1,0:T(8,128)(2,1)} collective-permute-done((bf16[1024,1024]{1,0:T(8,128)(2,1)}, bf16[1024,1024]{1,0:T(8,128)(2,1)}, u32[]{:S(2)}, u32[]{:S(2)}) %collective-permute-start.11) | collective-permute-done | bytes 2097184 | tf_op jit(solution)/shard_map/ppermute | solution.py:65
  591.6 4.0 convolution_convert_fusion.2
  609.3 4.7 fusion.5
  621.4 4.7 add_convert_fusion
  633.6 4.3 pad_maximum_fusion
  637.9 43.2 %collective-permute-done.13 = bf16[2,2,256,1024]{3,2,1,0:T(8,128)(2,1)S(1)} collective-permute-done((bf16[2,2,256,1024]{3,2,1,0:T(8,128)(2,1)S(1)}, bf16[2,2,256,1024]{3,2,1,0:T(8,128)(2,1)S(1)}, u32[]{:S(2)}, u32[]{:S(2)}) %collective-permute-start.13) | collective-permute-done | bytes 2097184 | tf_op jit(solution)/shard_map/ppermute | solution.py:65
  700.8 6.0 all-to-all-start.4
  706.8 4.3 add_add_fusion.4
  711.1 77.3 %scatter_rows.1 = f32[32,3072]{1,0:T(8,128)} custom-call(bf16[2,2,2,2,2,32,3072]{6,5,4,3,2,1,0:T(8,128)(2,1)} %bitcast.321), custom_call_target="tpu_custom_call" | custom-call | bytes 157286400 | tf_op jit(solution)/shard_map/scatter_rows/pallas_call | solution.py:494
  789.0 5.6 add_bitcast_fusion
  797.5 4.2 maximum_bitcast_fusion
  806.6 4.5 reshape.410
  (480 shorter events, 302.7 us)
Async XLA Ops:
  7.2 220.3 %all-gather.2.cloned.1.call-start = ((), (), s32[]{:S(2)}) async-start(), calls=%async_computation.7 | async-start | bytes 19464192 | tf_op jit(solution)/shard_map/all_gather | solution.py:559
  80.8 151.1 %copy-start.55 = (f32[1,1024]{1,0:T(1,128)}, f32[1,1024]{1,0:T(1,128)S(1)}, u32[]{:S(2)}) copy-start(f32[1,1024]{1,0:T(1,128)S(1)} %get-tuple-element.135) | copy-start | bytes 12292
  87.1 55.4 %collective-permute-start = (bf16[2,256,2048]{2,1,0:T(8,128)(2,1)S(1)}, bf16[2,256,2048]{2,1,0:T(8,128)(2,1)}, u32[]{:S(2)}, u32[]{:S(2)}) collective-permute-start(bf16[2,256,2048]{2,1,0:T(8,128)(2,1)S(1)} %bitcast.331), channel_id=1, source_target_pairs={{0,16},{8,24},{1,17},{9,25},{2,18},{10,26},{3,19},{11,27},{4,20},{... | collective-permute-start | bytes 6291464 | tf_op jit(solution)/shard_map/ppermute | solution.py:65
  91.2 58.3 %copy-start.63 = (s32[2,1024]{1,0:T(2,128)S(1)}, s32[2,1024]{1,0:T(2,128)}, u32[]{:S(2)}) copy-start(s32[2,1024]{1,0:T(2,128)} %param.15) | copy-start | bytes 24580
  144.0 14.4 %collective-permute-start.1 = (bf16[2,256,2048]{2,1,0:T(8,128)(2,1)}, bf16[2,256,2048]{2,1,0:T(8,128)(2,1)}, u32[]{:S(2)}, u32[]{:S(2)}) collective-permute-start(bf16[2,256,2048]{2,1,0:T(8,128)(2,1)} %broadcast_select_fusion), channel_id=1, source_target_pairs={{0,8},{16,24},{24,16},{1,9},{17,25},{25,17},{2,10},{18,26},{26,18}... | collective-permute-start | bytes 6291464 | tf_op jit(solution)/shard_map/ppermute | solution.py:65
  227.1 58.1 %collective-permute-start.2 = (bf16[1024,1024]{1,0:T(8,128)(2,1)}, bf16[1024,1024]{1,0:T(8,128)(2,1)}, u32[]{:S(2)}, u32[]{:S(2)}) collective-permute-start(bf16[1024,1024]{1,0:T(8,128)(2,1)} %get-tuple-element.63), channel_id=1, source_target_pairs={{0,16},{16,0},{8,24},{24,8},{1,17},{17,1},{9,25},{25,9},{2,18},{18... | collective-permute-start | bytes 6291464 | tf_op jit(solution)/shard_map/ppermute | solution.py:65
  249.8 31.8 %all-to-all-start = ((bf16[8,64,1024]{2,1,0:T(8,128)(2,1)}), bf16[8,64,1024]{2,1,0:T(8,128)(2,1)S(1)}, u32[]{:S(2)}, u32[]{:S(2)}) async-start(bf16[8,64,1024]{2,1,0:T(8,128)(2,1)} %bitcast.18), calls=%async_computation | async-start | bytes 2097152 | tf_op jit(solution)/shard_map/all_to_all | solution.py:617
  258.9 37.4 %collective-permute-start.3 = (bf16[1024,1024]{1,0:T(8,128)(2,1)}, bf16[1024,1024]{1,0:T(8,128)(2,1)}, u32[]{:S(2)}, u32[]{:S(2)}) collective-permute-start(bf16[1024,1024]{1,0:T(8,128)(2,1)} %get-tuple-element.69), channel_id=1, source_target_pairs={{0,8},{8,0},{16,24},{24,16},{1,9},{9,1},{17,25},{25,17},{2,10},{10... | collective-permute-start | bytes 6291464 | tf_op jit(solution)/shard_map/ppermute | solution.py:65
  259.0 46.1 %collective-permute-start.4 = (bf16[1024,1024]{1,0:T(8,128)(2,1)}, bf16[1024,1024]{1,0:T(8,128)(2,1)}, u32[]{:S(2)}, u32[]{:S(2)}) collective-permute-start(bf16[1024,1024]{1,0:T(8,128)(2,1)} %get-tuple-element.70), channel_id=1, source_target_pairs={{0,8},{8,0},{16,24},{24,16},{1,9},{9,1},{17,25},{25,17},{2,10},{10... | collective-permute-start | bytes 6291464 | tf_op jit(solution)/shard_map/ppermute | solution.py:65
  259.5 63.2 %collective-permute-start.5 = (bf16[1024,1024]{1,0:T(8,128)(2,1)}, bf16[1024,1024]{1,0:T(8,128)(2,1)}, u32[]{:S(2)}, u32[]{:S(2)}) collective-permute-start(bf16[1024,1024]{1,0:T(8,128)(2,1)} %get-tuple-element.72), channel_id=1, source_target_pairs={{0,16},{16,0},{8,24},{24,8},{1,17},{17,1},{9,25},{25,9},{2,18},{18... | collective-permute-start | bytes 6291464 | tf_op jit(solution)/shard_map/ppermute | solution.py:65
  281.6 29.4 %all-to-all-start.2 = ((bf16[8,64,1024]{2,1,0:T(8,128)(2,1)}), bf16[8,64,1024]{2,1,0:T(8,128)(2,1)S(1)}, u32[]{:S(2)}, u32[]{:S(2)}) async-start(bf16[8,64,1024]{2,1,0:T(8,128)(2,1)} %bitcast.325), calls=%async_computation.2 | async-start | bytes 2097152 | tf_op jit(solution)/shard_map/all_to_all | solution.py:650
  285.2 509.5 %reduce-scatter.5.cloned.1.call-start = ((), (), s32[]{:S(2)}) async-start(), calls=%async_computation.9 | async-start | bytes 10485760 | tf_op jit(solution)/shard_map/reduce_scatter | solution.py:678
  336.6 22.9 %collective-permute-start.7 = (bf16[1024,1024]{1,0:T(8,128)(2,1)}, bf16[1024,1024]{1,0:T(8,128)(2,1)}, u32[]{:S(2)}, u32[]{:S(2)}) collective-permute-start(bf16[1024,1024]{1,0:T(8,128)(2,1)} %collective-permute-done.5), channel_id=1, source_target_pairs={{0,8},{8,0},{16,24},{24,16},{1,9},{9,1},{17,25},{25,17},{2,10},{10... | collective-permute-start | bytes 6291464 | tf_op jit(solution)/shard_map/ppermute | solution.py:65
  336.7 21.3 %collective-permute-start.6 = (bf16[1024,1024]{1,0:T(8,128)(2,1)}, bf16[1024,1024]{1,0:T(8,128)(2,1)S(1)}, u32[]{:S(2)}, u32[]{:S(2)}) collective-permute-start(bf16[1024,1024]{1,0:T(8,128)(2,1)} %collective-permute-done.2), channel_id=1, source_target_pairs={{0,8},{8,0},{16,24},{24,16},{1,9},{9,1},{17,25},{25,17},{2,10},{10... | collective-permute-start | bytes 6291464 | tf_op jit(solution)/shard_map/ppermute | solution.py:65
  383.3 28.3 %collective-permute-start.8 = (bf16[1024,1024]{1,0:T(8,128)(2,1)}, bf16[1024,1024]{1,0:T(8,128)(2,1)S(1)}, u32[]{:S(2)}, u32[]{:S(2)}) collective-permute-start(bf16[1024,1024]{1,0:T(8,128)(2,1)} %convolution_convert_fusion.9), channel_id=1, source_target_pairs={{0,8},{8,0},{16,24},{24,16},{1,9},{9,1},{17,25},{25,17},{2,10},{10... | collective-permute-start | bytes 6291464 | tf_op jit(solution)/shard_map/ppermute | solution.py:65
  414.2 31.3 %all-to-all-start.3 = ((bf16[8,64,1024]{2,1,0:T(8,128)(2,1)}), bf16[8,64,1024]{2,1,0:T(8,128)(2,1)S(1)}, u32[]{:S(2)}, u32[]{:S(2)}) async-start(bf16[8,64,1024]{2,1,0:T(8,128)(2,1)} %bitcast.329), calls=%async_computation.3 | async-start | bytes 2097152 | tf_op jit(solution)/shard_map/all_to_all | solution.py:684
  419.3 382.4 %reduce-scatter.3.cloned.1.call-start = ((), (), s32[]{:S(2)}) async-start(), calls=%async_computation.8 | async-start | bytes 19464192 | tf_op jit(solution)/shard_map/reduce_scatter | solution.py:720
  437.3 59.6 %collective-permute-start.9 = (bf16[1024,1024]{1,0:T(8,128)(2,1)}, bf16[1024,1024]{1,0:T(8,128)(2,1)}, u32[]{:S(2)}, u32[]{:S(2)}) collective-permute-start(bf16[1024,1024]{1,0:T(8,128)(2,1)} %add_convert_fusion.2), channel_id=1, source_target_pairs={{0,16},{16,0},{8,24},{24,8},{1,17},{17,1},{9,25},{25,9},{2,18},{18... | collective-permute-start | bytes 6291464 | tf_op jit(solution)/shard_map/ppermute | solution.py:65
  525.4 9.4 %collective-permute-start.10 = (bf16[1024,1024]{1,0:T(8,128)(2,1)}, bf16[1024,1024]{1,0:T(8,128)(2,1)}, u32[]{:S(2)}, u32[]{:S(2)}) collective-permute-start(bf16[1024,1024]{1,0:T(8,128)(2,1)} %convolution_convert_fusion.8), channel_id=1, source_target_pairs={{0,8},{8,0},{16,24},{24,16},{1,9},{9,1},{17,25},{25,17},{2,10},{10... | collective-permute-start | bytes 6291464 | tf_op jit(solution)/shard_map/ppermute | solution.py:65
  529.2 73.4 %all-to-all-start.1 = ((bf16[8,64,1024]{2,1,0:T(8,128)(2,1)}), bf16[8,64,1024]{2,1,0:T(8,128)(2,1)S(1)}, u32[]{:S(2)}, u32[]{:S(2)}) async-start(bf16[8,64,1024]{2,1,0:T(8,128)(2,1)} %bitcast.330), calls=%async_computation.1 | async-start | bytes 2097152 | tf_op jit(solution)/shard_map/all_to_all | solution.py:643
  539.9 47.3 %collective-permute-start.11 = (bf16[1024,1024]{1,0:T(8,128)(2,1)}, bf16[1024,1024]{1,0:T(8,128)(2,1)}, u32[]{:S(2)}, u32[]{:S(2)}) collective-permute-start(bf16[1024,1024]{1,0:T(8,128)(2,1)} %add_convert_fusion.1), channel_id=1, source_target_pairs={{0,16},{16,0},{8,24},{24,8},{1,17},{17,1},{9,25},{25,9},{2,18},{18... | collective-permute-start | bytes 6291464 | tf_op jit(solution)/shard_map/ppermute | solution.py:65
  587.2 22.1 %collective-permute-start.12 = (bf16[2,2,256,1024]{3,2,1,0:T(8,128)(2,1)}, bf16[2,2,256,1024]{3,2,1,0:T(8,128)(2,1)}, u32[]{:S(2)}, u32[]{:S(2)}) collective-permute-start(bf16[2,2,256,1024]{3,2,1,0:T(8,128)(2,1)} %get-tuple-element.90), channel_id=1, source_target_pairs={{8,0},{24,16},{16,24},{9,1},{25,17},{17,25},{10,2},{26,18},{18,26}... | collective-permute-start | bytes 6291464 | tf_op jit(solution)/shard_map/ppermute | solution.py:65
  589.1 6.5 collective-permute-start.17
  595.6 3.8 collective-permute-start.18
  595.7 25.7 %collective-permute-start.14 = (bf16[1024,1024]{1,0:T(8,128)(2,1)}, bf16[1024,1024]{1,0:T(8,128)(2,1)}, u32[]{:S(2)}, u32[]{:S(2)}) collective-permute-start(bf16[1024,1024]{1,0:T(8,128)(2,1)} %convolution_convert_fusion.7), channel_id=1, source_target_pairs={{0,8},{8,0},{16,24},{24,16},{1,9},{9,1},{17,25},{25,17},{2,10},{10... | collective-permute-start | bytes 6291464 | tf_op jit(solution)/shard_map/ppermute | solution.py:65
  599.5 26.6 %collective-permute-start.16 = (bf16[1024,1024]{1,0:T(8,128)(2,1)}, bf16[1024,1024]{1,0:T(8,128)(2,1)}, u32[]{:S(2)}, u32[]{:S(2)}) collective-permute-start(bf16[1024,1024]{1,0:T(8,128)(2,1)} %convolution_convert_fusion.6), channel_id=1, source_target_pairs={{0,8},{8,0},{16,24},{24,16},{1,9},{9,1},{17,25},{25,17},{2,10},{10... | collective-permute-start | bytes 6291464 | tf_op jit(solution)/shard_map/ppermute | solution.py:65
  605.4 24.5 %collective-permute-start.15 = (bf16[1024,1024]{1,0:T(8,128)(2,1)}, bf16[1024,1024]{1,0:T(8,128)(2,1)}, u32[]{:S(2)}, u32[]{:S(2)}) collective-permute-start(bf16[1024,1024]{1,0:T(8,128)(2,1)} %convolution_convert_fusion.5), channel_id=1, source_target_pairs={{0,8},{8,0},{16,24},{24,16},{1,9},{9,1},{17,25},{25,17},{2,10},{10... | collective-permute-start | bytes 6291464 | tf_op jit(solution)/shard_map/ppermute | solution.py:65
  609.2 179.8 %collective-permute-start.19 = (bf16[1024,1024]{1,0:T(8,128)(2,1)}, bf16[1024,1024]{1,0:T(8,128)(2,1)}, u32[]{:S(2)}, u32[]{:S(2)}) collective-permute-start(bf16[1024,1024]{1,0:T(8,128)(2,1)} %convolution_convert_fusion.4), channel_id=1, source_target_pairs={{0,8},{8,0},{16,24},{24,16},{1,9},{9,1},{17,25},{25,17},{2,10},{10... | collective-permute-start | bytes 6291464 | tf_op jit(solution)/shard_map/ppermute | solution.py:65
  614.0 67.1 %collective-permute-start.13 = (bf16[2,2,256,1024]{3,2,1,0:T(8,128)(2,1)S(1)}, bf16[2,2,256,1024]{3,2,1,0:T(8,128)(2,1)S(1)}, u32[]{:S(2)}, u32[]{:S(2)}) collective-permute-start(bf16[2,2,256,1024]{3,2,1,0:T(8,128)(2,1)S(1)} %fusion.5), channel_id=1, source_target_pairs={{16,0},{24,8},{17,1},{25,9},{18,2},{26,10},{19,3},{27,11},{20,4},{... | collective-permute-start | bytes 6291464 | tf_op jit(solution)/shard_map/ppermute | solution.py:65
  694.2 94.8 %collective-permute-start.20 = (bf16[1024,1024]{1,0:T(8,128)(2,1)}, bf16[1024,1024]{1,0:T(8,128)(2,1)}, u32[]{:S(2)}, u32[]{:S(2)}) collective-permute-start(bf16[1024,1024]{1,0:T(8,128)(2,1)} %add_convert_fusion), channel_id=1, source_target_pairs={{0,16},{16,0},{8,24},{24,8},{1,17},{17,1},{9,25},{25,9},{2,18},{18... | collective-permute-start | bytes 6291464 | tf_op jit(solution)/shard_map/ppermute | solution.py:65
  700.8 87.6 %all-to-all-start.4 = ((f32[32,2,32]{2,1,0:T(2,128)}), f32[32,2,32]{2,1,0:T(2,128)S(1)}, u32[]{:S(2)}, u32[]{:S(2)}) async-start(f32[32,2,32]{2,1,0:T(2,128)} %maximum_bitcast_fusion.1), calls=%async_computation.4 | async-start | bytes 65536 | tf_op jit(solution)/shard_map/all_to_all | solution.py:754
  711.1 77.9 %copy-start.25 = (bf16[1024,1024]{1,0:T(8,128)(2,1)S(1)}, bf16[1024,1024]{1,0:T(8,128)(2,1)}, u32[]{:S(2)}) copy-start(bf16[1024,1024]{1,0:T(8,128)(2,1)} %convolution_convert_fusion.2) | copy-start | bytes 6291460
  (119 other events, 620.7 us)
Sparse Core Ops, SparseCore 0:
  78.4 139.1 all-gather.1
  381.5 83.4 reduce-scatter.4
  525.5 240.2 reduce-scatter.2

commit v10 on v9

--- a/solution.py
+++ b/solution.py
@@ -704,19 +704,20 @@
     grad_pres, grad_normed_ffn = ffn_backward(dense_kept, up_parts, down_parts, grad_down_in)
     grad_hidden_norm, grad_gain_ffn = norm_back(hidden, gain_ffn, grad_normed_ffn)
     grad_hidden = grad_dense + grad_hidden_norm
-    grad_hidden, outer1.got_chip = together(grad_hidden, outer1.got_chip)
+    grad_down_late, outer1.got_chip, held = together(
+        grad_down_in, outer1.got_chip, outer0.chip_sum()
+    )
+    outer0.send_chip(held)
     grad_proj = grad_hidden.astype(bf16)
     rest_grad = jnp.concatenate(
         [weight_grad(attended, grad_proj)]
         + [weight_grad(normed_ffn, grad_pre) for grad_pre in grad_pres]
-        + [weight_grad(act, grad_down_in) for act, _ in dense_kept],
+        + [weight_grad(act, grad_down_late) for act, _ in dense_kept],
         axis=1,
     )
     rest_grad = row_major(rest_grad)
     grad_attended = product_bt(grad_proj, proj_full).astype(bf16)
     grad_attended, rest_grad = together(grad_attended, rest_grad)
-    grad_attended, held = together(grad_attended, outer0.chip_sum())
-    outer0.send_chip(held)
     rest_sum = lax.psum_scatter(rest_grad, every, scatter_dimension=0, tiled=True).astype(f32)
     grad_query, grad_kv0, grad_kv1, grad_kv2 = attend_back(
         query, kv_blocks, bias, grad_attended.reshape(query.shape)

time: 832 us -> 813 us (0.977)
  waiting for transfers between devices: 152 us -> 141 us
    ppermute x21, waiting for transfers between devices: 124 us -> 112 us  [seq_send(): return lax.ppermute(values, 'seq', pairs)]
    unnamed x251 -> x277, local copies, waits for them, and re-layouts: 20.6 us -> 25 us
  transfers between devices with their start and end apart: 29 -> 29, of which waited for: 8 -> 8; matrix products, arithmetic and copies ran while one was open for 35% -> 35% of each run, Pallas kernels for 22% -> 23%
where the time goes in v10:
time: 813 us; the launch traced here: 805 us
  Pallas kernels  246 us (30%)
  matrix products  220 us (27%)
  waiting for transfers between devices  141 us (17%)
  other arithmetic  71.5 us (9%)
  local copies, waits for them, and re-layouts  65.3 us (8%)
  starting transfers between devices  41.5 us (5%)
  between operations  19.5 us (2%)
    ppermute x21, waiting for transfers between devices, seq_send(): return lax.ppermute(values, 'seq', pairs)  112 us
    dot_general x28, matrix products, product_at(): lax.dot_general(left_side, right_side, (((0,), (0,)), ((), ())), preferre...  80.2 us
    pallas_call x1, Pallas kernels, scatter_rows(): pl.pallas_call(functools.partial(scatter_kernel, bits, orders), in_specs=...  76.6 us
    dot_general x28, matrix products, product_bt(): lax.dot_general(left_side, right_side, (((1,), (1,)), ((), ())), preferre...  72.8 us
    pallas_call x1, Pallas kernels, attend(): pl.pallas_call(functools.partial(attend_kernel, 1.0 / math.sqrt(HEAD_DIM)...  68.5 us
    dot_general x27, matrix products, product(): return jnp.dot(left_side, right_side, preferred_element_type=f32)  65.9 us
    pallas_call x1, Pallas kernels, gather_rows(): pl.pallas_call(functools.partial(gather_kernel, bits, orders), in_specs=[...  64.9 us
    pallas_call x1, Pallas kernels, attend_back(): pl.pallas_call(functools.partial(attend_back_kernel, 1.0 / math.sqrt(HEAD...  36.4 us
  transfers between devices with their start and end apart: 29, of which 8 were waited for; matrix products, arithmetic and copies ran while one was open for 35% of the time, Pallas kernels for 23%

profile of v10, /device:TPU:0, one launch (start us, length us, event | category | flops | bytes accessed | tf_op | source)
XLA Modules:
  0.0 804.5 jit_solution(2568294052822921357)
XLA Ops:
  13.3 64.9 %gather_rows.1 = (bf16[2,2,2,2,2,32,3328]{6,5,4,3,2,1,0:T(8,128)(2,1)}, bf16[2,1024,1024]{2,1,0:T(8,128)(2,1)}, bf16[2,1024,1024]{2,1,0:T(8,128)(2,1)}, bf16[1024,1024]{1,0:T(8,128)(2,1)}) custom-call(bf16[32,3328]{1,0:T(8,128)(2,1)} %fusion.149.own_ref, bf16[1,2,1024,1024]{3,2,1,0:T(8,128)(2,1)} %inner_ref.1, bf16[1,2,1024,1024]{3,2,1,0:T(8,128)(2,1)} %outer_ref.1), custom_call_target="tpu_custom_call" | custom-call | bytes 85196800 | tf_op jit(solution)/shard_map/gather_rows/pallas_call | solution.py:404
  81.8 5.2 fusion.10
  91.2 51.3 %collective-permute-done.k2.v2 = bf16[2,256,2048]{2,1,0:T(8,128)(2,1)} collective-permute-done((bf16[2,256,2048]{2,1,0:T(8,128)(2,1)S(1)}, bf16[2,256,2048]{2,1,0:T(8,128)(2,1)}, u32[]{:S(2)}, u32[]{:S(2)}) %collective-permute-start) | collective-permute-done | bytes 2097184 | tf_op jit(solution)/shard_map/ppermute | solution.py:65
  151.2 4.3 fusion.122
  158.4 68.5 %attend.1 = (bf16[2,256,1024]{2,1,0:T(8,128)(2,1)}, bf16[1024,1024]{1,0:T(8,128)(2,1)}) custom-call(bf16[2,256,1024]{2,1,0:T(8,128)(2,1)} %bitcast.406, bf16[2,256,2048]{2,1,0:T(8,128)(2,1)} %bitcast.333, bf16[2,256,2048]{2,1,0:T(8,128)(2,1)} %bitcast.334, bf16[2,256,2048]{2,1,0:T(8,128)(2,1)} %collective-permute-done.1.k1.v1, ...), custom_call_target="tpu_custom_call" | custom-call | flops 9663676416 | bytes 8388608 | tf_op jit(solution)/shard_map/attend/pallas_call | solution.py:191
  232.0 4.0 fusion.74
  249.5 6.3 all-to-all-start
  260.8 20.6 %all-to-all-done = bf16[8,64,1024]{2,1,0:T(8,128)(2,1)S(1)} async-done(((bf16[8,64,1024]{2,1,0:T(8,128)(2,1)}), bf16[8,64,1024]{2,1,0:T(8,128)(2,1)S(1)}, u32[]{:S(2)}, u32[]{:S(2)}) %all-to-all-start) | async-done | bytes 1048608 | tf_op jit(solution)/shard_map/all_to_all | solution.py:617
  296.0 4.5 multiply_convert_fusion.18
  313.1 4.4 multiply_convert_fusion.14
  337.0 4.5 broadcast_in_dim.99
  382.0 4.1 multiply_convert_fusion.5
  395.9 3.9 multiply_convert_fusion.4
  411.9 4.2 add_convert_fusion.2
  416.2 4.2 all-to-all-start.3
  420.6 4.3 convolution_convert_fusion.6
  440.1 6.8 all-to-all-done.3
  492.2 4.2 add_convert_fusion.1
  512.5 5.5 all-to-all-start.1
  518.6 36.4 %attend_back.1 = (bf16[2,256,1024]{2,1,0:T(8,128)(2,1)}, bf16[2,2,256,1024]{3,2,1,0:T(8,128)(2,1)}, bf16[2,2,256,1024]{3,2,1,0:T(8,128)(2,1)}, bf16[2,2,256,1024]{3,2,1,0:T(8,128)(2,1)}) custom-call(bf16[2,256,1024]{2,1,0:T(8,128)(2,1)} %bitcast.407, bf16[2,256,2048]{2,1,0:T(8,128)(2,1)} %bitcast.335, bf16[2,256,2048]{2,1,0:T(8,128)(2,1)} %bitcast.336, ...), custom_call_target="tpu_custom_call" | custom-call | flops 24159191040 | bytes 16777216 | tf_op jit(solution)/shard_map/attend_back/pallas_call | solution.py:216
  555.0 10.5 %collective-permute-done.11 = bf16[1024,1024]{1,0:T(8,128)(2,1)} collective-permute-done((bf16[1024,1024]{1,0:T(8,128)(2,1)}, bf16[1024,1024]{1,0:T(8,128)(2,1)}, u32[]{:S(2)}, u32[]{:S(2)}) %collective-permute-start.11) | collective-permute-done | bytes 2097184 | tf_op jit(solution)/shard_map/ppermute | solution.py:65
  569.8 4.0 convolution_convert_fusion.2
  588.0 4.5 fusion.5
  600.1 4.6 add_convert_fusion
  612.1 4.3 pad_maximum_fusion
  616.3 48.0 %collective-permute-done.13 = bf16[2,2,256,1024]{3,2,1,0:T(8,128)(2,1)S(1)} collective-permute-done((bf16[2,2,256,1024]{3,2,1,0:T(8,128)(2,1)S(1)}, bf16[2,2,256,1024]{3,2,1,0:T(8,128)(2,1)S(1)}, u32[]{:S(2)}, u32[]{:S(2)}) %collective-permute-start.13) | collective-permute-done | bytes 2097184 | tf_op jit(solution)/shard_map/ppermute | solution.py:65
  684.2 4.1 all-to-all-start.4
  688.4 4.3 add_add_fusion.4
  692.6 76.6 %scatter_rows.1 = f32[32,3072]{1,0:T(8,128)} custom-call(bf16[2,2,2,2,2,32,3072]{6,5,4,3,2,1,0:T(8,128)(2,1)} %bitcast.321), custom_call_target="tpu_custom_call" | custom-call | bytes 157286400 | tf_op jit(solution)/shard_map/scatter_rows/pallas_call | solution.py:494
  769.9 5.6 add_bitcast_fusion
  778.3 4.2 maximum_bitcast_fusion
  787.4 4.5 reshape.410
  (507 shorter events, 297.9 us)
Async XLA Ops:
  7.2 220.1 %all-gather.2.cloned.1.call-start = ((), (), s32[]{:S(2)}) async-start(), calls=%async_computation.7 | async-start | bytes 19464192 | tf_op jit(solution)/shard_map/all_gather | solution.py:559
  80.9 150.8 %copy-start.56 = (f32[1,1024]{1,0:T(1,128)}, f32[1,1024]{1,0:T(1,128)S(1)}, u32[]{:S(2)}) copy-start(f32[1,1024]{1,0:T(1,128)S(1)} %get-tuple-element.133) | copy-start | bytes 12292
  87.1 55.4 %collective-permute-start = (bf16[2,256,2048]{2,1,0:T(8,128)(2,1)S(1)}, bf16[2,256,2048]{2,1,0:T(8,128)(2,1)}, u32[]{:S(2)}, u32[]{:S(2)}) collective-permute-start(bf16[2,256,2048]{2,1,0:T(8,128)(2,1)S(1)} %bitcast.331), channel_id=1, source_target_pairs={{0,16},{8,24},{1,17},{9,25},{2,18},{10,26},{3,19},{11,27},{4,20},{... | collective-permute-start | bytes 6291464 | tf_op jit(solution)/shard_map/ppermute | solution.py:65
  91.2 58.3 %copy-start.64 = (s32[2,1024]{1,0:T(2,128)S(1)}, s32[2,1024]{1,0:T(2,128)}, u32[]{:S(2)}) copy-start(s32[2,1024]{1,0:T(2,128)} %param.15) | copy-start | bytes 24580
  144.0 14.4 %collective-permute-start.1 = (bf16[2,256,2048]{2,1,0:T(8,128)(2,1)}, bf16[2,256,2048]{2,1,0:T(8,128)(2,1)}, u32[]{:S(2)}, u32[]{:S(2)}) collective-permute-start(bf16[2,256,2048]{2,1,0:T(8,128)(2,1)} %broadcast_select_fusion), channel_id=1, source_target_pairs={{0,8},{16,24},{24,16},{1,9},{17,25},{25,17},{2,10},{18,26},{26,18}... | collective-permute-start | bytes 6291464 | tf_op jit(solution)/shard_map/ppermute | solution.py:65
  226.8 58.1 %collective-permute-start.2 = (bf16[1024,1024]{1,0:T(8,128)(2,1)}, bf16[1024,1024]{1,0:T(8,128)(2,1)}, u32[]{:S(2)}, u32[]{:S(2)}) collective-permute-start(bf16[1024,1024]{1,0:T(8,128)(2,1)} %get-tuple-element.62), channel_id=1, source_target_pairs={{0,16},{16,0},{8,24},{24,8},{1,17},{17,1},{9,25},{25,9},{2,18},{18... | collective-permute-start | bytes 6291464 | tf_op jit(solution)/shard_map/ppermute | solution.py:65
  249.5 31.8 %all-to-all-start = ((bf16[8,64,1024]{2,1,0:T(8,128)(2,1)}), bf16[8,64,1024]{2,1,0:T(8,128)(2,1)S(1)}, u32[]{:S(2)}, u32[]{:S(2)}) async-start(bf16[8,64,1024]{2,1,0:T(8,128)(2,1)} %bitcast.18), calls=%async_computation | async-start | bytes 2097152 | tf_op jit(solution)/shard_map/all_to_all | solution.py:617
  258.7 37.2 %collective-permute-start.3 = (bf16[1024,1024]{1,0:T(8,128)(2,1)}, bf16[1024,1024]{1,0:T(8,128)(2,1)}, u32[]{:S(2)}, u32[]{:S(2)}) collective-permute-start(bf16[1024,1024]{1,0:T(8,128)(2,1)} %get-tuple-element.68), channel_id=1, source_target_pairs={{0,8},{8,0},{16,24},{24,16},{1,9},{9,1},{17,25},{25,17},{2,10},{10... | collective-permute-start | bytes 6291464 | tf_op jit(solution)/shard_map/ppermute | solution.py:65
  258.8 46.0 %collective-permute-start.4 = (bf16[1024,1024]{1,0:T(8,128)(2,1)}, bf16[1024,1024]{1,0:T(8,128)(2,1)}, u32[]{:S(2)}, u32[]{:S(2)}) collective-permute-start(bf16[1024,1024]{1,0:T(8,128)(2,1)} %get-tuple-element.69), channel_id=1, source_target_pairs={{0,8},{8,0},{16,24},{24,16},{1,9},{9,1},{17,25},{25,17},{2,10},{10... | collective-permute-start | bytes 6291464 | tf_op jit(solution)/shard_map/ppermute | solution.py:65
  259.3 63.1 %collective-permute-start.5 = (bf16[1024,1024]{1,0:T(8,128)(2,1)}, bf16[1024,1024]{1,0:T(8,128)(2,1)}, u32[]{:S(2)}, u32[]{:S(2)}) collective-permute-start(bf16[1024,1024]{1,0:T(8,128)(2,1)} %get-tuple-element.71), channel_id=1, source_target_pairs={{0,16},{16,0},{8,24},{24,8},{1,17},{17,1},{9,25},{25,9},{2,18},{18... | collective-permute-start | bytes 6291464 | tf_op jit(solution)/shard_map/ppermute | solution.py:65
  281.4 29.4 %all-to-all-start.2 = ((bf16[8,64,1024]{2,1,0:T(8,128)(2,1)}), bf16[8,64,1024]{2,1,0:T(8,128)(2,1)S(1)}, u32[]{:S(2)}, u32[]{:S(2)}) async-start(bf16[8,64,1024]{2,1,0:T(8,128)(2,1)} %bitcast.325), calls=%async_computation.2 | async-start | bytes 2097152 | tf_op jit(solution)/shard_map/all_to_all | solution.py:650
  284.9 490.5 %reduce-scatter.5.cloned.1.call-start = ((), (), s32[]{:S(2)}) async-start(), calls=%async_computation.9 | async-start | bytes 10485760 | tf_op jit(solution)/shard_map/reduce_scatter | solution.py:678
  336.4 22.9 %collective-permute-start.7 = (bf16[1024,1024]{1,0:T(8,128)(2,1)}, bf16[1024,1024]{1,0:T(8,128)(2,1)}, u32[]{:S(2)}, u32[]{:S(2)}) collective-permute-start(bf16[1024,1024]{1,0:T(8,128)(2,1)} %collective-permute-done.5), channel_id=1, source_target_pairs={{0,8},{8,0},{16,24},{24,16},{1,9},{9,1},{17,25},{25,17},{2,10},{10... | collective-permute-start | bytes 6291464 | tf_op jit(solution)/shard_map/ppermute | solution.py:65
  336.5 21.3 %collective-permute-start.6 = (bf16[1024,1024]{1,0:T(8,128)(2,1)}, bf16[1024,1024]{1,0:T(8,128)(2,1)S(1)}, u32[]{:S(2)}, u32[]{:S(2)}) collective-permute-start(bf16[1024,1024]{1,0:T(8,128)(2,1)} %collective-permute-done.2), channel_id=1, source_target_pairs={{0,8},{8,0},{16,24},{24,16},{1,9},{9,1},{17,25},{25,17},{2,10},{10... | collective-permute-start | bytes 6291464 | tf_op jit(solution)/shard_map/ppermute | solution.py:65
  381.8 30.1 %collective-permute-start.8 = (bf16[1024,1024]{1,0:T(8,128)(2,1)}, bf16[1024,1024]{1,0:T(8,128)(2,1)}, u32[]{:S(2)}, u32[]{:S(2)}) collective-permute-start(bf16[1024,1024]{1,0:T(8,128)(2,1)} %convolution_convert_fusion.9), channel_id=1, source_target_pairs={{0,8},{8,0},{16,24},{24,16},{1,9},{9,1},{17,25},{25,17},{2,10},{10... | collective-permute-start | bytes 6291464 | tf_op jit(solution)/shard_map/ppermute | solution.py:65
  416.2 30.8 %all-to-all-start.3 = ((bf16[8,64,1024]{2,1,0:T(8,128)(2,1)}), bf16[8,64,1024]{2,1,0:T(8,128)(2,1)S(1)}, u32[]{:S(2)}, u32[]{:S(2)}) async-start(bf16[8,64,1024]{2,1,0:T(8,128)(2,1)} %bitcast.329), calls=%async_computation.3 | async-start | bytes 2097152 | tf_op jit(solution)/shard_map/all_to_all | solution.py:684
  420.4 362.2 %reduce-scatter.3.cloned.1.call-start = ((), (), s32[]{:S(2)}) async-start(), calls=%async_computation.8 | async-start | bytes 19464192 | tf_op jit(solution)/shard_map/reduce_scatter | solution.py:721
  438.4 59.0 %collective-permute-start.9 = (bf16[1024,1024]{1,0:T(8,128)(2,1)}, bf16[1024,1024]{1,0:T(8,128)(2,1)}, u32[]{:S(2)}, u32[]{:S(2)}) collective-permute-start(bf16[1024,1024]{1,0:T(8,128)(2,1)} %add_convert_fusion.2), channel_id=1, source_target_pairs={{0,16},{16,0},{8,24},{24,8},{1,17},{17,1},{9,25},{25,9},{2,18},{18... | collective-permute-start | bytes 6291464 | tf_op jit(solution)/shard_map/ppermute | solution.py:65
  446.9 45.3 %collective-permute-start.10 = (bf16[1024,1024]{1,0:T(8,128)(2,1)}, bf16[1024,1024]{1,0:T(8,128)(2,1)}, u32[]{:S(2)}, u32[]{:S(2)}) collective-permute-start(bf16[1024,1024]{1,0:T(8,128)(2,1)} %convolution_convert_fusion.8), channel_id=1, source_target_pairs={{0,8},{8,0},{16,24},{24,16},{1,9},{9,1},{17,25},{25,17},{2,10},{10... | collective-permute-start | bytes 6291464 | tf_op jit(solution)/shard_map/ppermute | solution.py:65
  512.5 68.8 %all-to-all-start.1 = ((bf16[8,64,1024]{2,1,0:T(8,128)(2,1)}), bf16[8,64,1024]{2,1,0:T(8,128)(2,1)S(1)}, u32[]{:S(2)}, u32[]{:S(2)}) async-start(bf16[8,64,1024]{2,1,0:T(8,128)(2,1)} %bitcast.330), calls=%async_computation.1 | async-start | bytes 2097152 | tf_op jit(solution)/shard_map/all_to_all | solution.py:643
  518.1 47.4 %collective-permute-start.11 = (bf16[1024,1024]{1,0:T(8,128)(2,1)}, bf16[1024,1024]{1,0:T(8,128)(2,1)}, u32[]{:S(2)}, u32[]{:S(2)}) collective-permute-start(bf16[1024,1024]{1,0:T(8,128)(2,1)} %add_convert_fusion.1), channel_id=1, source_target_pairs={{0,16},{16,0},{8,24},{24,8},{1,17},{17,1},{9,25},{25,9},{2,18},{18... | collective-permute-start | bytes 6291464 | tf_op jit(solution)/shard_map/ppermute | solution.py:65
  565.5 22.5 %collective-permute-start.12 = (bf16[2,2,256,1024]{3,2,1,0:T(8,128)(2,1)}, bf16[2,2,256,1024]{3,2,1,0:T(8,128)(2,1)}, u32[]{:S(2)}, u32[]{:S(2)}) collective-permute-start(bf16[2,2,256,1024]{3,2,1,0:T(8,128)(2,1)} %get-tuple-element.88), channel_id=1, source_target_pairs={{8,0},{24,16},{16,24},{9,1},{25,17},{17,25},{10,2},{26,18},{18,26}... | collective-permute-start | bytes 6291464 | tf_op jit(solution)/shard_map/ppermute | solution.py:65
  567.3 6.5 collective-permute-start.17
  573.8 4.3 collective-permute-start.18
  573.9 26.1 %collective-permute-start.14 = (bf16[1024,1024]{1,0:T(8,128)(2,1)}, bf16[1024,1024]{1,0:T(8,128)(2,1)}, u32[]{:S(2)}, u32[]{:S(2)}) collective-permute-start(bf16[1024,1024]{1,0:T(8,128)(2,1)} %convolution_convert_fusion.7), channel_id=1, source_target_pairs={{0,8},{8,0},{16,24},{24,16},{1,9},{9,1},{17,25},{25,17},{2,10},{10... | collective-permute-start | bytes 6291464 | tf_op jit(solution)/shard_map/ppermute | solution.py:65
  578.1 26.5 %collective-permute-start.16 = (bf16[1024,1024]{1,0:T(8,128)(2,1)}, bf16[1024,1024]{1,0:T(8,128)(2,1)}, u32[]{:S(2)}, u32[]{:S(2)}) collective-permute-start(bf16[1024,1024]{1,0:T(8,128)(2,1)} %convolution_convert_fusion.6), channel_id=1, source_target_pairs={{0,8},{8,0},{16,24},{24,16},{1,9},{9,1},{17,25},{25,17},{2,10},{10... | collective-permute-start | bytes 6291464 | tf_op jit(solution)/shard_map/ppermute | solution.py:65
  584.1 24.3 %collective-permute-start.15 = (bf16[1024,1024]{1,0:T(8,128)(2,1)}, bf16[1024,1024]{1,0:T(8,128)(2,1)}, u32[]{:S(2)}, u32[]{:S(2)}) collective-permute-start(bf16[1024,1024]{1,0:T(8,128)(2,1)} %convolution_convert_fusion.5), channel_id=1, source_target_pairs={{0,8},{8,0},{16,24},{24,16},{1,9},{9,1},{17,25},{25,17},{2,10},{10... | collective-permute-start | bytes 6291464 | tf_op jit(solution)/shard_map/ppermute | solution.py:65
  587.9 182.0 %collective-permute-start.19 = (bf16[1024,1024]{1,0:T(8,128)(2,1)}, bf16[1024,1024]{1,0:T(8,128)(2,1)}, u32[]{:S(2)}, u32[]{:S(2)}) collective-permute-start(bf16[1024,1024]{1,0:T(8,128)(2,1)} %convolution_convert_fusion.4), channel_id=1, source_target_pairs={{0,8},{8,0},{16,24},{24,16},{1,9},{9,1},{17,25},{25,17},{2,10},{10... | collective-permute-start | bytes 6291464 | tf_op jit(solution)/shard_map/ppermute | solution.py:65
  592.5 71.9 %collective-permute-start.13 = (bf16[2,2,256,1024]{3,2,1,0:T(8,128)(2,1)S(1)}, bf16[2,2,256,1024]{3,2,1,0:T(8,128)(2,1)S(1)}, u32[]{:S(2)}, u32[]{:S(2)}) collective-permute-start(bf16[2,2,256,1024]{3,2,1,0:T(8,128)(2,1)S(1)} %fusion.5), channel_id=1, source_target_pairs={{16,0},{24,8},{17,1},{25,9},{18,2},{26,10},{19,3},{27,11},{20,4},{... | collective-permute-start | bytes 6291464 | tf_op jit(solution)/shard_map/ppermute | solution.py:65
  677.5 92.4 %collective-permute-start.20 = (bf16[1024,1024]{1,0:T(8,128)(2,1)}, bf16[1024,1024]{1,0:T(8,128)(2,1)}, u32[]{:S(2)}, u32[]{:S(2)}) collective-permute-start(bf16[1024,1024]{1,0:T(8,128)(2,1)} %add_convert_fusion), channel_id=1, source_target_pairs={{0,16},{16,0},{8,24},{24,8},{1,17},{17,1},{9,25},{25,9},{2,18},{18... | collective-permute-start | bytes 6291464 | tf_op jit(solution)/shard_map/ppermute | solution.py:65
  684.2 85.1 %all-to-all-start.4 = ((f32[32,2,32]{2,1,0:T(2,128)}), f32[32,2,32]{2,1,0:T(2,128)S(1)}, u32[]{:S(2)}, u32[]{:S(2)}) async-start(f32[32,2,32]{2,1,0:T(2,128)} %maximum_bitcast_fusion.1), calls=%async_computation.4 | async-start | bytes 65536 | tf_op jit(solution)/shard_map/all_to_all | solution.py:755
  692.6 77.2 %copy-start.25 = (bf16[1024,1024]{1,0:T(8,128)(2,1)S(1)}, bf16[1024,1024]{1,0:T(8,128)(2,1)}, u32[]{:S(2)}) copy-start(bf16[1024,1024]{1,0:T(8,128)(2,1)} %convolution_convert_fusion.2) | copy-start | bytes 6291460
  (132 other events, 646.6 us)
Sparse Core Ops, SparseCore 0:
  78.4 138.6 all-gather.1
  382.1 82.7 reduce-scatter.4
  508.8 240.0 reduce-scatter.2
